TPU v7x, 256 devices: a whole 4x4x8 slice. The times are simulated.
256 devices in a mesh: dp: 4 (over x_hi, core), vocab: 64 (over y, z, x_lo).
Axes of the slice: x: 4 (x_hi: 2, x_lo: 2; x = x_hi * 2 + x_lo), y: 4, z: 8, core: 2. Of those that a mesh axis runs over, the one named last changes fastest.
Arguments:
- hidden: bfloat16 [1024, 2048], P('dp', 'vocab'), may hold values from -30 to 30
- table: bfloat16 [128000, 2048], P('vocab'), may hold values from -20 to 20
- targets: int32 [1024], P('dp'), may hold values from 0 to 127999
- input_ids: int32 [16384], P(('dp', 'vocab')), may hold values from 0 to 127999, as said below
- cotangent: bfloat16 [16384, 2048], P(('dp', 'vocab')), may hold values from -0.4375 to 0.4375
Outputs:
- token_loss: float32 [1024], P('dp')
- hidden_grad: bfloat16 [1024, 2048], P('dp', 'vocab')
- table_grad: bfloat16 [128000, 2048], P('vocab', 'dp')
Inputs may be any that keep to these rules, and one draw needn't show every extreme that they name: `input_ids`: within the 64 rows of one device, at most 2 ids fall in any one block of 2000 consecutive ids (the rows of one index of vocab); in every draw some block receives exactly 2 ids from every device.
All inputs are finite; a program needn't handle non-finite values.
Results may differ from a plain program's by a relative error of at most 0.0034.
Values may be sent and summed in bfloat16 or wider, within the bound.
No kernel may reach another device: no remote copies, remote signals or barrier semaphores. Data moves between devices by JAX's collectives and lax.ppermute only.
A program may use at most 128 MiB of HBM per device.

v0:
```python
import jax
import jax.numpy as jnp
from jax import lax
from jax.sharding import PartitionSpec as P


def copy_for_each(value, axis):
    copies = jnp.broadcast_to(value, (lax.axis_size(axis), *value.shape))
    return lax.all_to_all(copies, axis, split_axis=0, concat_axis=0, tiled=True)


def joined_along(pieces, dim):
    pieces = jnp.moveaxis(pieces, 0, dim)
    shape = pieces.shape
    return pieces.reshape(*shape[:dim], shape[dim] * shape[dim + 1], *shape[dim + 2 :])


def collect(value, axis, dim):
    pieces = copy_for_each(value, axis)
    return joined_along(pieces, dim)


def gathered_once(value, axis):
    leaves = jax.tree.leaves(value)
    turns = sorted(range(len(leaves)), key=lambda k: -leaves[k].size)
    width = (1, *leaves[turns[0]].shape)[-1]
    lines = [
        jnp.pad(leaves[k].reshape(-1), (0, -leaves[k].size % width)).reshape(-1, width)
        for k in turns
    ]
    both, at, found = (copy_for_each(jnp.concatenate(lines), axis), 0, {})
    for k, line in zip(turns, lines):
        section = both[:, at : at + len(line)].reshape(len(both), -1)
        found[k] = section[:, : leaves[k].size].reshape(-1, *leaves[k].shape)
        at += len(line)
    numbers = iter(range(len(leaves)))
    return jax.tree.map(lambda _: found[next(numbers)], value)


def combined_pairwise(pieces, combine):
    while len(jax.tree.leaves(pieces)[0]) > 1:
        pieces = jax.vmap(combine)(
            *(jax.tree.map(lambda part: part[side::2], pieces) for side in (0, 1))
        )
    return jax.tree.map(lambda part: part[0], pieces)


def merged(value, axis, combine):
    pieces = gathered_once(value, axis)
    return combined_pairwise(pieces, combine)


def cut_along(value, dim, peers):
    shape = value.shape
    pieces = value.reshape(*shape[:dim], peers, shape[dim] // peers, *shape[dim + 1 :])
    return jnp.moveaxis(pieces, dim, 0)


def sent_and_summed(value, axis, dim):
    peers = lax.axis_size(axis)
    pieces = lax.all_to_all(cut_along(value, dim, peers), axis, 0, 0, tiled=True)
    return jnp.sum(pieces, axis=0)


def combine_stats(former, latter):
    highest = jnp.maximum(former[0], latter[0])
    summed = former[1] * jnp.exp(former[0] - highest) + latter[1] * jnp.exp(latter[0] - highest)
    return (highest, summed, former[2] + latter[2])


def body(hidden, table, targets, input_ids, cotangent):
    vocab_rows = table.shape[0]
    model_width = table.shape[1]
    data_count = lax.axis_size("dp")
    vocab_count = lax.axis_size("vocab")
    first_row = lax.axis_index("vocab") * vocab_rows
    hidden_full = collect(hidden, "vocab", 1)
    logits = lax.dot_general(
        hidden_full, table, (((1,), (1,)), ((), ())), preferred_element_type=jnp.float32
    )
    columns = lax.broadcasted_iota(jnp.int32, logits.shape, 1)
    is_target = columns == (targets - first_row)[:, None]
    picked = jnp.sum(jnp.where(is_target, logits, 0.0), axis=1)
    local_max = jnp.max(logits, axis=1)
    local_sum = jnp.sum(jnp.exp(logits - local_max[:, None]), axis=1)
    row_max, row_sum, target_logit = merged((local_max, local_sum, picked), "vocab", combine_stats)
    shifted = jnp.exp(logits - row_max[:, None])
    token_loss = row_max + jnp.log(row_sum) - target_logit
    residual = (shifted / row_sum[:, None] - jnp.where(is_target, 1.0, 0.0)).astype(jnp.bfloat16)
    hidden_part = jnp.dot(residual, table, preferred_element_type=jnp.float32)
    hidden_grad = sent_and_summed(hidden_part, "vocab", 1).astype(jnp.bfloat16)
    row_count = input_ids.shape[0]
    capacity = max(2, 2 * row_count // vocab_count)
    slot_total = vocab_count * capacity
    owners = input_ids // vocab_rows
    offsets = input_ids - owners * vocab_rows
    later_rows = lax.broadcasted_iota(jnp.int32, (row_count, row_count), 0)
    earlier_rows = lax.broadcasted_iota(jnp.int32, (row_count, row_count), 1)
    earlier = (owners[:, None] == owners[None, :]) & (earlier_rows < later_rows)
    position = jnp.sum(earlier.astype(jnp.int32), axis=1)
    slot_index = owners * capacity + position
    selector = lax.broadcasted_iota(jnp.int32, (slot_total, row_count), 0) == slot_index[None, :]
    send_rows = jnp.dot(
        selector.astype(jnp.bfloat16), cotangent, preferred_element_type=jnp.float32
    ).astype(jnp.bfloat16)
    send_rows = send_rows.reshape(vocab_count, capacity, model_width)
    send_offsets = jnp.sum(jnp.where(selector, offsets[None, :] + 1, 0), axis=1) - 1
    offset_copies = jnp.broadcast_to(
        send_offsets.reshape(vocab_count, capacity, 1), (vocab_count, capacity, data_count)
    )
    got_rows, got_offsets = (
        lax.all_to_all(
            lax.all_to_all(send_rows, "dp", split_axis=2, concat_axis=1, tiled=True),
            "vocab",
            split_axis=0,
            concat_axis=0,
            tiled=True,
        ),
        lax.all_to_all(
            lax.all_to_all(offset_copies, "dp", split_axis=2, concat_axis=1, tiled=True),
            "vocab",
            split_axis=0,
            concat_axis=0,
            tiled=True,
        ),
    )
    block_width = model_width // data_count
    flat_rows = got_rows.reshape(-1, block_width)
    flat_offsets = got_offsets.reshape(-1)
    matches = (
        lax.broadcasted_iota(jnp.int32, (vocab_rows, flat_offsets.shape[0]), 0)
        == flat_offsets[None, :]
    )
    start_sum = jnp.dot(matches.astype(jnp.bfloat16), flat_rows, preferred_element_type=jnp.float32)
    hidden_block = lax.all_to_all(hidden_full, "dp", split_axis=1, concat_axis=0, tiled=True)
    table_sum = start_sum + lax.dot_general(
        lax.all_gather(residual, "dp", axis=0, tiled=True),
        hidden_block,
        (((0,), (0,)), ((), ())),
        preferred_element_type=jnp.float32,
    )
    return (token_loss, hidden_grad, table_sum.astype(jnp.bfloat16))


def solution(mesh):
    placed = (
        P("dp", "vocab"),
        P("vocab", None),
        P("dp"),
        P(("dp", "vocab")),
        P(("dp", "vocab"), None),
    )
    return jax.shard_map(
        body,
        mesh=mesh,
        in_specs=placed,
        out_specs=(P("dp"), P("dp", "vocab"), P("vocab", "dp")),
        check_vma=False,
    )
```

profile of v0, /device:TPU:8, one launch (start us, length us, event | category | flops | bytes accessed | tf_op | source)
XLA Modules:
  0.0 226.3 jit_solution(1768518006500221207)
XLA Ops:
  7.2 1.9 broadcast_in_dim.39
  9.1 13.2 %all-to-all-start = ((bf16[64,256,32]{1,2,0:T(8,128)(2,1)}), bf16[64,256,32]{1,2,0:T(8,128)(2,1)}, u32[]{:S(2)}, u32[]{:S(2)}) async-start(bf16[64,256,32]{1,2,0:T(8,128)(2,1)} %broadcast_in_dim.39), calls=%async_computation | async-start | bytes 2097152 | tf_op jit(solution)/shard_map/all_to_all | solution.py:9
  22.8 27.4 %all-to-all-done = bf16[64,256,32]{1,2,0:T(8,128)(2,1)} async-done(((bf16[64,256,32]{1,2,0:T(8,128)(2,1)}), bf16[64,256,32]{1,2,0:T(8,128)(2,1)}, u32[]{:S(2)}, u32[]{:S(2)}) %all-to-all-start) | async-done | bytes 1048608 | tf_op jit(solution)/shard_map/all_to_all | solution.py:9
  50.3 5.9 %fusion.7 = (f32[256]{0:T(256)S(1)}, f32[256,2000]{0,1:T(8,128)S(1)}) fusion(bf16[2000,2048]{1,0:T(8,128)(2,1)} %param.6, bf16[256,2048]{0,1:T(8,128)(2,1)} %bitcast.1), kind=kOutput, calls=%fused_computation.37 | convolution fusion | flops 2097663744 | bytes 11289600 | tf_op jit(solution)/shard_map/dot_general | solution.py:78
  56.7 0.7 broadcast_in_dim.41
  57.4 7.0 %all-to-all-start.1 = ((f32[64,3,256]{2,1,0:T(4,128)}), f32[64,3,256]{2,1,0:T(4,128)}, u32[]{:S(2)}, u32[]{:S(2)}) async-start(f32[64,3,256]{2,1,0:T(4,128)} %broadcast_in_dim.41), calls=%async_computation.1 | async-start | bytes 524288 | tf_op jit(solution)/shard_map/all_to_all | solution.py:9
  65.6 1.1 reshape.66
  66.7 2.6 %copy.36 = bf16[64,2,2048]{0,1,2:T(2,128)(2,1)S(1)} copy(bf16[64,2,2048]{2,1,0:T(2,128)(2,1)} %reshape.66) | data formatting | bytes 1048576 | tf_op jit(solution)/shard_map/reshape | solution.py:106
  69.3 1.5 reshape.79
  70.9 4.8 %all-to-all-done.1 = f32[64,3,256]{2,1,0:T(4,128)} async-done(((f32[64,3,256]{2,1,0:T(4,128)}), f32[64,3,256]{2,1,0:T(4,128)}, u32[]{:S(2)}, u32[]{:S(2)}) %all-to-all-start.1) | async-done | bytes 196640 | tf_op jit(solution)/shard_map/all_to_all | solution.py:9
  75.6 4.0 %all-to-all-start.3 = ((s32[4,1,128]{2,1,0:T(1,128)}), s32[4,1,128]{2,1,0:T(1,128)S(1)}, u32[]{:S(2)}, u32[]{:S(2)}) async-start(s32[4,1,128]{2,1,0:T(1,128)} %reshape.77), calls=%async_computation.3 | async-start | bytes 4096 | tf_op jit(solution)/shard_map/all_to_all | solution.py:120
  79.6 1.4 fusion.6
  81.6 3.3 %all-to-all-done.3 = s32[4,1,128]{2,1,0:T(1,128)S(1)} async-done(((s32[4,1,128]{2,1,0:T(1,128)}), s32[4,1,128]{2,1,0:T(1,128)S(1)}, u32[]{:S(2)}, u32[]{:S(2)}) %all-to-all-start.3) | async-done | bytes 2080 | tf_op jit(solution)/shard_map/all_to_all | solution.py:120
  84.8 3.5 %all-to-all-start.5 = ((bf16[4,2,32768]{2,1,0:T(2,128)(2,1)}), bf16[4,2,32768]{2,1,0:T(2,128)(2,1)S(1)}, u32[]{:S(2)}, u32[]{:S(2)}) async-start(bf16[4,2,32768]{2,1,0:T(2,128)(2,1)} %reshape.79), calls=%async_computation.5 | async-start | bytes 1048576 | tf_op jit(solution)/shard_map/all_to_all | solution.py:113
  88.4 1.5 subtract_convert_fusion
  91.2 0.7 copy.35
  91.9 6.7 %all-to-all-done.5 = bf16[4,2,32768]{2,1,0:T(2,128)(2,1)S(1)} async-done(((bf16[4,2,32768]{2,1,0:T(2,128)(2,1)}), bf16[4,2,32768]{2,1,0:T(2,128)(2,1)S(1)}, u32[]{:S(2)}, u32[]{:S(2)}) %all-to-all-start.5) | async-done | bytes 524320 | tf_op jit(solution)/shard_map/all_to_all | solution.py:113
  98.6 6.5 %all-to-all-start.4 = ((s32[64,8,1]{1,2,0:T(1,128)}), s32[64,8,1]{1,2,0:T(1,128)S(1)}, u32[]{:S(2)}, u32[]{:S(2)}) async-start(s32[64,8,1]{1,2,0:T(1,128)} %copy.35), calls=%async_computation.4 | async-start | bytes 65536 | tf_op jit(solution)/shard_map/all_to_all | solution.py:119
  105.1 0.7 reshape.80
  105.8 0.9 copy.42
  107.1 7.4 %all-to-all-done.4 = s32[64,8,1]{1,2,0:T(1,128)S(1)} async-done(((s32[64,8,1]{1,2,0:T(1,128)}), s32[64,8,1]{1,2,0:T(1,128)S(1)}, u32[]{:S(2)}, u32[]{:S(2)}) %all-to-all-start.4) | async-done | bytes 2080 | tf_op jit(solution)/shard_map/all_to_all | solution.py:119
  114.5 20.8 %all_to_all.80 = bf16[64,8,512]{2,1,0:T(8,128)(2,1)} all-to-all(bf16[64,8,512]{2,1,0:T(8,128)(2,1)S(1)} %copy.39), channel_id=1, replica_groups=mesh['dp'=4,'vocab'=64] {'vocab'}, dimensions={0} | all-to-all | bytes 1048576 | tf_op jit(solution)/shard_map/all_to_all | solution.py:112
  135.4 3.7 %all-to-all-start.7 = ((bf16[256,4,512]{0,2,1:T(8,128)(2,1)}), bf16[256,4,512]{0,2,1:T(8,128)(2,1)S(1)}, u32[]{:S(2)}, u32[]{:S(2)}) async-start(bf16[256,4,512]{0,2,1:T(8,128)(2,1)} %bitcast.18), calls=%async_computation.7 | async-start | bytes 2097152 | tf_op jit(solution)/shard_map/all_to_all | solution.py:135
  139.1 8.1 %fusion.8 = f32[256,2048]{0,1:T(8,128)} fusion(bf16[256,2000]{0,1:T(8,128)(2,1)S(1)} %copy-done.1, bf16[2000,2048]{1,0:T(8,128)(2,1)} %param.6), kind=kOutput, calls=%fused_computation.39 | convolution fusion | flops 2097152000 | bytes 11313152 | tf_op jit(solution)/shard_map/dot_general | solution.py:90
  147.2 7.6 %all-to-all-done.7 = bf16[256,4,512]{0,2,1:T(8,128)(2,1)S(1)} async-done(((bf16[256,4,512]{0,2,1:T(8,128)(2,1)}), bf16[256,4,512]{0,2,1:T(8,128)(2,1)S(1)}, u32[]{:S(2)}, u32[]{:S(2)}) %all-to-all-start.7) | async-done | bytes 1048608 | tf_op jit(solution)/shard_map/all_to_all | solution.py:135
  154.8 6.8 %all-to-all-start.2 = ((f32[64,256,32]{1,2,0:T(8,128)}), f32[64,256,32]{1,2,0:T(8,128)S(1)}, u32[]{:S(2)}, u32[]{:S(2)}) async-start(f32[64,256,32]{1,2,0:T(8,128)} %bitcast.51), calls=%async_computation.2 | async-start | bytes 4194304 | tf_op jit(solution)/shard_map/all_to_all | solution.py:61
  162.1 0.7 reduce.3
  162.9 4.2 %fusion = f32[2000,512]{1,0:T(8,128)} fusion(s32[512]{0:T(512)S(1)} %eq.46, bf16[64,8,512]{2,1,0:T(8,128)(2,1)} %all_to_all.80), kind=kOutput, calls=%fused_computation.2 | convolution fusion | flops 1049600000 | bytes 4622336 | tf_op jit(solution)/shard_map/dot_general | solution.py:134
  168.0 1.3 copy.40
  169.3 42.4 %all-to-all-done.2 = f32[64,256,32]{1,2,0:T(8,128)S(1)} async-done(((f32[64,256,32]{1,2,0:T(8,128)}), f32[64,256,32]{1,2,0:T(8,128)S(1)}, u32[]{:S(2)}, u32[]{:S(2)}) %all-to-all-start.2) | async-done | bytes 2097184 | tf_op jit(solution)/shard_map/all_to_all | solution.py:61
  211.7 0.7 reduce_sum.47
  212.5 7.0 %add_convert_fusion = bf16[2000,512]{1,0:T(8,128)(2,1)} fusion(f32[2000,512]{1,0:T(8,128)} %fusion, bf16[1024,2000]{0,1:T(8,128)(2,1)} %all-gather.2.cloned.1.call-done, bf16[1024,512]{1,0:T(8,128)(2,1)S(1)} %bitcast.53), kind=kOutput, calls=%fused_computation | convolution fusion | flops 2099200000 | bytes 11288576 | tf_op jit(solution)/shard_map/dot_general | solution.py:136
  (78 shorter events, 5.8 us)
Async XLA Ops:
  7.2 58.0 %copy-start = (bf16[64,2048]{1,0:T(8,128)(2,1)S(1)}, bf16[64,2048]{1,0:T(8,128)(2,1)}, u32[]{:S(2)}) copy-start(bf16[64,2048]{1,0:T(8,128)(2,1)} %param.9) | copy-start | bytes 786436
  7.2 15.1 %copy-start.4 = (s32[64]{0:T(128)S(1)}, s32[64]{0:T(128)}, u32[]{:S(2)}) copy-start(s32[64]{0:T(128)} %param.8) | copy-start | bytes 772
  7.2 15.6 %copy-start.3 = (s32[256]{0:T(256)S(1)}, s32[256]{0:T(256)}, u32[]{:S(2)}) copy-start(s32[256]{0:T(256)} %param.7) | copy-start | bytes 3076
  9.1 41.2 %all-to-all-start = ((bf16[64,256,32]{1,2,0:T(8,128)(2,1)}), bf16[64,256,32]{1,2,0:T(8,128)(2,1)}, u32[]{:S(2)}, u32[]{:S(2)}) async-start(bf16[64,256,32]{1,2,0:T(8,128)(2,1)} %broadcast_in_dim.39), calls=%async_computation | async-start | bytes 2097152 | tf_op jit(solution)/shard_map/all_to_all | solution.py:9
  57.4 18.2 %all-to-all-start.1 = ((f32[64,3,256]{2,1,0:T(4,128)}), f32[64,3,256]{2,1,0:T(4,128)}, u32[]{:S(2)}, u32[]{:S(2)}) async-start(f32[64,3,256]{2,1,0:T(4,128)} %broadcast_in_dim.41), calls=%async_computation.1 | async-start | bytes 524288 | tf_op jit(solution)/shard_map/all_to_all | solution.py:9
  75.6 9.2 %all-to-all-start.3 = ((s32[4,1,128]{2,1,0:T(1,128)}), s32[4,1,128]{2,1,0:T(1,128)S(1)}, u32[]{:S(2)}, u32[]{:S(2)}) async-start(s32[4,1,128]{2,1,0:T(1,128)} %reshape.77), calls=%async_computation.3 | async-start | bytes 4096 | tf_op jit(solution)/shard_map/all_to_all | solution.py:120
  84.8 13.8 %all-to-all-start.5 = ((bf16[4,2,32768]{2,1,0:T(2,128)(2,1)}), bf16[4,2,32768]{2,1,0:T(2,128)(2,1)S(1)}, u32[]{:S(2)}, u32[]{:S(2)}) async-start(bf16[4,2,32768]{2,1,0:T(2,128)(2,1)} %reshape.79), calls=%async_computation.5 | async-start | bytes 1048576 | tf_op jit(solution)/shard_map/all_to_all | solution.py:113
  88.3 124.2 %all-gather.2.cloned.1.call-start = ((), (), s32[]{:S(2)}) async-start(), calls=%async_computation.8 | async-start | bytes 5120000 | tf_op jit(solution)/shard_map/all_gather | solution.py:137
  98.6 16.0 %all-to-all-start.4 = ((s32[64,8,1]{1,2,0:T(1,128)}), s32[64,8,1]{1,2,0:T(1,128)S(1)}, u32[]{:S(2)}, u32[]{:S(2)}) async-start(s32[64,8,1]{1,2,0:T(1,128)} %copy.35), calls=%async_computation.4 | async-start | bytes 65536 | tf_op jit(solution)/shard_map/all_to_all | solution.py:119
  106.8 32.3 %copy-start.1 = (bf16[256,2000]{0,1:T(8,128)(2,1)S(1)}, bf16[256,2000]{0,1:T(8,128)(2,1)}, u32[]{:S(2)}) copy-start(bf16[256,2000]{0,1:T(8,128)(2,1)} %subtract_convert_fusion) | copy-start | bytes 3072004
  135.4 19.4 %all-to-all-start.7 = ((bf16[256,4,512]{0,2,1:T(8,128)(2,1)}), bf16[256,4,512]{0,2,1:T(8,128)(2,1)S(1)}, u32[]{:S(2)}, u32[]{:S(2)}) async-start(bf16[256,4,512]{0,2,1:T(8,128)(2,1)} %bitcast.18), calls=%async_computation.7 | async-start | bytes 2097152 | tf_op jit(solution)/shard_map/all_to_all | solution.py:135
  154.8 56.9 %all-to-all-start.2 = ((f32[64,256,32]{1,2,0:T(8,128)}), f32[64,256,32]{1,2,0:T(8,128)S(1)}, u32[]{:S(2)}, u32[]{:S(2)}) async-start(f32[64,256,32]{1,2,0:T(8,128)} %bitcast.51), calls=%async_computation.2 | async-start | bytes 4194304 | tf_op jit(solution)/shard_map/all_to_all | solution.py:61
  169.3 43.2 %copy-start.2 = (bf16[4,256,512]{2,1,0:T(8,128)(2,1)S(1)}, bf16[4,256,512]{2,1,0:T(8,128)(2,1)}, u32[]{:S(2)}) copy-start(bf16[4,256,512]{2,1,0:T(8,128)(2,1)} %copy.40) | copy-start | bytes 3145732
Sparse Core Ops, SparseCore 0:
  90.9 44.4 all-gather.1
where the time goes:
time: 227 us; the launch traced here: 226 us
  waiting for transfers between devices  99.7 us (44%)
  starting transfers between devices  44.7 us (20%)
  matrix products  25.6 us (11%)
  blocking collectives  20.8 us (9%)
  local copies, waits for them, and re-layouts  15.9 us (7%)
  between operations  14.3 us (6%)
  other arithmetic  5.25 us (2%)
    all_to_all x1, waiting for transfers between devices, sent_and_summed(): lax.all_to_all(cut_along(value, dim, peers), axis, 0, 0, tiled=True)  42.4 us
    all_to_all x2, waiting for transfers between devices, copy_for_each(): return lax.all_to_all(copies, axis, split_axis=0, concat_axis=0, tiled=True)  32.2 us
    all_to_all x1, blocking collectives, body(): lax.all_to_all(lax.all_to_all(send_rows, 'dp', split_axis=2, concat_axis=...  20.8 us
    all_to_all x2, starting transfers between devices, copy_for_each(): return lax.all_to_all(copies, axis, split_axis=0, concat_axis=0, tiled=True)  20.3 us
    dot_general x1, matrix products, body(): hidden_part = jnp.dot(residual, table, preferred_element_type=jnp.float32)  8.1 us
    all_to_all x1, waiting for transfers between devices, body(): lax.all_to_all(hidden_full, 'dp', split_axis=1, concat_axis=0, tiled=True)  7.61 us
    all_to_all x1, waiting for transfers between devices, body(): lax.all_to_all(lax.all_to_all(offset_copies, 'dp', split_axis=2, concat_a...  7.45 us
    dot_general x1, matrix products, body(): lax.dot_general(lax.all_gather(residual, 'dp', axis=0, tiled=True), hidde...  7 us
  transfers between devices with their start and end apart: 8, of which 7 were waited for; matrix products, arithmetic and copies ran while one was open for 14% of the time, Pallas kernels for 0%

commit v1 on v0

v1 whole, which is shorter than its diff:
```python
import jax
import jax.numpy as jnp
from jax import lax
from jax.sharding import Mesh, PartitionSpec as P

BF16 = jnp.bfloat16
F32 = jnp.float32
ALL = ("xh", "c", "y", "z", "xl")
DP = ("xh", "c")
VOCAB = ("y", "z", "xl")
PLANE = ("y", "xl")


def exchange(pieces, axes):
    return lax.all_to_all(pieces, axes, 0, 0, tiled=True)


def to_each(value, count):
    return jnp.broadcast_to(value, (count, *value.shape))


def swap(value, axis):
    return lax.ppermute(value, axis, [(0, 1), (1, 0)])


def by_plane(rows, ny, nz, nx):
    tail = rows.shape[1:]
    rows = rows.reshape(ny, nz, nx, -1, *tail)
    return rows.transpose(0, 2, 1, 3, *range(4, 4 + len(tail)))


def body(hidden, table, targets, input_ids, cotangent):
    vocab_rows, width = table.shape
    ny, nz, nx = (lax.axis_size(a) for a in VOCAB)
    plane = ny * nx
    vocab_count = plane * nz
    data_count = lax.axis_size(DP)
    block = width // data_count
    first_row = lax.axis_index(VOCAB) * vocab_rows
    xh, c = lax.axis_index("xh"), lax.axis_index("c")

    owners = input_ids // vocab_rows
    offsets = input_ids - owners * vocab_rows
    count = input_ids.shape[0]
    later = lax.broadcasted_iota(jnp.int32, (count, count), 0)
    early = lax.broadcasted_iota(jnp.int32, (count, count), 1)
    before = (owners[:, None] == owners[None, :]) & (early < later)
    slot = owners * 2 + jnp.sum(before.astype(jnp.int32), axis=1)
    chosen = lax.broadcasted_iota(jnp.int32, (2 * vocab_count, count), 0) == slot[None, :]
    sent = jnp.dot(chosen.astype(BF16), cotangent, preferred_element_type=F32).astype(BF16)
    spots = jnp.sum(jnp.where(chosen, offsets[None, :] + 1, 0), axis=1)
    lane = lax.broadcasted_iota(jnp.int32, (2 * vocab_count, 128), 1)
    code = jnp.where(lane == 0, (spots // 64)[:, None], jnp.where(lane == 1, (spots % 64)[:, None], 0))
    code = code.astype(BF16)
    sent = jnp.stack(
        [jnp.concatenate([sent[:, d * block : (d + 1) * block], code], axis=1) for d in range(data_count)]
    )
    sent = sent.reshape(data_count * vocab_count, 2, block + 128)

    mine = hidden.T
    stage = exchange(to_each(mine, nz), "z").reshape(-1, mine.shape[1])
    stage = exchange(to_each(stage, plane), PLANE)
    tokens = mine.shape[1]
    hid = stage.reshape(ny, nx, nz, -1, tokens).transpose(0, 2, 1, 3, 4).reshape(width, tokens)
    logits = jnp.dot(table, hid, preferred_element_type=F32)
    rows = lax.broadcasted_iota(jnp.int32, logits.shape, 0)
    hit = rows == (targets - first_row)[None, :]
    picked = jnp.sum(jnp.where(hit, logits, 0.0), axis=0)
    top = jnp.max(logits, axis=0)
    total = jnp.sum(jnp.exp(logits - top[None]), axis=0)
    stats = exchange(to_each(jnp.stack([top, total, picked]), vocab_count), VOCAB)
    row_max = jnp.max(stats[:, 0], axis=0)
    row_sum = jnp.sum(stats[:, 1] * jnp.exp(stats[:, 0] - row_max[None]), axis=0)
    token_loss = row_max + jnp.log(row_sum) - jnp.sum(stats[:, 2], axis=0)
    residual = (jnp.exp(logits - row_max[None]) / row_sum[None] - jnp.where(hit, 1.0, 0.0)).astype(BF16)

    part = lax.dot_general(table, residual, (((0,), (0,)), ((), ())), preferred_element_type=F32)
    part = by_plane(part.astype(BF16), ny, nz, nx).reshape(plane, -1, tokens)
    part = exchange(part, PLANE)
    part = jnp.sum(part.astype(F32), axis=0).reshape(nz, -1, tokens)
    part = jnp.sum(exchange(part, "z"), axis=0)
    hidden_grad = part.astype(BF16).T

    res_far = swap(residual, "xh")
    res_sib = swap(residual, "c")
    res_far_sib = swap(res_far, "c")

    def cut(value, start, size):
        return lax.dynamic_slice_in_dim(value, start, size, 0)

    hb_own = cut(hid, (2 * xh + c) * block, block)
    hb_sib = swap(cut(hid, (2 * xh + 1 - c) * block, block), "c")
    far = swap(cut(hid, 2 * (1 - xh) * block, 2 * block), "xh")
    hb_far = cut(far, c * block, block)
    hb_far_sib = swap(cut(far, (1 - c) * block, block), "c")
    res_all = jnp.concatenate([residual, res_sib, res_far, res_far_sib], axis=1)
    hid_all = jnp.concatenate([hb_own, hb_sib, hb_far, hb_far_sib], axis=1)

    got = exchange(sent, ALL).reshape(-1, block + 128)
    code = got[:, block:].astype(F32)
    place = (code[:, 0] * 64 + code[:, 1]).astype(jnp.int32) - 1
    match = lax.broadcasted_iota(jnp.int32, (vocab_rows, place.shape[0]), 0) == place[None, :]
    start = jnp.dot(match.astype(BF16), got[:, :block], preferred_element_type=F32)
    table_grad = start + lax.dot_general(
        res_all, hid_all, (((1,), (1,)), ((), ())), preferred_element_type=F32
    )
    return token_loss, hidden_grad, table_grad.astype(BF16)


def solution(mesh):
    fine = Mesh(mesh.devices.reshape(2, 2, 4, 8, 2), ALL)
    placed = (P(DP, VOCAB), P(VOCAB, None), P(DP), P(ALL), P(ALL, None))
    return jax.shard_map(
        body,
        mesh=fine,
        in_specs=placed,
        out_specs=(P(DP), P(DP, VOCAB), P(VOCAB, DP)),
        check_vma=False,
    )
```

time: 227 us -> 158 us (0.70)
  waiting for transfers between devices: 99.7 us -> 69.4 us
  blocking collectives: 20.8 us -> 0 us
  between operations: 14.3 us -> 0.9 us
  matrix products: 25.6 us -> 22.2 us
  local copies, waits for them, and re-layouts: 15.9 us -> 13.6 us
    all_to_all x7 -> x6, waiting for transfers between devices: 99.7 us -> 46.1 us  [exchange(): return lax.all_to_all(pieces, axes, 0, 0, tiled=True)]
    ppermute x0 -> x6, waiting for transfers between devices: none -> 23.3 us  [swap(): return lax.ppermute(value, axis, [(0, 1), (1, 0)])]
    all_to_all x1 -> x0, blocking collectives: 20.8 us -> none  [body(): lax.all_to_all(lax.all_to_all(send_rows, 'dp', split_axis=2, concat_axis=...]
    ppermute x0 -> x6, starting transfers between devices: none -> 4.34 us  [swap(): return lax.ppermute(value, axis, [(0, 1), (1, 0)])]
    all_to_all x7 -> x0, local copies, waits for them, and re-layouts: 4.3 us -> none  [the longest x1 1.31 us: body(): lax.all_to_all(hidden_full, 'dp', split_axis=1, concat_axis=0, tiled=True)]
    all_to_all x7 -> x6, starting transfers between devices: 44.7 us -> 41 us  [exchange(): return lax.all_to_all(pieces, axes, 0, 0, tiled=True)]
    dot_general x5, matrix products: 25.6 us -> 22.2 us  [the longest x1 6.9 us: body(): lax.dot_general(res_all, hid_all, (((1,), (1,)), ((), ())), preferred_ele...]
    unnamed x16, local copies, waits for them, and re-layouts: 3.06 us -> 0.04 us
  transfers between devices with their start and end apart: 8 -> 12, of which waited for: 7 -> 7; matrix products, arithmetic and copies ran while one was open for 14% -> 15% of each run, Pallas kernels for 0% -> 0%
where the time goes in v1:
time: 158 us; the launch traced here: 156 us
  waiting for transfers between devices  69.4 us (44%)
  starting transfers between devices  45.3 us (29%)
  matrix products  22.2 us (14%)
  local copies, waits for them, and re-layouts  13.6 us (9%)
  other arithmetic  4.9 us (3%)
    all_to_all x6, waiting for transfers between devices, exchange(): return lax.all_to_all(pieces, axes, 0, 0, tiled=True)  46.1 us
    all_to_all x6, starting transfers between devices, exchange(): return lax.all_to_all(pieces, axes, 0, 0, tiled=True)  41 us
    ppermute x6, waiting for transfers between devices, swap(): return lax.ppermute(value, axis, [(0, 1), (1, 0)])  23.3 us
    dot_general x1, matrix products, body(): lax.dot_general(res_all, hid_all, (((1,), (1,)), ((), ())), preferred_ele...  6.9 us
    dot_general x1, matrix products, body(): logits = jnp.dot(table, hid, preferred_element_type=F32)  6.11 us
    dot_general x1, matrix products, body(): lax.dot_general(table, residual, (((0,), (0,)), ((), ())), preferred_elem...  5.67 us
    ppermute x6, starting transfers between devices, swap(): return lax.ppermute(value, axis, [(0, 1), (1, 0)])  4.34 us
    broadcast_in_dim x3, local copies, waits for them, and re-layouts, to_each(): return jnp.broadcast_to(value, (count, *value.shape))  3.21 us
  transfers between devices with their start and end apart: 12, of which 7 were waited for; matrix products, arithmetic and copies ran while one was open for 15% of the time, Pallas kernels for 0%

profile of v1, /device:TPU:8, one launch (start us, length us, event | category | flops | bytes accessed | tf_op | source)
XLA Modules:
  0.0 156.4 jit_solution(9327452353162883754)
XLA Ops:
  0.7 1.4 broadcast_in_dim.61
  2.1 8.5 %all-to-all-start = ((bf16[8,32,256]{2,1,0:T(8,128)(2,1)}), bf16[8,32,256]{2,1,0:T(8,128)(2,1)S(1)}, u32[]{:S(2)}, u32[]{:S(2)}) async-start(bf16[8,32,256]{2,1,0:T(8,128)(2,1)} %broadcast_in_dim.61), calls=%async_computation | async-start | bytes 262144 | tf_op jit(solution)/shard_map/all_to_all | solution.py:15
  10.6 0.7 subtract_add_fusion
  11.5 8.1 %all-to-all-done = bf16[8,32,256]{2,1,0:T(8,128)(2,1)S(1)} async-done(((bf16[8,32,256]{2,1,0:T(8,128)(2,1)}), bf16[8,32,256]{2,1,0:T(8,128)(2,1)S(1)}, u32[]{:S(2)}, u32[]{:S(2)}) %all-to-all-start) | async-done | bytes 131104 | tf_op jit(solution)/shard_map/all_to_all | solution.py:15
  19.6 1.0 broadcast_in_dim.62
  20.7 5.8 %all-to-all-start.1 = ((bf16[8,256,256]{2,1,0:T(8,128)(2,1)}), bf16[8,256,256]{2,1,0:T(8,128)(2,1)S(1)}, u32[]{:S(2)}, u32[]{:S(2)}) async-start(bf16[8,256,256]{2,1,0:T(8,128)(2,1)} %broadcast_in_dim.62), calls=%async_computation.1 | async-start | bytes 2097152 | tf_op jit(solution)/shard_map/all_to_all | solution.py:15
  27.0 0.8 fusion.35
  27.7 10.8 %all-to-all-done.1 = bf16[8,256,256]{2,1,0:T(8,128)(2,1)S(1)} async-done(((bf16[8,256,256]{2,1,0:T(8,128)(2,1)}), bf16[8,256,256]{2,1,0:T(8,128)(2,1)S(1)}, u32[]{:S(2)}, u32[]{:S(2)}) %all-to-all-start.1) | async-done | bytes 1048608 | tf_op jit(solution)/shard_map/all_to_all | solution.py:15
  38.6 6.1 %fusion.36 = (f32[256]{0:T(256)S(1)}, f32[2000,256]{1,0:T(8,128)S(1)}) fusion(bf16[2000,2048]{1,0:T(8,128)(2,1)} %param.6, bf16[2048,256]{1,0:T(8,128)(2,1)S(1)} %bitcast.44), kind=kOutput, calls=%fused_computation.78 | convolution fusion | flops 2097663744 | bytes 11289600 | tf_op jit(solution)/shard_map/dot_general | solution.py:65
  45.4 0.7 broadcast_in_dim.64
  46.1 6.3 %all-to-all-start.2 = ((f32[64,3,256]{2,1,0:T(4,128)}), f32[64,3,256]{2,1,0:T(4,128)S(1)}, u32[]{:S(2)}, u32[]{:S(2)}) async-start(f32[64,3,256]{2,1,0:T(4,128)} %broadcast_in_dim.64), calls=%async_computation.2 | async-start | bytes 524288 | tf_op jit(solution)/shard_map/all_to_all | solution.py:15
  52.7 1.1 reshape.93
  53.8 9.5 %all-to-all-done.2 = f32[64,3,256]{2,1,0:T(4,128)S(1)} async-done(((f32[64,3,256]{2,1,0:T(4,128)}), f32[64,3,256]{2,1,0:T(4,128)S(1)}, u32[]{:S(2)}, u32[]{:S(2)}) %all-to-all-start.2) | async-done | bytes 196640 | tf_op jit(solution)/shard_map/all_to_all | solution.py:15
  63.3 9.5 %all-to-all-start.5 = ((bf16[256,2,640]{2,1,0:T(2,128)(2,1)}), bf16[256,2,640]{2,1,0:T(2,128)(2,1)}, u32[]{:S(2)}, u32[]{:S(2)}) async-start(bf16[256,2,640]{2,1,0:T(2,128)(2,1)} %reshape.93), calls=%async_computation.5 | async-start | bytes 1310720 | tf_op jit(solution)/shard_map/all_to_all | solution.py:15
  73.6 3.1 %collective-permute-start.1 = (bf16[2000,256]{1,0:T(8,128)(2,1)S(1)}, bf16[2000,256]{1,0:T(8,128)(2,1)}, u32[]{:S(2)}, u32[]{:S(2)}) collective-permute-start(bf16[2000,256]{1,0:T(8,128)(2,1)S(1)} %subtract_convert_fusion), channel_id=1, source_target_pairs={{0,128},{128,0},{1,129},{129,1},{2,130},{130,2},{3,131},{131,3},{4... | collective-permute-start | bytes 3072008 | tf_op jit(solution)/shard_map/ppermute | solution.py:23
  76.6 5.7 %fusion.11 = bf16[2048,256]{0,1:T(8,128)(2,1)S(1)} fusion(bf16[2000,256]{1,0:T(8,128)(2,1)S(1)} %subtract_convert_fusion, bf16[2000,2048]{1,0:T(8,128)(2,1)} %param.6), kind=kOutput, calls=%fused_computation.12 | convolution fusion | flops 2097676288 | bytes 10264576 | tf_op jit(solution)/shard_map/dot_general | solution.py:77
  82.3 1.3 copy.23
  83.6 2.4 %copy.24 = bf16[4,2,8,32,256]{4,3,2,1,0:T(8,128)(2,1)} copy(bf16[4,2,8,32,256]{4,3,1,2,0:T(8,128)(2,1)} %bitcast.49) | data formatting | bytes 2097152 | tf_op jit(solution)/shard_map/transpose | solution.py:29
  86.0 8.9 %all-to-all-done.5 = bf16[256,2,640]{2,1,0:T(2,128)(2,1)} async-done(((bf16[256,2,640]{2,1,0:T(2,128)(2,1)}), bf16[256,2,640]{2,1,0:T(2,128)(2,1)}, u32[]{:S(2)}, u32[]{:S(2)}) %all-to-all-start.5) | async-done | bytes 655392 | tf_op jit(solution)/shard_map/all_to_all | solution.py:15
  94.9 4.9 %all-to-all-start.3 = ((bf16[8,256,256]{2,1,0:T(8,128)(2,1)}), bf16[8,256,256]{2,1,0:T(8,128)(2,1)S(1)}, u32[]{:S(2)}, u32[]{:S(2)}) async-start(bf16[8,256,256]{2,1,0:T(8,128)(2,1)} %bitcast.47), calls=%async_computation.3 | async-start | bytes 2097152 | tf_op jit(solution)/shard_map/all_to_all | solution.py:15
  99.7 0.8 constant_dynamic-slice_fusion.2
  101.1 0.8 constant_dynamic-slice_fusion.4
  102.0 2.1 %reshape.94 = bf16[512,640]{1,0:T(8,128)(2,1)S(1)} reshape(bf16[256,2,640]{2,1,0:T(2,128)(2,1)} %all-to-all-done.5) | data formatting | bytes 1310720 | tf_op jit(solution)/shard_map/reshape | solution.py:99
  104.7 1.5 collective-permute-done.1
  106.4 21.7 %collective-permute-done.4 = bf16[1024,256]{1,0:T(8,128)(2,1)} collective-permute-done((bf16[1024,256]{1,0:T(8,128)(2,1)}, bf16[1024,256]{1,0:T(8,128)(2,1)}, u32[]{:S(2)}, u32[]{:S(2)}) %collective-permute-start.4) | collective-permute-done | bytes 524320 | tf_op jit(solution)/shard_map/ppermute | solution.py:23
  128.2 1.1 constant_dynamic-slice_fusion.1
  129.3 0.8 convert_reduce_fusion
  130.2 6.1 %all-to-all-start.4 = ((f32[8,32,256]{2,1,0:T(8,128)}), f32[8,32,256]{2,1,0:T(8,128)S(1)}, u32[]{:S(2)}, u32[]{:S(2)}) async-start(f32[8,32,256]{2,1,0:T(8,128)} %bitcast.13), calls=%async_computation.4 | async-start | bytes 524288 | tf_op jit(solution)/shard_map/all_to_all | solution.py:15
  136.3 3.1 %fusion.8 = f32[2000,512]{1,0:T(8,128)} fusion(s32[512]{0:T(512)S(1)} %fusion.23, bf16[512,640]{1,0:T(8,128)(2,1)S(1)} %reshape.94), kind=kOutput, calls=%fused_computation.10 | convolution fusion | flops 1049600000 | bytes 4622336 | tf_op jit(solution)/shard_map/dot_general | solution.py:103
  140.0 8.8 %all-to-all-done.4 = f32[8,32,256]{2,1,0:T(8,128)S(1)} async-done(((f32[8,32,256]{2,1,0:T(8,128)}), f32[8,32,256]{2,1,0:T(8,128)S(1)}, u32[]{:S(2)}, u32[]{:S(2)}) %all-to-all-start.4) | async-done | bytes 262176 | tf_op jit(solution)/shard_map/all_to_all | solution.py:15
  148.8 0.6 reduce_sum.77
  149.5 6.9 %add_convert_fusion = bf16[2000,512]{1,0:T(8,128)(2,1)} fusion(f32[2000,512]{1,0:T(8,128)} %fusion.8, bf16[2000,256]{1,0:T(8,128)(2,1)} %collective-permute-done.2, bf16[2000,256]{1,0:T(8,128)(2,1)} %collective-permute-done.1, bf16[2000,256]{1,0:T(8,128)(2,1)} %collective-permute-done, bf16[2000,256]{1,0:T(8,128)(2,1)S(1)} %subtract_convert_fusion, ...), kind=kOutput, calls=%fused_computation.8 | convolution fusion | flops 2119778304 | bytes 11288576 | tf_op jit(solution)/shard_map/dot_general | solution.py:104
  (45 shorter events, 4.6 us)
Async XLA Ops:
  0.6 25.9 %copy-start = (bf16[64,2048]{1,0:T(8,128)(2,1)S(1)}, bf16[64,2048]{1,0:T(8,128)(2,1)}, u32[]{:S(2)}) copy-start(bf16[64,2048]{1,0:T(8,128)(2,1)} %param.9) | copy-start | bytes 786436
  0.6 25.9 %copy-start.7 = (s32[256]{0:T(256)S(1)}, s32[256]{0:T(256)}, u32[]{:S(2)}) copy-start(s32[256]{0:T(256)} %param.7) | copy-start | bytes 3076
  2.1 17.6 %all-to-all-start = ((bf16[8,32,256]{2,1,0:T(8,128)(2,1)}), bf16[8,32,256]{2,1,0:T(8,128)(2,1)S(1)}, u32[]{:S(2)}, u32[]{:S(2)}) async-start(bf16[8,32,256]{2,1,0:T(8,128)(2,1)} %broadcast_in_dim.61), calls=%async_computation | async-start | bytes 262144 | tf_op jit(solution)/shard_map/all_to_all | solution.py:15
  20.7 17.9 %all-to-all-start.1 = ((bf16[8,256,256]{2,1,0:T(8,128)(2,1)}), bf16[8,256,256]{2,1,0:T(8,128)(2,1)S(1)}, u32[]{:S(2)}, u32[]{:S(2)}) async-start(bf16[8,256,256]{2,1,0:T(8,128)(2,1)} %broadcast_in_dim.62), calls=%async_computation.1 | async-start | bytes 2097152 | tf_op jit(solution)/shard_map/all_to_all | solution.py:15
  38.6 6.1 %copy-start.1 = (bf16[4,8,2,32,256]{4,3,2,1,0:T(8,128)(2,1)}, bf16[4,8,2,32,256]{4,3,2,1,0:T(8,128)(2,1)S(1)}, u32[]{:S(2)}) copy-start(bf16[4,8,2,32,256]{4,3,2,1,0:T(8,128)(2,1)S(1)} %copy.20) | copy-start | bytes 3145732
  44.8 7.7 %copy-start.3 = (bf16[128,512]{1,0:T(8,128)(2,1)S(1)}, bf16[128,512]{1,0:T(8,128)(2,1)}, u32[]{:S(2)}) copy-start(bf16[128,512]{1,0:T(8,128)(2,1)} %get-tuple-element.14) | copy-start | bytes 393220
  44.8 7.7 %copy-start.4 = (bf16[128,512]{1,0:T(8,128)(2,1)S(1)}, bf16[128,512]{1,0:T(8,128)(2,1)}, u32[]{:S(2)}) copy-start(bf16[128,512]{1,0:T(8,128)(2,1)} %get-tuple-element.15) | copy-start | bytes 393220
  44.8 7.7 %copy-start.5 = (bf16[128,512]{1,0:T(8,128)(2,1)S(1)}, bf16[128,512]{1,0:T(8,128)(2,1)}, u32[]{:S(2)}) copy-start(bf16[128,512]{1,0:T(8,128)(2,1)} %get-tuple-element.16) | copy-start | bytes 393220
  46.1 17.2 %all-to-all-start.2 = ((f32[64,3,256]{2,1,0:T(4,128)}), f32[64,3,256]{2,1,0:T(4,128)S(1)}, u32[]{:S(2)}, u32[]{:S(2)}) async-start(f32[64,3,256]{2,1,0:T(4,128)} %broadcast_in_dim.64), calls=%async_computation.2 | async-start | bytes 524288 | tf_op jit(solution)/shard_map/all_to_all | solution.py:15
  63.3 31.6 %all-to-all-start.5 = ((bf16[256,2,640]{2,1,0:T(2,128)(2,1)}), bf16[256,2,640]{2,1,0:T(2,128)(2,1)}, u32[]{:S(2)}, u32[]{:S(2)}) async-start(bf16[256,2,640]{2,1,0:T(2,128)(2,1)} %reshape.93), calls=%async_computation.5 | async-start | bytes 1310720 | tf_op jit(solution)/shard_map/all_to_all | solution.py:15
  73.6 32.6 %collective-permute-start.1 = (bf16[2000,256]{1,0:T(8,128)(2,1)S(1)}, bf16[2000,256]{1,0:T(8,128)(2,1)}, u32[]{:S(2)}, u32[]{:S(2)}) collective-permute-start(bf16[2000,256]{1,0:T(8,128)(2,1)S(1)} %subtract_convert_fusion), channel_id=1, source_target_pairs={{0,128},{128,0},{1,129},{129,1},{2,130},{130,2},{3,131},{131,3},{4... | collective-permute-start | bytes 3072008 | tf_op jit(solution)/shard_map/ppermute | solution.py:23
  83.6 16.1 %copy-start.2 = (bf16[4,8,2,32,256]{4,3,2,1,0:T(8,128)(2,1)S(1)}, bf16[4,8,2,32,256]{4,3,2,1,0:T(8,128)(2,1)}, u32[]{:S(2)}) copy-start(bf16[4,8,2,32,256]{4,3,2,1,0:T(8,128)(2,1)} %copy-done.1) | copy-start | bytes 3145732
  94.9 34.5 %all-to-all-start.3 = ((bf16[8,256,256]{2,1,0:T(8,128)(2,1)}), bf16[8,256,256]{2,1,0:T(8,128)(2,1)S(1)}, u32[]{:S(2)}, u32[]{:S(2)}) async-start(bf16[8,256,256]{2,1,0:T(8,128)(2,1)} %bitcast.47), calls=%async_computation.3 | async-start | bytes 2097152 | tf_op jit(solution)/shard_map/all_to_all | solution.py:15
  100.6 27.6 %collective-permute-start.4 = (bf16[1024,256]{1,0:T(8,128)(2,1)}, bf16[1024,256]{1,0:T(8,128)(2,1)}, u32[]{:S(2)}, u32[]{:S(2)}) collective-permute-start(bf16[1024,256]{1,0:T(8,128)(2,1)} %constant_dynamic-slice_fusion.2), channel_id=1, source_target_pairs={{0,128},{128,0},{1,129},{129,1},{2,130},{130,2},{3,131},{131,3},{4... | collective-permute-start | bytes 1572872 | tf_op jit(solution)/shard_map/ppermute | solution.py:23
  102.0 47.4 %collective-permute-start.3 = (bf16[512,256]{1,0:T(8,128)(2,1)}, bf16[512,256]{1,0:T(8,128)(2,1)}, u32[]{:S(2)}, u32[]{:S(2)}) collective-permute-start(bf16[512,256]{1,0:T(8,128)(2,1)} %get-tuple-element.10), channel_id=1, source_target_pairs={{0,64},{64,0},{1,65},{65,1},{2,66},{66,2},{3,67},{67,3},{4,68},{68... | collective-permute-start | bytes 786440 | tf_op jit(solution)/shard_map/ppermute | solution.py:23
  104.1 45.4 %collective-permute-start = (bf16[2000,256]{1,0:T(8,128)(2,1)S(1)}, bf16[2000,256]{1,0:T(8,128)(2,1)}, u32[]{:S(2)}, u32[]{:S(2)}) collective-permute-start(bf16[2000,256]{1,0:T(8,128)(2,1)S(1)} %subtract_convert_fusion), channel_id=1, source_target_pairs={{0,64},{64,0},{1,65},{65,1},{2,66},{66,2},{3,67},{67,3},{4,68},{68... | collective-permute-start | bytes 3072008 | tf_op jit(solution)/shard_map/ppermute | solution.py:23
  106.2 43.3 %collective-permute-start.2 = (bf16[2000,256]{1,0:T(8,128)(2,1)}, bf16[2000,256]{1,0:T(8,128)(2,1)}, u32[]{:S(2)}, u32[]{:S(2)}) collective-permute-start(bf16[2000,256]{1,0:T(8,128)(2,1)} %collective-permute-done.1), channel_id=1, source_target_pairs={{0,64},{64,0},{1,65},{65,1},{2,66},{66,2},{3,67},{67,3},{4,68},{68... | collective-permute-start | bytes 3072008 | tf_op jit(solution)/shard_map/ppermute | solution.py:23
  129.2 20.2 %collective-permute-start.5 = (bf16[512,256]{1,0:T(8,128)(2,1)S(1)}, bf16[512,256]{1,0:T(8,128)(2,1)}, u32[]{:S(2)}, u32[]{:S(2)}) collective-permute-start(bf16[512,256]{1,0:T(8,128)(2,1)S(1)} %get-tuple-element.12), channel_id=1, source_target_pairs={{0,64},{64,0},{1,65},{65,1},{2,66},{66,2},{3,67},{67,3},{4,68},{68... | collective-permute-start | bytes 786440 | tf_op jit(solution)/shard_map/ppermute | solution.py:23
  130.2 18.6 %all-to-all-start.4 = ((f32[8,32,256]{2,1,0:T(8,128)}), f32[8,32,256]{2,1,0:T(8,128)S(1)}, u32[]{:S(2)}, u32[]{:S(2)}) async-start(f32[8,32,256]{2,1,0:T(8,128)} %bitcast.13), calls=%async_computation.4 | async-start | bytes 524288 | tf_op jit(solution)/shard_map/all_to_all | solution.py:15
  136.3 13.2 %copy-start.6 = (bf16[512,256]{1,0:T(8,128)(2,1)S(1)}, bf16[512,256]{1,0:T(8,128)(2,1)}, u32[]{:S(2)}) copy-start(bf16[512,256]{1,0:T(8,128)(2,1)} %get-tuple-element.9) | copy-start | bytes 786436

commit v2 on v1

v2 whole, which is shorter than its diff:
```python
import functools

import jax
import jax.numpy as jnp
from jax import lax
from jax.experimental import pallas as pl
from jax.experimental.pallas import tpu as pltpu
from jax.sharding import Mesh, PartitionSpec as P

BF16 = jnp.bfloat16
F32 = jnp.float32
I32 = jnp.int32
ALL = ("xh", "c", "y", "z", "xl")
DP = ("xh", "c")
VOCAB = ("y", "z", "xl")
PLANE = ("y", "xl")
CHUNK = 400
PARAMS = pltpu.CompilerParams(vmem_limit_bytes=48 * 1024 * 1024)


def exchange(pieces, axes):
    return lax.all_to_all(pieces, axes, 0, 0, tiled=True)


def to_each(value, count):
    return jnp.broadcast_to(value, (count, *value.shape))


def swap(value, axis):
    return lax.ppermute(value, axis, [(0, 1), (1, 0)])


def cost(flops, moved, special=0):
    return pl.CostEstimate(flops=flops, bytes_accessed=moved, transcendentals=special)


def logits_kernel(where_ref, tgt_ref, got_ref, table_ref, near_ref, far_ref, stats_ref, hid, log, acc):
    step = pl.program_id(0)
    rows, tokens = table_ref.shape[0], hid.shape[1]
    width = hid.shape[0]
    half = width // 2

    @pl.when(step == 0)
    def _():
        plane, depth, _ = got_ref.shape
        nz = depth // 32
        nx = 2
        for p in range(plane):
            y, x = p // nx, p % nx
            for z in range(nz):
                at = ((y * nz + z) * nx + x) * 32
                hid[at : at + 32, :] = got_ref[p, z * 32 : z * 32 + 32, :]
        acc[0:1, :] = jnp.full((1, tokens), -jnp.inf, F32)
        acc[1:2, :] = jnp.zeros((1, tokens), F32)

    values = jnp.dot(table_ref[...], hid[...], preferred_element_type=F32)
    log[pl.ds(pl.multiple_of(step * rows, rows), rows), :] = values
    index = lax.broadcasted_iota(I32, values.shape, 0) + (where_ref[0] + step * rows)
    acc[1:2, :] += jnp.sum(jnp.where(index == tgt_ref[...], values, 0.0), axis=0, keepdims=True)
    acc[0:1, :] = jnp.maximum(acc[0:1, :], jnp.max(values, axis=0, keepdims=True))

    @pl.when(step == pl.num_programs(0) - 1)
    def _():
        top = acc[0:1, :]
        piece = 80

        def one(i, total):
            at = pl.ds(pl.multiple_of(i * piece, piece), piece)
            e = jnp.exp(log[at, :] - top)
            near_ref[at, :] = e.astype(BF16)
            far_ref[at, :] = e.astype(BF16)
            return total + jnp.sum(e, axis=0, keepdims=True)

        count = log.shape[0]
        total = lax.fori_loop(0, count // piece, one, jnp.zeros((1, tokens), F32))
        base = near_ref.shape[0] - half
        near_ref[count:base, :] = jnp.zeros((base - count, tokens), BF16)
        far_ref[count:base, :] = jnp.zeros((base - count, tokens), BF16)
        near_ref[base:, :] = hid[pl.ds(pl.multiple_of(where_ref[1] * half, half), half), :]
        far_ref[base:, :] = hid[pl.ds(pl.multiple_of((1 - where_ref[1]) * half, half), half), :]
        line = jnp.concatenate([top, total, acc[1:2, :], jnp.zeros((1, tokens), F32)], axis=0)
        stats_ref[...] = jnp.broadcast_to(line[None], stats_ref.shape)


def logits_call(where, targets, got, table, copies):
    count, width = table.shape
    tokens = got.shape[2]
    span = 2048 + width // 2
    return pl.pallas_call(
        logits_kernel,
        grid_spec=pltpu.PrefetchScalarGridSpec(
            num_scalar_prefetch=1,
            grid=(count // CHUNK,),
            in_specs=[
                pl.BlockSpec((1, tokens), lambda i, s: (0, 0)),
                pl.BlockSpec(got.shape, lambda i, s: (0, 0, 0)),
                pl.BlockSpec((CHUNK, width), lambda i, s: (i, 0)),
            ],
            out_specs=[
                pl.BlockSpec((span, tokens), lambda i, s: (0, 0)),
                pl.BlockSpec((span, tokens), lambda i, s: (0, 0)),
                pl.BlockSpec((copies, 4, tokens), lambda i, s: (0, 0, 0)),
            ],
            scratch_shapes=[
                pltpu.VMEM((width, tokens), BF16),
                pltpu.VMEM((count, tokens), F32),
                pltpu.VMEM((8, tokens), F32),
            ],
        ),
        out_shape=[
            jax.ShapeDtypeStruct((span, tokens), BF16),
            jax.ShapeDtypeStruct((span, tokens), BF16),
            jax.ShapeDtypeStruct((copies, 4, tokens), F32),
        ],
        compiler_params=PARAMS,
        cost_estimate=cost(2 * count * width * tokens, 2 * count * width + 4 * span * tokens),
        name="logits",
    )(where, targets, got, table)


def part_kernel(where_ref, tgt_ref, e_ref, table_ref, soft_ref, hard_ref, lhs):
    tokens = tgt_ref.shape[1]
    count = table_ref.shape[0]

    @pl.when(pl.program_id(0) == 0)
    def _():
        index = lax.broadcasted_iota(I32, (count, tokens), 0) + where_ref[0]
        hit = jnp.where(index == tgt_ref[...], 1.0, 0.0).astype(BF16)
        lhs[0:tokens, :] = e_ref[...].T
        lhs[tokens:, :] = hit.T

    both = jnp.dot(lhs[...], table_ref[...], preferred_element_type=F32)
    soft = both[0:tokens, :].T
    hard = both[tokens:, :].T
    for k in range(soft.shape[0] // 32):
        z, x = k // 2, k % 2
        soft_ref[x, z * 32 : z * 32 + 32, :] = soft[k * 32 : k * 32 + 32, :]
        hard_ref[x, z * 32 : z * 32 + 32, :] = hard[k * 32 : k * 32 + 32, :].astype(BF16)


def part_call(where, targets, near, table):
    count, width = table.shape
    tokens = targets.shape[1]
    wide = 256
    spec = pl.BlockSpec((2, wide // 2, tokens), lambda j, s: (j // 2, j % 2, 0))
    return pl.pallas_call(
        part_kernel,
        grid_spec=pltpu.PrefetchScalarGridSpec(
            num_scalar_prefetch=1,
            grid=(width // wide,),
            in_specs=[
                pl.BlockSpec((1, tokens), lambda j, s: (0, 0)),
                pl.BlockSpec((count, tokens), lambda j, s: (0, 0)),
                pl.BlockSpec((count, wide), lambda j, s: (0, j)),
            ],
            out_specs=[spec, spec],
            scratch_shapes=[pltpu.VMEM((2 * tokens, count), BF16)],
        ),
        out_shape=[
            jax.ShapeDtypeStruct((8, width // 8, tokens), F32),
            jax.ShapeDtypeStruct((8, width // 8, tokens), BF16),
        ],
        compiler_params=PARAMS,
        cost_estimate=cost(4 * count * width * tokens, 2 * count * width + 6 * width * tokens),
        name="part",
    )(where, targets, near, table)


def scale_kernel(where_ref, tgt_ref, own_ref, stats_ref, soft_ref, hard_ref, out_ref, loss_ref, w_ref, keep):
    @pl.when(pl.program_id(0) == 0)
    def _():
        stats = stats_ref[...]
        peak = jnp.max(stats, axis=0)
        top = peak[0:1, :]
        sums = jnp.sum(stats[:, 1:2, :] * jnp.exp(stats[:, 0:1, :] - top[None]), axis=0)
        picks = jnp.sum(stats, axis=0)[2:3, :]
        loss_ref[...] = top + jnp.log(sums) - picks
        local_top, local_pick = own_ref[0, 0:1, :], own_ref[0, 2:3, :]
        w = jnp.exp(local_top - top) / sums
        prob = jnp.exp(local_pick - top) / sums
        soft = jnp.exp(local_pick - local_top).astype(BF16).astype(F32) * w
        gap = (prob - 1.0).astype(BF16).astype(F32) - soft
        keep[0:1, :] = w
        keep[1:2, :] = gap
        w_ref[...] = jnp.concatenate(
            [w, tgt_ref[...].astype(F32), jnp.zeros((6, w.shape[1]), F32)], axis=0
        )

    out_ref[...] = (
        soft_ref[...] * keep[0:1, :][None] + hard_ref[...].astype(F32) * keep[1:2, :][None]
    ).astype(BF16)


def scale_call(where, targets, own, stats, soft, hard):
    plane, depth, tokens = soft.shape
    spec = pl.BlockSpec((2, depth, tokens), lambda p, s: (p, 0, 0))
    return pl.pallas_call(
        scale_kernel,
        grid_spec=pltpu.PrefetchScalarGridSpec(
            num_scalar_prefetch=1,
            grid=(plane // 2,),
            in_specs=[
                pl.BlockSpec((1, tokens), lambda p, s: (0, 0)),
                pl.BlockSpec((1, 4, tokens), lambda p, s: (0, 0, 0)),
                pl.BlockSpec(stats.shape, lambda p, s: (0, 0, 0)),
                spec,
                spec,
            ],
            out_specs=[
                spec,
                pl.BlockSpec((1, tokens), lambda p, s: (0, 0)),
                pl.BlockSpec((8, tokens), lambda p, s: (0, 0)),
            ],
            scratch_shapes=[pltpu.VMEM((8, tokens), F32)],
        ),
        out_shape=[
            jax.ShapeDtypeStruct((plane, depth, tokens), BF16),
            jax.ShapeDtypeStruct((1, tokens), F32),
            jax.ShapeDtypeStruct((8, tokens), F32),
        ],
        compiler_params=PARAMS,
        cost_estimate=cost(4 * plane * depth * tokens, 8 * plane * depth * tokens),
        name="scale",
    )(where, targets, own, stats, soft, hard)


def table_kernel(where_ref, w_ref, place_ref, rows_ref, *refs):
    out_ref = refs[-1]
    count = out_ref.shape[0]
    first = pl.program_id(0) * count
    index = lax.broadcasted_iota(I32, (count, 256), 0) + first
    near = index + where_ref[0]
    slots = place_ref.shape[1]
    match = jnp.concatenate(
        [
            jnp.where(index == place_ref[:, k : k + 256], 1.0, 0.0).astype(BF16)
            for k in range(0, slots, 256)
        ],
        axis=1,
    )
    total = jnp.dot(match, rows_ref[...], preferred_element_type=F32)
    for g in range(4):
        e = refs[2 * g][...].astype(F32)
        w = w_ref[g, 0:1, :]
        target = w_ref[g, 1:2, :].astype(I32)
        res = (e * w - jnp.where(near == target, 1.0, 0.0)).astype(BF16)
        total += lax.dot_general(
            res, refs[2 * g + 1][...], (((1,), (1,)), ((), ())), preferred_element_type=F32
        )
    out_ref[...] = total.astype(BF16)


def table_call(where, w, place, rows, packs, count):
    tokens = packs[0].shape[1]
    block = rows.shape[1] // 128 * 128
    block = 512
    specs, operands = [], []
    for pack in packs:
        specs.append(pl.BlockSpec((CHUNK, tokens), lambda i, s: (i, 0)))
        specs.append(pl.BlockSpec((block, tokens), lambda i, s: (4 + s[2], 0)))
        operands += [pack, pack]
    return pl.pallas_call(
        table_kernel,
        grid_spec=pltpu.PrefetchScalarGridSpec(
            num_scalar_prefetch=1,
            grid=(count // CHUNK,),
            in_specs=[
                pl.BlockSpec(w.shape, lambda i, s: (0, 0, 0)),
                pl.BlockSpec(place.shape, lambda i, s: (0, 0)),
                pl.BlockSpec((rows.shape[0], block), lambda i, s: (0, 0)),
                *specs,
            ],
            out_specs=pl.BlockSpec((CHUNK, block), lambda i, s: (i, 0)),
        ),
        out_shape=jax.ShapeDtypeStruct((count, block), BF16),
        compiler_params=PARAMS,
        cost_estimate=cost(2 * count * block * 1536, 8 * count * 256 + 2 * count * block),
        name="table_grad",
    )(where, w, place, rows, *operands)


def body(hidden, table, targets, input_ids, cotangent):
    vocab_rows, width = table.shape
    ny, nz, nx = (lax.axis_size(a) for a in VOCAB)
    plane = ny * nx
    vocab_count = plane * nz
    data_count = lax.axis_size(DP)
    block = width // data_count
    xh, c = lax.axis_index("xh"), lax.axis_index("c")
    where = jnp.stack([lax.axis_index(VOCAB) * vocab_rows, xh, c]).astype(I32)
    tokens = hidden.shape[0]
    goal = targets.reshape(1, tokens)

    owners = input_ids // vocab_rows
    offsets = input_ids - owners * vocab_rows
    count = input_ids.shape[0]
    later = lax.broadcasted_iota(I32, (count, count), 0)
    early = lax.broadcasted_iota(I32, (count, count), 1)
    before = (owners[:, None] == owners[None, :]) & (early < later)
    slot = owners * 2 + jnp.sum(before.astype(I32), axis=1)
    chosen = lax.broadcasted_iota(I32, (2 * vocab_count, count), 0) == slot[None, :]
    sent = jnp.dot(chosen.astype(BF16), cotangent, preferred_element_type=F32).astype(BF16)
    spots = jnp.sum(jnp.where(chosen, offsets[None, :] + 1, 0), axis=1)
    lane = lax.broadcasted_iota(I32, (2 * vocab_count, 128), 1)
    code = jnp.where(lane == 0, (spots // 64)[:, None], jnp.where(lane == 1, (spots % 64)[:, None], 0))
    code = code.astype(BF16)
    sent = jnp.stack(
        [jnp.concatenate([sent[:, d * block : (d + 1) * block], code], axis=1) for d in range(data_count)]
    )
    sent = sent.reshape(data_count * vocab_count, 2, block + 128)

    mine = hidden.T
    stage = exchange(to_each(mine, nz), "z").reshape(-1, tokens)
    stage = exchange(to_each(stage, plane), PLANE)

    near, far, own = logits_call(where, goal, stage, table, vocab_count)
    stats = exchange(own, VOCAB)
    near_sib = swap(near, "c")
    far = swap(far, "xh")
    far_sib = swap(far, "c")
    soft, hard = part_call(where, goal, near, table)
    part, loss, w = scale_call(where, goal, own, stats, soft, hard)

    part = exchange(part, PLANE)
    part = jnp.sum(part.astype(F32), axis=0).reshape(nz, -1, tokens)
    part = jnp.sum(exchange(part, "z"), axis=0)
    hidden_grad = part.astype(BF16).T

    w_near = jnp.stack([w, swap(w, "c")])
    w_all = jnp.concatenate([w_near, swap(w_near, "xh")], axis=0)

    got = exchange(sent, ALL).reshape(-1, block + 128)
    code = got[:, block:].astype(F32)
    place = (code[:, 0] * 64 + code[:, 1]).astype(I32) - 1
    table_grad = table_call(
        where, w_all, place.reshape(1, -1), got, (near, near_sib, far, far_sib), vocab_rows
    )
    return loss.reshape(tokens), hidden_grad, table_grad


def solution(mesh):
    fine = Mesh(mesh.devices.reshape(2, 2, 4, 8, 2), ALL)
    placed = (P(DP, VOCAB), P(VOCAB, None), P(DP), P(ALL), P(ALL, None))
    return jax.shard_map(
        body,
        mesh=fine,
        in_specs=placed,
        out_specs=(P(DP), P(DP, VOCAB), P(VOCAB, DP)),
        check_vma=False,
    )
```

time: 158 us -> 155 us (0.981)
  Pallas kernels: 0 us -> 28.9 us
  matrix products: 22.2 us -> 1.2 us
  waiting for transfers between devices: 69.4 us -> 55.4 us
  starting transfers between devices: 45.3 us -> 47.6 us
  other arithmetic: 4.9 us -> 6.99 us
    pallas_call x0 -> x4, Pallas kernels: none -> 28.9 us  [the longest x1 10.5 us: part_call(): pl.pallas_call(part_kernel, grid_spec=pltpu.PrefetchScalarGridSpec(num_sc...]
    dot_general x4 -> x0, matrix products: 21.8 us -> none  [the longest x1 6.9 us: body(): lax.dot_general(res_all, hid_all, (((1,), (1,)), ((), ())), preferred_ele...]
    ppermute x6 -> x5, waiting for transfers between devices: 23.3 us -> 3.16 us  [swap(): return lax.ppermute(value, axis, [(0, 1), (1, 0)])]
    all_to_all x6, waiting for transfers between devices: 46.1 us -> 52.2 us  [exchange(): return lax.all_to_all(pieces, axes, 0, 0, tiled=True)]
    unnamed x16 -> x10, local copies, waits for them, and re-layouts: 0.04 us -> 3.21 us
    dynamic_slice x3 -> x0, local copies, waits for them, and re-layouts: 2.72 us -> none  [cut(): return lax.dynamic_slice_in_dim(value, start, size, 0)]
    transpose x2 -> x0, local copies, waits for them, and re-layouts: 2.46 us -> none  [the longest x1 2.37 us: by_plane(): return rows.transpose(0, 2, 1, 3, *range(4, 4 + len(tail)))]
    ppermute x6 -> x5, starting transfers between devices: 4.34 us -> 5.36 us  [swap(): return lax.ppermute(value, axis, [(0, 1), (1, 0)])]
  transfers between devices with their start and end apart: 12 -> 11, of which waited for: 7 -> 7; matrix products, arithmetic and copies ran while one was open for 15% -> 10% of each run, Pallas kernels for 0% -> 9%
where the time goes in v2:
time: 155 us; the launch traced here: 153 us
  waiting for transfers between devices  55.4 us (36%)
  starting transfers between devices  47.6 us (31%)
  Pallas kernels  28.9 us (19%)
  local copies, waits for them, and re-layouts  12.1 us (8%)
  other arithmetic  6.99 us (5%)
    all_to_all x6, waiting for transfers between devices, exchange(): return lax.all_to_all(pieces, axes, 0, 0, tiled=True)  52.2 us
    all_to_all x6, starting transfers between devices, exchange(): return lax.all_to_all(pieces, axes, 0, 0, tiled=True)  42.2 us
    pallas_call x1, Pallas kernels, part_call(): pl.pallas_call(part_kernel, grid_spec=pltpu.PrefetchScalarGridSpec(num_sc...  10.5 us
    pallas_call x1, Pallas kernels, logits_call(): pl.pallas_call(logits_kernel, grid_spec=pltpu.PrefetchScalarGridSpec(num_...  8.32 us
    pallas_call x1, Pallas kernels, table_call(): pl.pallas_call(table_kernel, grid_spec=pltpu.PrefetchScalarGridSpec(num_s...  7.53 us
    ppermute x5, starting transfers between devices, swap(): return lax.ppermute(value, axis, [(0, 1), (1, 0)])  5.36 us
    unnamed x10, local copies, waits for them, and re-layouts  3.21 us
    ppermute x5, waiting for transfers between devices, swap(): return lax.ppermute(value, axis, [(0, 1), (1, 0)])  3.16 us
  transfers between devices with their start and end apart: 11, of which 7 were waited for; matrix products, arithmetic and copies ran while one was open for 10% of the time, Pallas kernels for 9%

profile of v2, /device:TPU:8, one launch (start us, length us, event | category | flops | bytes accessed | tf_op | source)
XLA Modules:
  0.0 153.0 jit_solution(6230481956190333054)
XLA Ops:
  0.6 1.4 broadcast_in_dim.42
  2.1 8.5 %all-to-all-start = ((bf16[8,32,256]{2,1,0:T(8,128)(2,1)}), bf16[8,32,256]{2,1,0:T(8,128)(2,1)S(1)}, u32[]{:S(2)}, u32[]{:S(2)}) async-start(bf16[8,32,256]{2,1,0:T(8,128)(2,1)} %broadcast_in_dim.42), calls=%async_computation | async-start | bytes 262144 | tf_op jit(solution)/shard_map/all_to_all | solution.py:22
  11.4 8.2 %all-to-all-done = bf16[8,32,256]{2,1,0:T(8,128)(2,1)S(1)} async-done(((bf16[8,32,256]{2,1,0:T(8,128)(2,1)}), bf16[8,32,256]{2,1,0:T(8,128)(2,1)S(1)}, u32[]{:S(2)}, u32[]{:S(2)}) %all-to-all-start) | async-done | bytes 131104 | tf_op jit(solution)/shard_map/all_to_all | solution.py:22
  19.6 1.0 broadcast_in_dim.43
  20.7 6.0 %all-to-all-start.1 = ((bf16[8,256,256]{2,1,0:T(8,128)(2,1)}), bf16[8,256,256]{2,1,0:T(8,128)(2,1)S(1)}, u32[]{:S(2)}, u32[]{:S(2)}) async-start(bf16[8,256,256]{2,1,0:T(8,128)(2,1)} %broadcast_in_dim.43), calls=%async_computation.1 | async-start | bytes 2097152 | tf_op jit(solution)/shard_map/all_to_all | solution.py:22
  26.9 1.2 convolution_convert_fusion
  28.1 10.6 %all-to-all-done.1.got_ref = bf16[8,256,256]{2,1,0:T(8,128)(2,1)S(1)} async-done(((bf16[8,256,256]{2,1,0:T(8,128)(2,1)}), bf16[8,256,256]{2,1,0:T(8,128)(2,1)S(1)}, u32[]{:S(2)}, u32[]{:S(2)}) %all-to-all-start.1) | async-done | bytes 1048608 | tf_op jit(solution)/shard_map/all_to_all | solution.py:22
  38.7 8.3 %logits.1 = (bf16[3072,256]{1,0:T(8,128)(2,1)S(1)}, bf16[3072,256]{1,0:T(8,128)(2,1)S(1)}, f32[64,4,256]{2,1,0:T(4,128)}) custom-call(s32[3]{0:T(128)S(1)} %pad_add_fusion.where_ref, s32[1,256]{1,0:T(1,128)S(1)} %bitcast.26, bf16[8,256,256]{2,1,0:T(8,128)(2,1)S(1)} %all-to-all-done.1.got_ref, bf16[2000,2048]{1,0:T(8,128)(2,1)} %table_ref.3), custom_call_target="tpu_custom_call" | custom-call | flops 2097152000 | bytes 11337728 | tf_op jit(solution)/shard_map/logits/pallas_call | solution.py:89
  47.0 1.1 copy-done.4
  48.1 7.0 %all-to-all-start.2 = ((f32[64,4,256]{2,1,0:T(4,128)}), f32[64,4,256]{2,1,0:T(4,128)}, u32[]{:S(2)}, u32[]{:S(2)}) async-start(f32[64,4,256]{2,1,0:T(4,128)} %get-tuple-element.11.own_ref), calls=%async_computation.2 | async-start | bytes 524288 | tf_op jit(solution)/shard_map/all_to_all | solution.py:22
  55.3 1.1 fusion.9
  56.4 2.8 %collective-permute-start.3 = (bf16[3072,256]{1,0:T(8,128)(2,1)}, bf16[3072,256]{1,0:T(8,128)(2,1)S(1)}, u32[]{:S(2)}, u32[]{:S(2)}) collective-permute-start(bf16[3072,256]{1,0:T(8,128)(2,1)} %copy-done.4), channel_id=1, source_target_pairs={{0,128},{128,0},{1,129},{129,1},{2,130},{130,2},{3,131},{131,3},{4... | collective-permute-start | bytes 4718600 | tf_op jit(solution)/shard_map/ppermute | solution.py:30
  59.3 1.0 pad_maximum_fusion
  60.3 2.6 %reshape.96 = bf16[256,2,640]{2,1,0:T(2,128)(2,1)} reshape(bf16[4,128,640]{2,1,0:T(8,128)(2,1)} %pad_maximum_fusion) | data formatting | bytes 1310720 | tf_op jit(solution)/shard_map/reshape | solution.py:310
  62.9 2.7 %all-to-all-done.2.stats_ref = f32[64,4,256]{2,1,0:T(4,128)} async-done(((f32[64,4,256]{2,1,0:T(4,128)}), f32[64,4,256]{2,1,0:T(4,128)}, u32[]{:S(2)}, u32[]{:S(2)}) %all-to-all-start.2) | async-done | bytes 262176 | tf_op jit(solution)/shard_map/all_to_all | solution.py:22
  65.6 9.4 %all-to-all-start.5 = ((bf16[256,2,640]{2,1,0:T(2,128)(2,1)}), bf16[256,2,640]{2,1,0:T(2,128)(2,1)}, u32[]{:S(2)}, u32[]{:S(2)}) async-start(bf16[256,2,640]{2,1,0:T(2,128)(2,1)} %reshape.96), calls=%async_computation.5 | async-start | bytes 1310720 | tf_op jit(solution)/shard_map/all_to_all | solution.py:22
  75.0 10.5 %part.1 = (f32[8,256,256]{2,1,0:T(8,128)S(1)}, bf16[8,256,256]{2,1,0:T(8,128)(2,1)S(1)}) custom-call(s32[3]{0:T(128)S(1)} %pad_add_fusion.where_ref, s32[1,256]{1,0:T(1,128)S(1)} %bitcast.27, bf16[3072,256]{1,0:T(8,128)(2,1)S(1)} %get-tuple-element.12.e_ref.refs_0_.refs_1_, bf16[2000,2048]{1,0:T(8,128)(2,1)} %table_ref.3), custom_call_target="tpu_custom_call" | custom-call | flops 4194304000 | bytes 11337728 | tf_op jit(solution)/shard_map/part/pallas_call | solution.py:146
  85.5 2.6 %scale.1 = (bf16[8,256,256]{2,1,0:T(8,128)(2,1)S(1)}, f32[1,256]{1,0:T(1,128)}, f32[8,256]{1,0:T(8,128)S(1)}) custom-call(s32[3]{0:T(128)S(1)} %pad_add_fusion.where_ref, s32[1,256]{1,0:T(1,128)S(1)} %bitcast.28, f32[64,4,256]{2,1,0:T(4,128)} %get-tuple-element.11.own_ref, f32[64,4,256]{2,1,0:T(4,128)} %all-to-all-done.2.stats_ref, ...), custom_call_target="tpu_custom_call" | custom-call | flops 2097152 | bytes 4194304 | tf_op jit(solution)/shard_map/scale/pallas_call | solution.py:197
  88.1 1.0 copy-done.2
  89.1 14.6 %all-to-all-done.5 = bf16[256,2,640]{2,1,0:T(2,128)(2,1)} async-done(((bf16[256,2,640]{2,1,0:T(2,128)(2,1)}), bf16[256,2,640]{2,1,0:T(2,128)(2,1)}, u32[]{:S(2)}, u32[]{:S(2)}) %all-to-all-start.5) | async-done | bytes 655392 | tf_op jit(solution)/shard_map/all_to_all | solution.py:22
  103.6 5.4 %all-to-all-start.3 = ((bf16[8,256,256]{2,1,0:T(8,128)(2,1)}), bf16[8,256,256]{2,1,0:T(8,128)(2,1)}, u32[]{:S(2)}, u32[]{:S(2)}) async-start(bf16[8,256,256]{2,1,0:T(8,128)(2,1)} %copy-done.2), calls=%async_computation.3 | async-start | bytes 2097152 | tf_op jit(solution)/shard_map/all_to_all | solution.py:22
  109.6 2.7 %reshape.97.rows_ref = bf16[512,640]{1,0:T(8,128)(2,1)} reshape(bf16[256,2,640]{2,1,0:T(2,128)(2,1)} %all-to-all-done.5) | data formatting | bytes 1310720 | tf_op jit(solution)/shard_map/reshape | solution.py:332
  112.4 11.0 %all-to-all-done.3 = bf16[8,256,256]{2,1,0:T(8,128)(2,1)} async-done(((bf16[8,256,256]{2,1,0:T(8,128)(2,1)}), bf16[8,256,256]{2,1,0:T(8,128)(2,1)}, u32[]{:S(2)}, u32[]{:S(2)}) %all-to-all-start.3) | async-done | bytes 1048608 | tf_op jit(solution)/shard_map/all_to_all | solution.py:22
  123.4 2.1 %convert_reduce_fusion = f32[256,256]{1,0:T(8,128)} fusion(bf16[8,256,256]{2,1,0:T(8,128)(2,1)} %all-to-all-done.3), kind=kLoop, calls=%fused_computation.1 | loop fusion | flops 983040 | bytes 1310720 | tf_op jit(solution)/shard_map/reduce_sum | solution.py:325
  125.5 5.9 %all-to-all-start.4 = ((f32[8,32,256]{2,1,0:T(8,128)}), f32[8,32,256]{2,1,0:T(8,128)}, u32[]{:S(2)}, u32[]{:S(2)}) async-start(f32[8,32,256]{2,1,0:T(8,128)} %bitcast.29), calls=%async_computation.4 | async-start | bytes 524288 | tf_op jit(solution)/shard_map/all_to_all | solution.py:22
  131.4 0.9 slice_convert_fusion
  132.3 1.9 %collective-permute-start.1 = (f32[2,8,256]{2,1,0:T(8,128)S(1)}, f32[2,8,256]{2,1,0:T(8,128)S(1)}, u32[]{:S(2)}, u32[]{:S(2)}) collective-permute-start(f32[2,8,256]{2,1,0:T(8,128)S(1)} %pad_maximum_fusion.6), channel_id=1, source_target_pairs={{0,128},{128,0},{1,129},{129,1},{2,130},{130,2},{3,131},{131,3},{4... | collective-permute-start | bytes 49160 | tf_op jit(solution)/shard_map/ppermute | solution.py:30
  134.5 3.1 %collective-permute-done.1 = f32[2,8,256]{2,1,0:T(8,128)S(1)} collective-permute-done((f32[2,8,256]{2,1,0:T(8,128)S(1)}, f32[2,8,256]{2,1,0:T(8,128)S(1)}, u32[]{:S(2)}, u32[]{:S(2)}) %collective-permute-start.1) | collective-permute-done | bytes 16416 | tf_op jit(solution)/shard_map/ppermute | solution.py:30
  137.7 5.1 %all-to-all-done.4 = f32[8,32,256]{2,1,0:T(8,128)} async-done(((f32[8,32,256]{2,1,0:T(8,128)}), f32[8,32,256]{2,1,0:T(8,128)}, u32[]{:S(2)}, u32[]{:S(2)}) %all-to-all-start.4) | async-done | bytes 262176 | tf_op jit(solution)/shard_map/all_to_all | solution.py:22
  142.8 1.6 %reduce_sum.37 = bf16[32,256]{1,0:T(8,128)(2,1)} reduce(f32[8,32,256]{2,1,0:T(8,128)} %all-to-all-done.4, f32[]{:T(128)} %constant.65.clone.1), dimensions={0}, to_apply=%region_1.2 | reduce | flops 57344 | bytes 278532 | tf_op jit(solution)/shard_map/reduce_sum | solution.py:326
  144.4 1.1 copy-done.1
  145.5 7.5 %table_grad.1 = bf16[2000,512]{1,0:T(8,128)(2,1)} custom-call(s32[3]{0:T(128)S(1)} %pad_add_fusion.where_ref, f32[4,8,256]{2,1,0:T(8,128)S(1)} %pad_maximum_fusion.5.w_ref, s32[1,512]{1,0:T(1,128)S(1)} %bitcast.25, bf16[512,640]{1,0:T(8,128)(2,1)S(1)} %copy-done.1, bf16[3072,256]{1,0:T(8,128)(2,1)S(1)} %get-tuple-element.12.e_ref.refs_0_.refs_1_, ...), custom_call_target="tpu_custom_call" | custom-call | flops 3145728000 | bytes 6144000 | tf_op jit(solution)/shard_map/table_grad/pallas_call | solution.py:262
  (26 shorter events, 2.1 us)
Async XLA Ops:
  0.6 26.2 %copy-start = (bf16[64,2048]{1,0:T(8,128)(2,1)S(1)}, bf16[64,2048]{1,0:T(8,128)(2,1)}, u32[]{:S(2)}) copy-start(bf16[64,2048]{1,0:T(8,128)(2,1)} %param.9) | copy-start | bytes 786436
  2.1 17.6 %all-to-all-start = ((bf16[8,32,256]{2,1,0:T(8,128)(2,1)}), bf16[8,32,256]{2,1,0:T(8,128)(2,1)S(1)}, u32[]{:S(2)}, u32[]{:S(2)}) async-start(bf16[8,32,256]{2,1,0:T(8,128)(2,1)} %broadcast_in_dim.42), calls=%async_computation | async-start | bytes 262144 | tf_op jit(solution)/shard_map/all_to_all | solution.py:22
  20.7 18.0 %copy-start.3 = (s32[256]{0:T(256)S(1)}, s32[256]{0:T(256)}, u32[]{:S(2)}) copy-start(s32[256]{0:T(256)} %param.7) | copy-start | bytes 3076
  20.7 18.0 %all-to-all-start.1 = ((bf16[8,256,256]{2,1,0:T(8,128)(2,1)}), bf16[8,256,256]{2,1,0:T(8,128)(2,1)S(1)}, u32[]{:S(2)}, u32[]{:S(2)}) async-start(bf16[8,256,256]{2,1,0:T(8,128)(2,1)} %broadcast_in_dim.43), calls=%async_computation.1 | async-start | bytes 2097152 | tf_op jit(solution)/shard_map/all_to_all | solution.py:22
  47.0 1.1 copy-start.4
  48.1 17.5 %all-to-all-start.2 = ((f32[64,4,256]{2,1,0:T(4,128)}), f32[64,4,256]{2,1,0:T(4,128)}, u32[]{:S(2)}, u32[]{:S(2)}) async-start(f32[64,4,256]{2,1,0:T(4,128)} %get-tuple-element.11.own_ref), calls=%async_computation.2 | async-start | bytes 524288 | tf_op jit(solution)/shard_map/all_to_all | solution.py:22
  56.4 52.6 %collective-permute-start.3 = (bf16[3072,256]{1,0:T(8,128)(2,1)}, bf16[3072,256]{1,0:T(8,128)(2,1)S(1)}, u32[]{:S(2)}, u32[]{:S(2)}) collective-permute-start(bf16[3072,256]{1,0:T(8,128)(2,1)} %copy-done.4), channel_id=1, source_target_pairs={{0,128},{128,0},{1,129},{129,1},{2,130},{130,2},{3,131},{131,3},{4... | collective-permute-start | bytes 4718600 | tf_op jit(solution)/shard_map/ppermute | solution.py:30
  65.6 38.1 %all-to-all-start.5 = ((bf16[256,2,640]{2,1,0:T(2,128)(2,1)}), bf16[256,2,640]{2,1,0:T(2,128)(2,1)}, u32[]{:S(2)}, u32[]{:S(2)}) async-start(bf16[256,2,640]{2,1,0:T(2,128)(2,1)} %reshape.96), calls=%async_computation.5 | async-start | bytes 1310720 | tf_op jit(solution)/shard_map/all_to_all | solution.py:22
  88.1 1.0 copy-start.2
  103.6 19.8 %all-to-all-start.3 = ((bf16[8,256,256]{2,1,0:T(8,128)(2,1)}), bf16[8,256,256]{2,1,0:T(8,128)(2,1)}, u32[]{:S(2)}, u32[]{:S(2)}) async-start(bf16[8,256,256]{2,1,0:T(8,128)(2,1)} %copy-done.2), calls=%async_computation.3 | async-start | bytes 2097152 | tf_op jit(solution)/shard_map/all_to_all | solution.py:22
  109.1 35.3 %collective-permute-start.2 = (bf16[3072,256]{1,0:T(8,128)(2,1)S(1)}, bf16[3072,256]{1,0:T(8,128)(2,1)}, u32[]{:S(2)}, u32[]{:S(2)}) collective-permute-start(bf16[3072,256]{1,0:T(8,128)(2,1)S(1)} %get-tuple-element.12.e_ref.refs_0_.refs_1_), channel_id=1, source_target_pairs={{0,64},{64,0},{1,65},{65,1},{2,66},{66,2},{3,67},{67,3},{4,68},{68... | collective-permute-start | bytes 4718600 | tf_op jit(solution)/shard_map/ppermute | solution.py:30
  109.1 35.3 %collective-permute-start.4 = (bf16[3072,256]{1,0:T(8,128)(2,1)S(1)}, bf16[3072,256]{1,0:T(8,128)(2,1)}, u32[]{:S(2)}, u32[]{:S(2)}) collective-permute-start(bf16[3072,256]{1,0:T(8,128)(2,1)S(1)} %collective-permute-done.3.refs_4_.refs_5_), channel_id=1, source_target_pairs={{0,64},{64,0},{1,65},{65,1},{2,66},{66,2},{3,67},{67,3},{4,68},{68... | collective-permute-start | bytes 4718600 | tf_op jit(solution)/shard_map/ppermute | solution.py:30
  112.3 20.0 %collective-permute-start = (f32[8,256]{1,0:T(8,128)S(1)}, f32[8,256]{1,0:T(8,128)S(1)}, u32[]{:S(2)}, u32[]{:S(2)}) collective-permute-start(f32[8,256]{1,0:T(8,128)S(1)} %get-tuple-element.17), channel_id=1, source_target_pairs={{0,64},{64,0},{1,65},{65,1},{2,66},{66,2},{3,67},{67,3},{4,68},{68... | collective-permute-start | bytes 24584 | tf_op jit(solution)/shard_map/ppermute | solution.py:30
  125.5 17.3 %all-to-all-start.4 = ((f32[8,32,256]{2,1,0:T(8,128)}), f32[8,32,256]{2,1,0:T(8,128)}, u32[]{:S(2)}, u32[]{:S(2)}) async-start(f32[8,32,256]{2,1,0:T(8,128)} %bitcast.29), calls=%async_computation.4 | async-start | bytes 524288 | tf_op jit(solution)/shard_map/all_to_all | solution.py:22
  132.3 5.3 %collective-permute-start.1 = (f32[2,8,256]{2,1,0:T(8,128)S(1)}, f32[2,8,256]{2,1,0:T(8,128)S(1)}, u32[]{:S(2)}, u32[]{:S(2)}) collective-permute-start(f32[2,8,256]{2,1,0:T(8,128)S(1)} %pad_maximum_fusion.6), channel_id=1, source_target_pairs={{0,128},{128,0},{1,129},{129,1},{2,130},{130,2},{3,131},{131,3},{4... | collective-permute-start | bytes 49160 | tf_op jit(solution)/shard_map/ppermute | solution.py:30
  144.4 1.1 copy-start.1

commit v3 on v2

--- a/solution.py
+++ b/solution.py
@@ -15,7 +15,7 @@
 VOCAB = ("y", "z", "xl")
 PLANE = ("y", "xl")
 CHUNK = 400
-PARAMS = pltpu.CompilerParams(vmem_limit_bytes=48 * 1024 * 1024)
+PARAMS = pltpu.CompilerParams(vmem_limit_bytes=24 * 1024 * 1024)
 
 
 def exchange(pieces, axes):
@@ -32,6 +32,98 @@
 
 def cost(flops, moved, special=0):
     return pl.CostEstimate(flops=flops, bytes_accessed=moved, transcendentals=special)
+
+
+def shift(value, axis, by):
+    size = lax.axis_size(axis)
+    return lax.ppermute(value, axis, [(i, (i + by) % size) for i in range(size)])
+
+
+def select_kernel(vocab_rows, where_ref, ids_ref, *refs):
+    packs, outs = refs[:4], refs[4:]
+    groups, count = ids_ref.shape
+    total = groups * count
+    line = jnp.concatenate([ids_ref[g : g + 1, :] for g in range(groups)], axis=1).astype(F32)
+    tall = jnp.broadcast_to(line, (8, total)).T[:, 0:1]
+
+    def parts(ids):
+        owner = jnp.floor((ids + 0.5) * (1.0 / vocab_rows))
+        spot = (ids - owner * vocab_rows).astype(I32) + 1
+        owner = owner.astype(I32)
+        plane = (owner >> 4) * 2 + (owner & 1)
+        turn = (((owner >> 1) & 7) - where_ref[3]) & 7
+        return owner, plane, turn, spot
+
+    owner, plane, turn, _ = parts(line)
+    owner_t, plane_t, turn_t, spot_t = parts(tall)
+    early = lax.broadcasted_iota(I32, (total, total), 0)
+    later = lax.broadcasted_iota(I32, (total, total), 1)
+    before = (owner_t == owner) & (early < later) & ((early >> 6) == (later >> 6))
+    rank = jnp.sum(jnp.where(before, 1.0, 0.0), axis=0, keepdims=True).astype(I32)
+    token = lax.broadcasted_iota(I32, (1, total), 1)
+    row = (token >> 6) * 2 + rank
+    slots = turn * 64 + plane * 8 + row
+    chosen = lax.broadcasted_iota(I32, (512, total), 0) == slots
+    cot = jnp.concatenate([p[...] for p in packs], axis=0)
+    picked = jnp.dot(jnp.where(chosen, 1.0, 0.0).astype(BF16), cot, preferred_element_type=F32)
+    picked = picked.astype(BF16)
+    lane = lax.broadcasted_iota(I32, (total, 128), 1)
+    base = turn_t * 16 + plane_t
+    digits = jnp.where(lane == base, spot_t >> 6, jnp.where(lane == base + 8, spot_t & 63, 0))
+    mark = lax.broadcasted_iota(I32, (64, total), 0) == turn * 8 + row
+    code = jnp.dot(
+        jnp.where(mark, 1.0, 0.0).astype(BF16),
+        digits.astype(F32).astype(BF16),
+        preferred_element_type=F32,
+    )
+    width = cot.shape[1]
+    code = jnp.concatenate([code, jnp.zeros((64, width - 128), F32)], axis=1).astype(BF16)
+    for k, out in enumerate(outs):
+        out[0:64, :] = picked[k * 64 : k * 64 + 64, :]
+        out[64:72, :] = code[k * 8 : k * 8 + 8, :]
+
+
+def select_call(where, ids, packs, vocab_rows):
+    count, wide = packs[0].shape
+    block = wide // 2
+    out = pl.BlockSpec((72, block), lambda i, s: (0, 0))
+    return pl.pallas_call(
+        functools.partial(select_kernel, vocab_rows),
+        grid_spec=pltpu.PrefetchScalarGridSpec(
+            num_scalar_prefetch=1,
+            grid=(1,),
+            in_specs=[
+                pl.BlockSpec(ids.shape, lambda i, s: (0, 0)),
+                *[pl.BlockSpec((count, block), lambda i, s: (0, s[2]))] * 4,
+            ],
+            out_specs=[out] * 8,
+        ),
+        out_shape=[jax.ShapeDtypeStruct((72, block), BF16)] * 8,
+        compiler_params=PARAMS,
+        cost_estimate=cost(2 * 512 * 256 * block, 2**20),
+        name="select",
+    )(where, ids, *packs)
+
+
+def regroup_kernel(*refs):
+    turns, out_ref = refs[:-1], refs[-1]
+    code = turns[0][64:72, :].astype(F32)
+    for turn in turns[1:]:
+        code += turn[64:72, :].astype(F32)
+    for p in range(out_ref.shape[0]):
+        for k, turn in enumerate(turns):
+            out_ref[p, k * 8 : k * 8 + 8, :] = turn[p * 8 : p * 8 + 8, :]
+        out_ref[p, 64:72, :] = code.astype(BF16)
+
+
+def regroup_call(turns):
+    return pl.pallas_call(
+        regroup_kernel,
+        out_shape=jax.ShapeDtypeStruct((8, *turns[0].shape), BF16),
+        compiler_params=PARAMS,
+        cost_estimate=cost(0, 2**20),
+        name="regroup",
+    )(*turns)
 
 
 def logits_kernel(where_ref, tgt_ref, got_ref, table_ref, near_ref, far_ref, stats_ref, hid, log, acc):
@@ -228,16 +320,9 @@
     out_ref = refs[-1]
     count = out_ref.shape[0]
     first = pl.program_id(0) * count
-    index = lax.broadcasted_iota(I32, (count, 256), 0) + first
-    near = index + where_ref[0]
-    slots = place_ref.shape[1]
-    match = jnp.concatenate(
-        [
-            jnp.where(index == place_ref[:, k : k + 256], 1.0, 0.0).astype(BF16)
-            for k in range(0, slots, 256)
-        ],
-        axis=1,
-    )
+    near = lax.broadcasted_iota(I32, (count, 256), 0) + (first + where_ref[0])
+    spots = lax.broadcasted_iota(I32, (count, place_ref.shape[1]), 0) + first
+    match = jnp.where(spots == place_ref[...], 1.0, 0.0).astype(BF16)
     total = jnp.dot(match, rows_ref[...], preferred_element_type=F32)
     for g in range(4):
         e = refs[2 * g][...].astype(F32)
@@ -252,8 +337,7 @@
 
 def table_call(where, w, place, rows, packs, count):
     tokens = packs[0].shape[1]
-    block = rows.shape[1] // 128 * 128
-    block = 512
+    block = rows.shape[1]
     specs, operands = [], []
     for pack in packs:
         specs.append(pl.BlockSpec((CHUNK, tokens), lambda i, s: (i, 0)))
@@ -279,44 +363,41 @@
     )(where, w, place, rows, *operands)
 
 
-def body(hidden, table, targets, input_ids, cotangent):
+def inner(hidden, table, targets, input_ids, cotangent):
     vocab_rows, width = table.shape
     ny, nz, nx = (lax.axis_size(a) for a in VOCAB)
     plane = ny * nx
     vocab_count = plane * nz
-    data_count = lax.axis_size(DP)
-    block = width // data_count
+    block = width // lax.axis_size(DP)
     xh, c = lax.axis_index("xh"), lax.axis_index("c")
-    where = jnp.stack([lax.axis_index(VOCAB) * vocab_rows, xh, c]).astype(I32)
+    where = jnp.stack([lax.axis_index(VOCAB) * vocab_rows, xh, c, lax.axis_index("z")]).astype(I32)
     tokens = hidden.shape[0]
     goal = targets.reshape(1, tokens)
 
-    owners = input_ids // vocab_rows
-    offsets = input_ids - owners * vocab_rows
-    count = input_ids.shape[0]
-    later = lax.broadcasted_iota(I32, (count, count), 0)
-    early = lax.broadcasted_iota(I32, (count, count), 1)
-    before = (owners[:, None] == owners[None, :]) & (early < later)
-    slot = owners * 2 + jnp.sum(before.astype(I32), axis=1)
-    chosen = lax.broadcasted_iota(I32, (2 * vocab_count, count), 0) == slot[None, :]
-    sent = jnp.dot(chosen.astype(BF16), cotangent, preferred_element_type=F32).astype(BF16)
-    spots = jnp.sum(jnp.where(chosen, offsets[None, :] + 1, 0), axis=1)
-    lane = lax.broadcasted_iota(I32, (2 * vocab_count, 128), 1)
-    code = jnp.where(lane == 0, (spots // 64)[:, None], jnp.where(lane == 1, (spots % 64)[:, None], 0))
-    code = code.astype(BF16)
-    sent = jnp.stack(
-        [jnp.concatenate([sent[:, d * block : (d + 1) * block], code], axis=1) for d in range(data_count)]
-    )
-    sent = sent.reshape(data_count * vocab_count, 2, block + 128)
+    half = width // 2
+    near_rows = lax.dynamic_slice_in_dim(cotangent, xh * half, half, 1)
+    far_rows = lax.dynamic_slice_in_dim(cotangent, (1 - xh) * half, half, 1)
+    far_rows = swap(far_rows, "xh")
+    ids = input_ids.reshape(1, -1)
+    ids = jnp.concatenate([ids, swap(ids, "c")], axis=0)
+    ids = jnp.concatenate([ids, swap(ids, "xh")], axis=0)
+    packs = (near_rows, swap(near_rows, "c"), far_rows, swap(far_rows, "c"))
+    turns = select_call(where, ids, packs, vocab_rows)
 
     mine = hidden.T
     stage = exchange(to_each(mine, nz), "z").reshape(-1, tokens)
+    stage, *turns = lax.optimization_barrier((stage, *turns))
     stage = exchange(to_each(stage, plane), PLANE)
-
+    turns = [shift(turn, "z", k) if k else turn for k, turn in enumerate(turns)]
+    mixed = regroup_call(turns)
+    stage, mixed = lax.optimization_barrier((stage, mixed))
+    got = exchange(mixed, PLANE)
     near, far, own = logits_call(where, goal, stage, table, vocab_count)
+    own, got = lax.optimization_barrier((own, got))
+
     stats = exchange(own, VOCAB)
+    far = swap(far, "xh")
     near_sib = swap(near, "c")
-    far = swap(far, "xh")
     far_sib = swap(far, "c")
     soft, hard = part_call(where, goal, near, table)
     part, loss, w = scale_call(where, goal, own, stats, soft, hard)
@@ -328,12 +409,15 @@
 
     w_near = jnp.stack([w, swap(w, "c")])
     w_all = jnp.concatenate([w_near, swap(w_near, "xh")], axis=0)
-
-    got = exchange(sent, ALL).reshape(-1, block + 128)
-    code = got[:, block:].astype(F32)
-    place = (code[:, 0] * 64 + code[:, 1]).astype(I32) - 1
+    code = got[:, -8:, :128].astype(F32).reshape(plane, 8, nz, 2, plane)
+    spot = lax.axis_index("y") * nx + lax.axis_index("xl")
+    here = lax.broadcasted_iota(I32, code.shape, 4) == spot
+    code = jnp.sum(jnp.where(here, code, 0.0), axis=4)
+    place = (code[..., 0] * 64 + code[..., 1]).astype(I32) - 1
+    place = place.transpose(0, 2, 1).reshape(plane, -1)
+    place = jnp.concatenate([place, jnp.full((plane, 8), -1, I32)], axis=1).reshape(1, -1)
     table_grad = table_call(
-        where, w_all, place.reshape(1, -1), got, (near, near_sib, far, far_sib), vocab_rows
+        where, w_all, place, got.reshape(-1, block), (near, near_sib, far, far_sib), vocab_rows
     )
     return loss.reshape(tokens), hidden_grad, table_grad
 
@@ -342,7 +426,7 @@
     fine = Mesh(mesh.devices.reshape(2, 2, 4, 8, 2), ALL)
     placed = (P(DP, VOCAB), P(VOCAB, None), P(DP), P(ALL), P(ALL, None))
     return jax.shard_map(
-        body,
+        inner,
         mesh=fine,
         in_specs=placed,
         out_specs=(P(DP), P(DP, VOCAB), P(VOCAB, DP)),

time: 155 us -> 184 us (1.19)
  blocking collectives: 0 us -> 41.6 us
  waiting for transfers between devices: 55.4 us -> 24.8 us
  starting transfers between devices: 47.6 us -> 60.5 us
  local copies, waits for them, and re-layouts: 12.1 us -> 19.9 us
  Pallas kernels: 28.9 us -> 26.2 us
    all_to_all x0 -> x1, blocking collectives: none -> 41.6 us  [exchange(): return lax.all_to_all(pieces, axes, 0, 0, tiled=True)]
    all_to_all x6 -> x5, waiting for transfers between devices: 52.2 us -> 12.3 us  [exchange(): return lax.all_to_all(pieces, axes, 0, 0, tiled=True)]
    ppermute x0 -> x7, starting transfers between devices: none -> 16.9 us  [shift(): lax.ppermute(value, axis, [(i, (i + by) % size) for i in range(size)])]
    unnamed x10 -> x22, local copies, waits for them, and re-layouts: 3.21 us -> 14.7 us
    all_to_all x6 -> x5, starting transfers between devices: 42.2 us -> 34.2 us  [exchange(): return lax.all_to_all(pieces, axes, 0, 0, tiled=True)]
    ppermute x0 -> x7, waiting for transfers between devices: none -> 5.9 us  [shift(): lax.ppermute(value, axis, [(i, (i + by) % size) for i in range(size)])]
    ppermute x5 -> x10, starting transfers between devices: 5.36 us -> 9.27 us  [swap(): return lax.ppermute(value, axis, [(0, 1), (1, 0)])]
    reshape x2 -> x3, local copies, waits for them, and re-layouts: 5.34 us -> 1.77 us  [the longest x1 1.61 us: inner(): code = got[:, -8:, :128].astype(F32).reshape(plane, 8, nz, 2, plane)]
  transfers between devices with their start and end apart: 11 -> 22, of which waited for: 7 -> 9; matrix products, arithmetic and copies ran while one was open for 10% -> 6% of each run, Pallas kernels for 9% -> 7%
where the time goes in v3:
time: 184 us; the launch traced here: 182 us
  starting transfers between devices  60.5 us (33%)
  blocking collectives  41.6 us (23%)
  Pallas kernels  26.2 us (14%)
  waiting for transfers between devices  24.8 us (13%)
  local copies, waits for them, and re-layouts  19.9 us (11%)
  other arithmetic  7.76 us (4%)
    all_to_all x1, blocking collectives, exchange(): return lax.all_to_all(pieces, axes, 0, 0, tiled=True)  41.6 us
    all_to_all x5, starting transfers between devices, exchange(): return lax.all_to_all(pieces, axes, 0, 0, tiled=True)  34.2 us
    ppermute x7, starting transfers between devices, shift(): lax.ppermute(value, axis, [(i, (i + by) % size) for i in range(size)])  16.9 us
    unnamed x22, local copies, waits for them, and re-layouts  14.7 us
    all_to_all x5, waiting for transfers between devices, exchange(): return lax.all_to_all(pieces, axes, 0, 0, tiled=True)  12.3 us
    ppermute x10, starting transfers between devices, swap(): return lax.ppermute(value, axis, [(0, 1), (1, 0)])  9.27 us
    pallas_call x1, Pallas kernels, part_call(): pl.pallas_call(part_kernel, grid_spec=pltpu.PrefetchScalarGridSpec(num_sc...  9.18 us
    pallas_call x1, Pallas kernels, table_call(): pl.pallas_call(table_kernel, grid_spec=pltpu.PrefetchScalarGridSpec(num_s...  7.84 us
  transfers between devices with their start and end apart: 22, of which 9 were waited for; matrix products, arithmetic and copies ran while one was open for 6% of the time, Pallas kernels for 7%

profile of v3, /device:TPU:8, one launch (start us, length us, event | category | flops | bytes accessed | tf_op | source)
XLA Modules:
  0.0 181.6 jit_solution(3413700081003734920)
XLA Ops:
  1.6 3.1 %collective-permute-start.3 = (bf16[64,1024]{1,0:T(8,128)(2,1)S(1)}, bf16[64,1024]{1,0:T(8,128)(2,1)S(1)}, u32[]{:S(2)}, u32[]{:S(2)}) collective-permute-start(bf16[64,1024]{1,0:T(8,128)(2,1)S(1)} %get-tuple-element.61), channel_id=1, source_target_pairs={{0,128},{128,0},{1,129},{129,1},{2,130},{130,2},{3,131},{131,3},{4... | collective-permute-start | bytes 393224 | tf_op jit(solution)/shard_map/ppermute | solution.py:30
  4.7 1.4 broadcast_in_dim.11
  6.1 8.5 %all-to-all-start = ((bf16[8,32,256]{2,1,0:T(8,128)(2,1)}), bf16[8,32,256]{2,1,0:T(8,128)(2,1)S(1)}, u32[]{:S(2)}, u32[]{:S(2)}) async-start(bf16[8,32,256]{2,1,0:T(8,128)(2,1)} %broadcast_in_dim.11), calls=%async_computation | async-start | bytes 262144 | tf_op jit(solution)/shard_map/all_to_all | solution.py:22
  17.1 4.5 %collective-permute-done.1 = s32[2,64]{1,0:T(2,128)S(1)} collective-permute-done((s32[2,64]{1,0:T(2,128)S(1)}, s32[2,64]{1,0:T(2,128)S(1)}, u32[]{:S(2)}, u32[]{:S(2)}) %collective-permute-start.1) | collective-permute-done | bytes 544 | tf_op jit(solution)/shard_map/ppermute | solution.py:30
  24.7 5.1 %all-to-all-start.1 = ((bf16[8,256,256]{2,1,0:T(8,128)(2,1)}), bf16[8,256,256]{2,1,0:T(8,128)(2,1)S(1)}, u32[]{:S(2)}, u32[]{:S(2)}) async-start(bf16[8,256,256]{2,1,0:T(8,128)(2,1)} %broadcast_in_dim.12), calls=%async_computation.1 | async-start | bytes 2097152 | tf_op jit(solution)/shard_map/all_to_all | solution.py:22
  29.8 1.8 %collective-permute-start.5 = (bf16[72,512]{1,0:T(8,128)(2,1)S(1)}, bf16[72,512]{1,0:T(8,128)(2,1)S(1)}, u32[]{:S(2)}, u32[]{:S(2)}) collective-permute-start(bf16[72,512]{1,0:T(8,128)(2,1)S(1)} %get-tuple-element.42), channel_id=1, source_target_pairs={{0,2},{2,4},{4,6},{6,8},{8,10},{10,12},{12,14},{14,0},{1,3},{3,5},... | collective-permute-start | bytes 221192 | tf_op jit(solution)/shard_map/ppermute | solution.py:39
  31.6 2.4 %collective-permute-start.6 = (bf16[72,512]{1,0:T(8,128)(2,1)S(1)}, bf16[72,512]{1,0:T(8,128)(2,1)S(1)}, u32[]{:S(2)}, u32[]{:S(2)}) collective-permute-start(bf16[72,512]{1,0:T(8,128)(2,1)S(1)} %get-tuple-element.43), channel_id=1, source_target_pairs={{0,4},{2,6},{4,8},{6,10},{8,12},{10,14},{12,0},{14,2},{1,5},{3,7},... | collective-permute-start | bytes 221192 | tf_op jit(solution)/shard_map/ppermute | solution.py:39
  34.0 2.7 %collective-permute-start.7 = (bf16[72,512]{1,0:T(8,128)(2,1)S(1)}, bf16[72,512]{1,0:T(8,128)(2,1)S(1)}, u32[]{:S(2)}, u32[]{:S(2)}) collective-permute-start(bf16[72,512]{1,0:T(8,128)(2,1)S(1)} %get-tuple-element.44), channel_id=1, source_target_pairs={{0,6},{2,8},{4,10},{6,12},{8,14},{10,0},{12,2},{14,4},{1,7},{3,9},... | collective-permute-start | bytes 221192 | tf_op jit(solution)/shard_map/ppermute | solution.py:39
  36.7 2.4 %collective-permute-start.8 = (bf16[72,512]{1,0:T(8,128)(2,1)S(1)}, bf16[72,512]{1,0:T(8,128)(2,1)S(1)}, u32[]{:S(2)}, u32[]{:S(2)}) collective-permute-start(bf16[72,512]{1,0:T(8,128)(2,1)S(1)} %get-tuple-element.45), channel_id=1, source_target_pairs={{0,8},{2,10},{4,12},{6,14},{8,0},{10,2},{12,4},{14,6},{1,9},{3,11}... | collective-permute-start | bytes 221192 | tf_op jit(solution)/shard_map/ppermute | solution.py:39
  39.0 2.7 %collective-permute-start.9 = (bf16[72,512]{1,0:T(8,128)(2,1)S(1)}, bf16[72,512]{1,0:T(8,128)(2,1)S(1)}, u32[]{:S(2)}, u32[]{:S(2)}) collective-permute-start(bf16[72,512]{1,0:T(8,128)(2,1)S(1)} %get-tuple-element.46), channel_id=1, source_target_pairs={{0,10},{2,12},{4,14},{6,0},{8,2},{10,4},{12,6},{14,8},{1,11},{3,13... | collective-permute-start | bytes 221192 | tf_op jit(solution)/shard_map/ppermute | solution.py:39
  41.7 3.6 %collective-permute-start.10 = (bf16[72,512]{1,0:T(8,128)(2,1)S(1)}, bf16[72,512]{1,0:T(8,128)(2,1)S(1)}, u32[]{:S(2)}, u32[]{:S(2)}) collective-permute-start(bf16[72,512]{1,0:T(8,128)(2,1)S(1)} %get-tuple-element.47), channel_id=1, source_target_pairs={{0,12},{2,14},{4,0},{6,2},{8,4},{10,6},{12,8},{14,10},{1,13},{3,15... | collective-permute-start | bytes 221192 | tf_op jit(solution)/shard_map/ppermute | solution.py:39
  45.3 1.5 collective-permute-start.11
  46.7 3.8 %collective-permute-done.9.refs_5_ = bf16[72,512]{1,0:T(8,128)(2,1)S(1)} collective-permute-done((bf16[72,512]{1,0:T(8,128)(2,1)S(1)}, bf16[72,512]{1,0:T(8,128)(2,1)S(1)}, u32[]{:S(2)}, u32[]{:S(2)}) %collective-permute-start.9) | collective-permute-done | bytes 73760 | tf_op jit(solution)/shard_map/ppermute | solution.py:39
  50.5 1.4 collective-permute-done.10.refs_6_
  53.5 3.3 %copy-done = bf16[2000,2048]{1,0:T(8,128)(2,1)S(1)} copy-done((bf16[2000,2048]{1,0:T(8,128)(2,1)S(1)}, bf16[2000,2048]{1,0:T(8,128)(2,1)}, u32[]{:S(2)}) %copy-start) | copy-done | bytes 8192024
  56.8 5.8 %logits.1 = (bf16[3072,256]{1,0:T(8,128)(2,1)S(1)}, bf16[3072,256]{1,0:T(8,128)(2,1)}, f32[64,4,256]{2,1,0:T(4,128)}) custom-call(s32[4]{0:T(128)S(1)} %pad_add_fusion.2.where_ref, s32[1,256]{1,0:T(1,128)S(1)} %bitcast.20, bf16[8,256,256]{2,1,0:T(8,128)(2,1)S(1)} %all-to-all-done.1.got_ref, bf16[2000,2048]{1,0:T(8,128)(2,1)S(1)} %copy-done), custom_call_target="tpu_custom_call" | custom-call | flops 2097152000 | bytes 11337728 | tf_op jit(solution)/shard_map/logits/pallas_call | solution.py:181
  62.6 2.0 %collective-permute-start.15 = (bf16[3072,256]{1,0:T(8,128)(2,1)}, bf16[3072,256]{1,0:T(8,128)(2,1)S(1)}, u32[]{:S(2)}, u32[]{:S(2)}) collective-permute-start(bf16[3072,256]{1,0:T(8,128)(2,1)} %get-tuple-element.60), channel_id=1, source_target_pairs={{0,128},{128,0},{1,129},{129,1},{2,130},{130,2},{3,131},{131,3},{4... | collective-permute-start | bytes 4718600 | tf_op jit(solution)/shard_map/ppermute | solution.py:30
  64.6 41.6 %all_to_all.30 = bf16[8,72,512]{2,1,0:T(8,128)(2,1)} all-to-all(bf16[8,72,512]{2,1,0:T(8,128)(2,1)S(1)} %copy-done.4), channel_id=1, replica_groups=mesh['xh'=2,'c'=2,'y'=4,'z'=8,'xl'=2] {'y','xl'}, dimensions={0} | all-to-all | bytes 1179648 | tf_op jit(solution)/shard_map/all_to_all | solution.py:22
  106.2 8.2 %all-to-all-start.3 = ((f32[64,4,256]{2,1,0:T(4,128)}), f32[64,4,256]{2,1,0:T(4,128)S(1)}, u32[]{:S(2)}, u32[]{:S(2)}) async-start(f32[64,4,256]{2,1,0:T(4,128)} %get-tuple-element.52.own_ref), calls=%async_computation.3 | async-start | bytes 524288 | tf_op jit(solution)/shard_map/all_to_all | solution.py:22
  114.4 3.3 %copy-done.1 = bf16[2000,2048]{1,0:T(8,128)(2,1)S(1)} copy-done((bf16[2000,2048]{1,0:T(8,128)(2,1)S(1)}, bf16[2000,2048]{1,0:T(8,128)(2,1)}, u32[]{:S(2)}) %copy-start.1) | copy-done | bytes 8192024
  117.7 9.2 %part.1 = (f32[8,256,256]{2,1,0:T(8,128)S(1)}, bf16[8,256,256]{2,1,0:T(8,128)(2,1)S(1)}) custom-call(s32[4]{0:T(128)S(1)} %pad_add_fusion.2.where_ref, s32[1,256]{1,0:T(1,128)S(1)} %bitcast.21, bf16[3072,256]{1,0:T(8,128)(2,1)S(1)} %get-tuple-element.53.e_ref.refs_0_.refs_1_, bf16[2000,2048]{1,0:T(8,128)(2,1)S(1)} %copy-done.1), custom_call_target="tpu_custom_call" | custom-call | flops 4194304000 | bytes 11337728 | tf_op jit(solution)/shard_map/part/pallas_call | solution.py:238
  129.3 1.6 copy-done.6
  132.1 2.3 %scale.1 = (bf16[8,256,256]{2,1,0:T(8,128)(2,1)S(1)}, f32[1,256]{1,0:T(1,128)}, f32[8,256]{1,0:T(8,128)S(1)}) custom-call(s32[4]{0:T(128)S(1)} %pad_add_fusion.2.where_ref, s32[1,256]{1,0:T(1,128)S(1)} %bitcast.22, f32[64,4,256]{2,1,0:T(4,128)} %get-tuple-element.52.own_ref, f32[64,4,256]{2,1,0:T(4,128)S(1)} %all-to-all-done.3.stats_ref, ...), custom_call_target="tpu_custom_call" | custom-call | flops 2097152 | bytes 4194304 | tf_op jit(solution)/shard_map/scale/pallas_call | solution.py:289
  135.4 5.8 %all-to-all-start.4 = ((bf16[8,256,256]{2,1,0:T(8,128)(2,1)}), bf16[8,256,256]{2,1,0:T(8,128)(2,1)}, u32[]{:S(2)}, u32[]{:S(2)}) async-start(bf16[8,256,256]{2,1,0:T(8,128)(2,1)} %copy-done.9), calls=%async_computation.4 | async-start | bytes 2097152 | tf_op jit(solution)/shard_map/all_to_all | solution.py:22
  142.4 1.6 reshape.53
  144.1 8.6 %all-to-all-done.4 = bf16[8,256,256]{2,1,0:T(8,128)(2,1)} async-done(((bf16[8,256,256]{2,1,0:T(8,128)(2,1)}), bf16[8,256,256]{2,1,0:T(8,128)(2,1)}, u32[]{:S(2)}, u32[]{:S(2)}) %all-to-all-start.4) | async-done | bytes 1048608 | tf_op jit(solution)/shard_map/all_to_all | solution.py:22
  152.8 2.1 %convert_reduce_fusion = f32[256,256]{1,0:T(8,128)} fusion(bf16[8,256,256]{2,1,0:T(8,128)(2,1)} %all-to-all-done.4), kind=kLoop, calls=%fused_computation | loop fusion | flops 983040 | bytes 1310720 | tf_op jit(solution)/shard_map/reduce_sum | solution.py:406
  154.9 6.7 %all-to-all-start.5 = ((f32[8,32,256]{2,1,0:T(8,128)}), f32[8,32,256]{2,1,0:T(8,128)S(1)}, u32[]{:S(2)}, u32[]{:S(2)}) async-start(f32[8,32,256]{2,1,0:T(8,128)} %bitcast.9), calls=%async_computation.5 | async-start | bytes 524288 | tf_op jit(solution)/shard_map/all_to_all | solution.py:22
  161.6 1.7 select_reduce_fusion
  163.3 2.5 %collective-permute-start.13 = (f32[2,8,256]{2,1,0:T(8,128)S(1)}, f32[2,8,256]{2,1,0:T(8,128)S(1)}, u32[]{:S(2)}, u32[]{:S(2)}) collective-permute-start(f32[2,8,256]{2,1,0:T(8,128)S(1)} %pad_maximum_fusion.1), channel_id=1, source_target_pairs={{0,128},{128,0},{1,129},{129,1},{2,130},{130,2},{3,131},{131,3},{4... | collective-permute-start | bytes 49160 | tf_op jit(solution)/shard_map/ppermute | solution.py:30
  168.6 3.5 %all-to-all-done.5 = f32[8,32,256]{2,1,0:T(8,128)S(1)} async-done(((f32[8,32,256]{2,1,0:T(8,128)}), f32[8,32,256]{2,1,0:T(8,128)S(1)}, u32[]{:S(2)}, u32[]{:S(2)}) %all-to-all-start.5) | async-done | bytes 262176 | tf_op jit(solution)/shard_map/all_to_all | solution.py:22
  173.7 7.8 %table_grad.1 = bf16[2000,512]{1,0:T(8,128)(2,1)} custom-call(s32[4]{0:T(128)S(1)} %pad_add_fusion.2.where_ref, f32[4,8,256]{2,1,0:T(8,128)S(1)} %pad_maximum_fusion.w_ref, s32[1,576]{1,0:T(1,128)S(1)} %reshape.50.place_ref, bf16[576,512]{1,0:T(8,128)(2,1)S(1)} %bitcast.17, bf16[3072,256]{1,0:T(8,128)(2,1)S(1)} %get-tuple-element.53.e_ref.refs_0_.refs_1_, ...), custom_call_target="tpu_custom_call" | custom-call | flops 3145728000 | bytes 6144000 | tf_op jit(solution)/shard_map/table_grad/pallas_call | solution.py:346
  (60 shorter events, 18.5 us)
Async XLA Ops:
  1.6 15.4 %collective-permute-start.3 = (bf16[64,1024]{1,0:T(8,128)(2,1)S(1)}, bf16[64,1024]{1,0:T(8,128)(2,1)S(1)}, u32[]{:S(2)}, u32[]{:S(2)}) collective-permute-start(bf16[64,1024]{1,0:T(8,128)(2,1)S(1)} %get-tuple-element.61), channel_id=1, source_target_pairs={{0,128},{128,0},{1,129},{129,1},{2,130},{130,2},{3,131},{131,3},{4... | collective-permute-start | bytes 393224 | tf_op jit(solution)/shard_map/ppermute | solution.py:30
  6.1 17.5 %all-to-all-start = ((bf16[8,32,256]{2,1,0:T(8,128)(2,1)}), bf16[8,32,256]{2,1,0:T(8,128)(2,1)S(1)}, u32[]{:S(2)}, u32[]{:S(2)}) async-start(bf16[8,32,256]{2,1,0:T(8,128)(2,1)} %broadcast_in_dim.11), calls=%async_computation | async-start | bytes 262144 | tf_op jit(solution)/shard_map/all_to_all | solution.py:22
  14.6 1.3 collective-permute-start
  14.6 7.7 %collective-permute-start.2 = (bf16[64,1024]{1,0:T(8,128)(2,1)S(1)}, bf16[64,1024]{1,0:T(8,128)(2,1)S(1)}, u32[]{:S(2)}, u32[]{:S(2)}) collective-permute-start(bf16[64,1024]{1,0:T(8,128)(2,1)S(1)} %get-tuple-element.62.refs_0_), channel_id=1, source_target_pairs={{0,64},{64,0},{1,65},{65,1},{2,66},{66,2},{3,67},{67,3},{4,68},{68... | collective-permute-start | bytes 393224 | tf_op jit(solution)/shard_map/ppermute | solution.py:30
  16.5 5.1 %collective-permute-start.1 = (s32[2,64]{1,0:T(2,128)S(1)}, s32[2,64]{1,0:T(2,128)S(1)}, u32[]{:S(2)}, u32[]{:S(2)}) collective-permute-start(s32[2,64]{1,0:T(2,128)S(1)} %pad_add_fusion.1), channel_id=1, source_target_pairs={{0,128},{128,0},{1,129},{129,1},{2,130},{130,2},{3,131},{131,3},{4... | collective-permute-start | bytes 1544 | tf_op jit(solution)/shard_map/ppermute | solution.py:30
  17.1 5.2 %collective-permute-start.4 = (bf16[64,1024]{1,0:T(8,128)(2,1)S(1)}, bf16[64,1024]{1,0:T(8,128)(2,1)S(1)}, u32[]{:S(2)}, u32[]{:S(2)}) collective-permute-start(bf16[64,1024]{1,0:T(8,128)(2,1)S(1)} %collective-permute-done.3.refs_2_), channel_id=1, source_target_pairs={{0,64},{64,0},{1,65},{65,1},{2,66},{66,2},{3,67},{67,3},{4,68},{68... | collective-permute-start | bytes 393224 | tf_op jit(solution)/shard_map/ppermute | solution.py:30
  24.7 28.8 %copy-start.10 = (s32[256]{0:T(256)S(1)}, s32[256]{0:T(256)}, u32[]{:S(2)}) copy-start(s32[256]{0:T(256)} %param.7) | copy-start | bytes 3076
  24.7 28.8 %all-to-all-start.1 = ((bf16[8,256,256]{2,1,0:T(8,128)(2,1)}), bf16[8,256,256]{2,1,0:T(8,128)(2,1)S(1)}, u32[]{:S(2)}, u32[]{:S(2)}) async-start(bf16[8,256,256]{2,1,0:T(8,128)(2,1)} %broadcast_in_dim.12), calls=%async_computation.1 | async-start | bytes 2097152 | tf_op jit(solution)/shard_map/all_to_all | solution.py:22
  29.8 11.9 %collective-permute-start.5 = (bf16[72,512]{1,0:T(8,128)(2,1)S(1)}, bf16[72,512]{1,0:T(8,128)(2,1)S(1)}, u32[]{:S(2)}, u32[]{:S(2)}) collective-permute-start(bf16[72,512]{1,0:T(8,128)(2,1)S(1)} %get-tuple-element.42), channel_id=1, source_target_pairs={{0,2},{2,4},{4,6},{6,8},{8,10},{10,12},{12,14},{14,0},{1,3},{3,5},... | collective-permute-start | bytes 221192 | tf_op jit(solution)/shard_map/ppermute | solution.py:39
  31.6 13.7 %collective-permute-start.6 = (bf16[72,512]{1,0:T(8,128)(2,1)S(1)}, bf16[72,512]{1,0:T(8,128)(2,1)S(1)}, u32[]{:S(2)}, u32[]{:S(2)}) collective-permute-start(bf16[72,512]{1,0:T(8,128)(2,1)S(1)} %get-tuple-element.43), channel_id=1, source_target_pairs={{0,4},{2,6},{4,8},{6,10},{8,12},{10,14},{12,0},{14,2},{1,5},{3,7},... | collective-permute-start | bytes 221192 | tf_op jit(solution)/shard_map/ppermute | solution.py:39
  34.0 12.7 %collective-permute-start.7 = (bf16[72,512]{1,0:T(8,128)(2,1)S(1)}, bf16[72,512]{1,0:T(8,128)(2,1)S(1)}, u32[]{:S(2)}, u32[]{:S(2)}) collective-permute-start(bf16[72,512]{1,0:T(8,128)(2,1)S(1)} %get-tuple-element.44), channel_id=1, source_target_pairs={{0,6},{2,8},{4,10},{6,12},{8,14},{10,0},{12,2},{14,4},{1,7},{3,9},... | collective-permute-start | bytes 221192 | tf_op jit(solution)/shard_map/ppermute | solution.py:39
  36.7 10.1 %collective-permute-start.8 = (bf16[72,512]{1,0:T(8,128)(2,1)S(1)}, bf16[72,512]{1,0:T(8,128)(2,1)S(1)}, u32[]{:S(2)}, u32[]{:S(2)}) collective-permute-start(bf16[72,512]{1,0:T(8,128)(2,1)S(1)} %get-tuple-element.45), channel_id=1, source_target_pairs={{0,8},{2,10},{4,12},{6,14},{8,0},{10,2},{12,4},{14,6},{1,9},{3,11}... | collective-permute-start | bytes 221192 | tf_op jit(solution)/shard_map/ppermute | solution.py:39
  39.0 11.5 %collective-permute-start.9 = (bf16[72,512]{1,0:T(8,128)(2,1)S(1)}, bf16[72,512]{1,0:T(8,128)(2,1)S(1)}, u32[]{:S(2)}, u32[]{:S(2)}) collective-permute-start(bf16[72,512]{1,0:T(8,128)(2,1)S(1)} %get-tuple-element.46), channel_id=1, source_target_pairs={{0,10},{2,12},{4,14},{6,0},{8,2},{10,4},{12,6},{14,8},{1,11},{3,13... | collective-permute-start | bytes 221192 | tf_op jit(solution)/shard_map/ppermute | solution.py:39
  41.7 10.2 %collective-permute-start.10 = (bf16[72,512]{1,0:T(8,128)(2,1)S(1)}, bf16[72,512]{1,0:T(8,128)(2,1)S(1)}, u32[]{:S(2)}, u32[]{:S(2)}) collective-permute-start(bf16[72,512]{1,0:T(8,128)(2,1)S(1)} %get-tuple-element.47), channel_id=1, source_target_pairs={{0,12},{2,14},{4,0},{6,2},{8,4},{10,6},{12,8},{14,10},{1,13},{3,15... | collective-permute-start | bytes 221192 | tf_op jit(solution)/shard_map/ppermute | solution.py:39
  45.3 7.4 %collective-permute-start.11 = (bf16[72,512]{1,0:T(8,128)(2,1)S(1)}, bf16[72,512]{1,0:T(8,128)(2,1)S(1)}, u32[]{:S(2)}, u32[]{:S(2)}) collective-permute-start(bf16[72,512]{1,0:T(8,128)(2,1)S(1)} %get-tuple-element.48), channel_id=1, source_target_pairs={{0,14},{2,0},{4,2},{6,4},{8,6},{10,8},{12,10},{14,12},{1,15},{3,1}... | collective-permute-start | bytes 221192 | tf_op jit(solution)/shard_map/ppermute | solution.py:39
  53.5 3.3 %copy-start = (bf16[2000,2048]{1,0:T(8,128)(2,1)S(1)}, bf16[2000,2048]{1,0:T(8,128)(2,1)}, u32[]{:S(2)}) copy-start(bf16[2000,2048]{1,0:T(8,128)(2,1)} %table_ref.3) | copy-start | bytes 24576004
  56.8 7.8 %copy-start.4 = (bf16[8,72,512]{2,1,0:T(8,128)(2,1)S(1)}, bf16[8,72,512]{2,1,0:T(8,128)(2,1)}, u32[]{:S(2)}) copy-start(bf16[8,72,512]{2,1,0:T(8,128)(2,1)} %copy-done.3) | copy-start | bytes 1769476
  62.6 78.6 %collective-permute-start.15 = (bf16[3072,256]{1,0:T(8,128)(2,1)}, bf16[3072,256]{1,0:T(8,128)(2,1)S(1)}, u32[]{:S(2)}, u32[]{:S(2)}) collective-permute-start(bf16[3072,256]{1,0:T(8,128)(2,1)} %get-tuple-element.60), channel_id=1, source_target_pairs={{0,128},{128,0},{1,129},{129,1},{2,130},{130,2},{3,131},{131,3},{4... | collective-permute-start | bytes 4718600 | tf_op jit(solution)/shard_map/ppermute | solution.py:30
  106.2 23.1 %all-to-all-start.3 = ((f32[64,4,256]{2,1,0:T(4,128)}), f32[64,4,256]{2,1,0:T(4,128)S(1)}, u32[]{:S(2)}, u32[]{:S(2)}) async-start(f32[64,4,256]{2,1,0:T(4,128)} %get-tuple-element.52.own_ref), calls=%async_computation.3 | async-start | bytes 524288 | tf_op jit(solution)/shard_map/all_to_all | solution.py:22
  114.4 3.3 %copy-start.1 = (bf16[2000,2048]{1,0:T(8,128)(2,1)S(1)}, bf16[2000,2048]{1,0:T(8,128)(2,1)}, u32[]{:S(2)}) copy-start(bf16[2000,2048]{1,0:T(8,128)(2,1)} %table_ref.3) | copy-start | bytes 24576004
  126.9 1.3 copy-start.5
  128.3 1.0 copy-start.7
  129.3 1.6 copy-start.6
  130.9 1.2 copy-start.8
  134.4 1.0 copy-start.9
  135.4 17.4 %all-to-all-start.4 = ((bf16[8,256,256]{2,1,0:T(8,128)(2,1)}), bf16[8,256,256]{2,1,0:T(8,128)(2,1)}, u32[]{:S(2)}, u32[]{:S(2)}) async-start(bf16[8,256,256]{2,1,0:T(8,128)(2,1)} %copy-done.9), calls=%async_computation.4 | async-start | bytes 2097152 | tf_op jit(solution)/shard_map/all_to_all | solution.py:22
  141.2 31.5 %collective-permute-start.14 = (bf16[3072,256]{1,0:T(8,128)(2,1)S(1)}, bf16[3072,256]{1,0:T(8,128)(2,1)}, u32[]{:S(2)}, u32[]{:S(2)}) collective-permute-start(bf16[3072,256]{1,0:T(8,128)(2,1)S(1)} %get-tuple-element.53.e_ref.refs_0_.refs_1_), channel_id=1, source_target_pairs={{0,64},{64,0},{1,65},{65,1},{2,66},{66,2},{3,67},{67,3},{4,68},{68... | collective-permute-start | bytes 4718600 | tf_op jit(solution)/shard_map/ppermute | solution.py:30
  141.2 31.5 %collective-permute-start.16 = (bf16[3072,256]{1,0:T(8,128)(2,1)S(1)}, bf16[3072,256]{1,0:T(8,128)(2,1)}, u32[]{:S(2)}, u32[]{:S(2)}) collective-permute-start(bf16[3072,256]{1,0:T(8,128)(2,1)S(1)} %collective-permute-done.15.refs_4_.refs_5_), channel_id=1, source_target_pairs={{0,64},{64,0},{1,65},{65,1},{2,66},{66,2},{3,67},{67,3},{4,68},{68... | collective-permute-start | bytes 4718600 | tf_op jit(solution)/shard_map/ppermute | solution.py:30
  144.0 19.2 %collective-permute-start.12 = (f32[8,256]{1,0:T(8,128)S(1)}, f32[8,256]{1,0:T(8,128)S(1)}, u32[]{:S(2)}, u32[]{:S(2)}) collective-permute-start(f32[8,256]{1,0:T(8,128)S(1)} %get-tuple-element.58), channel_id=1, source_target_pairs={{0,64},{64,0},{1,65},{65,1},{2,66},{66,2},{3,67},{67,3},{4,68},{68... | collective-permute-start | bytes 24584 | tf_op jit(solution)/shard_map/ppermute | solution.py:30
  154.9 17.2 %all-to-all-start.5 = ((f32[8,32,256]{2,1,0:T(8,128)}), f32[8,32,256]{2,1,0:T(8,128)S(1)}, u32[]{:S(2)}, u32[]{:S(2)}) async-start(f32[8,32,256]{2,1,0:T(8,128)} %bitcast.9), calls=%async_computation.5 | async-start | bytes 524288 | tf_op jit(solution)/shard_map/all_to_all | solution.py:22
  163.3 5.3 %collective-permute-start.13 = (f32[2,8,256]{2,1,0:T(8,128)S(1)}, f32[2,8,256]{2,1,0:T(8,128)S(1)}, u32[]{:S(2)}, u32[]{:S(2)}) collective-permute-start(f32[2,8,256]{2,1,0:T(8,128)S(1)} %pad_maximum_fusion.1), channel_id=1, source_target_pairs={{0,128},{128,0},{1,129},{129,1},{2,130},{130,2},{3,131},{131,3},{4... | collective-permute-start | bytes 49160 | tf_op jit(solution)/shard_map/ppermute | solution.py:30
  172.7 1.1 copy-start.2
  (1 other events, 0.8 us)

commit v4 on v3

--- a/solution.py
+++ b/solution.py
@@ -15,7 +15,7 @@
 VOCAB = ("y", "z", "xl")
 PLANE = ("y", "xl")
 CHUNK = 400
-PARAMS = pltpu.CompilerParams(vmem_limit_bytes=24 * 1024 * 1024)
+PARAMS = pltpu.CompilerParams(vmem_limit_bytes=16 * 1024 * 1024)
 
 
 def exchange(pieces, axes):
@@ -34,16 +34,43 @@
     return pl.CostEstimate(flops=flops, bytes_accessed=moved, transcendentals=special)
 
 
-def shift(value, axis, by):
-    size = lax.axis_size(axis)
-    return lax.ppermute(value, axis, [(i, (i + by) % size) for i in range(size)])
-
-
-def select_kernel(vocab_rows, where_ref, ids_ref, *refs):
-    packs, outs = refs[:4], refs[4:]
-    groups, count = ids_ref.shape
-    total = groups * count
-    line = jnp.concatenate([ids_ref[g : g + 1, :] for g in range(groups)], axis=1).astype(F32)
+def partner(value, bit):
+    size = lax.axis_size("z")
+    return lax.ppermute(value, "z", [(i, i ^ bit) for i in range(size)])
+
+
+def join_kernel(cuts, *refs):
+    out, at = refs[-1], 0
+    for ref, (first, size) in zip(refs, cuts):
+        out[at : at + size, :] = ref[first : first + size, :]
+        at += size
+
+
+def join_call(*parts):
+    cuts = tuple((first, size) for _, first, size in parts)
+    shape = (sum(size for _, size in cuts), parts[0][0].shape[1])
+    return pl.pallas_call(
+        functools.partial(join_kernel, cuts),
+        out_shape=jax.ShapeDtypeStruct(shape, BF16),
+        compiler_params=PARAMS,
+        cost_estimate=cost(10**6, 2**19),
+        name="join",
+    )(*(array for array, _, _ in parts))
+
+
+def select_kernel(vocab_rows, where_ref, *refs):
+    packs = refs[:4]
+    outs = refs[4:]
+    count = packs[0].shape[0] - 8
+    total = 4 * count
+    line = jnp.concatenate(
+        [
+            p[count : count + 8, 0:128].astype(F32)[:, 0:count]
+            for p in packs
+        ],
+        axis=1,
+    )
+    line = line[0:1, :] * 16384.0 + line[1:2, :] * 128.0 + line[2:3, :]
     tall = jnp.broadcast_to(line, (8, total)).T[:, 0:1]
 
     def parts(ids):
@@ -51,7 +78,7 @@
         spot = (ids - owner * vocab_rows).astype(I32) + 1
         owner = owner.astype(I32)
         plane = (owner >> 4) * 2 + (owner & 1)
-        turn = (((owner >> 1) & 7) - where_ref[3]) & 7
+        turn = ((owner >> 1) & 7) ^ where_ref[3]
         return owner, plane, turn, spot
 
     owner, plane, turn, _ = parts(line)
@@ -64,66 +91,46 @@
     row = (token >> 6) * 2 + rank
     slots = turn * 64 + plane * 8 + row
     chosen = lax.broadcasted_iota(I32, (512, total), 0) == slots
-    cot = jnp.concatenate([p[...] for p in packs], axis=0)
+    cot = jnp.concatenate([p[0:count, :] for p in packs], axis=0)
     picked = jnp.dot(jnp.where(chosen, 1.0, 0.0).astype(BF16), cot, preferred_element_type=F32)
-    picked = picked.astype(BF16)
     lane = lax.broadcasted_iota(I32, (total, 128), 1)
     base = turn_t * 16 + plane_t
     digits = jnp.where(lane == base, spot_t >> 6, jnp.where(lane == base + 8, spot_t & 63, 0))
-    mark = lax.broadcasted_iota(I32, (64, total), 0) == turn * 8 + row
+    mark = lax.broadcasted_iota(I32, (16, total), 0) == row
     code = jnp.dot(
         jnp.where(mark, 1.0, 0.0).astype(BF16),
         digits.astype(F32).astype(BF16),
         preferred_element_type=F32,
     )
-    width = cot.shape[1]
-    code = jnp.concatenate([code, jnp.zeros((64, width - 128), F32)], axis=1).astype(BF16)
-    for k, out in enumerate(outs):
-        out[0:64, :] = picked[k * 64 : k * 64 + 64, :]
-        out[64:72, :] = code[k * 8 : k * 8 + 8, :]
-
-
-def select_call(where, ids, packs, vocab_rows):
-    count, wide = packs[0].shape
+    code = jnp.concatenate([code, jnp.zeros((16, 128), F32)], axis=1).astype(BF16)
+    far, middle, one, own, mine = outs
+    for q in range(8):
+        out, at = ((own, 0), (one, 0), (middle, 0), (middle, 128))[q] if q < 4 else (far, (q - 4) * 128)
+        for p in range(8):
+            piece = picked[q * 64 + p * 8 : q * 64 + p * 8 + 8, :]
+            piece = jnp.concatenate([piece[:, 0:256], piece[:, 256:512]], axis=0)
+            out[at + p * 16 : at + p * 16 + 16, :] = piece.astype(BF16)
+    far[512:528, :] = code
+    mine[...] = code
+
+
+def select_call(where, packs, vocab_rows):
+    rows, wide = packs[0].shape
     block = wide // 2
-    out = pl.BlockSpec((72, block), lambda i, s: (0, 0))
+    sizes = (528, 256, 128, 128, 16)
     return pl.pallas_call(
         functools.partial(select_kernel, vocab_rows),
         grid_spec=pltpu.PrefetchScalarGridSpec(
             num_scalar_prefetch=1,
             grid=(1,),
-            in_specs=[
-                pl.BlockSpec(ids.shape, lambda i, s: (0, 0)),
-                *[pl.BlockSpec((count, block), lambda i, s: (0, s[2]))] * 4,
-            ],
-            out_specs=[out] * 8,
+            in_specs=[pl.BlockSpec((rows, block), lambda i, s: (0, s[2]))] * 4,
+            out_specs=[pl.BlockSpec((n, 256), lambda i, s: (0, 0)) for n in sizes],
         ),
-        out_shape=[jax.ShapeDtypeStruct((72, block), BF16)] * 8,
+        out_shape=[jax.ShapeDtypeStruct((n, 256), BF16) for n in sizes],
         compiler_params=PARAMS,
         cost_estimate=cost(2 * 512 * 256 * block, 2**20),
         name="select",
-    )(where, ids, *packs)
-
-
-def regroup_kernel(*refs):
-    turns, out_ref = refs[:-1], refs[-1]
-    code = turns[0][64:72, :].astype(F32)
-    for turn in turns[1:]:
-        code += turn[64:72, :].astype(F32)
-    for p in range(out_ref.shape[0]):
-        for k, turn in enumerate(turns):
-            out_ref[p, k * 8 : k * 8 + 8, :] = turn[p * 8 : p * 8 + 8, :]
-        out_ref[p, 64:72, :] = code.astype(BF16)
-
-
-def regroup_call(turns):
-    return pl.pallas_call(
-        regroup_kernel,
-        out_shape=jax.ShapeDtypeStruct((8, *turns[0].shape), BF16),
-        compiler_params=PARAMS,
-        cost_estimate=cost(0, 2**20),
-        name="regroup",
-    )(*turns)
+    )(where, *packs)
 
 
 def logits_kernel(where_ref, tgt_ref, got_ref, table_ref, near_ref, far_ref, stats_ref, hid, log, acc):
@@ -258,7 +265,15 @@
     )(where, targets, near, table)
 
 
-def scale_kernel(where_ref, tgt_ref, own_ref, stats_ref, soft_ref, hard_ref, out_ref, loss_ref, w_ref, keep):
+QUOTA = (0, 4, 2, 6, 1, 5, 3, 7)
+
+
+def scale_kernel(
+    where_ref, tgt_ref, own_ref, stats_ref, soft_ref, hard_ref, x0, r1, r2, r3, c0,
+    out_ref, loss_ref, w_ref, keep, code,
+):
+    step = pl.program_id(0)
+
     @pl.when(pl.program_id(0) == 0)
     def _():
         stats = stats_ref[...]
@@ -278,12 +293,27 @@
             [w, tgt_ref[...].astype(F32), jnp.zeros((6, w.shape[1]), F32)], axis=0
         )
 
-    out_ref[...] = (
+        marks = [c0[...], r1[512:528, :], r2[512:528, :], r2[528:544, :]]
+        marks += [r3[k : k + 16, :] for k in range(512, 576, 16)]
+        group = lax.broadcasted_iota(I32, (16, 256), 1) >> 4
+        mixed = jnp.zeros((16, 256), F32)
+        for q, mark in zip(QUOTA, marks):
+            mixed += jnp.where(group == q, mark.astype(F32), 0.0)
+        code[...] = mixed.astype(BF16)
+
+    depth = soft_ref.shape[1]
+    out_ref[:, 0:depth, :] = (
         soft_ref[...] * keep[0:1, :][None] + hard_ref[...].astype(F32) * keep[1:2, :][None]
     ).astype(BF16)
-
-
-def scale_call(where, targets, own, stats, soft, hard):
+    pieces = ((x0, 0), (r1, 0), (r2, 0), (r2, 256), (r3, 0), (r3, 128), (r3, 256), (r3, 384))
+    for j in range(2):
+        for i, (ref, at) in enumerate(pieces):
+            from_row = pl.multiple_of((2 * step + j) * 16 + at, 16)
+            out_ref[j, depth + 16 * i : depth + 16 * i + 16, :] = ref[pl.ds(from_row, 16), :]
+        out_ref[j, depth + 128 : depth + 144, :] = code[...]
+
+
+def scale_call(where, targets, own, stats, soft, hard, riders):
     plane, depth, tokens = soft.shape
     spec = pl.BlockSpec((2, depth, tokens), lambda p, s: (p, 0, 0))
     return pl.pallas_call(
@@ -297,33 +327,63 @@
                 pl.BlockSpec(stats.shape, lambda p, s: (0, 0, 0)),
                 spec,
                 spec,
+                *[pl.BlockSpec(rider.shape, lambda p, s: (0, 0)) for rider in riders],
             ],
             out_specs=[
-                spec,
+                pl.BlockSpec((2, depth + 144, tokens), lambda p, s: (p, 0, 0)),
                 pl.BlockSpec((1, tokens), lambda p, s: (0, 0)),
                 pl.BlockSpec((8, tokens), lambda p, s: (0, 0)),
             ],
-            scratch_shapes=[pltpu.VMEM((8, tokens), F32)],
+            scratch_shapes=[pltpu.VMEM((8, tokens), F32), pltpu.VMEM((16, tokens), BF16)],
         ),
         out_shape=[
-            jax.ShapeDtypeStruct((plane, depth, tokens), BF16),
+            jax.ShapeDtypeStruct((plane, depth + 144, tokens), BF16),
             jax.ShapeDtypeStruct((1, tokens), F32),
             jax.ShapeDtypeStruct((8, tokens), F32),
         ],
         compiler_params=PARAMS,
         cost_estimate=cost(4 * plane * depth * tokens, 8 * plane * depth * tokens),
         name="scale",
-    )(where, targets, own, stats, soft, hard)
-
-
-def table_kernel(where_ref, w_ref, place_ref, rows_ref, *refs):
-    out_ref = refs[-1]
+    )(where, targets, own, stats, soft, hard, *riders)
+
+
+def table_kernel(where_ref, w_ref, got_ref, *refs):
+    out_ref, rows, place = refs[-3:]
     count = out_ref.shape[0]
     first = pl.program_id(0) * count
+
+    @pl.when(pl.program_id(0) == 0)
+    def _():
+        plane = got_ref.shape[0]
+        depth = got_ref.shape[1] - 144
+        slots = rows.shape[0]
+        mark = lax.broadcasted_iota(I32, (128, slots), 0)
+        lane = lax.broadcasted_iota(I32, (128, slots), 1)
+        i = (lane >> 3) & 7
+        quota = ((i & 1) << 2) | (i & 2) | ((i >> 2) & 1)
+        at = quota * 16 + where_ref[4]
+        digit = jnp.where(mark == at, 64.0, jnp.where(mark == at + 8, 1.0, 0.0))
+        found = jnp.zeros((16, slots), F32)
+        for p in range(plane):
+            for k in range(0, 8, 2):
+                a = got_ref[p, depth + 16 * k : depth + 16 * k + 16, :].astype(F32)
+                b = got_ref[p, depth + 16 * k + 16 : depth + 16 * k + 32, :].astype(F32)
+                to = p * 64 + k * 8
+                rows[to : to + 16, 0:256] = jnp.concatenate([a[0:8], b[0:8]], axis=0).astype(BF16)
+                rows[to : to + 16, 256:512] = jnp.concatenate([a[8:16], b[8:16]], axis=0).astype(BF16)
+            code = got_ref[p, depth + 128 : depth + 144, 0:128]
+            these = jnp.where((lane >> 6) == p, digit, 0.0).astype(BF16)
+            found += jnp.dot(code, these, preferred_element_type=F32)
+        mine = lax.broadcasted_iota(I32, (16, slots), 0) == (
+            lax.broadcasted_iota(I32, (16, slots), 1) & 7
+        )
+        spot = jnp.sum(jnp.where(mine, found, 0.0), axis=0, keepdims=True) - 1.0
+        place[...] = jnp.broadcast_to(spot, place.shape).astype(I32)
+
     near = lax.broadcasted_iota(I32, (count, 256), 0) + (first + where_ref[0])
-    spots = lax.broadcasted_iota(I32, (count, place_ref.shape[1]), 0) + first
-    match = jnp.where(spots == place_ref[...], 1.0, 0.0).astype(BF16)
-    total = jnp.dot(match, rows_ref[...], preferred_element_type=F32)
+    spots = lax.broadcasted_iota(I32, (count, place.shape[1]), 0) + first
+    match = jnp.where(spots == place[0:1, :], 1.0, 0.0).astype(BF16)
+    total = jnp.dot(match, rows[...], preferred_element_type=F32)
     for g in range(4):
         e = refs[2 * g][...].astype(F32)
         w = w_ref[g, 0:1, :]
@@ -335,9 +395,9 @@
     out_ref[...] = total.astype(BF16)
 
 
-def table_call(where, w, place, rows, packs, count):
+def table_call(where, w, got, packs, count):
     tokens = packs[0].shape[1]
-    block = rows.shape[1]
+    block = 512
     specs, operands = [], []
     for pack in packs:
         specs.append(pl.BlockSpec((CHUNK, tokens), lambda i, s: (i, 0)))
@@ -350,17 +410,17 @@
             grid=(count // CHUNK,),
             in_specs=[
                 pl.BlockSpec(w.shape, lambda i, s: (0, 0, 0)),
-                pl.BlockSpec(place.shape, lambda i, s: (0, 0)),
-                pl.BlockSpec((rows.shape[0], block), lambda i, s: (0, 0)),
+                pl.BlockSpec(got.shape, lambda i, s: (0, 0, 0)),
                 *specs,
             ],
             out_specs=pl.BlockSpec((CHUNK, block), lambda i, s: (i, 0)),
+            scratch_shapes=[pltpu.VMEM((512, block), BF16), pltpu.VMEM((8, 512), I32)],
         ),
         out_shape=jax.ShapeDtypeStruct((count, block), BF16),
         compiler_params=PARAMS,
         cost_estimate=cost(2 * count * block * 1536, 8 * count * 256 + 2 * count * block),
         name="table_grad",
-    )(where, w, place, rows, *operands)
+    )(where, w, got, *operands)
 
 
 def inner(hidden, table, targets, input_ids, cotangent):
@@ -370,54 +430,49 @@
     vocab_count = plane * nz
     block = width // lax.axis_size(DP)
     xh, c = lax.axis_index("xh"), lax.axis_index("c")
-    where = jnp.stack([lax.axis_index(VOCAB) * vocab_rows, xh, c, lax.axis_index("z")]).astype(I32)
+    spot = lax.axis_index("y") * nx + lax.axis_index("xl")
+    where = jnp.stack([lax.axis_index(VOCAB) * vocab_rows, xh, c, lax.axis_index("z"), spot]).astype(I32)
     tokens = hidden.shape[0]
     goal = targets.reshape(1, tokens)
 
     half = width // 2
+    ids = jnp.stack([input_ids >> 14, (input_ids >> 7) & 127, input_ids & 127]).astype(BF16)
+    ids = jnp.pad(ids, ((0, 5), (0, block - ids.shape[1])))
+    ids = jnp.concatenate([ids, ids], axis=1)
     near_rows = lax.dynamic_slice_in_dim(cotangent, xh * half, half, 1)
     far_rows = lax.dynamic_slice_in_dim(cotangent, (1 - xh) * half, half, 1)
-    far_rows = swap(far_rows, "xh")
-    ids = input_ids.reshape(1, -1)
-    ids = jnp.concatenate([ids, swap(ids, "c")], axis=0)
-    ids = jnp.concatenate([ids, swap(ids, "xh")], axis=0)
+    near_rows = jnp.concatenate([near_rows, ids], axis=0)
+    far_rows = swap(jnp.concatenate([far_rows, ids], axis=0), "xh")
     packs = (near_rows, swap(near_rows, "c"), far_rows, swap(far_rows, "c"))
-    turns = select_call(where, ids, packs, vocab_rows)
+    away, middle, one, x0, c0 = select_call(where, packs, vocab_rows)
+    r1 = partner(away, 4)
+    r2 = partner(join_call((middle, 0, 256), (r1, 256, 256), (c0, 0, 16), (r1, 512, 16)), 2)
+    r3 = join_call(
+        (one, 0, 128), (r1, 128, 128), (r2, 128, 128), (r2, 384, 128), (c0, 0, 16), (r1, 512, 16), (r2, 512, 32)
+    )
+    r3 = partner(r3, 1)
 
     mine = hidden.T
     stage = exchange(to_each(mine, nz), "z").reshape(-1, tokens)
-    stage, *turns = lax.optimization_barrier((stage, *turns))
     stage = exchange(to_each(stage, plane), PLANE)
-    turns = [shift(turn, "z", k) if k else turn for k, turn in enumerate(turns)]
-    mixed = regroup_call(turns)
-    stage, mixed = lax.optimization_barrier((stage, mixed))
-    got = exchange(mixed, PLANE)
     near, far, own = logits_call(where, goal, stage, table, vocab_count)
-    own, got = lax.optimization_barrier((own, got))
 
     stats = exchange(own, VOCAB)
     far = swap(far, "xh")
     near_sib = swap(near, "c")
     far_sib = swap(far, "c")
     soft, hard = part_call(where, goal, near, table)
-    part, loss, w = scale_call(where, goal, own, stats, soft, hard)
-
-    part = exchange(part, PLANE)
-    part = jnp.sum(part.astype(F32), axis=0).reshape(nz, -1, tokens)
+    part, loss, w = scale_call(where, goal, own, stats, soft, hard, (x0, r1, r2, r3, c0))
+
+    got = exchange(part, PLANE)
+    part = jnp.sum(got[:, : width // plane].astype(F32), axis=0).reshape(nz, -1, tokens)
     part = jnp.sum(exchange(part, "z"), axis=0)
     hidden_grad = part.astype(BF16).T
 
     w_near = jnp.stack([w, swap(w, "c")])
     w_all = jnp.concatenate([w_near, swap(w_near, "xh")], axis=0)
-    code = got[:, -8:, :128].astype(F32).reshape(plane, 8, nz, 2, plane)
-    spot = lax.axis_index("y") * nx + lax.axis_index("xl")
-    here = lax.broadcasted_iota(I32, code.shape, 4) == spot
-    code = jnp.sum(jnp.where(here, code, 0.0), axis=4)
-    place = (code[..., 0] * 64 + code[..., 1]).astype(I32) - 1
-    place = place.transpose(0, 2, 1).reshape(plane, -1)
-    place = jnp.concatenate([place, jnp.full((plane, 8), -1, I32)], axis=1).reshape(1, -1)
     table_grad = table_call(
-        where, w_all, place, got.reshape(-1, block), (near, near_sib, far, far_sib), vocab_rows
+        where, w_all, got, (near, near_sib, far, far_sib), vocab_rows
     )
     return loss.reshape(tokens), hidden_grad, table_grad
 

time: 184 us -> 161 us (0.88)
  waiting for transfers between devices: 24.8 us -> 60.3 us
  blocking collectives: 41.6 us -> 17.4 us
  starting transfers between devices: 60.5 us -> 37.2 us
  other arithmetic: 7.76 us -> 1.51 us
  local copies, waits for them, and re-layouts: 19.9 us -> 14.3 us
    all_to_all x1, blocking collectives: 41.6 us -> 17.4 us  [exchange(): return lax.all_to_all(pieces, axes, 0, 0, tiled=True)]
    ppermute x7 -> x3, waiting for transfers between devices: 5.9 us -> 21.3 us  [partner(): return lax.ppermute(value, 'z', [(i, i ^ bit) for i in range(size)])]
    ppermute x7 -> x3, starting transfers between devices: 16.9 us -> 4.89 us  [partner(): return lax.ppermute(value, 'z', [(i, i ^ bit) for i in range(size)])]
    all_to_all x5 -> x4, waiting for transfers between devices: 12.3 us -> 22.5 us  [exchange(): return lax.all_to_all(pieces, axes, 0, 0, tiled=True)]
    ppermute x10 -> x8, waiting for transfers between devices: 6.59 us -> 16.5 us  [swap(): return lax.ppermute(value, axis, [(0, 1), (1, 0)])]
    all_to_all x5 -> x4, starting transfers between devices: 34.2 us -> 25.4 us  [exchange(): return lax.all_to_all(pieces, axes, 0, 0, tiled=True)]
    reduce_sum x2 -> x1, other arithmetic: 3.76 us -> 0.84 us  [inner(): jnp.sum(got[:, :width // plane].astype(F32), axis=0).reshape(nz, -1, tokens)]
    ppermute x10 -> x8, starting transfers between devices: 9.27 us -> 6.91 us  [swap(): return lax.ppermute(value, axis, [(0, 1), (1, 0)])]
  transfers between devices with their start and end apart: 22 -> 15, of which waited for: 9 -> 7; matrix products, arithmetic and copies ran while one was open for 6% -> 1% of each run, Pallas kernels for 7% -> 12%
where the time goes in v4:
time: 161 us; the launch traced here: 158 us
  waiting for transfers between devices  60.3 us (37%)
  starting transfers between devices  37.2 us (23%)
  Pallas kernels  26.7 us (17%)
  blocking collectives  17.4 us (11%)
  local copies, waits for them, and re-layouts  14.3 us (9%)
    all_to_all x4, starting transfers between devices, exchange(): return lax.all_to_all(pieces, axes, 0, 0, tiled=True)  25.4 us
    all_to_all x4, waiting for transfers between devices, exchange(): return lax.all_to_all(pieces, axes, 0, 0, tiled=True)  22.5 us
    ppermute x3, waiting for transfers between devices, partner(): return lax.ppermute(value, 'z', [(i, i ^ bit) for i in range(size)])  21.3 us
    all_to_all x1, blocking collectives, exchange(): return lax.all_to_all(pieces, axes, 0, 0, tiled=True)  17.4 us
    ppermute x8, waiting for transfers between devices, swap(): return lax.ppermute(value, axis, [(0, 1), (1, 0)])  16.5 us
    unnamed x20, local copies, waits for them, and re-layouts  12.4 us
    pallas_call x1, Pallas kernels, part_call(): pl.pallas_call(part_kernel, grid_spec=pltpu.PrefetchScalarGridSpec(num_sc...  9.18 us
    pallas_call x1, Pallas kernels, table_call(): pl.pallas_call(table_kernel, grid_spec=pltpu.PrefetchScalarGridSpec(num_s...  8.17 us
  transfers between devices with their start and end apart: 15, of which 7 were waited for; matrix products, arithmetic and copies ran while one was open for 1% of the time, Pallas kernels for 12%

profile of v4, /device:TPU:8, one launch (start us, length us, event | category | flops | bytes accessed | tf_op | source)
XLA Modules:
  0.0 158.2 jit_solution(5890177542014654365)
XLA Ops:
  0.6 0.7 broadcast_in_dim.6
  1.4 17.4 %all_to_all.25 = bf16[8,32,256]{2,1,0:T(8,128)(2,1)S(1)} all-to-all(bf16[8,32,256]{2,1,0:T(8,128)(2,1)S(1)} %broadcast_in_dim.6), channel_id=1, replica_groups=mesh['xh'=2,'c'=2,'y'=4,'z'=8,'xl'=2] {'z'}, dimensions={0} | all-to-all | bytes 262144 | tf_op jit(solution)/shard_map/all_to_all | solution.py:22
  18.7 1.0 broadcast_in_dim.7
  19.8 6.0 %all-to-all-start.1 = ((bf16[8,256,256]{2,1,0:T(8,128)(2,1)}), bf16[8,256,256]{2,1,0:T(8,128)(2,1)S(1)}, u32[]{:S(2)}, u32[]{:S(2)}) async-start(bf16[8,256,256]{2,1,0:T(8,128)(2,1)} %broadcast_in_dim.7), calls=%async_computation.1 | async-start | bytes 2097152 | tf_op jit(solution)/shard_map/all_to_all | solution.py:22
  25.8 2.8 %collective-permute-start.1 = (bf16[72,1024]{1,0:T(8,128)(2,1)S(1)}, bf16[72,1024]{1,0:T(8,128)(2,1)S(1)}, u32[]{:S(2)}, u32[]{:S(2)}) collective-permute-start(bf16[72,1024]{1,0:T(8,128)(2,1)S(1)} %get-tuple-element.31), channel_id=1, source_target_pairs={{0,128},{128,0},{1,129},{129,1},{2,130},{130,2},{3,131},{131,3},{4... | collective-permute-start | bytes 442376 | tf_op jit(solution)/shard_map/ppermute | solution.py:30
  28.7 12.9 %collective-permute-done.1.refs_2_ = bf16[72,1024]{1,0:T(8,128)(2,1)S(1)} collective-permute-done((bf16[72,1024]{1,0:T(8,128)(2,1)S(1)}, bf16[72,1024]{1,0:T(8,128)(2,1)S(1)}, u32[]{:S(2)}, u32[]{:S(2)}) %collective-permute-start.1) | collective-permute-done | bytes 147488 | tf_op jit(solution)/shard_map/ppermute | solution.py:30
  41.6 3.3 %copy-done = bf16[2000,2048]{1,0:T(8,128)(2,1)S(1)} copy-done((bf16[2000,2048]{1,0:T(8,128)(2,1)S(1)}, bf16[2000,2048]{1,0:T(8,128)(2,1)}, u32[]{:S(2)}) %copy-start) | copy-done | bytes 8192024
  45.0 5.8 %logits.1 = (bf16[3072,256]{1,0:T(8,128)(2,1)S(1)}, bf16[3072,256]{1,0:T(8,128)(2,1)}, f32[64,4,256]{2,1,0:T(4,128)}) custom-call(s32[5]{0:T(128)S(1)} %stack.48.where_ref, s32[1,256]{1,0:T(1,128)S(1)} %bitcast.23, bf16[8,256,256]{2,1,0:T(8,128)(2,1)S(1)} %all-to-all-done.1.got_ref, bf16[2000,2048]{1,0:T(8,128)(2,1)S(1)} %copy-done), custom_call_target="tpu_custom_call" | custom-call | flops 2097152000 | bytes 11337728 | tf_op jit(solution)/shard_map/logits/pallas_call | solution.py:188
  50.8 0.8 collective-permute-start.9
  51.6 1.2 select.28
  52.7 0.9 collective-permute-start.3
  53.7 14.1 %collective-permute-done.3.refs_1_.refs_3_.refs_5_.r1 = bf16[528,256]{1,0:T(8,128)(2,1)S(1)} collective-permute-done((bf16[528,256]{1,0:T(8,128)(2,1)S(1)}, bf16[528,256]{1,0:T(8,128)(2,1)S(1)}, u32[]{:S(2)}, u32[]{:S(2)}) %collective-permute-start.3) | collective-permute-done | bytes 270368 | tf_op jit(solution)/shard_map/ppermute | solution.py:39
  67.8 3.8 %collective-permute-start.4 = (bf16[544,256]{1,0:T(8,128)(2,1)S(1)}, bf16[544,256]{1,0:T(8,128)(2,1)S(1)}, u32[]{:S(2)}, u32[]{:S(2)}) collective-permute-start(bf16[544,256]{1,0:T(8,128)(2,1)S(1)} %join.2), channel_id=1, source_target_pairs={{0,4},{2,6},{4,0},{6,2},{8,12},{10,14},{12,8},{14,10},{1,5},{3,7},... | collective-permute-start | bytes 835592 | tf_op jit(solution)/shard_map/ppermute | solution.py:39
  71.6 8.6 %all-to-all-start.2 = ((f32[64,4,256]{2,1,0:T(4,128)}), f32[64,4,256]{2,1,0:T(4,128)S(1)}, u32[]{:S(2)}, u32[]{:S(2)}) async-start(f32[64,4,256]{2,1,0:T(4,128)} %get-tuple-element.16.own_ref), calls=%async_computation.2 | async-start | bytes 524288 | tf_op jit(solution)/shard_map/all_to_all | solution.py:22
  80.2 7.2 %collective-permute-done.4.refs_2_.refs_3_.refs_6_.r2 = bf16[544,256]{1,0:T(8,128)(2,1)S(1)} collective-permute-done((bf16[544,256]{1,0:T(8,128)(2,1)S(1)}, bf16[544,256]{1,0:T(8,128)(2,1)S(1)}, u32[]{:S(2)}, u32[]{:S(2)}) %collective-permute-start.4) | collective-permute-done | bytes 278560 | tf_op jit(solution)/shard_map/ppermute | solution.py:39
  87.6 3.3 %copy-done.1 = bf16[2000,2048]{1,0:T(8,128)(2,1)S(1)} copy-done((bf16[2000,2048]{1,0:T(8,128)(2,1)S(1)}, bf16[2000,2048]{1,0:T(8,128)(2,1)}, u32[]{:S(2)}) %copy-start.1) | copy-done | bytes 8192024
  91.0 9.2 %part.1 = (f32[8,256,256]{2,1,0:T(8,128)S(1)}, bf16[8,256,256]{2,1,0:T(8,128)(2,1)S(1)}) custom-call(s32[5]{0:T(128)S(1)} %stack.48.where_ref, s32[1,256]{1,0:T(1,128)S(1)} %bitcast.24, bf16[3072,256]{1,0:T(8,128)(2,1)S(1)} %get-tuple-element.17.e_ref.refs_0_.refs_1_, bf16[2000,2048]{1,0:T(8,128)(2,1)S(1)} %copy-done.1), custom_call_target="tpu_custom_call" | custom-call | flops 4194304000 | bytes 11337728 | tf_op jit(solution)/shard_map/part/pallas_call | solution.py:245
  100.2 1.3 copy-done.2
  101.5 0.7 copy-done.5
  102.2 1.6 %copy-done.3 = f32[8,256,256]{2,1,0:T(8,128)S(1)} copy-done((f32[8,256,256]{2,1,0:T(8,128)S(1)}, f32[8,256,256]{2,1,0:T(8,128)}, u32[]{:S(2)}) %copy-start.3) | copy-done | bytes 2097176
  103.8 1.0 copy-done.6
  104.8 2.3 %scale.1 = (bf16[8,400,256]{2,1,0:T(8,128)(2,1)S(1)}, f32[1,256]{1,0:T(1,128)}, f32[8,256]{1,0:T(8,128)S(1)}) custom-call(s32[5]{0:T(128)S(1)} %stack.48.where_ref, s32[1,256]{1,0:T(1,128)S(1)} %bitcast.25, f32[64,4,256]{2,1,0:T(4,128)} %get-tuple-element.16.own_ref, f32[64,4,256]{2,1,0:T(4,128)S(1)} %all-to-all-done.2.stats_ref, ...), custom_call_target="tpu_custom_call" | custom-call | flops 2097152 | bytes 4194304 | tf_op jit(solution)/shard_map/scale/pallas_call | solution.py:319
  107.1 1.2 copy-done.4
  108.3 5.8 %all-to-all-start.3 = ((bf16[8,400,256]{2,1,0:T(8,128)(2,1)}), bf16[8,400,256]{2,1,0:T(8,128)(2,1)S(1)}, u32[]{:S(2)}, u32[]{:S(2)}) async-start(bf16[8,400,256]{2,1,0:T(8,128)(2,1)} %copy-done.4), calls=%async_computation.3 | async-start | bytes 3276800 | tf_op jit(solution)/shard_map/all_to_all | solution.py:22
  114.6 18.4 %all-to-all-done.3.got_ref = bf16[8,400,256]{2,1,0:T(8,128)(2,1)S(1)} async-done(((bf16[8,400,256]{2,1,0:T(8,128)(2,1)}), bf16[8,400,256]{2,1,0:T(8,128)(2,1)S(1)}, u32[]{:S(2)}, u32[]{:S(2)}) %all-to-all-start.3) | async-done | bytes 1638432 | tf_op jit(solution)/shard_map/all_to_all | solution.py:22
  133.1 0.8 convert_reduce_fusion
  133.9 5.0 %all-to-all-start.4 = ((f32[8,32,256]{2,1,0:T(8,128)}), f32[8,32,256]{2,1,0:T(8,128)S(1)}, u32[]{:S(2)}, u32[]{:S(2)}) async-start(f32[8,32,256]{2,1,0:T(8,128)} %bitcast.12), calls=%async_computation.4 | async-start | bytes 524288 | tf_op jit(solution)/shard_map/all_to_all | solution.py:22
  138.9 1.2 collective-permute-done.6
  140.1 2.8 %collective-permute-start.7 = (f32[2,8,256]{2,1,0:T(8,128)S(1)}, f32[2,8,256]{2,1,0:T(8,128)S(1)}, u32[]{:S(2)}, u32[]{:S(2)}) collective-permute-start(f32[2,8,256]{2,1,0:T(8,128)S(1)} %pad_maximum_fusion.2), channel_id=1, source_target_pairs={{0,128},{128,0},{1,129},{129,1},{2,130},{130,2},{3,131},{131,3},{4... | collective-permute-start | bytes 49160 | tf_op jit(solution)/shard_map/ppermute | solution.py:30
  142.9 2.5 %collective-permute-done.7 = f32[2,8,256]{2,1,0:T(8,128)S(1)} collective-permute-done((f32[2,8,256]{2,1,0:T(8,128)S(1)}, f32[2,8,256]{2,1,0:T(8,128)S(1)}, u32[]{:S(2)}, u32[]{:S(2)}) %collective-permute-start.7) | collective-permute-done | bytes 16416 | tf_op jit(solution)/shard_map/ppermute | solution.py:30
  145.3 4.1 %all-to-all-done.4 = f32[8,32,256]{2,1,0:T(8,128)S(1)} async-done(((f32[8,32,256]{2,1,0:T(8,128)}), f32[8,32,256]{2,1,0:T(8,128)S(1)}, u32[]{:S(2)}, u32[]{:S(2)}) %all-to-all-start.4) | async-done | bytes 262176 | tf_op jit(solution)/shard_map/all_to_all | solution.py:22
  150.0 8.2 %table_grad.1 = bf16[2000,512]{1,0:T(8,128)(2,1)} custom-call(s32[5]{0:T(128)S(1)} %stack.48.where_ref, f32[4,8,256]{2,1,0:T(8,128)S(1)} %pad_maximum_fusion.1.w_ref, bf16[8,400,256]{2,1,0:T(8,128)(2,1)S(1)} %all-to-all-done.3.got_ref, bf16[3072,256]{1,0:T(8,128)(2,1)S(1)} %get-tuple-element.17.e_ref.refs_0_.refs_1_, ...), custom_call_target="tpu_custom_call" | custom-call | flops 3145728000 | bytes 6144000 | tf_op jit(solution)/shard_map/table_grad/pallas_call | solution.py:406
  (37 shorter events, 1.5 us)
Async XLA Ops:
  18.7 7.0 %copy-start.9 = (s32[64]{0:T(128)S(1)}, s32[64]{0:T(128)}, u32[]{:S(2)}) copy-start(s32[64]{0:T(128)} %param.8) | copy-start | bytes 772
  18.7 7.0 %copy-start.8 = (bf16[64,2048]{1,0:T(8,128)(2,1)S(1)}, bf16[64,2048]{1,0:T(8,128)(2,1)}, u32[]{:S(2)}) copy-start(bf16[64,2048]{1,0:T(8,128)(2,1)} %param.9) | copy-start | bytes 786436
  19.8 21.9 %copy-start.7 = (s32[256]{0:T(256)S(1)}, s32[256]{0:T(256)}, u32[]{:S(2)}) copy-start(s32[256]{0:T(256)} %param.7) | copy-start | bytes 3076
  19.8 21.9 %all-to-all-start.1 = ((bf16[8,256,256]{2,1,0:T(8,128)(2,1)}), bf16[8,256,256]{2,1,0:T(8,128)(2,1)S(1)}, u32[]{:S(2)}, u32[]{:S(2)}) async-start(bf16[8,256,256]{2,1,0:T(8,128)(2,1)} %broadcast_in_dim.7), calls=%async_computation.1 | async-start | bytes 2097152 | tf_op jit(solution)/shard_map/all_to_all | solution.py:22
  25.8 15.8 %collective-permute-start.1 = (bf16[72,1024]{1,0:T(8,128)(2,1)S(1)}, bf16[72,1024]{1,0:T(8,128)(2,1)S(1)}, u32[]{:S(2)}, u32[]{:S(2)}) collective-permute-start(bf16[72,1024]{1,0:T(8,128)(2,1)S(1)} %get-tuple-element.31), channel_id=1, source_target_pairs={{0,128},{128,0},{1,129},{129,1},{2,130},{130,2},{3,131},{131,3},{4... | collective-permute-start | bytes 442376 | tf_op jit(solution)/shard_map/ppermute | solution.py:30
  28.7 22.9 %collective-permute-start = (bf16[72,1024]{1,0:T(8,128)(2,1)S(1)}, bf16[72,1024]{1,0:T(8,128)(2,1)S(1)}, u32[]{:S(2)}, u32[]{:S(2)}) collective-permute-start(bf16[72,1024]{1,0:T(8,128)(2,1)S(1)} %get-tuple-element.32.refs_0_), channel_id=1, source_target_pairs={{0,64},{64,0},{1,65},{65,1},{2,66},{66,2},{3,67},{67,3},{4,68},{68... | collective-permute-start | bytes 442376 | tf_op jit(solution)/shard_map/ppermute | solution.py:30
  41.6 10.0 %collective-permute-start.2 = (bf16[72,1024]{1,0:T(8,128)(2,1)S(1)}, bf16[72,1024]{1,0:T(8,128)(2,1)S(1)}, u32[]{:S(2)}, u32[]{:S(2)}) collective-permute-start(bf16[72,1024]{1,0:T(8,128)(2,1)S(1)} %collective-permute-done.1.refs_2_), channel_id=1, source_target_pairs={{0,64},{64,0},{1,65},{65,1},{2,66},{66,2},{3,67},{67,3},{4,68},{68... | collective-permute-start | bytes 442376 | tf_op jit(solution)/shard_map/ppermute | solution.py:30
  41.6 3.3 %copy-start = (bf16[2000,2048]{1,0:T(8,128)(2,1)S(1)}, bf16[2000,2048]{1,0:T(8,128)(2,1)}, u32[]{:S(2)}) copy-start(bf16[2000,2048]{1,0:T(8,128)(2,1)} %table_ref.3) | copy-start | bytes 24576004
  50.8 63.3 %collective-permute-start.9 = (bf16[3072,256]{1,0:T(8,128)(2,1)}, bf16[3072,256]{1,0:T(8,128)(2,1)}, u32[]{:S(2)}, u32[]{:S(2)}) collective-permute-start(bf16[3072,256]{1,0:T(8,128)(2,1)} %get-tuple-element.28), channel_id=1, source_target_pairs={{0,128},{128,0},{1,129},{129,1},{2,130},{130,2},{3,131},{131,3},{4... | collective-permute-start | bytes 4718600 | tf_op jit(solution)/shard_map/ppermute | solution.py:30
  52.7 15.0 %collective-permute-start.3 = (bf16[528,256]{1,0:T(8,128)(2,1)S(1)}, bf16[528,256]{1,0:T(8,128)(2,1)S(1)}, u32[]{:S(2)}, u32[]{:S(2)}) collective-permute-start(bf16[528,256]{1,0:T(8,128)(2,1)S(1)} %get-tuple-element.21), channel_id=1, source_target_pairs={{0,8},{2,10},{4,12},{6,14},{8,0},{10,2},{12,4},{14,6},{1,9},{3,11}... | collective-permute-start | bytes 811016 | tf_op jit(solution)/shard_map/ppermute | solution.py:39
  67.8 19.7 %collective-permute-start.4 = (bf16[544,256]{1,0:T(8,128)(2,1)S(1)}, bf16[544,256]{1,0:T(8,128)(2,1)S(1)}, u32[]{:S(2)}, u32[]{:S(2)}) collective-permute-start(bf16[544,256]{1,0:T(8,128)(2,1)S(1)} %join.2), channel_id=1, source_target_pairs={{0,4},{2,6},{4,0},{6,2},{8,12},{10,14},{12,8},{14,10},{1,5},{3,7},... | collective-permute-start | bytes 835592 | tf_op jit(solution)/shard_map/ppermute | solution.py:39
  71.6 30.6 %all-to-all-start.2 = ((f32[64,4,256]{2,1,0:T(4,128)}), f32[64,4,256]{2,1,0:T(4,128)S(1)}, u32[]{:S(2)}, u32[]{:S(2)}) async-start(f32[64,4,256]{2,1,0:T(4,128)} %get-tuple-element.16.own_ref), calls=%async_computation.2 | async-start | bytes 524288 | tf_op jit(solution)/shard_map/all_to_all | solution.py:22
  87.5 14.0 %collective-permute-start.5 = (bf16[576,256]{1,0:T(8,128)(2,1)S(1)}, bf16[576,256]{1,0:T(8,128)(2,1)S(1)}, u32[]{:S(2)}, u32[]{:S(2)}) collective-permute-start(bf16[576,256]{1,0:T(8,128)(2,1)S(1)} %join.3), channel_id=1, source_target_pairs={{0,2},{2,0},{4,6},{6,4},{8,10},{10,8},{12,14},{14,12},{1,3},{3,1},... | collective-permute-start | bytes 884744 | tf_op jit(solution)/shard_map/ppermute | solution.py:39
  87.6 3.3 %copy-start.1 = (bf16[2000,2048]{1,0:T(8,128)(2,1)S(1)}, bf16[2000,2048]{1,0:T(8,128)(2,1)}, u32[]{:S(2)}) copy-start(bf16[2000,2048]{1,0:T(8,128)(2,1)} %table_ref.3) | copy-start | bytes 24576004
  100.1 1.4 copy-start.2
  101.5 0.7 copy-start.5
  102.2 1.6 %copy-start.3 = (f32[8,256,256]{2,1,0:T(8,128)S(1)}, f32[8,256,256]{2,1,0:T(8,128)}, u32[]{:S(2)}) copy-start(f32[8,256,256]{2,1,0:T(8,128)} %copy-done.2) | copy-start | bytes 6291460
  103.8 1.0 copy-start.6
  107.1 1.2 copy-start.4
  108.3 24.8 %all-to-all-start.3 = ((bf16[8,400,256]{2,1,0:T(8,128)(2,1)}), bf16[8,400,256]{2,1,0:T(8,128)(2,1)S(1)}, u32[]{:S(2)}, u32[]{:S(2)}) async-start(bf16[8,400,256]{2,1,0:T(8,128)(2,1)} %copy-done.4), calls=%async_computation.3 | async-start | bytes 3276800 | tf_op jit(solution)/shard_map/all_to_all | solution.py:22
  114.1 35.9 %collective-permute-start.8 = (bf16[3072,256]{1,0:T(8,128)(2,1)S(1)}, bf16[3072,256]{1,0:T(8,128)(2,1)}, u32[]{:S(2)}, u32[]{:S(2)}) collective-permute-start(bf16[3072,256]{1,0:T(8,128)(2,1)S(1)} %get-tuple-element.17.e_ref.refs_0_.refs_1_), channel_id=1, source_target_pairs={{0,64},{64,0},{1,65},{65,1},{2,66},{66,2},{3,67},{67,3},{4,68},{68... | collective-permute-start | bytes 4718600 | tf_op jit(solution)/shard_map/ppermute | solution.py:30
  114.1 35.9 %collective-permute-start.10 = (bf16[3072,256]{1,0:T(8,128)(2,1)}, bf16[3072,256]{1,0:T(8,128)(2,1)}, u32[]{:S(2)}, u32[]{:S(2)}) collective-permute-start(bf16[3072,256]{1,0:T(8,128)(2,1)} %collective-permute-done.9.refs_4_.refs_5_), channel_id=1, source_target_pairs={{0,64},{64,0},{1,65},{65,1},{2,66},{66,2},{3,67},{67,3},{4,68},{68... | collective-permute-start | bytes 4718600 | tf_op jit(solution)/shard_map/ppermute | solution.py:30
  133.9 15.5 %all-to-all-start.4 = ((f32[8,32,256]{2,1,0:T(8,128)}), f32[8,32,256]{2,1,0:T(8,128)S(1)}, u32[]{:S(2)}, u32[]{:S(2)}) async-start(f32[8,32,256]{2,1,0:T(8,128)} %bitcast.12), calls=%async_computation.4 | async-start | bytes 524288 | tf_op jit(solution)/shard_map/all_to_all | solution.py:22
  138.9 1.2 collective-permute-start.6
  140.1 5.2 %collective-permute-start.7 = (f32[2,8,256]{2,1,0:T(8,128)S(1)}, f32[2,8,256]{2,1,0:T(8,128)S(1)}, u32[]{:S(2)}, u32[]{:S(2)}) collective-permute-start(f32[2,8,256]{2,1,0:T(8,128)S(1)} %pad_maximum_fusion.2), channel_id=1, source_target_pairs={{0,128},{128,0},{1,129},{129,1},{2,130},{130,2},{3,131},{131,3},{4... | collective-permute-start | bytes 49160 | tf_op jit(solution)/shard_map/ppermute | solution.py:30

commit v5 on v4

--- a/solution.py
+++ b/solution.py
@@ -15,7 +15,7 @@
 VOCAB = ("y", "z", "xl")
 PLANE = ("y", "xl")
 CHUNK = 400
-PARAMS = pltpu.CompilerParams(vmem_limit_bytes=16 * 1024 * 1024)
+PARAMS = pltpu.CompilerParams(vmem_limit_bytes=60 * 1024 * 1024)
 
 
 def exchange(pieces, axes):
@@ -217,52 +217,45 @@
     )(where, targets, got, table)
 
 
-def part_kernel(where_ref, tgt_ref, e_ref, table_ref, soft_ref, hard_ref, lhs):
-    tokens = tgt_ref.shape[1]
+def part_kernel(hot, where_ref, side_ref, table_ref, out_ref, lhs):
+    tokens = out_ref.shape[2]
     count = table_ref.shape[0]
 
     @pl.when(pl.program_id(0) == 0)
     def _():
-        index = lax.broadcasted_iota(I32, (count, tokens), 0) + where_ref[0]
-        hit = jnp.where(index == tgt_ref[...], 1.0, 0.0).astype(BF16)
-        lhs[0:tokens, :] = e_ref[...].T
-        lhs[tokens:, :] = hit.T
-
-    both = jnp.dot(lhs[...], table_ref[...], preferred_element_type=F32)
-    soft = both[0:tokens, :].T
-    hard = both[tokens:, :].T
-    for k in range(soft.shape[0] // 32):
+        if hot:
+            index = lax.broadcasted_iota(I32, (count, tokens), 0) + where_ref[0]
+            lhs[...] = jnp.where(index == side_ref[...], 1.0, 0.0).astype(BF16).T
+        else:
+            lhs[...] = side_ref[...].T
+
+    part = jnp.dot(lhs[...], table_ref[...], preferred_element_type=F32).T
+    for k in range(part.shape[0] // 32):
         z, x = k // 2, k % 2
-        soft_ref[x, z * 32 : z * 32 + 32, :] = soft[k * 32 : k * 32 + 32, :]
-        hard_ref[x, z * 32 : z * 32 + 32, :] = hard[k * 32 : k * 32 + 32, :].astype(BF16)
-
-
-def part_call(where, targets, near, table):
+        out_ref[x, z * 32 : z * 32 + 32, :] = part[k * 32 : k * 32 + 32, :].astype(out_ref.dtype)
+
+
+def part_call(hot, where, side, table):
     count, width = table.shape
-    tokens = targets.shape[1]
+    tokens = side.shape[1]
     wide = 256
-    spec = pl.BlockSpec((2, wide // 2, tokens), lambda j, s: (j // 2, j % 2, 0))
-    return pl.pallas_call(
-        part_kernel,
+    return pl.pallas_call(
+        functools.partial(part_kernel, hot),
         grid_spec=pltpu.PrefetchScalarGridSpec(
             num_scalar_prefetch=1,
             grid=(width // wide,),
             in_specs=[
-                pl.BlockSpec((1, tokens), lambda j, s: (0, 0)),
-                pl.BlockSpec((count, tokens), lambda j, s: (0, 0)),
+                pl.BlockSpec((1 if hot else count, tokens), lambda j, s: (0, 0)),
                 pl.BlockSpec((count, wide), lambda j, s: (0, j)),
             ],
-            out_specs=[spec, spec],
-            scratch_shapes=[pltpu.VMEM((2 * tokens, count), BF16)],
+            out_specs=pl.BlockSpec((2, wide // 2, tokens), lambda j, s: (j // 2, j % 2, 0)),
+            scratch_shapes=[pltpu.VMEM((tokens, count), BF16)],
         ),
-        out_shape=[
-            jax.ShapeDtypeStruct((8, width // 8, tokens), F32),
-            jax.ShapeDtypeStruct((8, width // 8, tokens), BF16),
-        ],
-        compiler_params=PARAMS,
-        cost_estimate=cost(4 * count * width * tokens, 2 * count * width + 6 * width * tokens),
-        name="part",
-    )(where, targets, near, table)
+        out_shape=jax.ShapeDtypeStruct((8, width // 8, tokens), BF16 if hot else F32),
+        compiler_params=PARAMS,
+        cost_estimate=cost(2 * count * width * tokens, 2 * count * width + 4 * width * tokens),
+        name="hard" if hot else "soft",
+    )(where, side, table)
 
 
 QUOTA = (0, 4, 2, 6, 1, 5, 3, 7)
@@ -445,6 +438,7 @@
     far_rows = swap(jnp.concatenate([far_rows, ids], axis=0), "xh")
     packs = (near_rows, swap(near_rows, "c"), far_rows, swap(far_rows, "c"))
     away, middle, one, x0, c0 = select_call(where, packs, vocab_rows)
+    hard = part_call(True, where, goal, table)
     r1 = partner(away, 4)
     r2 = partner(join_call((middle, 0, 256), (r1, 256, 256), (c0, 0, 16), (r1, 512, 16)), 2)
     r3 = join_call(
@@ -461,7 +455,7 @@
     far = swap(far, "xh")
     near_sib = swap(near, "c")
     far_sib = swap(far, "c")
-    soft, hard = part_call(where, goal, near, table)
+    soft = part_call(False, where, near, table)
     part, loss, w = scale_call(where, goal, own, stats, soft, hard, (x0, r1, r2, r3, c0))
 
     got = exchange(part, PLANE)

time: 161 us -> 178 us (1.11)
  Pallas kernels: 26.7 us -> 50.9 us
  local copies, waits for them, and re-layouts: 14.3 us -> 7.03 us
    pallas_call x1 -> x2, Pallas kernels: 9.18 us -> 19.8 us  [part_call(): pl.pallas_call(functools.partial(part_kernel, hot), grid_spec=pltpu.Prefe...]
    unnamed x20 -> x28, local copies, waits for them, and re-layouts: 12.4 us -> 4.56 us
    pallas_call x1, Pallas kernels: 5.82 us -> 9.8 us  [logits_call(): pl.pallas_call(logits_kernel, grid_spec=pltpu.PrefetchScalarGridSpec(num_...]
    pallas_call x2, Pallas kernels: 0.04 us -> 3.98 us  [join_call(): pl.pallas_call(functools.partial(join_kernel, cuts), out_shape=jax.ShapeD...]
    pallas_call x1, Pallas kernels: 2.34 us -> 5.22 us  [scale_call(): pl.pallas_call(scale_kernel, grid_spec=pltpu.PrefetchScalarGridSpec(num_s...]
    pallas_call x1, Pallas kernels: 1.16 us -> 2.97 us  [select_call(): pl.pallas_call(functools.partial(select_kernel, vocab_rows), grid_spec=pl...]
  transfers between devices with their start and end apart: 15 -> 15, of which waited for: 7 -> 7; matrix products, arithmetic and copies ran while one was open for 1% -> 2% of each run, Pallas kernels for 12% -> 24%
where the time goes in v5:
time: 178 us; the launch traced here: 175 us
  waiting for transfers between devices  59.5 us (33%)
  Pallas kernels  50.9 us (29%)
  starting transfers between devices  36.9 us (21%)
  blocking collectives  17.4 us (10%)
  local copies, waits for them, and re-layouts  7.03 us (4%)
  other arithmetic  2.28 us (1%)
    all_to_all x4, starting transfers between devices, exchange(): return lax.all_to_all(pieces, axes, 0, 0, tiled=True)  25.1 us
    all_to_all x4, waiting for transfers between devices, exchange(): return lax.all_to_all(pieces, axes, 0, 0, tiled=True)  21.9 us
    ppermute x3, waiting for transfers between devices, partner(): return lax.ppermute(value, 'z', [(i, i ^ bit) for i in range(size)])  21.7 us
    pallas_call x2, Pallas kernels, part_call(): pl.pallas_call(functools.partial(part_kernel, hot), grid_spec=pltpu.Prefe...  19.8 us
    all_to_all x1, blocking collectives, exchange(): return lax.all_to_all(pieces, axes, 0, 0, tiled=True)  17.4 us
    ppermute x8, waiting for transfers between devices, swap(): return lax.ppermute(value, axis, [(0, 1), (1, 0)])  15.9 us
    pallas_call x1, Pallas kernels, logits_call(): pl.pallas_call(logits_kernel, grid_spec=pltpu.PrefetchScalarGridSpec(num_...  9.8 us
    pallas_call x1, Pallas kernels, table_call(): pl.pallas_call(table_kernel, grid_spec=pltpu.PrefetchScalarGridSpec(num_s...  9.1 us
  transfers between devices with their start and end apart: 15, of which 7 were waited for; matrix products, arithmetic and copies ran while one was open for 2% of the time, Pallas kernels for 24%

profile of v5, /device:TPU:8, one launch (start us, length us, event | category | flops | bytes accessed | tf_op | source)
XLA Modules:
  0.0 174.7 jit_solution(13753753286706372001)
XLA Ops:
  0.6 0.7 broadcast_in_dim.6
  1.4 17.4 %all_to_all.25 = bf16[8,32,256]{2,1,0:T(8,128)(2,1)S(1)} all-to-all(bf16[8,32,256]{2,1,0:T(8,128)(2,1)S(1)} %broadcast_in_dim.6), channel_id=1, replica_groups=mesh['xh'=2,'c'=2,'y'=4,'z'=8,'xl'=2] {'z'}, dimensions={0} | all-to-all | bytes 262144 | tf_op jit(solution)/shard_map/all_to_all | solution.py:22
  18.7 1.0 broadcast_in_dim.7
  19.8 5.8 %all-to-all-start.1 = ((bf16[8,256,256]{2,1,0:T(8,128)(2,1)}), bf16[8,256,256]{2,1,0:T(8,128)(2,1)S(1)}, u32[]{:S(2)}, u32[]{:S(2)}) async-start(bf16[8,256,256]{2,1,0:T(8,128)(2,1)} %broadcast_in_dim.7), calls=%async_computation.1 | async-start | bytes 2097152 | tf_op jit(solution)/shard_map/all_to_all | solution.py:22
  25.7 2.8 %collective-permute-start.1 = (bf16[72,1024]{1,0:T(8,128)(2,1)S(1)}, bf16[72,1024]{1,0:T(8,128)(2,1)S(1)}, u32[]{:S(2)}, u32[]{:S(2)}) collective-permute-start(bf16[72,1024]{1,0:T(8,128)(2,1)S(1)} %get-tuple-element.27), channel_id=1, source_target_pairs={{0,128},{128,0},{1,129},{129,1},{2,130},{130,2},{3,131},{131,3},{4... | collective-permute-start | bytes 442376 | tf_op jit(solution)/shard_map/ppermute | solution.py:30
  29.2 12.3 %collective-permute-done.1.refs_2_ = bf16[72,1024]{1,0:T(8,128)(2,1)S(1)} collective-permute-done((bf16[72,1024]{1,0:T(8,128)(2,1)S(1)}, bf16[72,1024]{1,0:T(8,128)(2,1)S(1)}, u32[]{:S(2)}, u32[]{:S(2)}) %collective-permute-start.1) | collective-permute-done | bytes 147488 | tf_op jit(solution)/shard_map/ppermute | solution.py:30
  41.5 1.0 copy-done.4
  42.5 9.8 %logits.1 = (bf16[3072,256]{1,0:T(8,128)(2,1)}, bf16[3072,256]{1,0:T(8,128)(2,1)}, f32[64,4,256]{2,1,0:T(4,128)}) custom-call(s32[5]{0:T(128)} %stack.48.where_ref, s32[1,256]{1,0:T(1,128)} %bitcast.28, bf16[8,256,256]{2,1,0:T(8,128)(2,1)} %copy-done.4, bf16[2000,2048]{1,0:T(8,128)(2,1)} %table_ref.5), custom_call_target="tpu_custom_call" | custom-call | flops 2097152000 | bytes 11337728 | tf_op jit(solution)/shard_map/logits/pallas_call | solution.py:188
  52.3 0.8 collective-permute-start.9
  54.4 3.0 %select.28 = (bf16[528,256]{1,0:T(8,128)(2,1)}, bf16[256,256]{1,0:T(8,128)(2,1)}, bf16[128,256]{1,0:T(8,128)(2,1)}, bf16[128,256]{1,0:T(8,128)(2,1)}, bf16[16,256]{1,0:T(8,128)(2,1)}) custom-call(s32[5]{0:T(128)} %stack.48.where_ref, bf16[72,1024]{1,0:T(8,128)(2,1)} %copy-done.6, bf16[72,1024]{1,0:T(8,128)(2,1)} %copy-done.10, bf16[72,1024]{1,0:T(8,128)(2,1)} %copy-done.9, ...), custom_call_target="tpu_custom_call" | custom-call | flops 134217728 | bytes 1048576 | tf_op jit(solution)/shard_map/select/pallas_call | solution.py:121
  57.4 0.9 collective-permute-start.3
  58.2 14.2 %collective-permute-done.3.refs_1_.refs_3_.refs_5_.r1 = bf16[528,256]{1,0:T(8,128)(2,1)S(1)} collective-permute-done((bf16[528,256]{1,0:T(8,128)(2,1)}, bf16[528,256]{1,0:T(8,128)(2,1)S(1)}, u32[]{:S(2)}, u32[]{:S(2)}) %collective-permute-start.3) | collective-permute-done | bytes 270368 | tf_op jit(solution)/shard_map/ppermute | solution.py:39
  72.5 0.7 copy-done.2
  73.2 1.8 %join.2 = bf16[544,256]{1,0:T(8,128)(2,1)} custom-call(bf16[256,256]{1,0:T(8,128)(2,1)} %get-tuple-element.18.refs_0_, bf16[528,256]{1,0:T(8,128)(2,1)} %copy-done.2, bf16[16,256]{1,0:T(8,128)(2,1)} %get-tuple-element.19.refs_2_.refs_4_.c0, bf16[528,256]{1,0:T(8,128)(2,1)} %copy-done.2), custom_call_target="tpu_custom_call" | custom-call | flops 1000000 | bytes 524288 | tf_op jit(solution)/shard_map/join/pallas_call | solution.py:52
  75.0 3.7 %collective-permute-start.4 = (bf16[544,256]{1,0:T(8,128)(2,1)}, bf16[544,256]{1,0:T(8,128)(2,1)S(1)}, u32[]{:S(2)}, u32[]{:S(2)}) collective-permute-start(bf16[544,256]{1,0:T(8,128)(2,1)} %join.2), channel_id=1, source_target_pairs={{0,4},{2,6},{4,0},{6,2},{8,12},{10,14},{12,8},{14,10},{1,5},{3,7},... | collective-permute-start | bytes 835592 | tf_op jit(solution)/shard_map/ppermute | solution.py:39
  78.8 8.6 %all-to-all-start.2 = ((f32[64,4,256]{2,1,0:T(4,128)}), f32[64,4,256]{2,1,0:T(4,128)S(1)}, u32[]{:S(2)}, u32[]{:S(2)}) async-start(f32[64,4,256]{2,1,0:T(4,128)} %get-tuple-element.14.own_ref), calls=%async_computation.2 | async-start | bytes 524288 | tf_op jit(solution)/shard_map/all_to_all | solution.py:22
  87.4 7.5 %collective-permute-done.4.refs_2_.refs_3_.refs_6_.r2 = bf16[544,256]{1,0:T(8,128)(2,1)S(1)} collective-permute-done((bf16[544,256]{1,0:T(8,128)(2,1)}, bf16[544,256]{1,0:T(8,128)(2,1)S(1)}, u32[]{:S(2)}, u32[]{:S(2)}) %collective-permute-start.4) | collective-permute-done | bytes 278560 | tf_op jit(solution)/shard_map/ppermute | solution.py:39
  94.9 0.7 copy-done.3
  95.6 2.1 %join.3 = bf16[576,256]{1,0:T(8,128)(2,1)} custom-call(bf16[128,256]{1,0:T(8,128)(2,1)} %get-tuple-element.20.refs_0_, bf16[528,256]{1,0:T(8,128)(2,1)} %copy-done.2, bf16[544,256]{1,0:T(8,128)(2,1)} %copy-done.3, bf16[544,256]{1,0:T(8,128)(2,1)} %copy-done.3, bf16[16,256]{1,0:T(8,128)(2,1)} %get-tuple-element.19.refs_2_.refs_4_.c0, ...), custom_call_target="tpu_custom_call" | custom-call | flops 1000000 | bytes 524288 | tf_op jit(solution)/shard_map/join/pallas_call | solution.py:52
  97.9 9.6 %hard.1.hard_ref = bf16[8,256,256]{2,1,0:T(8,128)(2,1)} custom-call(s32[5]{0:T(128)} %stack.48.where_ref, s32[1,256]{1,0:T(1,128)} %bitcast.29, bf16[2000,2048]{1,0:T(8,128)(2,1)} %table_ref.5), custom_call_target="tpu_custom_call" | custom-call | flops 2097152000 | bytes 10289152 | tf_op jit(solution)/shard_map/hard/pallas_call | solution.py:242
  107.5 10.2 %soft.1.soft_ref = f32[8,256,256]{2,1,0:T(8,128)} custom-call(s32[5]{0:T(128)} %stack.48.where_ref, bf16[3072,256]{1,0:T(8,128)(2,1)} %get-tuple-element.15.side_ref.refs_0_.refs_1_, bf16[2000,2048]{1,0:T(8,128)(2,1)} %table_ref.5), custom_call_target="tpu_custom_call" | custom-call | flops 2097152000 | bytes 10289152 | tf_op jit(solution)/shard_map/soft/pallas_call | solution.py:242
  117.7 0.7 copy-done.7
  118.5 5.2 %scale.1 = (bf16[8,400,256]{2,1,0:T(8,128)(2,1)}, f32[1,256]{1,0:T(1,128)}, f32[8,256]{1,0:T(8,128)}) custom-call(s32[5]{0:T(128)} %stack.48.where_ref, s32[1,256]{1,0:T(1,128)} %bitcast.30, f32[64,4,256]{2,1,0:T(4,128)} %get-tuple-element.14.own_ref, f32[64,4,256]{2,1,0:T(4,128)} %copy-done.5, f32[8,256,256]{2,1,0:T(8,128)} %soft.1.soft_ref, ...), custom_call_target="tpu_custom_call" | custom-call | flops 2097152 | bytes 4194304 | tf_op jit(solution)/shard_map/scale/pallas_call | solution.py:312
  123.7 5.9 %all-to-all-start.3 = ((bf16[8,400,256]{2,1,0:T(8,128)(2,1)}), bf16[8,400,256]{2,1,0:T(8,128)(2,1)S(1)}, u32[]{:S(2)}, u32[]{:S(2)}) async-start(bf16[8,400,256]{2,1,0:T(8,128)(2,1)} %get-tuple-element.22), calls=%async_computation.3 | async-start | bytes 3276800 | tf_op jit(solution)/shard_map/all_to_all | solution.py:22
  130.2 18.5 %all-to-all-done.3.got_ref = bf16[8,400,256]{2,1,0:T(8,128)(2,1)S(1)} async-done(((bf16[8,400,256]{2,1,0:T(8,128)(2,1)}), bf16[8,400,256]{2,1,0:T(8,128)(2,1)S(1)}, u32[]{:S(2)}, u32[]{:S(2)}) %all-to-all-start.3) | async-done | bytes 1638432 | tf_op jit(solution)/shard_map/all_to_all | solution.py:22
  148.7 1.0 convert_reduce_fusion
  149.7 4.8 %all-to-all-start.4 = ((f32[8,32,256]{2,1,0:T(8,128)}), f32[8,32,256]{2,1,0:T(8,128)S(1)}, u32[]{:S(2)}, u32[]{:S(2)}) async-start(f32[8,32,256]{2,1,0:T(8,128)} %bitcast.12), calls=%async_computation.4 | async-start | bytes 524288 | tf_op jit(solution)/shard_map/all_to_all | solution.py:22
  154.6 1.2 collective-permute-done.6
  155.8 2.8 %collective-permute-start.7 = (f32[2,8,256]{2,1,0:T(8,128)S(1)}, f32[2,8,256]{2,1,0:T(8,128)S(1)}, u32[]{:S(2)}, u32[]{:S(2)}) collective-permute-start(f32[2,8,256]{2,1,0:T(8,128)S(1)} %pad_maximum_fusion.2), channel_id=1, source_target_pairs={{0,128},{128,0},{1,129},{129,1},{2,130},{130,2},{3,131},{131,3},{4... | collective-permute-start | bytes 49160 | tf_op jit(solution)/shard_map/ppermute | solution.py:30
  158.5 2.5 %collective-permute-done.7 = f32[2,8,256]{2,1,0:T(8,128)S(1)} collective-permute-done((f32[2,8,256]{2,1,0:T(8,128)S(1)}, f32[2,8,256]{2,1,0:T(8,128)S(1)}, u32[]{:S(2)}, u32[]{:S(2)}) %collective-permute-start.7) | collective-permute-done | bytes 16416 | tf_op jit(solution)/shard_map/ppermute | solution.py:30
  161.6 3.4 %all-to-all-done.4 = f32[8,32,256]{2,1,0:T(8,128)S(1)} async-done(((f32[8,32,256]{2,1,0:T(8,128)}), f32[8,32,256]{2,1,0:T(8,128)S(1)}, u32[]{:S(2)}, u32[]{:S(2)}) %all-to-all-start.4) | async-done | bytes 262176 | tf_op jit(solution)/shard_map/all_to_all | solution.py:22
  165.6 9.1 %table_grad.1 = bf16[2000,512]{1,0:T(8,128)(2,1)} custom-call(s32[5]{0:T(128)} %stack.48.where_ref, f32[4,8,256]{2,1,0:T(8,128)} %pad_maximum_fusion.1.w_ref, bf16[8,400,256]{2,1,0:T(8,128)(2,1)} %copy-done.1, bf16[3072,256]{1,0:T(8,128)(2,1)} %get-tuple-element.15.side_ref.refs_0_.refs_1_, bf16[3072,256]{1,0:T(8,128)(2,1)} %get-tuple-element.15.side_ref.refs_0_.refs_1_, ...), custom_call_target="tpu_custom_call" | custom-call | flops 3145728000 | bytes 6144000 | tf_op jit(solution)/shard_map/table_grad/pallas_call | solution.py:399
  (46 shorter events, 4.2 us)
Async XLA Ops:
  18.7 6.9 %copy-start.13 = (s32[64]{0:T(128)S(1)}, s32[64]{0:T(128)}, u32[]{:S(2)}) copy-start(s32[64]{0:T(128)} %param.8) | copy-start | bytes 772
  18.7 6.9 %copy-start.8 = (bf16[64,2048]{1,0:T(8,128)(2,1)S(1)}, bf16[64,2048]{1,0:T(8,128)(2,1)}, u32[]{:S(2)}) copy-start(bf16[64,2048]{1,0:T(8,128)(2,1)} %param.9) | copy-start | bytes 786436
  19.8 21.7 %all-to-all-start.1 = ((bf16[8,256,256]{2,1,0:T(8,128)(2,1)}), bf16[8,256,256]{2,1,0:T(8,128)(2,1)S(1)}, u32[]{:S(2)}, u32[]{:S(2)}) async-start(bf16[8,256,256]{2,1,0:T(8,128)(2,1)} %broadcast_in_dim.7), calls=%async_computation.1 | async-start | bytes 2097152 | tf_op jit(solution)/shard_map/all_to_all | solution.py:22
  25.7 27.4 %copy-start.6 = (bf16[72,1024]{1,0:T(8,128)(2,1)}, bf16[72,1024]{1,0:T(8,128)(2,1)S(1)}, u32[]{:S(2)}) copy-start(bf16[72,1024]{1,0:T(8,128)(2,1)S(1)} %get-tuple-element.28.refs_0_) | copy-start | bytes 442372
  25.7 15.8 %collective-permute-start.1 = (bf16[72,1024]{1,0:T(8,128)(2,1)S(1)}, bf16[72,1024]{1,0:T(8,128)(2,1)S(1)}, u32[]{:S(2)}, u32[]{:S(2)}) collective-permute-start(bf16[72,1024]{1,0:T(8,128)(2,1)S(1)} %get-tuple-element.27), channel_id=1, source_target_pairs={{0,128},{128,0},{1,129},{129,1},{2,130},{130,2},{3,131},{131,3},{4... | collective-permute-start | bytes 442376 | tf_op jit(solution)/shard_map/ppermute | solution.py:30
  28.5 24.6 %collective-permute-start = (bf16[72,1024]{1,0:T(8,128)(2,1)S(1)}, bf16[72,1024]{1,0:T(8,128)(2,1)S(1)}, u32[]{:S(2)}, u32[]{:S(2)}) collective-permute-start(bf16[72,1024]{1,0:T(8,128)(2,1)S(1)} %get-tuple-element.28.refs_0_), channel_id=1, source_target_pairs={{0,64},{64,0},{1,65},{65,1},{2,66},{66,2},{3,67},{67,3},{4,68},{68... | collective-permute-start | bytes 442376 | tf_op jit(solution)/shard_map/ppermute | solution.py:30
  41.5 11.7 %copy-start.9 = (bf16[72,1024]{1,0:T(8,128)(2,1)}, bf16[72,1024]{1,0:T(8,128)(2,1)S(1)}, u32[]{:S(2)}) copy-start(bf16[72,1024]{1,0:T(8,128)(2,1)S(1)} %collective-permute-done.1.refs_2_) | copy-start | bytes 442372
  41.5 11.6 %collective-permute-start.2 = (bf16[72,1024]{1,0:T(8,128)(2,1)S(1)}, bf16[72,1024]{1,0:T(8,128)(2,1)S(1)}, u32[]{:S(2)}, u32[]{:S(2)}) collective-permute-start(bf16[72,1024]{1,0:T(8,128)(2,1)S(1)} %collective-permute-done.1.refs_2_), channel_id=1, source_target_pairs={{0,64},{64,0},{1,65},{65,1},{2,66},{66,2},{3,67},{67,3},{4,68},{68... | collective-permute-start | bytes 442376 | tf_op jit(solution)/shard_map/ppermute | solution.py:30
  41.5 1.0 copy-start.4
  52.3 77.4 %collective-permute-start.9 = (bf16[3072,256]{1,0:T(8,128)(2,1)}, bf16[3072,256]{1,0:T(8,128)(2,1)}, u32[]{:S(2)}, u32[]{:S(2)}) collective-permute-start(bf16[3072,256]{1,0:T(8,128)(2,1)} %get-tuple-element.24), channel_id=1, source_target_pairs={{0,128},{128,0},{1,129},{129,1},{2,130},{130,2},{3,131},{131,3},{4... | collective-permute-start | bytes 4718600 | tf_op jit(solution)/shard_map/ppermute | solution.py:30
  53.1 0.7 copy-start.10
  53.8 0.7 copy-start.11
  57.4 15.1 %collective-permute-start.3 = (bf16[528,256]{1,0:T(8,128)(2,1)}, bf16[528,256]{1,0:T(8,128)(2,1)S(1)}, u32[]{:S(2)}, u32[]{:S(2)}) collective-permute-start(bf16[528,256]{1,0:T(8,128)(2,1)} %get-tuple-element.17), channel_id=1, source_target_pairs={{0,8},{2,10},{4,12},{6,14},{8,0},{10,2},{12,4},{14,6},{1,9},{3,11}... | collective-permute-start | bytes 811016 | tf_op jit(solution)/shard_map/ppermute | solution.py:39
  72.5 0.7 copy-start.2
  75.0 19.9 %collective-permute-start.4 = (bf16[544,256]{1,0:T(8,128)(2,1)}, bf16[544,256]{1,0:T(8,128)(2,1)S(1)}, u32[]{:S(2)}, u32[]{:S(2)}) collective-permute-start(bf16[544,256]{1,0:T(8,128)(2,1)} %join.2), channel_id=1, source_target_pairs={{0,4},{2,6},{4,0},{6,2},{8,12},{10,14},{12,8},{14,10},{1,5},{3,7},... | collective-permute-start | bytes 835592 | tf_op jit(solution)/shard_map/ppermute | solution.py:39
  78.8 38.9 %all-to-all-start.2 = ((f32[64,4,256]{2,1,0:T(4,128)}), f32[64,4,256]{2,1,0:T(4,128)S(1)}, u32[]{:S(2)}, u32[]{:S(2)}) async-start(f32[64,4,256]{2,1,0:T(4,128)} %get-tuple-element.14.own_ref), calls=%async_computation.2 | async-start | bytes 524288 | tf_op jit(solution)/shard_map/all_to_all | solution.py:22
  94.9 0.7 copy-start.3
  97.8 19.9 %collective-permute-start.5 = (bf16[576,256]{1,0:T(8,128)(2,1)}, bf16[576,256]{1,0:T(8,128)(2,1)S(1)}, u32[]{:S(2)}, u32[]{:S(2)}) collective-permute-start(bf16[576,256]{1,0:T(8,128)(2,1)} %join.3), channel_id=1, source_target_pairs={{0,2},{2,0},{4,6},{6,4},{8,10},{10,8},{12,14},{14,12},{1,3},{3,1},... | collective-permute-start | bytes 884744 | tf_op jit(solution)/shard_map/ppermute | solution.py:39
  117.7 0.7 copy-start.7
  117.7 0.8 copy-start.5
  123.7 5.9 %copy-start = (bf16[3072,256]{1,0:T(8,128)(2,1)S(1)}, bf16[3072,256]{1,0:T(8,128)(2,1)}, u32[]{:S(2)}) copy-start(bf16[3072,256]{1,0:T(8,128)(2,1)} %get-tuple-element.15.side_ref.refs_0_.refs_1_) | copy-start | bytes 4718596
  123.7 25.0 %all-to-all-start.3 = ((bf16[8,400,256]{2,1,0:T(8,128)(2,1)}), bf16[8,400,256]{2,1,0:T(8,128)(2,1)S(1)}, u32[]{:S(2)}, u32[]{:S(2)}) async-start(bf16[8,400,256]{2,1,0:T(8,128)(2,1)} %get-tuple-element.22), calls=%async_computation.3 | async-start | bytes 3276800 | tf_op jit(solution)/shard_map/all_to_all | solution.py:22
  129.6 24.9 %copy-start.12 = (f32[8,256]{1,0:T(8,128)S(1)}, f32[8,256]{1,0:T(8,128)}, u32[]{:S(2)}) copy-start(f32[8,256]{1,0:T(8,128)} %get-tuple-element.23) | copy-start | bytes 24580
  129.6 36.0 %collective-permute-start.8 = (bf16[3072,256]{1,0:T(8,128)(2,1)S(1)}, bf16[3072,256]{1,0:T(8,128)(2,1)}, u32[]{:S(2)}, u32[]{:S(2)}) collective-permute-start(bf16[3072,256]{1,0:T(8,128)(2,1)S(1)} %copy-done), channel_id=1, source_target_pairs={{0,64},{64,0},{1,65},{65,1},{2,66},{66,2},{3,67},{67,3},{4,68},{68... | collective-permute-start | bytes 4718600 | tf_op jit(solution)/shard_map/ppermute | solution.py:30
  129.7 35.9 %collective-permute-start.10 = (bf16[3072,256]{1,0:T(8,128)(2,1)}, bf16[3072,256]{1,0:T(8,128)(2,1)}, u32[]{:S(2)}, u32[]{:S(2)}) collective-permute-start(bf16[3072,256]{1,0:T(8,128)(2,1)} %collective-permute-done.9.refs_4_.refs_5_), channel_id=1, source_target_pairs={{0,64},{64,0},{1,65},{65,1},{2,66},{66,2},{3,67},{67,3},{4,68},{68... | collective-permute-start | bytes 4718600 | tf_op jit(solution)/shard_map/ppermute | solution.py:30
  148.7 16.9 %copy-start.1 = (bf16[8,400,256]{2,1,0:T(8,128)(2,1)}, bf16[8,400,256]{2,1,0:T(8,128)(2,1)S(1)}, u32[]{:S(2)}) copy-start(bf16[8,400,256]{2,1,0:T(8,128)(2,1)S(1)} %all-to-all-done.3.got_ref) | copy-start | bytes 4915204
  149.7 15.3 %all-to-all-start.4 = ((f32[8,32,256]{2,1,0:T(8,128)}), f32[8,32,256]{2,1,0:T(8,128)S(1)}, u32[]{:S(2)}, u32[]{:S(2)}) async-start(f32[8,32,256]{2,1,0:T(8,128)} %bitcast.12), calls=%async_computation.4 | async-start | bytes 524288 | tf_op jit(solution)/shard_map/all_to_all | solution.py:22
  154.5 1.3 collective-permute-start.6
  155.8 5.2 %collective-permute-start.7 = (f32[2,8,256]{2,1,0:T(8,128)S(1)}, f32[2,8,256]{2,1,0:T(8,128)S(1)}, u32[]{:S(2)}, u32[]{:S(2)}) collective-permute-start(f32[2,8,256]{2,1,0:T(8,128)S(1)} %pad_maximum_fusion.2), channel_id=1, source_target_pairs={{0,128},{128,0},{1,129},{129,1},{2,130},{130,2},{3,131},{131,3},{4... | collective-permute-start | bytes 49160 | tf_op jit(solution)/shard_map/ppermute | solution.py:30

commit v6 on v5

--- a/solution.py
+++ b/solution.py
@@ -15,7 +15,9 @@
 VOCAB = ("y", "z", "xl")
 PLANE = ("y", "xl")
 CHUNK = 400
-PARAMS = pltpu.CompilerParams(vmem_limit_bytes=60 * 1024 * 1024)
+PARAMS = pltpu.CompilerParams(vmem_limit_bytes=16 * 1024 * 1024)
+WIDE = pltpu.CompilerParams(vmem_limit_bytes=57 * 1024 * 1024)
+FULL = pltpu.CompilerParams(vmem_limit_bytes=62 * 1024 * 1024)
 
 
 def exchange(pieces, axes):
@@ -133,211 +135,158 @@
     )(where, *packs)
 
 
-def logits_kernel(where_ref, tgt_ref, got_ref, table_ref, near_ref, far_ref, stats_ref, hid, log, acc):
-    step = pl.program_id(0)
-    rows, tokens = table_ref.shape[0], hid.shape[1]
-    width = hid.shape[0]
-    half = width // 2
-
-    @pl.when(step == 0)
-    def _():
-        plane, depth, _ = got_ref.shape
-        nz = depth // 32
-        nx = 2
-        for p in range(plane):
-            y, x = p // nx, p % nx
-            for z in range(nz):
-                at = ((y * nz + z) * nx + x) * 32
-                hid[at : at + 32, :] = got_ref[p, z * 32 : z * 32 + 32, :]
-        acc[0:1, :] = jnp.full((1, tokens), -jnp.inf, F32)
-        acc[1:2, :] = jnp.zeros((1, tokens), F32)
-
-    values = jnp.dot(table_ref[...], hid[...], preferred_element_type=F32)
-    log[pl.ds(pl.multiple_of(step * rows, rows), rows), :] = values
-    index = lax.broadcasted_iota(I32, values.shape, 0) + (where_ref[0] + step * rows)
-    acc[1:2, :] += jnp.sum(jnp.where(index == tgt_ref[...], values, 0.0), axis=0, keepdims=True)
-    acc[0:1, :] = jnp.maximum(acc[0:1, :], jnp.max(values, axis=0, keepdims=True))
-
-    @pl.when(step == pl.num_programs(0) - 1)
-    def _():
-        top = acc[0:1, :]
-        piece = 80
-
-        def one(i, total):
-            at = pl.ds(pl.multiple_of(i * piece, piece), piece)
-            e = jnp.exp(log[at, :] - top)
-            near_ref[at, :] = e.astype(BF16)
-            far_ref[at, :] = e.astype(BF16)
-            return total + jnp.sum(e, axis=0, keepdims=True)
-
-        count = log.shape[0]
-        total = lax.fori_loop(0, count // piece, one, jnp.zeros((1, tokens), F32))
-        base = near_ref.shape[0] - half
-        near_ref[count:base, :] = jnp.zeros((base - count, tokens), BF16)
-        far_ref[count:base, :] = jnp.zeros((base - count, tokens), BF16)
-        near_ref[base:, :] = hid[pl.ds(pl.multiple_of(where_ref[1] * half, half), half), :]
-        far_ref[base:, :] = hid[pl.ds(pl.multiple_of((1 - where_ref[1]) * half, half), half), :]
-        line = jnp.concatenate([top, total, acc[1:2, :], jnp.zeros((1, tokens), F32)], axis=0)
-        stats_ref[...] = jnp.broadcast_to(line[None], stats_ref.shape)
+def logits_kernel(where_ref, tgt_ref, got_ref, table_ref, pack_ref, stats_ref, hid, log, tab, sems):
+    count, tokens = log.shape
+    half = hid.shape[0] // 2
+    plane, depth, _ = got_ref.shape
+    loads = []
+    for i in range(count // CHUNK):
+        at = pl.ds(i * CHUNK, CHUNK)
+        loads.append(pltpu.make_async_copy(table_ref.at[at], tab.at[at], sems.at[i]))
+        loads[i].start()
+    for p in range(plane):
+        y, x = p // 2, p % 2
+        for z in range(depth // 32):
+            at = ((y * (depth // 32) + z) * 2 + x) * 32
+            hid[at : at + 32, :] = got_ref[p, z * 32 : z * 32 + 32, :]
+    top = jnp.full((1, tokens), -jnp.inf, F32)
+    picked = jnp.zeros((1, tokens), F32)
+    for i, load in enumerate(loads):
+        load.wait()
+        values = jnp.dot(tab[i * CHUNK : (i + 1) * CHUNK, :], hid[...], preferred_element_type=F32)
+        log[i * CHUNK : (i + 1) * CHUNK, :] = values
+        index = lax.broadcasted_iota(I32, values.shape, 0) + (where_ref[0] + i * CHUNK)
+        picked += jnp.sum(jnp.where(index == tgt_ref[...], values, 0.0), axis=0, keepdims=True)
+        top = jnp.maximum(top, jnp.max(values, axis=0, keepdims=True))
+    piece = 80
+
+    def one(i, total):
+        at = pl.ds(pl.multiple_of(i * piece, piece), piece)
+        e = jnp.exp(log[at, :] - top)
+        pack_ref[at, :] = e.astype(BF16)
+        return total + jnp.sum(e, axis=0, keepdims=True)
+
+    total = lax.fori_loop(0, count // piece, one, jnp.zeros((1, tokens), F32))
+    base = pack_ref.shape[0] - half
+    pack_ref[count:base, :] = jnp.zeros((base - count, tokens), BF16)
+    pack_ref[base:, :] = hid[pl.ds(pl.multiple_of(where_ref[1] * half, half), half), :]
+    line = jnp.concatenate([top, total, picked, jnp.zeros((1, tokens), F32)], axis=0)
+    stats_ref[...] = jnp.broadcast_to(line[None], stats_ref.shape)
 
 
 def logits_call(where, targets, got, table, copies):
     count, width = table.shape
     tokens = got.shape[2]
     span = 2048 + width // 2
+    whole = pl.BlockSpec(memory_space=pltpu.VMEM)
     return pl.pallas_call(
         logits_kernel,
-        grid_spec=pltpu.PrefetchScalarGridSpec(
-            num_scalar_prefetch=1,
-            grid=(count // CHUNK,),
-            in_specs=[
-                pl.BlockSpec((1, tokens), lambda i, s: (0, 0)),
-                pl.BlockSpec(got.shape, lambda i, s: (0, 0, 0)),
-                pl.BlockSpec((CHUNK, width), lambda i, s: (i, 0)),
-            ],
-            out_specs=[
-                pl.BlockSpec((span, tokens), lambda i, s: (0, 0)),
-                pl.BlockSpec((span, tokens), lambda i, s: (0, 0)),
-                pl.BlockSpec((copies, 4, tokens), lambda i, s: (0, 0, 0)),
-            ],
-            scratch_shapes=[
-                pltpu.VMEM((width, tokens), BF16),
-                pltpu.VMEM((count, tokens), F32),
-                pltpu.VMEM((8, tokens), F32),
-            ],
-        ),
+        in_specs=[pl.BlockSpec(memory_space=pltpu.SMEM), whole, whole, pl.BlockSpec(memory_space=pl.ANY)],
+        out_specs=[whole, whole],
+        scratch_shapes=[
+            pltpu.VMEM((width, tokens), BF16),
+            pltpu.VMEM((count, tokens), F32),
+            pltpu.VMEM((count, width), BF16),
+            pltpu.SemaphoreType.DMA((count // CHUNK,)),
+        ],
         out_shape=[
-            jax.ShapeDtypeStruct((span, tokens), BF16),
             jax.ShapeDtypeStruct((span, tokens), BF16),
             jax.ShapeDtypeStruct((copies, 4, tokens), F32),
         ],
-        compiler_params=PARAMS,
+        compiler_params=WIDE,
         cost_estimate=cost(2 * count * width * tokens, 2 * count * width + 4 * span * tokens),
         name="logits",
     )(where, targets, got, table)
 
 
-def part_kernel(hot, where_ref, side_ref, table_ref, out_ref, lhs):
-    tokens = out_ref.shape[2]
-    count = table_ref.shape[0]
-
-    @pl.when(pl.program_id(0) == 0)
-    def _():
-        if hot:
-            index = lax.broadcasted_iota(I32, (count, tokens), 0) + where_ref[0]
-            lhs[...] = jnp.where(index == side_ref[...], 1.0, 0.0).astype(BF16).T
-        else:
-            lhs[...] = side_ref[...].T
-
-    part = jnp.dot(lhs[...], table_ref[...], preferred_element_type=F32).T
-    for k in range(part.shape[0] // 32):
-        z, x = k // 2, k % 2
-        out_ref[x, z * 32 : z * 32 + 32, :] = part[k * 32 : k * 32 + 32, :].astype(out_ref.dtype)
-
-
-def part_call(hot, where, side, table):
+QUOTA = (0, 4, 2, 6, 1, 5, 3, 7)
+
+
+def part_kernel(
+    where_ref, tgt_ref, own_ref, stats_ref, near_ref, x0, r1, r2, r3, c0, table_ref,
+    out_ref, loss_ref, w_ref, lhs, tab, buf, sems, out_sems,
+):
+    tokens = tgt_ref.shape[1]
+    count, width = table_ref.shape
+    plane = buf.shape[0]
+    depth = width // plane
+    wide = tab.shape[2]
+    loads = []
+    for j in range(width // wide):
+        at = table_ref.at[:, pl.ds(j * wide, wide)]
+        loads.append(pltpu.make_async_copy(at, tab.at[j], sems.at[j]))
+        loads[j].start()
+
+    stats = stats_ref[...]
+    top = jnp.max(stats, axis=0)[0:1, :]
+    sums = jnp.sum(stats[:, 1:2, :] * jnp.exp(stats[:, 0:1, :] - top[None]), axis=0)
+    picks = jnp.sum(stats, axis=0)[2:3, :]
+    loss_ref[...] = top + jnp.log(sums) - picks
+    w = jnp.exp(own_ref[0, 0:1, :] - top) / sums
+    w_ref[...] = jnp.concatenate([w, tgt_ref[...].astype(F32), jnp.zeros((6, tokens), F32)], axis=0)
+    for i in range(0, count, CHUNK):
+        index = lax.broadcasted_iota(I32, (CHUNK, tokens), 0) + (where_ref[0] + i)
+        e = near_ref[i : i + CHUNK, :].astype(F32)
+        residual = e * w - jnp.where(index == tgt_ref[...], 1.0, 0.0)
+        lhs[i : i + CHUNK, :] = residual.astype(BF16)
+    rows = lhs[...].T
+
+    marks = [c0[...], r1[512:528, :], r2[512:528, :], r2[528:544, :]]
+    marks += [r3[k : k + 16, :] for k in range(512, 576, 16)]
+    group = lax.broadcasted_iota(I32, (16, tokens), 1) >> 4
+    mixed = jnp.zeros((16, tokens), F32)
+    for q, mark in zip(QUOTA, marks):
+        mixed += jnp.where(group == q, mark.astype(F32), 0.0)
+    pieces = ((x0, 0), (r1, 0), (r2, 0), (r2, 256), (r3, 0), (r3, 128), (r3, 256), (r3, 384))
+    for p in range(plane):
+        for i, (ref, at) in enumerate(pieces):
+            to = depth + 16 * i
+            buf[p, to : to + 16, :] = ref[at + p * 16 : at + p * 16 + 16, :]
+        buf[p, depth + 128 : depth + 144, :] = mixed.astype(BF16)
+
+    stores = []
+    for j, load in enumerate(loads):
+        load.wait()
+        part = jnp.dot(rows, tab[j], preferred_element_type=F32).T
+        for k in range(wide // 32):
+            z, x = k // 2, k % 2
+            at = (j % 2) * 128 + z * 32
+            buf[j // 2 * 2 + x, at : at + 32, :] = part[k * 32 : k * 32 + 32, :].astype(BF16)
+        if j % 2:
+            at = pl.ds(j // 2 * 2, 2)
+            stores.append(pltpu.make_async_copy(buf.at[at], out_ref.at[at], out_sems.at[j // 2]))
+            stores[-1].start()
+    for store in stores:
+        store.wait()
+
+
+def part_call(where, targets, own, stats, near, riders, table):
     count, width = table.shape
-    tokens = side.shape[1]
-    wide = 256
+    tokens = targets.shape[1]
+    plane, wide = 8, 256
+    whole = pl.BlockSpec(memory_space=pltpu.VMEM)
+    anywhere = pl.BlockSpec(memory_space=pl.ANY)
+    shape = (plane, width // plane + 144, tokens)
     return pl.pallas_call(
-        functools.partial(part_kernel, hot),
-        grid_spec=pltpu.PrefetchScalarGridSpec(
-            num_scalar_prefetch=1,
-            grid=(width // wide,),
-            in_specs=[
-                pl.BlockSpec((1 if hot else count, tokens), lambda j, s: (0, 0)),
-                pl.BlockSpec((count, wide), lambda j, s: (0, j)),
-            ],
-            out_specs=pl.BlockSpec((2, wide // 2, tokens), lambda j, s: (j // 2, j % 2, 0)),
-            scratch_shapes=[pltpu.VMEM((tokens, count), BF16)],
-        ),
-        out_shape=jax.ShapeDtypeStruct((8, width // 8, tokens), BF16 if hot else F32),
-        compiler_params=PARAMS,
-        cost_estimate=cost(2 * count * width * tokens, 2 * count * width + 4 * width * tokens),
-        name="hard" if hot else "soft",
-    )(where, side, table)
-
-
-QUOTA = (0, 4, 2, 6, 1, 5, 3, 7)
-
-
-def scale_kernel(
-    where_ref, tgt_ref, own_ref, stats_ref, soft_ref, hard_ref, x0, r1, r2, r3, c0,
-    out_ref, loss_ref, w_ref, keep, code,
-):
-    step = pl.program_id(0)
-
-    @pl.when(pl.program_id(0) == 0)
-    def _():
-        stats = stats_ref[...]
-        peak = jnp.max(stats, axis=0)
-        top = peak[0:1, :]
-        sums = jnp.sum(stats[:, 1:2, :] * jnp.exp(stats[:, 0:1, :] - top[None]), axis=0)
-        picks = jnp.sum(stats, axis=0)[2:3, :]
-        loss_ref[...] = top + jnp.log(sums) - picks
-        local_top, local_pick = own_ref[0, 0:1, :], own_ref[0, 2:3, :]
-        w = jnp.exp(local_top - top) / sums
-        prob = jnp.exp(local_pick - top) / sums
-        soft = jnp.exp(local_pick - local_top).astype(BF16).astype(F32) * w
-        gap = (prob - 1.0).astype(BF16).astype(F32) - soft
-        keep[0:1, :] = w
-        keep[1:2, :] = gap
-        w_ref[...] = jnp.concatenate(
-            [w, tgt_ref[...].astype(F32), jnp.zeros((6, w.shape[1]), F32)], axis=0
-        )
-
-        marks = [c0[...], r1[512:528, :], r2[512:528, :], r2[528:544, :]]
-        marks += [r3[k : k + 16, :] for k in range(512, 576, 16)]
-        group = lax.broadcasted_iota(I32, (16, 256), 1) >> 4
-        mixed = jnp.zeros((16, 256), F32)
-        for q, mark in zip(QUOTA, marks):
-            mixed += jnp.where(group == q, mark.astype(F32), 0.0)
-        code[...] = mixed.astype(BF16)
-
-    depth = soft_ref.shape[1]
-    out_ref[:, 0:depth, :] = (
-        soft_ref[...] * keep[0:1, :][None] + hard_ref[...].astype(F32) * keep[1:2, :][None]
-    ).astype(BF16)
-    pieces = ((x0, 0), (r1, 0), (r2, 0), (r2, 256), (r3, 0), (r3, 128), (r3, 256), (r3, 384))
-    for j in range(2):
-        for i, (ref, at) in enumerate(pieces):
-            from_row = pl.multiple_of((2 * step + j) * 16 + at, 16)
-            out_ref[j, depth + 16 * i : depth + 16 * i + 16, :] = ref[pl.ds(from_row, 16), :]
-        out_ref[j, depth + 128 : depth + 144, :] = code[...]
-
-
-def scale_call(where, targets, own, stats, soft, hard, riders):
-    plane, depth, tokens = soft.shape
-    spec = pl.BlockSpec((2, depth, tokens), lambda p, s: (p, 0, 0))
-    return pl.pallas_call(
-        scale_kernel,
-        grid_spec=pltpu.PrefetchScalarGridSpec(
-            num_scalar_prefetch=1,
-            grid=(plane // 2,),
-            in_specs=[
-                pl.BlockSpec((1, tokens), lambda p, s: (0, 0)),
-                pl.BlockSpec((1, 4, tokens), lambda p, s: (0, 0, 0)),
-                pl.BlockSpec(stats.shape, lambda p, s: (0, 0, 0)),
-                spec,
-                spec,
-                *[pl.BlockSpec(rider.shape, lambda p, s: (0, 0)) for rider in riders],
-            ],
-            out_specs=[
-                pl.BlockSpec((2, depth + 144, tokens), lambda p, s: (p, 0, 0)),
-                pl.BlockSpec((1, tokens), lambda p, s: (0, 0)),
-                pl.BlockSpec((8, tokens), lambda p, s: (0, 0)),
-            ],
-            scratch_shapes=[pltpu.VMEM((8, tokens), F32), pltpu.VMEM((16, tokens), BF16)],
-        ),
+        part_kernel,
+        in_specs=[pl.BlockSpec(memory_space=pltpu.SMEM), *[whole] * 9, anywhere],
+        out_specs=[anywhere, whole, whole],
+        scratch_shapes=[
+            pltpu.VMEM((count, tokens), BF16),
+            pltpu.VMEM((width // wide, count, wide), BF16),
+            pltpu.VMEM(shape, BF16),
+            pltpu.SemaphoreType.DMA((width // wide,)),
+            pltpu.SemaphoreType.DMA((plane // 2,)),
+        ],
         out_shape=[
-            jax.ShapeDtypeStruct((plane, depth + 144, tokens), BF16),
+            jax.ShapeDtypeStruct(shape, BF16),
             jax.ShapeDtypeStruct((1, tokens), F32),
             jax.ShapeDtypeStruct((8, tokens), F32),
         ],
-        compiler_params=PARAMS,
-        cost_estimate=cost(4 * plane * depth * tokens, 8 * plane * depth * tokens),
-        name="scale",
-    )(where, targets, own, stats, soft, hard, *riders)
+        compiler_params=FULL,
+        cost_estimate=cost(2 * count * width * tokens, 2 * count * width + 2 * width * tokens),
+        name="part",
+    )(where, targets, own, stats, near, *riders, table)
 
 
 def table_kernel(where_ref, w_ref, got_ref, *refs):
@@ -435,10 +384,10 @@
     near_rows = lax.dynamic_slice_in_dim(cotangent, xh * half, half, 1)
     far_rows = lax.dynamic_slice_in_dim(cotangent, (1 - xh) * half, half, 1)
     near_rows = jnp.concatenate([near_rows, ids], axis=0)
-    far_rows = swap(jnp.concatenate([far_rows, ids], axis=0), "xh")
+    far_rows = jnp.concatenate([far_rows, ids], axis=0)
+    far_rows = swap(far_rows, "xh")
     packs = (near_rows, swap(near_rows, "c"), far_rows, swap(far_rows, "c"))
     away, middle, one, x0, c0 = select_call(where, packs, vocab_rows)
-    hard = part_call(True, where, goal, table)
     r1 = partner(away, 4)
     r2 = partner(join_call((middle, 0, 256), (r1, 256, 256), (c0, 0, 16), (r1, 512, 16)), 2)
     r3 = join_call(
@@ -449,14 +398,14 @@
     mine = hidden.T
     stage = exchange(to_each(mine, nz), "z").reshape(-1, tokens)
     stage = exchange(to_each(stage, plane), PLANE)
-    near, far, own = logits_call(where, goal, stage, table, vocab_count)
+    far_stage = swap(stage, "xh")
+    near, own = logits_call(where, goal, stage, table, vocab_count)
 
     stats = exchange(own, VOCAB)
-    far = swap(far, "xh")
+    far, _ = logits_call(where, goal, far_stage, table, 1)
     near_sib = swap(near, "c")
     far_sib = swap(far, "c")
-    soft = part_call(False, where, near, table)
-    part, loss, w = scale_call(where, goal, own, stats, soft, hard, (x0, r1, r2, r3, c0))
+    part, loss, w = part_call(where, goal, own[0:1], stats, near, (x0, r1, r2, r3, c0), table)
 
     got = exchange(part, PLANE)
     part = jnp.sum(got[:, : width // plane].astype(F32), axis=0).reshape(nz, -1, tokens)

time: 178 us -> 161 us (0.904)
  blocking collectives: 17.4 us -> 0 us
  Pallas kernels: 50.9 us -> 38.1 us
  starting transfers between devices: 36.9 us -> 48.5 us
  waiting for transfers between devices: 59.5 us -> 63.3 us
    all_to_all x1 -> x0, blocking collectives: 17.4 us -> none  [exchange(): return lax.all_to_all(pieces, axes, 0, 0, tiled=True)]
    all_to_all x4 -> x5, starting transfers between devices: 25.1 us -> 35 us  [exchange(): return lax.all_to_all(pieces, axes, 0, 0, tiled=True)]
    pallas_call x4 -> x3, Pallas kernels: 34.8 us -> 29.2 us  [the longest x2 18.7 us: logits_call(): pl.pallas_call(logits_kernel, in_specs=[pl.BlockSpec(memory_space=pltpu.S...]
    pallas_call x2, Pallas kernels: 3.98 us -> 0.04 us  [join_call(): pl.pallas_call(functools.partial(join_kernel, cuts), out_shape=jax.ShapeD...]
    unnamed x28 -> x24, local copies, waits for them, and re-layouts: 4.56 us -> 2.25 us
    ppermute x3, waiting for transfers between devices: 21.7 us -> 23.9 us  [partner(): return lax.ppermute(value, 'z', [(i, i ^ bit) for i in range(size)])]
    ppermute x8, waiting for transfers between devices: 15.9 us -> 17.9 us  [swap(): return lax.ppermute(value, axis, [(0, 1), (1, 0)])]
    pallas_call x1, Pallas kernels: 2.97 us -> 1.15 us  [select_call(): pl.pallas_call(functools.partial(select_kernel, vocab_rows), grid_spec=pl...]
  transfers between devices with their start and end apart: 15 -> 16, of which waited for: 7 -> 9; matrix products, arithmetic and copies ran while one was open for 2% -> 2% of each run, Pallas kernels for 24% -> 19%
where the time goes in v6:
time: 161 us; the launch traced here: 159 us
  waiting for transfers between devices  63.3 us (39%)
  starting transfers between devices  48.5 us (30%)
  Pallas kernels  38.1 us (24%)
  local copies, waits for them, and re-layouts  6.05 us (4%)
  other arithmetic  2.16 us (1%)
    all_to_all x5, starting transfers between devices, exchange(): return lax.all_to_all(pieces, axes, 0, 0, tiled=True)  35 us
    ppermute x3, waiting for transfers between devices, partner(): return lax.ppermute(value, 'z', [(i, i ^ bit) for i in range(size)])  23.9 us
    all_to_all x5, waiting for transfers between devices, exchange(): return lax.all_to_all(pieces, axes, 0, 0, tiled=True)  21.5 us
    pallas_call x2, Pallas kernels, logits_call(): pl.pallas_call(logits_kernel, in_specs=[pl.BlockSpec(memory_space=pltpu.S...  18.7 us
    ppermute x8, waiting for transfers between devices, swap(): return lax.ppermute(value, axis, [(0, 1), (1, 0)])  17.9 us
    pallas_call x1, Pallas kernels, part_call(): pl.pallas_call(part_kernel, in_specs=[pl.BlockSpec(memory_space=pltpu.SME...  10.5 us
    pallas_call x1, Pallas kernels, table_call(): pl.pallas_call(table_kernel, grid_spec=pltpu.PrefetchScalarGridSpec(num_s...  7.8 us
    ppermute x8, starting transfers between devices, swap(): return lax.ppermute(value, axis, [(0, 1), (1, 0)])  7.02 us
  transfers between devices with their start and end apart: 16, of which 9 were waited for; matrix products, arithmetic and copies ran while one was open for 2% of the time, Pallas kernels for 19%

profile of v6, /device:TPU:8, one launch (start us, length us, event | category | flops | bytes accessed | tf_op | source)
XLA Modules:
  0.0 159.1 jit_solution(10317265920819572016)
XLA Ops:
  0.6 1.4 broadcast_in_dim.6
  2.0 8.5 %all-to-all-start = ((bf16[8,32,256]{2,1,0:T(8,128)(2,1)}), bf16[8,32,256]{2,1,0:T(8,128)(2,1)S(1)}, u32[]{:S(2)}, u32[]{:S(2)}) async-start(bf16[8,32,256]{2,1,0:T(8,128)(2,1)} %broadcast_in_dim.6), calls=%async_computation | async-start | bytes 262144 | tf_op jit(solution)/shard_map/all_to_all | solution.py:24
  10.5 0.7 convert_bitcast_fusion.3
  11.1 8.4 %all-to-all-done = bf16[8,32,256]{2,1,0:T(8,128)(2,1)S(1)} async-done(((bf16[8,32,256]{2,1,0:T(8,128)(2,1)}), bf16[8,32,256]{2,1,0:T(8,128)(2,1)S(1)}, u32[]{:S(2)}, u32[]{:S(2)}) %all-to-all-start) | async-done | bytes 131104 | tf_op jit(solution)/shard_map/all_to_all | solution.py:24
  19.6 1.0 broadcast_in_dim.7
  20.6 5.8 %all-to-all-start.1 = ((bf16[8,256,256]{2,1,0:T(8,128)(2,1)}), bf16[8,256,256]{2,1,0:T(8,128)(2,1)}, u32[]{:S(2)}, u32[]{:S(2)}) async-start(bf16[8,256,256]{2,1,0:T(8,128)(2,1)} %broadcast_in_dim.7), calls=%async_computation.1 | async-start | bytes 2097152 | tf_op jit(solution)/shard_map/all_to_all | solution.py:24
  26.5 2.8 %collective-permute-start.1 = (bf16[72,1024]{1,0:T(8,128)(2,1)S(1)}, bf16[72,1024]{1,0:T(8,128)(2,1)S(1)}, u32[]{:S(2)}, u32[]{:S(2)}) collective-permute-start(bf16[72,1024]{1,0:T(8,128)(2,1)S(1)} %get-tuple-element.27), channel_id=1, source_target_pairs={{0,128},{128,0},{1,129},{129,1},{2,130},{130,2},{3,131},{131,3},{4... | collective-permute-start | bytes 442376 | tf_op jit(solution)/shard_map/ppermute | solution.py:32
  29.4 13.0 %collective-permute-done.1.refs_2_ = bf16[72,1024]{1,0:T(8,128)(2,1)S(1)} collective-permute-done((bf16[72,1024]{1,0:T(8,128)(2,1)S(1)}, bf16[72,1024]{1,0:T(8,128)(2,1)S(1)}, u32[]{:S(2)}, u32[]{:S(2)}) %collective-permute-start.1) | collective-permute-done | bytes 147488 | tf_op jit(solution)/shard_map/ppermute | solution.py:32
  42.4 1.3 collective-permute-done.2.refs_3_
  43.7 1.2 select.28
  44.9 0.9 collective-permute-start.3
  45.8 14.0 %collective-permute-done.3.refs_1_.refs_3_.refs_5_.r1 = bf16[528,256]{1,0:T(8,128)(2,1)S(1)} collective-permute-done((bf16[528,256]{1,0:T(8,128)(2,1)S(1)}, bf16[528,256]{1,0:T(8,128)(2,1)S(1)}, u32[]{:S(2)}, u32[]{:S(2)}) %collective-permute-start.3) | collective-permute-done | bytes 270368 | tf_op jit(solution)/shard_map/ppermute | solution.py:41
  59.8 3.8 %collective-permute-start.4 = (bf16[544,256]{1,0:T(8,128)(2,1)S(1)}, bf16[544,256]{1,0:T(8,128)(2,1)S(1)}, u32[]{:S(2)}, u32[]{:S(2)}) collective-permute-start(bf16[544,256]{1,0:T(8,128)(2,1)S(1)} %join.2), channel_id=1, source_target_pairs={{0,4},{2,6},{4,0},{6,2},{8,12},{10,14},{12,8},{14,10},{1,5},{3,7},... | collective-permute-start | bytes 835592 | tf_op jit(solution)/shard_map/ppermute | solution.py:41
  63.7 0.8 collective-permute-start.9
  64.5 9.4 %logits.2 = (bf16[3072,256]{1,0:T(8,128)(2,1)}, f32[64,4,256]{2,1,0:T(4,128)}) custom-call(s32[5]{0:T(128)} %copy-done.6, s32[1,256]{1,0:T(1,128)} %bitcast.28, bf16[8,256,256]{2,1,0:T(8,128)(2,1)} %all-to-all-done.1.got_ref, bf16[2000,2048]{1,0:T(8,128)(2,1)} %table_ref.5), custom_call_target="tpu_custom_call" | custom-call | flops 2097152000 | bytes 11337728 | tf_op jit(solution)/shard_map/logits/pallas_call | solution.py:182
  73.9 8.7 %all-to-all-start.2 = ((f32[64,4,256]{2,1,0:T(4,128)}), f32[64,4,256]{2,1,0:T(4,128)S(1)}, u32[]{:S(2)}, u32[]{:S(2)}) async-start(f32[64,4,256]{2,1,0:T(4,128)} %get-tuple-element.14), calls=%async_computation.2 | async-start | bytes 524288 | tf_op jit(solution)/shard_map/all_to_all | solution.py:24
  82.6 1.7 %collective-permute-start.5 = (bf16[576,256]{1,0:T(8,128)(2,1)S(1)}, bf16[576,256]{1,0:T(8,128)(2,1)S(1)}, u32[]{:S(2)}, u32[]{:S(2)}) collective-permute-start(bf16[576,256]{1,0:T(8,128)(2,1)S(1)} %join.3), channel_id=1, source_target_pairs={{0,2},{2,0},{4,6},{6,4},{8,10},{10,8},{12,14},{14,12},{1,3},{3,1},... | collective-permute-start | bytes 884744 | tf_op jit(solution)/shard_map/ppermute | solution.py:41
  84.3 1.3 slice.6.own_ref
  85.6 9.9 %collective-permute-done.5.r3 = bf16[576,256]{1,0:T(8,128)(2,1)S(1)} collective-permute-done((bf16[576,256]{1,0:T(8,128)(2,1)S(1)}, bf16[576,256]{1,0:T(8,128)(2,1)S(1)}, u32[]{:S(2)}, u32[]{:S(2)}) %collective-permute-start.5) | collective-permute-done | bytes 294944 | tf_op jit(solution)/shard_map/ppermute | solution.py:41
  95.6 0.7 copy-done.9
  96.4 10.5 %part.1 = (bf16[8,400,256]{2,1,0:T(8,128)(2,1)}, f32[1,256]{1,0:T(1,128)}, f32[8,256]{1,0:T(8,128)}) custom-call(s32[5]{0:T(128)} %copy-done.6, s32[1,256]{1,0:T(1,128)} %bitcast.29, f32[1,4,256]{2,1,0:T(4,128)} %slice.6.own_ref, f32[64,4,256]{2,1,0:T(4,128)} %copy-done.8, bf16[3072,256]{1,0:T(8,128)(2,1)} %get-tuple-element.15.near_ref.refs_0_.refs_1_, ...), custom_call_target="tpu_custom_call" | custom-call | flops 2097152000 | bytes 9240576 | tf_op jit(solution)/shard_map/part/pallas_call | solution.py:270
  106.9 6.0 %all-to-all-start.3 = ((bf16[8,400,256]{2,1,0:T(8,128)(2,1)}), bf16[8,400,256]{2,1,0:T(8,128)(2,1)S(1)}, u32[]{:S(2)}, u32[]{:S(2)}) async-start(bf16[8,400,256]{2,1,0:T(8,128)(2,1)} %get-tuple-element.22), calls=%async_computation.3 | async-start | bytes 3276800 | tf_op jit(solution)/shard_map/all_to_all | solution.py:24
  112.8 9.3 %logits.3 = (bf16[3072,256]{1,0:T(8,128)(2,1)}, f32[1,4,256]{2,1,0:T(4,128)}) custom-call(s32[5]{0:T(128)} %copy-done.6, s32[1,256]{1,0:T(1,128)} %bitcast.30, bf16[8,256,256]{2,1,0:T(8,128)(2,1)} %collective-permute-done.9.got_ref, bf16[2000,2048]{1,0:T(8,128)(2,1)} %table_ref.5), custom_call_target="tpu_custom_call" | custom-call | flops 2097152000 | bytes 11337728 | tf_op jit(solution)/shard_map/logits/pallas_call | solution.py:182
  122.7 9.1 %all-to-all-done.3.got_ref = bf16[8,400,256]{2,1,0:T(8,128)(2,1)S(1)} async-done(((bf16[8,400,256]{2,1,0:T(8,128)(2,1)}), bf16[8,400,256]{2,1,0:T(8,128)(2,1)S(1)}, u32[]{:S(2)}, u32[]{:S(2)}) %all-to-all-start.3) | async-done | bytes 1638432 | tf_op jit(solution)/shard_map/all_to_all | solution.py:24
  131.8 0.8 convert_reduce_fusion
  132.7 6.1 %all-to-all-start.4 = ((f32[8,32,256]{2,1,0:T(8,128)}), f32[8,32,256]{2,1,0:T(8,128)S(1)}, u32[]{:S(2)}, u32[]{:S(2)}) async-start(f32[8,32,256]{2,1,0:T(8,128)} %bitcast.12), calls=%async_computation.4 | async-start | bytes 524288 | tf_op jit(solution)/shard_map/all_to_all | solution.py:24
  138.8 1.2 collective-permute-done.6
  140.0 2.7 %collective-permute-start.7 = (f32[2,8,256]{2,1,0:T(8,128)S(1)}, f32[2,8,256]{2,1,0:T(8,128)S(1)}, u32[]{:S(2)}, u32[]{:S(2)}) collective-permute-start(f32[2,8,256]{2,1,0:T(8,128)S(1)} %pad_maximum_fusion.2), channel_id=1, source_target_pairs={{0,128},{128,0},{1,129},{129,1},{2,130},{130,2},{3,131},{131,3},{4... | collective-permute-start | bytes 49160 | tf_op jit(solution)/shard_map/ppermute | solution.py:32
  142.7 2.5 %collective-permute-done.7 = f32[2,8,256]{2,1,0:T(8,128)S(1)} collective-permute-done((f32[2,8,256]{2,1,0:T(8,128)S(1)}, f32[2,8,256]{2,1,0:T(8,128)S(1)}, u32[]{:S(2)}, u32[]{:S(2)}) %collective-permute-start.7) | collective-permute-done | bytes 16416 | tf_op jit(solution)/shard_map/ppermute | solution.py:32
  145.2 4.0 %all-to-all-done.4 = f32[8,32,256]{2,1,0:T(8,128)S(1)} async-done(((f32[8,32,256]{2,1,0:T(8,128)}), f32[8,32,256]{2,1,0:T(8,128)S(1)}, u32[]{:S(2)}, u32[]{:S(2)}) %all-to-all-start.4) | async-done | bytes 262176 | tf_op jit(solution)/shard_map/all_to_all | solution.py:24
  149.9 1.4 copy-done.2
  151.3 7.8 %table_grad.1 = bf16[2000,512]{1,0:T(8,128)(2,1)} custom-call(s32[5]{0:T(128)S(1)} %copy-done.7, f32[4,8,256]{2,1,0:T(8,128)S(1)} %pad_maximum_fusion.1.w_ref, bf16[8,400,256]{2,1,0:T(8,128)(2,1)S(1)} %all-to-all-done.3.got_ref, bf16[3072,256]{1,0:T(8,128)(2,1)S(1)} %copy-done, bf16[3072,256]{1,0:T(8,128)(2,1)S(1)} %copy-done, ...), custom_call_target="tpu_custom_call" | custom-call | flops 3145728000 | bytes 6144000 | tf_op jit(solution)/shard_map/table_grad/pallas_call | solution.py:348
  (43 shorter events, 1.7 us)
Async XLA Ops:
  2.0 17.6 %all-to-all-start = ((bf16[8,32,256]{2,1,0:T(8,128)(2,1)}), bf16[8,32,256]{2,1,0:T(8,128)(2,1)S(1)}, u32[]{:S(2)}, u32[]{:S(2)}) async-start(bf16[8,32,256]{2,1,0:T(8,128)(2,1)} %broadcast_in_dim.6), calls=%async_computation | async-start | bytes 262144 | tf_op jit(solution)/shard_map/all_to_all | solution.py:24
  19.6 6.9 %copy-start.10 = (bf16[64,2048]{1,0:T(8,128)(2,1)S(1)}, bf16[64,2048]{1,0:T(8,128)(2,1)}, u32[]{:S(2)}) copy-start(bf16[64,2048]{1,0:T(8,128)(2,1)} %param.9) | copy-start | bytes 786436
  20.6 43.1 %all-to-all-start.1 = ((bf16[8,256,256]{2,1,0:T(8,128)(2,1)}), bf16[8,256,256]{2,1,0:T(8,128)(2,1)}, u32[]{:S(2)}, u32[]{:S(2)}) async-start(bf16[8,256,256]{2,1,0:T(8,128)(2,1)} %broadcast_in_dim.7), calls=%async_computation.1 | async-start | bytes 2097152 | tf_op jit(solution)/shard_map/all_to_all | solution.py:24
  26.5 15.8 %collective-permute-start.1 = (bf16[72,1024]{1,0:T(8,128)(2,1)S(1)}, bf16[72,1024]{1,0:T(8,128)(2,1)S(1)}, u32[]{:S(2)}, u32[]{:S(2)}) collective-permute-start(bf16[72,1024]{1,0:T(8,128)(2,1)S(1)} %get-tuple-element.27), channel_id=1, source_target_pairs={{0,128},{128,0},{1,129},{129,1},{2,130},{130,2},{3,131},{131,3},{4... | collective-permute-start | bytes 442376 | tf_op jit(solution)/shard_map/ppermute | solution.py:32
  29.4 13.1 %collective-permute-start = (bf16[72,1024]{1,0:T(8,128)(2,1)S(1)}, bf16[72,1024]{1,0:T(8,128)(2,1)S(1)}, u32[]{:S(2)}, u32[]{:S(2)}) collective-permute-start(bf16[72,1024]{1,0:T(8,128)(2,1)S(1)} %get-tuple-element.28.refs_0_), channel_id=1, source_target_pairs={{0,64},{64,0},{1,65},{65,1},{2,66},{66,2},{3,67},{67,3},{4,68},{68... | collective-permute-start | bytes 442376 | tf_op jit(solution)/shard_map/ppermute | solution.py:32
  42.3 1.4 collective-permute-start.2
  42.4 22.0 %copy-start.6 = (s32[5]{0:T(128)}, s32[5]{0:T(128)S(1)}, u32[]{:S(2)}) copy-start(s32[5]{0:T(128)S(1)} %stack.48.where_ref) | copy-start | bytes 64
  44.9 15.0 %copy-start.5 = (bf16[128,256]{1,0:T(8,128)(2,1)}, bf16[128,256]{1,0:T(8,128)(2,1)S(1)}, u32[]{:S(2)}) copy-start(bf16[128,256]{1,0:T(8,128)(2,1)S(1)} %get-tuple-element.16.x0) | copy-start | bytes 196612
  44.9 37.7 %copy-start.4 = (bf16[16,256]{1,0:T(8,128)(2,1)}, bf16[16,256]{1,0:T(8,128)(2,1)S(1)}, u32[]{:S(2)}) copy-start(bf16[16,256]{1,0:T(8,128)(2,1)S(1)} %get-tuple-element.19.refs_2_.refs_4_.c0) | copy-start | bytes 24580
  44.9 14.9 %collective-permute-start.3 = (bf16[528,256]{1,0:T(8,128)(2,1)S(1)}, bf16[528,256]{1,0:T(8,128)(2,1)S(1)}, u32[]{:S(2)}, u32[]{:S(2)}) collective-permute-start(bf16[528,256]{1,0:T(8,128)(2,1)S(1)} %get-tuple-element.17), channel_id=1, source_target_pairs={{0,8},{2,10},{4,12},{6,14},{8,0},{10,2},{12,4},{14,6},{1,9},{3,11}... | collective-permute-start | bytes 811016 | tf_op jit(solution)/shard_map/ppermute | solution.py:41
  59.8 22.8 %copy-start.1 = (bf16[528,256]{1,0:T(8,128)(2,1)}, bf16[528,256]{1,0:T(8,128)(2,1)S(1)}, u32[]{:S(2)}) copy-start(bf16[528,256]{1,0:T(8,128)(2,1)S(1)} %collective-permute-done.3.refs_1_.refs_3_.refs_5_.r1) | copy-start | bytes 811012
  59.8 22.7 %collective-permute-start.4 = (bf16[544,256]{1,0:T(8,128)(2,1)S(1)}, bf16[544,256]{1,0:T(8,128)(2,1)S(1)}, u32[]{:S(2)}, u32[]{:S(2)}) collective-permute-start(bf16[544,256]{1,0:T(8,128)(2,1)S(1)} %join.2), channel_id=1, source_target_pairs={{0,4},{2,6},{4,0},{6,2},{8,12},{10,14},{12,8},{14,10},{1,5},{3,7},... | collective-permute-start | bytes 835592 | tf_op jit(solution)/shard_map/ppermute | solution.py:41
  63.7 49.2 %collective-permute-start.9 = (bf16[8,256,256]{2,1,0:T(8,128)(2,1)}, bf16[8,256,256]{2,1,0:T(8,128)(2,1)}, u32[]{:S(2)}, u32[]{:S(2)}) collective-permute-start(bf16[8,256,256]{2,1,0:T(8,128)(2,1)} %all-to-all-done.1.got_ref), channel_id=1, source_target_pairs={{0,128},{128,0},{1,129},{129,1},{2,130},{130,2},{3,131},{131,3},{4... | collective-permute-start | bytes 3145736 | tf_op jit(solution)/shard_map/ppermute | solution.py:32
  73.9 21.7 %all-to-all-start.2 = ((f32[64,4,256]{2,1,0:T(4,128)}), f32[64,4,256]{2,1,0:T(4,128)S(1)}, u32[]{:S(2)}, u32[]{:S(2)}) async-start(f32[64,4,256]{2,1,0:T(4,128)} %get-tuple-element.14), calls=%async_computation.2 | async-start | bytes 524288 | tf_op jit(solution)/shard_map/all_to_all | solution.py:24
  82.5 13.0 %copy-start.3 = (bf16[544,256]{1,0:T(8,128)(2,1)}, bf16[544,256]{1,0:T(8,128)(2,1)S(1)}, u32[]{:S(2)}) copy-start(bf16[544,256]{1,0:T(8,128)(2,1)S(1)} %collective-permute-done.4.refs_2_.refs_3_.refs_6_.r2) | copy-start | bytes 835588
  82.6 12.9 %collective-permute-start.5 = (bf16[576,256]{1,0:T(8,128)(2,1)S(1)}, bf16[576,256]{1,0:T(8,128)(2,1)S(1)}, u32[]{:S(2)}, u32[]{:S(2)}) collective-permute-start(bf16[576,256]{1,0:T(8,128)(2,1)S(1)} %join.3), channel_id=1, source_target_pairs={{0,2},{2,0},{4,6},{6,4},{8,10},{10,8},{12,14},{14,12},{1,3},{3,1},... | collective-permute-start | bytes 884744 | tf_op jit(solution)/shard_map/ppermute | solution.py:41
  95.5 0.7 copy-start.9
  95.5 0.8 copy-start.8
  106.9 6.0 %copy-start = (bf16[3072,256]{1,0:T(8,128)(2,1)S(1)}, bf16[3072,256]{1,0:T(8,128)(2,1)}, u32[]{:S(2)}) copy-start(bf16[3072,256]{1,0:T(8,128)(2,1)} %get-tuple-element.15.near_ref.refs_0_.refs_1_) | copy-start | bytes 4718596
  106.9 25.0 %all-to-all-start.3 = ((bf16[8,400,256]{2,1,0:T(8,128)(2,1)}), bf16[8,400,256]{2,1,0:T(8,128)(2,1)S(1)}, u32[]{:S(2)}, u32[]{:S(2)}) async-start(bf16[8,400,256]{2,1,0:T(8,128)(2,1)} %get-tuple-element.22), calls=%async_computation.3 | async-start | bytes 3276800 | tf_op jit(solution)/shard_map/all_to_all | solution.py:24
  112.8 37.0 %collective-permute-start.8 = (bf16[3072,256]{1,0:T(8,128)(2,1)S(1)}, bf16[3072,256]{1,0:T(8,128)(2,1)}, u32[]{:S(2)}, u32[]{:S(2)}) collective-permute-start(bf16[3072,256]{1,0:T(8,128)(2,1)S(1)} %copy-done), channel_id=1, source_target_pairs={{0,64},{64,0},{1,65},{65,1},{2,66},{66,2},{3,67},{67,3},{4,68},{68... | collective-permute-start | bytes 4718600 | tf_op jit(solution)/shard_map/ppermute | solution.py:32
  122.1 16.6 %copy-start.11 = (f32[8,256]{1,0:T(8,128)S(1)}, f32[8,256]{1,0:T(8,128)}, u32[]{:S(2)}) copy-start(f32[8,256]{1,0:T(8,128)} %get-tuple-element.23) | copy-start | bytes 24580
  122.1 27.7 %copy-start.7 = (s32[5]{0:T(128)S(1)}, s32[5]{0:T(128)}, u32[]{:S(2)}) copy-start(s32[5]{0:T(128)} %copy-done.6) | copy-start | bytes 64
  122.1 27.7 %collective-permute-start.10 = (bf16[3072,256]{1,0:T(8,128)(2,1)}, bf16[3072,256]{1,0:T(8,128)(2,1)}, u32[]{:S(2)}, u32[]{:S(2)}) collective-permute-start(bf16[3072,256]{1,0:T(8,128)(2,1)} %get-tuple-element.24.refs_4_.refs_5_), channel_id=1, source_target_pairs={{0,64},{64,0},{1,65},{65,1},{2,66},{66,2},{3,67},{67,3},{4,68},{68... | collective-permute-start | bytes 4718600 | tf_op jit(solution)/shard_map/ppermute | solution.py:32
  132.7 16.5 %all-to-all-start.4 = ((f32[8,32,256]{2,1,0:T(8,128)}), f32[8,32,256]{2,1,0:T(8,128)S(1)}, u32[]{:S(2)}, u32[]{:S(2)}) async-start(f32[8,32,256]{2,1,0:T(8,128)} %bitcast.12), calls=%async_computation.4 | async-start | bytes 524288 | tf_op jit(solution)/shard_map/all_to_all | solution.py:24
  138.7 1.3 collective-permute-start.6
  140.0 5.2 %collective-permute-start.7 = (f32[2,8,256]{2,1,0:T(8,128)S(1)}, f32[2,8,256]{2,1,0:T(8,128)S(1)}, u32[]{:S(2)}, u32[]{:S(2)}) collective-permute-start(f32[2,8,256]{2,1,0:T(8,128)S(1)} %pad_maximum_fusion.2), channel_id=1, source_target_pairs={{0,128},{128,0},{1,129},{129,1},{2,130},{130,2},{3,131},{131,3},{4... | collective-permute-start | bytes 49160 | tf_op jit(solution)/shard_map/ppermute | solution.py:32
  149.9 1.4 copy-start.2

commit v7 on v6

--- a/solution.py
+++ b/solution.py
@@ -15,6 +15,7 @@
 VOCAB = ("y", "z", "xl")
 PLANE = ("y", "xl")
 CHUNK = 400
+DEPTH = 3
 PARAMS = pltpu.CompilerParams(vmem_limit_bytes=16 * 1024 * 1024)
 WIDE = pltpu.CompilerParams(vmem_limit_bytes=57 * 1024 * 1024)
 FULL = pltpu.CompilerParams(vmem_limit_bytes=62 * 1024 * 1024)
@@ -135,43 +136,70 @@
     )(where, *packs)
 
 
-def logits_kernel(where_ref, tgt_ref, got_ref, table_ref, pack_ref, stats_ref, hid, log, tab, sems):
-    count, tokens = log.shape
-    half = hid.shape[0] // 2
+def logits_kernel(
+    where_ref, tgt_ref, got_ref, table_ref, pack_ref, stats_ref, own_ref, hid, tab, buf, sems, out_sems
+):
+    count, width = tab.shape
+    tokens = hid.shape[1]
+    half = width // 2
     plane, depth, _ = got_ref.shape
-    loads = []
-    for i in range(count // CHUNK):
-        at = pl.ds(i * CHUNK, CHUNK)
-        loads.append(pltpu.make_async_copy(table_ref.at[at], tab.at[at], sems.at[i]))
-        loads[i].start()
+    chunks = count // CHUNK
+
+    def load(i):
+        at = pl.ds(pl.multiple_of(i * CHUNK, CHUNK), CHUNK)
+        return pltpu.make_async_copy(table_ref.at[at], tab.at[at], sems.at[i])
+
+    def store(i):
+        at = pl.ds(pl.multiple_of(i * CHUNK, CHUNK), CHUNK)
+        return pltpu.make_async_copy(buf.at[at], pack_ref.at[at], out_sems.at[i])
+
+    for i in range(DEPTH):
+        load(i).start()
     for p in range(plane):
         y, x = p // 2, p % 2
         for z in range(depth // 32):
             at = ((y * (depth // 32) + z) * 2 + x) * 32
             hid[at : at + 32, :] = got_ref[p, z * 32 : z * 32 + 32, :]
-    top = jnp.full((1, tokens), -jnp.inf, F32)
-    picked = jnp.zeros((1, tokens), F32)
-    for i, load in enumerate(loads):
-        load.wait()
-        values = jnp.dot(tab[i * CHUNK : (i + 1) * CHUNK, :], hid[...], preferred_element_type=F32)
-        log[i * CHUNK : (i + 1) * CHUNK, :] = values
+    base = buf.shape[0] - half
+    buf[base:, :] = hid[pl.ds(pl.multiple_of(where_ref[1] * half, half), half), :]
+    at = pl.ds(base, half)
+    side = pltpu.make_async_copy(buf.at[at], pack_ref.at[at], out_sems.at[chunks])
+    side.start()
+    own_ref[...] = jnp.zeros(own_ref.shape, F32)
+
+    def one(i, carry):
+        top, total, picked = carry
+        load(i).wait()
+
+        @pl.when(i + DEPTH < chunks)
+        def _():
+            load(i + DEPTH).start()
+
+        at = pl.ds(pl.multiple_of(i * CHUNK, CHUNK), CHUNK)
+        values = jnp.dot(tab[at, :], hid[...], preferred_element_type=F32)
         index = lax.broadcasted_iota(I32, values.shape, 0) + (where_ref[0] + i * CHUNK)
         picked += jnp.sum(jnp.where(index == tgt_ref[...], values, 0.0), axis=0, keepdims=True)
-        top = jnp.maximum(top, jnp.max(values, axis=0, keepdims=True))
-    piece = 80
-
-    def one(i, total):
-        at = pl.ds(pl.multiple_of(i * piece, piece), piece)
-        e = jnp.exp(log[at, :] - top)
-        pack_ref[at, :] = e.astype(BF16)
-        return total + jnp.sum(e, axis=0, keepdims=True)
-
-    total = lax.fori_loop(0, count // piece, one, jnp.zeros((1, tokens), F32))
-    base = pack_ref.shape[0] - half
-    pack_ref[count:base, :] = jnp.zeros((base - count, tokens), BF16)
-    pack_ref[base:, :] = hid[pl.ds(pl.multiple_of(where_ref[1] * half, half), half), :]
-    line = jnp.concatenate([top, total, picked, jnp.zeros((1, tokens), F32)], axis=0)
+        peak = jnp.max(values, axis=0, keepdims=True)
+        e = jnp.exp(values - peak)
+        buf[at, :] = e.astype(BF16)
+        store(i).start()
+        own_ref[pl.ds(i, 1), :] = peak
+        higher = jnp.maximum(top, peak)
+        total = total * jnp.exp(top - higher)
+        total += jnp.sum(e, axis=0, keepdims=True) * jnp.exp(peak - higher)
+        return higher, total, picked
+
+    blank = jnp.zeros((1, tokens), F32)
+    start = (jnp.full((1, tokens), -jnp.inf, F32), blank, blank)
+    line = jnp.concatenate([*lax.fori_loop(0, chunks, one, start), blank], axis=0)
     stats_ref[...] = jnp.broadcast_to(line[None], stats_ref.shape)
+    side.wait()
+
+    def end(i, carry):
+        store(i).wait()
+        return carry
+
+    lax.fori_loop(0, chunks, end, 0)
 
 
 def logits_call(where, targets, got, table, copies):
@@ -182,16 +210,18 @@
     return pl.pallas_call(
         logits_kernel,
         in_specs=[pl.BlockSpec(memory_space=pltpu.SMEM), whole, whole, pl.BlockSpec(memory_space=pl.ANY)],
-        out_specs=[whole, whole],
+        out_specs=[pl.BlockSpec(memory_space=pltpu.HBM), whole, whole],
         scratch_shapes=[
             pltpu.VMEM((width, tokens), BF16),
-            pltpu.VMEM((count, tokens), F32),
             pltpu.VMEM((count, width), BF16),
+            pltpu.VMEM((span, tokens), BF16),
             pltpu.SemaphoreType.DMA((count // CHUNK,)),
+            pltpu.SemaphoreType.DMA((count // CHUNK + 1,)),
         ],
         out_shape=[
-            jax.ShapeDtypeStruct((span, tokens), BF16),
+            pltpu.HBM((span, tokens), BF16),
             jax.ShapeDtypeStruct((copies, 4, tokens), F32),
+            jax.ShapeDtypeStruct((8, tokens), F32),
         ],
         compiler_params=WIDE,
         cost_estimate=cost(2 * count * width * tokens, 2 * count * width + 4 * span * tokens),
@@ -210,26 +240,34 @@
     count, width = table_ref.shape
     plane = buf.shape[0]
     depth = width // plane
-    wide = tab.shape[2]
-    loads = []
-    for j in range(width // wide):
-        at = table_ref.at[:, pl.ds(j * wide, wide)]
-        loads.append(pltpu.make_async_copy(at, tab.at[j], sems.at[j]))
-        loads[j].start()
+    turns, _, wide = tab.shape
+
+    def load(j):
+        at = table_ref.at[:, pl.ds(pl.multiple_of(j * wide, wide), wide)]
+        return pltpu.make_async_copy(at, tab.at[j], sems.at[j])
+
+    def store(j):
+        at = pl.ds(j * 2, 2)
+        return pltpu.make_async_copy(buf.at[at], out_ref.at[at], out_sems.at[j])
+
+    for j in range(DEPTH):
+        load(j).start()
 
     stats = stats_ref[...]
     top = jnp.max(stats, axis=0)[0:1, :]
     sums = jnp.sum(stats[:, 1:2, :] * jnp.exp(stats[:, 0:1, :] - top[None]), axis=0)
     picks = jnp.sum(stats, axis=0)[2:3, :]
     loss_ref[...] = top + jnp.log(sums) - picks
-    w = jnp.exp(own_ref[0, 0:1, :] - top) / sums
-    w_ref[...] = jnp.concatenate([w, tgt_ref[...].astype(F32), jnp.zeros((6, tokens), F32)], axis=0)
-    for i in range(0, count, CHUNK):
-        index = lax.broadcasted_iota(I32, (CHUNK, tokens), 0) + (where_ref[0] + i)
-        e = near_ref[i : i + CHUNK, :].astype(F32)
-        residual = e * w - jnp.where(index == tgt_ref[...], 1.0, 0.0)
-        lhs[i : i + CHUNK, :] = residual.astype(BF16)
-    rows = lhs[...].T
+    chunks = count // CHUNK
+    w = jnp.exp(own_ref[0:chunks, :] - top) / sums
+    w_ref[...] = jnp.concatenate(
+        [w, tgt_ref[...].astype(F32), jnp.zeros((7 - chunks, tokens), F32)], axis=0
+    )
+    for i in range(chunks):
+        index = lax.broadcasted_iota(I32, (CHUNK, tokens), 0) + (where_ref[0] + i * CHUNK)
+        e = near_ref[i * CHUNK : (i + 1) * CHUNK, :].astype(F32)
+        residual = e * w[i : i + 1, :] - jnp.where(index == tgt_ref[...], 1.0, 0.0)
+        lhs[i * CHUNK : (i + 1) * CHUNK, :] = residual.astype(BF16)
 
     marks = [c0[...], r1[512:528, :], r2[512:528, :], r2[528:544, :]]
     marks += [r3[k : k + 16, :] for k in range(512, 576, 16)]
@@ -244,33 +282,42 @@
             buf[p, to : to + 16, :] = ref[at + p * 16 : at + p * 16 + 16, :]
         buf[p, depth + 128 : depth + 144, :] = mixed.astype(BF16)
 
-    stores = []
-    for j, load in enumerate(loads):
-        load.wait()
-        part = jnp.dot(rows, tab[j], preferred_element_type=F32).T
+    def one(j, carry):
+        load(j).wait()
+
+        @pl.when(j + DEPTH < turns)
+        def _():
+            load(j + DEPTH).start()
+
+        part = lax.dot_general(
+            tab[j], lhs[...], (((0,), (0,)), ((), ())), preferred_element_type=F32
+        )
         for k in range(wide // 32):
             z, x = k // 2, k % 2
-            at = (j % 2) * 128 + z * 32
-            buf[j // 2 * 2 + x, at : at + 32, :] = part[k * 32 : k * 32 + 32, :].astype(BF16)
-        if j % 2:
-            at = pl.ds(j // 2 * 2, 2)
-            stores.append(pltpu.make_async_copy(buf.at[at], out_ref.at[at], out_sems.at[j // 2]))
-            stores[-1].start()
-    for store in stores:
-        store.wait()
+            buf[j * 2 + x, z * 32 : z * 32 + 32, :] = part[k * 32 : k * 32 + 32, :].astype(BF16)
+        store(j).start()
+        return carry
+
+    lax.fori_loop(0, turns, one, 0)
+
+    def end(j, carry):
+        store(j).wait()
+        return carry
+
+    lax.fori_loop(0, turns, end, 0)
 
 
 def part_call(where, targets, own, stats, near, riders, table):
     count, width = table.shape
     tokens = targets.shape[1]
-    plane, wide = 8, 256
+    plane, wide = 8, 512
     whole = pl.BlockSpec(memory_space=pltpu.VMEM)
     anywhere = pl.BlockSpec(memory_space=pl.ANY)
     shape = (plane, width // plane + 144, tokens)
     return pl.pallas_call(
         part_kernel,
         in_specs=[pl.BlockSpec(memory_space=pltpu.SMEM), *[whole] * 9, anywhere],
-        out_specs=[anywhere, whole, whole],
+        out_specs=[pl.BlockSpec(memory_space=pltpu.HBM), whole, whole],
         scratch_shapes=[
             pltpu.VMEM((count, tokens), BF16),
             pltpu.VMEM((width // wide, count, wide), BF16),
@@ -279,7 +326,7 @@
             pltpu.SemaphoreType.DMA((plane // 2,)),
         ],
         out_shape=[
-            jax.ShapeDtypeStruct(shape, BF16),
+            pltpu.HBM(shape, BF16),
             jax.ShapeDtypeStruct((1, tokens), F32),
             jax.ShapeDtypeStruct((8, tokens), F32),
         ],
@@ -328,8 +375,8 @@
     total = jnp.dot(match, rows[...], preferred_element_type=F32)
     for g in range(4):
         e = refs[2 * g][...].astype(F32)
-        w = w_ref[g, 0:1, :]
-        target = w_ref[g, 1:2, :].astype(I32)
+        w = w_ref[g, pl.ds(pl.program_id(0), 1), :]
+        target = w_ref[g, 5:6, :].astype(I32)
         res = (e * w - jnp.where(near == target, 1.0, 0.0)).astype(BF16)
         total += lax.dot_general(
             res, refs[2 * g + 1][...], (((1,), (1,)), ((), ())), preferred_element_type=F32
@@ -399,13 +446,13 @@
     stage = exchange(to_each(mine, nz), "z").reshape(-1, tokens)
     stage = exchange(to_each(stage, plane), PLANE)
     far_stage = swap(stage, "xh")
-    near, own = logits_call(where, goal, stage, table, vocab_count)
-
-    stats = exchange(own, VOCAB)
-    far, _ = logits_call(where, goal, far_stage, table, 1)
+    near, sums, own = logits_call(where, goal, stage, table, vocab_count)
+
+    stats = exchange(sums, VOCAB)
+    far, _, _ = logits_call(where, goal, far_stage, table, 1)
     near_sib = swap(near, "c")
     far_sib = swap(far, "c")
-    part, loss, w = part_call(where, goal, own[0:1], stats, near, (x0, r1, r2, r3, c0), table)
+    part, loss, w = part_call(where, goal, own, stats, near, (x0, r1, r2, r3, c0), table)
 
     got = exchange(part, PLANE)
     part = jnp.sum(got[:, : width // plane].astype(F32), axis=0).reshape(nz, -1, tokens)

time: 161 us -> 157 us (0.975)
  Pallas kernels: 38.1 us -> 32.4 us
  waiting for transfers between devices: 63.3 us -> 66.3 us
    pallas_call x2, Pallas kernels: 18.7 us -> 15.6 us  [logits_call(): pl.pallas_call(logits_kernel, in_specs=[pl.BlockSpec(memory_space=pltpu.S...]
    pallas_call x1, Pallas kernels: 10.5 us -> 7.8 us  [part_call(): pl.pallas_call(part_kernel, in_specs=[pl.BlockSpec(memory_space=pltpu.SME...]
  transfers between devices with their start and end apart: 16 -> 16, of which waited for: 9 -> 9; matrix products, arithmetic and copies ran while one was open for 2% -> 1% of each run, Pallas kernels for 19% -> 16%
where the time goes in v7:
time: 157 us; the launch traced here: 155 us
  waiting for transfers between devices  66.3 us (42%)
  starting transfers between devices  48.3 us (31%)
  Pallas kernels  32.4 us (21%)
  local copies, waits for them, and re-layouts  4.77 us (3%)
  other arithmetic  2.16 us (1%)
    all_to_all x5, starting transfers between devices, exchange(): return lax.all_to_all(pieces, axes, 0, 0, tiled=True)  35 us
    ppermute x3, waiting for transfers between devices, partner(): return lax.ppermute(value, 'z', [(i, i ^ bit) for i in range(size)])  25.4 us
    all_to_all x5, waiting for transfers between devices, exchange(): return lax.all_to_all(pieces, axes, 0, 0, tiled=True)  23 us
    ppermute x8, waiting for transfers between devices, swap(): return lax.ppermute(value, axis, [(0, 1), (1, 0)])  17.9 us
    pallas_call x2, Pallas kernels, logits_call(): pl.pallas_call(logits_kernel, in_specs=[pl.BlockSpec(memory_space=pltpu.S...  15.6 us
    pallas_call x1, Pallas kernels, part_call(): pl.pallas_call(part_kernel, in_specs=[pl.BlockSpec(memory_space=pltpu.SME...  7.8 us
    pallas_call x1, Pallas kernels, table_call(): pl.pallas_call(table_kernel, grid_spec=pltpu.PrefetchScalarGridSpec(num_s...  7.8 us
    ppermute x8, starting transfers between devices, swap(): return lax.ppermute(value, axis, [(0, 1), (1, 0)])  7.04 us
  transfers between devices with their start and end apart: 16, of which 9 were waited for; matrix products, arithmetic and copies ran while one was open for 1% of the time, Pallas kernels for 16%

profile of v7, /device:TPU:8, one launch (start us, length us, event | category | flops | bytes accessed | tf_op | source)
XLA Modules:
  0.0 154.8 jit_solution(15081807502963417783)
XLA Ops:
  0.6 1.4 broadcast_in_dim.6
  2.0 8.5 %all-to-all-start = ((bf16[8,32,256]{2,1,0:T(8,128)(2,1)}), bf16[8,32,256]{2,1,0:T(8,128)(2,1)S(1)}, u32[]{:S(2)}, u32[]{:S(2)}) async-start(bf16[8,32,256]{2,1,0:T(8,128)(2,1)} %broadcast_in_dim.6), calls=%async_computation | async-start | bytes 262144 | tf_op jit(solution)/shard_map/all_to_all | solution.py:25
  10.5 0.7 convert_bitcast_fusion.3
  11.1 8.4 %all-to-all-done = bf16[8,32,256]{2,1,0:T(8,128)(2,1)S(1)} async-done(((bf16[8,32,256]{2,1,0:T(8,128)(2,1)}), bf16[8,32,256]{2,1,0:T(8,128)(2,1)S(1)}, u32[]{:S(2)}, u32[]{:S(2)}) %all-to-all-start) | async-done | bytes 131104 | tf_op jit(solution)/shard_map/all_to_all | solution.py:25
  19.6 1.0 broadcast_in_dim.7
  20.6 5.8 %all-to-all-start.1 = ((bf16[8,256,256]{2,1,0:T(8,128)(2,1)}), bf16[8,256,256]{2,1,0:T(8,128)(2,1)}, u32[]{:S(2)}, u32[]{:S(2)}) async-start(bf16[8,256,256]{2,1,0:T(8,128)(2,1)} %broadcast_in_dim.7), calls=%async_computation.1 | async-start | bytes 2097152 | tf_op jit(solution)/shard_map/all_to_all | solution.py:25
  26.5 2.8 %collective-permute-start.1 = (bf16[72,1024]{1,0:T(8,128)(2,1)S(1)}, bf16[72,1024]{1,0:T(8,128)(2,1)S(1)}, u32[]{:S(2)}, u32[]{:S(2)}) collective-permute-start(bf16[72,1024]{1,0:T(8,128)(2,1)S(1)} %get-tuple-element.29), channel_id=1, source_target_pairs={{0,128},{128,0},{1,129},{129,1},{2,130},{130,2},{3,131},{131,3},{4... | collective-permute-start | bytes 442376 | tf_op jit(solution)/shard_map/ppermute | solution.py:33
  29.4 13.0 %collective-permute-done.1.refs_2_ = bf16[72,1024]{1,0:T(8,128)(2,1)S(1)} collective-permute-done((bf16[72,1024]{1,0:T(8,128)(2,1)S(1)}, bf16[72,1024]{1,0:T(8,128)(2,1)S(1)}, u32[]{:S(2)}, u32[]{:S(2)}) %collective-permute-start.1) | collective-permute-done | bytes 147488 | tf_op jit(solution)/shard_map/ppermute | solution.py:33
  42.4 1.3 collective-permute-done.2.refs_3_
  43.7 1.1 select.28
  44.9 1.0 collective-permute-start.3
  45.8 14.0 %collective-permute-done.3.refs_1_.refs_3_.refs_5_.r1 = bf16[528,256]{1,0:T(8,128)(2,1)S(1)} collective-permute-done((bf16[528,256]{1,0:T(8,128)(2,1)S(1)}, bf16[528,256]{1,0:T(8,128)(2,1)S(1)}, u32[]{:S(2)}, u32[]{:S(2)}) %collective-permute-start.3) | collective-permute-done | bytes 270368 | tf_op jit(solution)/shard_map/ppermute | solution.py:42
  59.8 3.8 %collective-permute-start.4 = (bf16[544,256]{1,0:T(8,128)(2,1)S(1)}, bf16[544,256]{1,0:T(8,128)(2,1)S(1)}, u32[]{:S(2)}, u32[]{:S(2)}) collective-permute-start(bf16[544,256]{1,0:T(8,128)(2,1)S(1)} %join.2), channel_id=1, source_target_pairs={{0,4},{2,6},{4,0},{6,2},{8,12},{10,14},{12,8},{14,10},{1,5},{3,7},... | collective-permute-start | bytes 835592 | tf_op jit(solution)/shard_map/ppermute | solution.py:42
  63.7 0.8 collective-permute-start.9
  64.5 7.9 %logits.2 = (bf16[3072,256]{1,0:T(8,128)(2,1)}, f32[64,4,256]{2,1,0:T(4,128)}, f32[8,256]{1,0:T(8,128)}) custom-call(s32[5]{0:T(128)} %copy-done.6, s32[1,256]{1,0:T(1,128)} %bitcast.28, bf16[8,256,256]{2,1,0:T(8,128)(2,1)} %all-to-all-done.1.got_ref, bf16[2000,2048]{1,0:T(8,128)(2,1)} %table_ref.5), custom_call_target="tpu_custom_call" | custom-call | flops 2097152000 | bytes 11337728 | tf_op jit(solution)/shard_map/logits/pallas_call | solution.py:210
  72.3 8.6 %all-to-all-start.2 = ((f32[64,4,256]{2,1,0:T(4,128)}), f32[64,4,256]{2,1,0:T(4,128)S(1)}, u32[]{:S(2)}, u32[]{:S(2)}) async-start(f32[64,4,256]{2,1,0:T(4,128)} %get-tuple-element.16), calls=%async_computation.2 | async-start | bytes 524288 | tf_op jit(solution)/shard_map/all_to_all | solution.py:25
  81.1 1.6 %collective-permute-start.5 = (bf16[576,256]{1,0:T(8,128)(2,1)S(1)}, bf16[576,256]{1,0:T(8,128)(2,1)S(1)}, u32[]{:S(2)}, u32[]{:S(2)}) collective-permute-start(bf16[576,256]{1,0:T(8,128)(2,1)S(1)} %join.3), channel_id=1, source_target_pairs={{0,2},{2,0},{4,6},{6,4},{8,10},{10,8},{12,14},{14,12},{1,3},{3,1},... | collective-permute-start | bytes 884744 | tf_op jit(solution)/shard_map/ppermute | solution.py:42
  82.6 11.4 %collective-permute-done.5.r3 = bf16[576,256]{1,0:T(8,128)(2,1)S(1)} collective-permute-done((bf16[576,256]{1,0:T(8,128)(2,1)S(1)}, bf16[576,256]{1,0:T(8,128)(2,1)S(1)}, u32[]{:S(2)}, u32[]{:S(2)}) %collective-permute-start.5) | collective-permute-done | bytes 294944 | tf_op jit(solution)/shard_map/ppermute | solution.py:42
  94.0 0.7 copy-done.9
  94.8 7.8 %part.1 = (bf16[8,400,256]{2,1,0:T(8,128)(2,1)}, f32[1,256]{1,0:T(1,128)}, f32[8,256]{1,0:T(8,128)}) custom-call(s32[5]{0:T(128)} %copy-done.6, s32[1,256]{1,0:T(1,128)} %bitcast.29, f32[8,256]{1,0:T(8,128)} %get-tuple-element.15.own_ref, f32[64,4,256]{2,1,0:T(4,128)} %copy-done.8, bf16[3072,256]{1,0:T(8,128)(2,1)} %get-tuple-element.17.near_ref.refs_0_.refs_1_, ...), custom_call_target="tpu_custom_call" | custom-call | flops 2097152000 | bytes 9240576 | tf_op jit(solution)/shard_map/part/pallas_call | solution.py:317
  102.6 6.0 %all-to-all-start.3 = ((bf16[8,400,256]{2,1,0:T(8,128)(2,1)}), bf16[8,400,256]{2,1,0:T(8,128)(2,1)S(1)}, u32[]{:S(2)}, u32[]{:S(2)}) async-start(bf16[8,400,256]{2,1,0:T(8,128)(2,1)} %get-tuple-element.24), calls=%async_computation.3 | async-start | bytes 3276800 | tf_op jit(solution)/shard_map/all_to_all | solution.py:25
  108.6 7.8 %logits.3 = (bf16[3072,256]{1,0:T(8,128)(2,1)}, f32[1,4,256]{2,1,0:T(4,128)}, f32[8,256]{1,0:T(8,128)}) custom-call(s32[5]{0:T(128)} %copy-done.6, s32[1,256]{1,0:T(1,128)} %bitcast.30, bf16[8,256,256]{2,1,0:T(8,128)(2,1)} %collective-permute-done.9.got_ref, bf16[2000,2048]{1,0:T(8,128)(2,1)} %table_ref.5), custom_call_target="tpu_custom_call" | custom-call | flops 2097152000 | bytes 11337728 | tf_op jit(solution)/shard_map/logits/pallas_call | solution.py:210
  117.0 10.6 %all-to-all-done.3.got_ref = bf16[8,400,256]{2,1,0:T(8,128)(2,1)S(1)} async-done(((bf16[8,400,256]{2,1,0:T(8,128)(2,1)}), bf16[8,400,256]{2,1,0:T(8,128)(2,1)S(1)}, u32[]{:S(2)}, u32[]{:S(2)}) %all-to-all-start.3) | async-done | bytes 1638432 | tf_op jit(solution)/shard_map/all_to_all | solution.py:25
  127.6 0.8 convert_reduce_fusion
  128.5 6.1 %all-to-all-start.4 = ((f32[8,32,256]{2,1,0:T(8,128)}), f32[8,32,256]{2,1,0:T(8,128)S(1)}, u32[]{:S(2)}, u32[]{:S(2)}) async-start(f32[8,32,256]{2,1,0:T(8,128)} %bitcast.12), calls=%async_computation.4 | async-start | bytes 524288 | tf_op jit(solution)/shard_map/all_to_all | solution.py:25
  134.6 1.2 collective-permute-done.6
  135.8 2.7 %collective-permute-start.7 = (f32[2,8,256]{2,1,0:T(8,128)S(1)}, f32[2,8,256]{2,1,0:T(8,128)S(1)}, u32[]{:S(2)}, u32[]{:S(2)}) collective-permute-start(f32[2,8,256]{2,1,0:T(8,128)S(1)} %pad_maximum_fusion.2), channel_id=1, source_target_pairs={{0,128},{128,0},{1,129},{129,1},{2,130},{130,2},{3,131},{131,3},{4... | collective-permute-start | bytes 49160 | tf_op jit(solution)/shard_map/ppermute | solution.py:33
  138.5 2.5 %collective-permute-done.7 = f32[2,8,256]{2,1,0:T(8,128)S(1)} collective-permute-done((f32[2,8,256]{2,1,0:T(8,128)S(1)}, f32[2,8,256]{2,1,0:T(8,128)S(1)}, u32[]{:S(2)}, u32[]{:S(2)}) %collective-permute-start.7) | collective-permute-done | bytes 16416 | tf_op jit(solution)/shard_map/ppermute | solution.py:33
  141.0 4.0 %all-to-all-done.4 = f32[8,32,256]{2,1,0:T(8,128)S(1)} async-done(((f32[8,32,256]{2,1,0:T(8,128)}), f32[8,32,256]{2,1,0:T(8,128)S(1)}, u32[]{:S(2)}, u32[]{:S(2)}) %all-to-all-start.4) | async-done | bytes 262176 | tf_op jit(solution)/shard_map/all_to_all | solution.py:25
  145.0 0.6 reduce_sum.19
  145.6 1.4 copy-done.2
  147.0 7.8 %table_grad.1 = bf16[2000,512]{1,0:T(8,128)(2,1)} custom-call(s32[5]{0:T(128)S(1)} %copy-done.7, f32[4,8,256]{2,1,0:T(8,128)S(1)} %pad_maximum_fusion.1.w_ref, bf16[8,400,256]{2,1,0:T(8,128)(2,1)S(1)} %all-to-all-done.3.got_ref, bf16[3072,256]{1,0:T(8,128)(2,1)S(1)} %copy-done, bf16[3072,256]{1,0:T(8,128)(2,1)S(1)} %copy-done, ...), custom_call_target="tpu_custom_call" | custom-call | flops 3145728000 | bytes 6144000 | tf_op jit(solution)/shard_map/table_grad/pallas_call | solution.py:395
  (42 shorter events, 1.0 us)
Async XLA Ops:
  2.0 17.6 %all-to-all-start = ((bf16[8,32,256]{2,1,0:T(8,128)(2,1)}), bf16[8,32,256]{2,1,0:T(8,128)(2,1)S(1)}, u32[]{:S(2)}, u32[]{:S(2)}) async-start(bf16[8,32,256]{2,1,0:T(8,128)(2,1)} %broadcast_in_dim.6), calls=%async_computation | async-start | bytes 262144 | tf_op jit(solution)/shard_map/all_to_all | solution.py:25
  19.6 6.9 %copy-start.10 = (bf16[64,2048]{1,0:T(8,128)(2,1)S(1)}, bf16[64,2048]{1,0:T(8,128)(2,1)}, u32[]{:S(2)}) copy-start(bf16[64,2048]{1,0:T(8,128)(2,1)} %param.9) | copy-start | bytes 786436
  20.6 43.1 %all-to-all-start.1 = ((bf16[8,256,256]{2,1,0:T(8,128)(2,1)}), bf16[8,256,256]{2,1,0:T(8,128)(2,1)}, u32[]{:S(2)}, u32[]{:S(2)}) async-start(bf16[8,256,256]{2,1,0:T(8,128)(2,1)} %broadcast_in_dim.7), calls=%async_computation.1 | async-start | bytes 2097152 | tf_op jit(solution)/shard_map/all_to_all | solution.py:25
  26.5 15.8 %collective-permute-start.1 = (bf16[72,1024]{1,0:T(8,128)(2,1)S(1)}, bf16[72,1024]{1,0:T(8,128)(2,1)S(1)}, u32[]{:S(2)}, u32[]{:S(2)}) collective-permute-start(bf16[72,1024]{1,0:T(8,128)(2,1)S(1)} %get-tuple-element.29), channel_id=1, source_target_pairs={{0,128},{128,0},{1,129},{129,1},{2,130},{130,2},{3,131},{131,3},{4... | collective-permute-start | bytes 442376 | tf_op jit(solution)/shard_map/ppermute | solution.py:33
  29.4 13.1 %collective-permute-start = (bf16[72,1024]{1,0:T(8,128)(2,1)S(1)}, bf16[72,1024]{1,0:T(8,128)(2,1)S(1)}, u32[]{:S(2)}, u32[]{:S(2)}) collective-permute-start(bf16[72,1024]{1,0:T(8,128)(2,1)S(1)} %get-tuple-element.30.refs_0_), channel_id=1, source_target_pairs={{0,64},{64,0},{1,65},{65,1},{2,66},{66,2},{3,67},{67,3},{4,68},{68... | collective-permute-start | bytes 442376 | tf_op jit(solution)/shard_map/ppermute | solution.py:33
  42.3 1.4 collective-permute-start.2
  42.4 22.1 %copy-start.6 = (s32[5]{0:T(128)}, s32[5]{0:T(128)S(1)}, u32[]{:S(2)}) copy-start(s32[5]{0:T(128)S(1)} %stack.48.where_ref) | copy-start | bytes 64
  44.9 15.0 %copy-start.5 = (bf16[128,256]{1,0:T(8,128)(2,1)}, bf16[128,256]{1,0:T(8,128)(2,1)S(1)}, u32[]{:S(2)}) copy-start(bf16[128,256]{1,0:T(8,128)(2,1)S(1)} %get-tuple-element.18.x0) | copy-start | bytes 196612
  44.9 36.1 %copy-start.4 = (bf16[16,256]{1,0:T(8,128)(2,1)}, bf16[16,256]{1,0:T(8,128)(2,1)S(1)}, u32[]{:S(2)}) copy-start(bf16[16,256]{1,0:T(8,128)(2,1)S(1)} %get-tuple-element.21.refs_2_.refs_4_.c0) | copy-start | bytes 24580
  44.9 14.9 %collective-permute-start.3 = (bf16[528,256]{1,0:T(8,128)(2,1)S(1)}, bf16[528,256]{1,0:T(8,128)(2,1)S(1)}, u32[]{:S(2)}, u32[]{:S(2)}) collective-permute-start(bf16[528,256]{1,0:T(8,128)(2,1)S(1)} %get-tuple-element.19), channel_id=1, source_target_pairs={{0,8},{2,10},{4,12},{6,14},{8,0},{10,2},{12,4},{14,6},{1,9},{3,11}... | collective-permute-start | bytes 811016 | tf_op jit(solution)/shard_map/ppermute | solution.py:42
  59.8 21.2 %copy-start.1 = (bf16[528,256]{1,0:T(8,128)(2,1)}, bf16[528,256]{1,0:T(8,128)(2,1)S(1)}, u32[]{:S(2)}) copy-start(bf16[528,256]{1,0:T(8,128)(2,1)S(1)} %collective-permute-done.3.refs_1_.refs_3_.refs_5_.r1) | copy-start | bytes 811012
  59.8 21.2 %collective-permute-start.4 = (bf16[544,256]{1,0:T(8,128)(2,1)S(1)}, bf16[544,256]{1,0:T(8,128)(2,1)S(1)}, u32[]{:S(2)}, u32[]{:S(2)}) collective-permute-start(bf16[544,256]{1,0:T(8,128)(2,1)S(1)} %join.2), channel_id=1, source_target_pairs={{0,4},{2,6},{4,0},{6,2},{8,12},{10,14},{12,8},{14,10},{1,5},{3,7},... | collective-permute-start | bytes 835592 | tf_op jit(solution)/shard_map/ppermute | solution.py:42
  63.7 44.9 %collective-permute-start.9 = (bf16[8,256,256]{2,1,0:T(8,128)(2,1)}, bf16[8,256,256]{2,1,0:T(8,128)(2,1)}, u32[]{:S(2)}, u32[]{:S(2)}) collective-permute-start(bf16[8,256,256]{2,1,0:T(8,128)(2,1)} %all-to-all-done.1.got_ref), channel_id=1, source_target_pairs={{0,128},{128,0},{1,129},{129,1},{2,130},{130,2},{3,131},{131,3},{4... | collective-permute-start | bytes 3145736 | tf_op jit(solution)/shard_map/ppermute | solution.py:33
  72.3 21.7 %all-to-all-start.2 = ((f32[64,4,256]{2,1,0:T(4,128)}), f32[64,4,256]{2,1,0:T(4,128)S(1)}, u32[]{:S(2)}, u32[]{:S(2)}) async-start(f32[64,4,256]{2,1,0:T(4,128)} %get-tuple-element.16), calls=%async_computation.2 | async-start | bytes 524288 | tf_op jit(solution)/shard_map/all_to_all | solution.py:25
  81.0 13.0 %copy-start.3 = (bf16[544,256]{1,0:T(8,128)(2,1)}, bf16[544,256]{1,0:T(8,128)(2,1)S(1)}, u32[]{:S(2)}) copy-start(bf16[544,256]{1,0:T(8,128)(2,1)S(1)} %collective-permute-done.4.refs_2_.refs_3_.refs_6_.r2) | copy-start | bytes 835588
  81.1 12.9 %collective-permute-start.5 = (bf16[576,256]{1,0:T(8,128)(2,1)S(1)}, bf16[576,256]{1,0:T(8,128)(2,1)S(1)}, u32[]{:S(2)}, u32[]{:S(2)}) collective-permute-start(bf16[576,256]{1,0:T(8,128)(2,1)S(1)} %join.3), channel_id=1, source_target_pairs={{0,2},{2,0},{4,6},{6,4},{8,10},{10,8},{12,14},{14,12},{1,3},{3,1},... | collective-permute-start | bytes 884744 | tf_op jit(solution)/shard_map/ppermute | solution.py:42
  94.0 0.7 copy-start.9
  94.0 0.8 copy-start.8
  102.6 6.0 %copy-start = (bf16[3072,256]{1,0:T(8,128)(2,1)S(1)}, bf16[3072,256]{1,0:T(8,128)(2,1)}, u32[]{:S(2)}) copy-start(bf16[3072,256]{1,0:T(8,128)(2,1)} %get-tuple-element.17.near_ref.refs_0_.refs_1_) | copy-start | bytes 4718596
  102.6 25.0 %all-to-all-start.3 = ((bf16[8,400,256]{2,1,0:T(8,128)(2,1)}), bf16[8,400,256]{2,1,0:T(8,128)(2,1)S(1)}, u32[]{:S(2)}, u32[]{:S(2)}) async-start(bf16[8,400,256]{2,1,0:T(8,128)(2,1)} %get-tuple-element.24), calls=%async_computation.3 | async-start | bytes 3276800 | tf_op jit(solution)/shard_map/all_to_all | solution.py:25
  108.6 37.0 %collective-permute-start.8 = (bf16[3072,256]{1,0:T(8,128)(2,1)S(1)}, bf16[3072,256]{1,0:T(8,128)(2,1)}, u32[]{:S(2)}, u32[]{:S(2)}) collective-permute-start(bf16[3072,256]{1,0:T(8,128)(2,1)S(1)} %copy-done), channel_id=1, source_target_pairs={{0,64},{64,0},{1,65},{65,1},{2,66},{66,2},{3,67},{67,3},{4,68},{68... | collective-permute-start | bytes 4718600 | tf_op jit(solution)/shard_map/ppermute | solution.py:33
  116.4 18.1 %copy-start.11 = (f32[8,256]{1,0:T(8,128)S(1)}, f32[8,256]{1,0:T(8,128)}, u32[]{:S(2)}) copy-start(f32[8,256]{1,0:T(8,128)} %get-tuple-element.25) | copy-start | bytes 24580
  116.4 29.2 %copy-start.7 = (s32[5]{0:T(128)S(1)}, s32[5]{0:T(128)}, u32[]{:S(2)}) copy-start(s32[5]{0:T(128)} %copy-done.6) | copy-start | bytes 64
  116.4 29.2 %collective-permute-start.10 = (bf16[3072,256]{1,0:T(8,128)(2,1)}, bf16[3072,256]{1,0:T(8,128)(2,1)}, u32[]{:S(2)}, u32[]{:S(2)}) collective-permute-start(bf16[3072,256]{1,0:T(8,128)(2,1)} %get-tuple-element.26.refs_4_.refs_5_), channel_id=1, source_target_pairs={{0,64},{64,0},{1,65},{65,1},{2,66},{66,2},{3,67},{67,3},{4,68},{68... | collective-permute-start | bytes 4718600 | tf_op jit(solution)/shard_map/ppermute | solution.py:33
  128.5 16.5 %all-to-all-start.4 = ((f32[8,32,256]{2,1,0:T(8,128)}), f32[8,32,256]{2,1,0:T(8,128)S(1)}, u32[]{:S(2)}, u32[]{:S(2)}) async-start(f32[8,32,256]{2,1,0:T(8,128)} %bitcast.12), calls=%async_computation.4 | async-start | bytes 524288 | tf_op jit(solution)/shard_map/all_to_all | solution.py:25
  134.5 1.3 collective-permute-start.6
  135.8 5.2 %collective-permute-start.7 = (f32[2,8,256]{2,1,0:T(8,128)S(1)}, f32[2,8,256]{2,1,0:T(8,128)S(1)}, u32[]{:S(2)}, u32[]{:S(2)}) collective-permute-start(f32[2,8,256]{2,1,0:T(8,128)S(1)} %pad_maximum_fusion.2), channel_id=1, source_target_pairs={{0,128},{128,0},{1,129},{129,1},{2,130},{130,2},{3,131},{131,3},{4... | collective-permute-start | bytes 49160 | tf_op jit(solution)/shard_map/ppermute | solution.py:33
  145.6 1.4 copy-start.2

commit v8 on v7

--- a/solution.py
+++ b/solution.py
@@ -406,7 +406,7 @@
             scratch_shapes=[pltpu.VMEM((512, block), BF16), pltpu.VMEM((8, 512), I32)],
         ),
         out_shape=jax.ShapeDtypeStruct((count, block), BF16),
-        compiler_params=PARAMS,
+        compiler_params=WIDE,
         cost_estimate=cost(2 * count * block * 1536, 8 * count * 256 + 2 * count * block),
         name="table_grad",
     )(where, w, got, *operands)
@@ -459,8 +459,8 @@
     part = jnp.sum(exchange(part, "z"), axis=0)
     hidden_grad = part.astype(BF16).T
 
-    w_near = jnp.stack([w, swap(w, "c")])
-    w_all = jnp.concatenate([w_near, swap(w_near, "xh")], axis=0)
+    w_far = swap(w, "xh")
+    w_all = jnp.stack([w, swap(w, "c"), w_far, swap(w_far, "c")])
     table_grad = table_call(
         where, w_all, got, (near, near_sib, far, far_sib), vocab_rows
     )

time: 157 us -> 157 us (level)
    ppermute x8 -> x9, waiting for transfers between devices: 17.9 us -> 17.8 us  [swap(): return lax.ppermute(value, axis, [(0, 1), (1, 0)])]
    ppermute x8 -> x9, starting transfers between devices: 7.04 us -> 7.03 us  [swap(): return lax.ppermute(value, axis, [(0, 1), (1, 0)])]
  transfers between devices with their start and end apart: 16 -> 17, of which waited for: 9 -> 9; matrix products, arithmetic and copies ran while one was open for 1% -> 2% of each run, Pallas kernels for 16% -> 16%
where the time goes in v8:
time: 157 us; the launch traced here: 155 us
  waiting for transfers between devices  65.8 us (42%)
  starting transfers between devices  48.3 us (31%)
  Pallas kernels  33.7 us (21%)
  local copies, waits for them, and re-layouts  3.36 us (2%)
  other arithmetic  2.94 us (2%)
    all_to_all x5, starting transfers between devices, exchange(): return lax.all_to_all(pieces, axes, 0, 0, tiled=True)  35 us
    ppermute x3, waiting for transfers between devices, partner(): return lax.ppermute(value, 'z', [(i, i ^ bit) for i in range(size)])  25.4 us
    all_to_all x5, waiting for transfers between devices, exchange(): return lax.all_to_all(pieces, axes, 0, 0, tiled=True)  22.6 us
    ppermute x9, waiting for transfers between devices, swap(): return lax.ppermute(value, axis, [(0, 1), (1, 0)])  17.8 us
    pallas_call x2, Pallas kernels, logits_call(): pl.pallas_call(logits_kernel, in_specs=[pl.BlockSpec(memory_space=pltpu.S...  15.6 us
    pallas_call x1, Pallas kernels, table_call(): pl.pallas_call(table_kernel, grid_spec=pltpu.PrefetchScalarGridSpec(num_s...  9.11 us
    pallas_call x1, Pallas kernels, part_call(): pl.pallas_call(part_kernel, in_specs=[pl.BlockSpec(memory_space=pltpu.SME...  7.8 us
    ppermute x9, starting transfers between devices, swap(): return lax.ppermute(value, axis, [(0, 1), (1, 0)])  7.03 us
  transfers between devices with their start and end apart: 17, of which 9 were waited for; matrix products, arithmetic and copies ran while one was open for 2% of the time, Pallas kernels for 16%

profile of v8, /device:TPU:8, one launch (start us, length us, event | category | flops | bytes accessed | tf_op | source)
XLA Modules:
  0.0 154.9 jit_solution(8002547605060351519)
XLA Ops:
  0.6 1.4 broadcast_in_dim.6
  2.0 8.5 %all-to-all-start = ((bf16[8,32,256]{2,1,0:T(8,128)(2,1)}), bf16[8,32,256]{2,1,0:T(8,128)(2,1)S(1)}, u32[]{:S(2)}, u32[]{:S(2)}) async-start(bf16[8,32,256]{2,1,0:T(8,128)(2,1)} %broadcast_in_dim.6), calls=%async_computation | async-start | bytes 262144 | tf_op jit(solution)/shard_map/all_to_all | solution.py:25
  10.5 0.7 convert_bitcast_fusion.3
  11.1 8.4 %all-to-all-done = bf16[8,32,256]{2,1,0:T(8,128)(2,1)S(1)} async-done(((bf16[8,32,256]{2,1,0:T(8,128)(2,1)}), bf16[8,32,256]{2,1,0:T(8,128)(2,1)S(1)}, u32[]{:S(2)}, u32[]{:S(2)}) %all-to-all-start) | async-done | bytes 131104 | tf_op jit(solution)/shard_map/all_to_all | solution.py:25
  19.6 1.0 broadcast_in_dim.7
  20.6 5.8 %all-to-all-start.1 = ((bf16[8,256,256]{2,1,0:T(8,128)(2,1)}), bf16[8,256,256]{2,1,0:T(8,128)(2,1)}, u32[]{:S(2)}, u32[]{:S(2)}) async-start(bf16[8,256,256]{2,1,0:T(8,128)(2,1)} %broadcast_in_dim.7), calls=%async_computation.1 | async-start | bytes 2097152 | tf_op jit(solution)/shard_map/all_to_all | solution.py:25
  26.5 2.8 %collective-permute-start.1 = (bf16[72,1024]{1,0:T(8,128)(2,1)S(1)}, bf16[72,1024]{1,0:T(8,128)(2,1)S(1)}, u32[]{:S(2)}, u32[]{:S(2)}) collective-permute-start(bf16[72,1024]{1,0:T(8,128)(2,1)S(1)} %get-tuple-element.29), channel_id=1, source_target_pairs={{0,128},{128,0},{1,129},{129,1},{2,130},{130,2},{3,131},{131,3},{4... | collective-permute-start | bytes 442376 | tf_op jit(solution)/shard_map/ppermute | solution.py:33
  29.4 13.0 %collective-permute-done.1.refs_2_ = bf16[72,1024]{1,0:T(8,128)(2,1)S(1)} collective-permute-done((bf16[72,1024]{1,0:T(8,128)(2,1)S(1)}, bf16[72,1024]{1,0:T(8,128)(2,1)S(1)}, u32[]{:S(2)}, u32[]{:S(2)}) %collective-permute-start.1) | collective-permute-done | bytes 147488 | tf_op jit(solution)/shard_map/ppermute | solution.py:33
  42.4 1.3 collective-permute-done.2.refs_3_
  43.7 1.1 select.28
  44.9 1.0 collective-permute-start.3
  45.8 14.0 %collective-permute-done.3.refs_1_.refs_3_.refs_5_.r1 = bf16[528,256]{1,0:T(8,128)(2,1)S(1)} collective-permute-done((bf16[528,256]{1,0:T(8,128)(2,1)S(1)}, bf16[528,256]{1,0:T(8,128)(2,1)S(1)}, u32[]{:S(2)}, u32[]{:S(2)}) %collective-permute-start.3) | collective-permute-done | bytes 270368 | tf_op jit(solution)/shard_map/ppermute | solution.py:42
  59.8 3.8 %collective-permute-start.4 = (bf16[544,256]{1,0:T(8,128)(2,1)S(1)}, bf16[544,256]{1,0:T(8,128)(2,1)S(1)}, u32[]{:S(2)}, u32[]{:S(2)}) collective-permute-start(bf16[544,256]{1,0:T(8,128)(2,1)S(1)} %join.2), channel_id=1, source_target_pairs={{0,4},{2,6},{4,0},{6,2},{8,12},{10,14},{12,8},{14,10},{1,5},{3,7},... | collective-permute-start | bytes 835592 | tf_op jit(solution)/shard_map/ppermute | solution.py:42
  63.7 0.8 collective-permute-start.10
  64.5 7.9 %logits.2 = (bf16[3072,256]{1,0:T(8,128)(2,1)}, f32[64,4,256]{2,1,0:T(4,128)}, f32[8,256]{1,0:T(8,128)}) custom-call(s32[5]{0:T(128)} %copy-done.4, s32[1,256]{1,0:T(1,128)} %bitcast.26, bf16[8,256,256]{2,1,0:T(8,128)(2,1)} %all-to-all-done.1.got_ref, bf16[2000,2048]{1,0:T(8,128)(2,1)} %table_ref.5), custom_call_target="tpu_custom_call" | custom-call | flops 2097152000 | bytes 11337728 | tf_op jit(solution)/shard_map/logits/pallas_call | solution.py:210
  72.3 8.6 %all-to-all-start.2 = ((f32[64,4,256]{2,1,0:T(4,128)}), f32[64,4,256]{2,1,0:T(4,128)S(1)}, u32[]{:S(2)}, u32[]{:S(2)}) async-start(f32[64,4,256]{2,1,0:T(4,128)} %get-tuple-element.16), calls=%async_computation.2 | async-start | bytes 524288 | tf_op jit(solution)/shard_map/all_to_all | solution.py:25
  81.1 1.6 %collective-permute-start.5 = (bf16[576,256]{1,0:T(8,128)(2,1)S(1)}, bf16[576,256]{1,0:T(8,128)(2,1)S(1)}, u32[]{:S(2)}, u32[]{:S(2)}) collective-permute-start(bf16[576,256]{1,0:T(8,128)(2,1)S(1)} %join.3), channel_id=1, source_target_pairs={{0,2},{2,0},{4,6},{6,4},{8,10},{10,8},{12,14},{14,12},{1,3},{3,1},... | collective-permute-start | bytes 884744 | tf_op jit(solution)/shard_map/ppermute | solution.py:42
  82.6 11.4 %collective-permute-done.5.r3 = bf16[576,256]{1,0:T(8,128)(2,1)S(1)} collective-permute-done((bf16[576,256]{1,0:T(8,128)(2,1)S(1)}, bf16[576,256]{1,0:T(8,128)(2,1)S(1)}, u32[]{:S(2)}, u32[]{:S(2)}) %collective-permute-start.5) | collective-permute-done | bytes 294944 | tf_op jit(solution)/shard_map/ppermute | solution.py:42
  94.0 0.7 copy-done.8
  94.8 7.8 %part.1 = (bf16[8,400,256]{2,1,0:T(8,128)(2,1)}, f32[1,256]{1,0:T(1,128)}, f32[8,256]{1,0:T(8,128)}) custom-call(s32[5]{0:T(128)} %copy-done.4, s32[1,256]{1,0:T(1,128)} %bitcast.27, f32[8,256]{1,0:T(8,128)} %get-tuple-element.15.own_ref, f32[64,4,256]{2,1,0:T(4,128)} %copy-done.7, bf16[3072,256]{1,0:T(8,128)(2,1)} %get-tuple-element.17.near_ref.refs_0_.refs_1_, ...), custom_call_target="tpu_custom_call" | custom-call | flops 2097152000 | bytes 9240576 | tf_op jit(solution)/shard_map/part/pallas_call | solution.py:317
  102.6 6.0 %all-to-all-start.3 = ((bf16[8,400,256]{2,1,0:T(8,128)(2,1)}), bf16[8,400,256]{2,1,0:T(8,128)(2,1)S(1)}, u32[]{:S(2)}, u32[]{:S(2)}) async-start(bf16[8,400,256]{2,1,0:T(8,128)(2,1)} %get-tuple-element.24), calls=%async_computation.3 | async-start | bytes 3276800 | tf_op jit(solution)/shard_map/all_to_all | solution.py:25
  108.6 7.7 %logits.3 = (bf16[3072,256]{1,0:T(8,128)(2,1)}, f32[1,4,256]{2,1,0:T(4,128)}, f32[8,256]{1,0:T(8,128)}) custom-call(s32[5]{0:T(128)} %copy-done.4, s32[1,256]{1,0:T(1,128)} %bitcast.28, bf16[8,256,256]{2,1,0:T(8,128)(2,1)} %collective-permute-done.10.got_ref, bf16[2000,2048]{1,0:T(8,128)(2,1)} %table_ref.5), custom_call_target="tpu_custom_call" | custom-call | flops 2097152000 | bytes 11337728 | tf_op jit(solution)/shard_map/logits/pallas_call | solution.py:210
  116.9 10.7 %all-to-all-done.3.got_ref = bf16[8,400,256]{2,1,0:T(8,128)(2,1)S(1)} async-done(((bf16[8,400,256]{2,1,0:T(8,128)(2,1)}), bf16[8,400,256]{2,1,0:T(8,128)(2,1)S(1)}, u32[]{:S(2)}, u32[]{:S(2)}) %all-to-all-start.3) | async-done | bytes 1638432 | tf_op jit(solution)/shard_map/all_to_all | solution.py:25
  127.6 1.0 convert_reduce_fusion
  128.6 6.1 %all-to-all-start.4 = ((f32[8,32,256]{2,1,0:T(8,128)}), f32[8,32,256]{2,1,0:T(8,128)S(1)}, u32[]{:S(2)}, u32[]{:S(2)}) async-start(f32[8,32,256]{2,1,0:T(8,128)} %bitcast.12), calls=%async_computation.4 | async-start | bytes 524288 | tf_op jit(solution)/shard_map/all_to_all | solution.py:25
  134.7 2.8 %collective-permute-start.7 = (f32[8,256]{1,0:T(8,128)S(1)}, f32[8,256]{1,0:T(8,128)S(1)}, u32[]{:S(2)}, u32[]{:S(2)}) collective-permute-start(f32[8,256]{1,0:T(8,128)S(1)} %copy-done.10), channel_id=1, source_target_pairs={{0,128},{128,0},{1,129},{129,1},{2,130},{130,2},{3,131},{131,3},{4... | collective-permute-start | bytes 24584 | tf_op jit(solution)/shard_map/ppermute | solution.py:33
  137.5 2.4 %collective-permute-done.7 = f32[8,256]{1,0:T(8,128)S(1)} collective-permute-done((f32[8,256]{1,0:T(8,128)S(1)}, f32[8,256]{1,0:T(8,128)S(1)}, u32[]{:S(2)}, u32[]{:S(2)}) %collective-permute-start.7) | collective-permute-done | bytes 8224 | tf_op jit(solution)/shard_map/ppermute | solution.py:33
  139.9 1.2 collective-permute-done.8
  141.1 0.6 pad_maximum_fusion.1.w_ref
  141.7 3.4 %all-to-all-done.4 = f32[8,32,256]{2,1,0:T(8,128)S(1)} async-done(((f32[8,32,256]{2,1,0:T(8,128)}), f32[8,32,256]{2,1,0:T(8,128)S(1)}, u32[]{:S(2)}, u32[]{:S(2)}) %all-to-all-start.4) | async-done | bytes 262176 | tf_op jit(solution)/shard_map/all_to_all | solution.py:25
  145.1 0.6 reduce_sum.19
  145.8 9.1 %table_grad.1 = bf16[2000,512]{1,0:T(8,128)(2,1)} custom-call(s32[5]{0:T(128)} %copy-done.4, f32[4,8,256]{2,1,0:T(8,128)} %pad_maximum_fusion.1.w_ref, bf16[8,400,256]{2,1,0:T(8,128)(2,1)} %copy-done.6, bf16[3072,256]{1,0:T(8,128)(2,1)} %get-tuple-element.17.near_ref.refs_0_.refs_1_, bf16[3072,256]{1,0:T(8,128)(2,1)} %get-tuple-element.17.near_ref.refs_0_.refs_1_, ...), custom_call_target="tpu_custom_call" | custom-call | flops 3145728000 | bytes 6144000 | tf_op jit(solution)/shard_map/table_grad/pallas_call | solution.py:395
  (41 shorter events, 0.9 us)
Async XLA Ops:
  2.0 17.6 %all-to-all-start = ((bf16[8,32,256]{2,1,0:T(8,128)(2,1)}), bf16[8,32,256]{2,1,0:T(8,128)(2,1)S(1)}, u32[]{:S(2)}, u32[]{:S(2)}) async-start(bf16[8,32,256]{2,1,0:T(8,128)(2,1)} %broadcast_in_dim.6), calls=%async_computation | async-start | bytes 262144 | tf_op jit(solution)/shard_map/all_to_all | solution.py:25
  19.6 6.9 %copy-start.9 = (bf16[64,2048]{1,0:T(8,128)(2,1)S(1)}, bf16[64,2048]{1,0:T(8,128)(2,1)}, u32[]{:S(2)}) copy-start(bf16[64,2048]{1,0:T(8,128)(2,1)} %param.9) | copy-start | bytes 786436
  20.6 43.1 %all-to-all-start.1 = ((bf16[8,256,256]{2,1,0:T(8,128)(2,1)}), bf16[8,256,256]{2,1,0:T(8,128)(2,1)}, u32[]{:S(2)}, u32[]{:S(2)}) async-start(bf16[8,256,256]{2,1,0:T(8,128)(2,1)} %broadcast_in_dim.7), calls=%async_computation.1 | async-start | bytes 2097152 | tf_op jit(solution)/shard_map/all_to_all | solution.py:25
  26.5 15.8 %collective-permute-start.1 = (bf16[72,1024]{1,0:T(8,128)(2,1)S(1)}, bf16[72,1024]{1,0:T(8,128)(2,1)S(1)}, u32[]{:S(2)}, u32[]{:S(2)}) collective-permute-start(bf16[72,1024]{1,0:T(8,128)(2,1)S(1)} %get-tuple-element.29), channel_id=1, source_target_pairs={{0,128},{128,0},{1,129},{129,1},{2,130},{130,2},{3,131},{131,3},{4... | collective-permute-start | bytes 442376 | tf_op jit(solution)/shard_map/ppermute | solution.py:33
  29.4 13.1 %collective-permute-start = (bf16[72,1024]{1,0:T(8,128)(2,1)S(1)}, bf16[72,1024]{1,0:T(8,128)(2,1)S(1)}, u32[]{:S(2)}, u32[]{:S(2)}) collective-permute-start(bf16[72,1024]{1,0:T(8,128)(2,1)S(1)} %get-tuple-element.30.refs_0_), channel_id=1, source_target_pairs={{0,64},{64,0},{1,65},{65,1},{2,66},{66,2},{3,67},{67,3},{4,68},{68... | collective-permute-start | bytes 442376 | tf_op jit(solution)/shard_map/ppermute | solution.py:33
  42.3 1.4 collective-permute-start.2
  42.4 22.1 %copy-start.4 = (s32[5]{0:T(128)}, s32[5]{0:T(128)S(1)}, u32[]{:S(2)}) copy-start(s32[5]{0:T(128)S(1)} %stack.54.where_ref) | copy-start | bytes 64
  44.9 15.0 %copy-start.3 = (bf16[128,256]{1,0:T(8,128)(2,1)}, bf16[128,256]{1,0:T(8,128)(2,1)S(1)}, u32[]{:S(2)}) copy-start(bf16[128,256]{1,0:T(8,128)(2,1)S(1)} %get-tuple-element.18.x0) | copy-start | bytes 196612
  44.9 36.1 %copy-start.2 = (bf16[16,256]{1,0:T(8,128)(2,1)}, bf16[16,256]{1,0:T(8,128)(2,1)S(1)}, u32[]{:S(2)}) copy-start(bf16[16,256]{1,0:T(8,128)(2,1)S(1)} %get-tuple-element.21.refs_2_.refs_4_.c0) | copy-start | bytes 24580
  44.9 14.9 %collective-permute-start.3 = (bf16[528,256]{1,0:T(8,128)(2,1)S(1)}, bf16[528,256]{1,0:T(8,128)(2,1)S(1)}, u32[]{:S(2)}, u32[]{:S(2)}) collective-permute-start(bf16[528,256]{1,0:T(8,128)(2,1)S(1)} %get-tuple-element.19), channel_id=1, source_target_pairs={{0,8},{2,10},{4,12},{6,14},{8,0},{10,2},{12,4},{14,6},{1,9},{3,11}... | collective-permute-start | bytes 811016 | tf_op jit(solution)/shard_map/ppermute | solution.py:42
  59.8 21.2 %copy-start = (bf16[528,256]{1,0:T(8,128)(2,1)}, bf16[528,256]{1,0:T(8,128)(2,1)S(1)}, u32[]{:S(2)}) copy-start(bf16[528,256]{1,0:T(8,128)(2,1)S(1)} %collective-permute-done.3.refs_1_.refs_3_.refs_5_.r1) | copy-start | bytes 811012
  59.8 21.2 %collective-permute-start.4 = (bf16[544,256]{1,0:T(8,128)(2,1)S(1)}, bf16[544,256]{1,0:T(8,128)(2,1)S(1)}, u32[]{:S(2)}, u32[]{:S(2)}) collective-permute-start(bf16[544,256]{1,0:T(8,128)(2,1)S(1)} %join.2), channel_id=1, source_target_pairs={{0,4},{2,6},{4,0},{6,2},{8,12},{10,14},{12,8},{14,10},{1,5},{3,7},... | collective-permute-start | bytes 835592 | tf_op jit(solution)/shard_map/ppermute | solution.py:42
  63.7 44.9 %collective-permute-start.10 = (bf16[8,256,256]{2,1,0:T(8,128)(2,1)}, bf16[8,256,256]{2,1,0:T(8,128)(2,1)}, u32[]{:S(2)}, u32[]{:S(2)}) collective-permute-start(bf16[8,256,256]{2,1,0:T(8,128)(2,1)} %all-to-all-done.1.got_ref), channel_id=1, source_target_pairs={{0,128},{128,0},{1,129},{129,1},{2,130},{130,2},{3,131},{131,3},{4... | collective-permute-start | bytes 3145736 | tf_op jit(solution)/shard_map/ppermute | solution.py:33
  72.3 21.7 %all-to-all-start.2 = ((f32[64,4,256]{2,1,0:T(4,128)}), f32[64,4,256]{2,1,0:T(4,128)S(1)}, u32[]{:S(2)}, u32[]{:S(2)}) async-start(f32[64,4,256]{2,1,0:T(4,128)} %get-tuple-element.16), calls=%async_computation.2 | async-start | bytes 524288 | tf_op jit(solution)/shard_map/all_to_all | solution.py:25
  81.0 13.0 %copy-start.1 = (bf16[544,256]{1,0:T(8,128)(2,1)}, bf16[544,256]{1,0:T(8,128)(2,1)S(1)}, u32[]{:S(2)}) copy-start(bf16[544,256]{1,0:T(8,128)(2,1)S(1)} %collective-permute-done.4.refs_2_.refs_3_.refs_6_.r2) | copy-start | bytes 835588
  81.1 12.9 %collective-permute-start.5 = (bf16[576,256]{1,0:T(8,128)(2,1)S(1)}, bf16[576,256]{1,0:T(8,128)(2,1)S(1)}, u32[]{:S(2)}, u32[]{:S(2)}) collective-permute-start(bf16[576,256]{1,0:T(8,128)(2,1)S(1)} %join.3), channel_id=1, source_target_pairs={{0,2},{2,0},{4,6},{6,4},{8,10},{10,8},{12,14},{14,12},{1,3},{3,1},... | collective-permute-start | bytes 884744 | tf_op jit(solution)/shard_map/ppermute | solution.py:42
  94.0 0.7 copy-start.8
  94.0 0.8 copy-start.7
  102.6 6.0 %copy-start.5 = (bf16[3072,256]{1,0:T(8,128)(2,1)S(1)}, bf16[3072,256]{1,0:T(8,128)(2,1)}, u32[]{:S(2)}) copy-start(bf16[3072,256]{1,0:T(8,128)(2,1)} %get-tuple-element.17.near_ref.refs_0_.refs_1_) | copy-start | bytes 4718596
  102.6 25.0 %all-to-all-start.3 = ((bf16[8,400,256]{2,1,0:T(8,128)(2,1)}), bf16[8,400,256]{2,1,0:T(8,128)(2,1)S(1)}, u32[]{:S(2)}, u32[]{:S(2)}) async-start(bf16[8,400,256]{2,1,0:T(8,128)(2,1)} %get-tuple-element.24), calls=%async_computation.3 | async-start | bytes 3276800 | tf_op jit(solution)/shard_map/all_to_all | solution.py:25
  108.6 37.2 %collective-permute-start.9 = (bf16[3072,256]{1,0:T(8,128)(2,1)S(1)}, bf16[3072,256]{1,0:T(8,128)(2,1)}, u32[]{:S(2)}, u32[]{:S(2)}) collective-permute-start(bf16[3072,256]{1,0:T(8,128)(2,1)S(1)} %copy-done.5), channel_id=1, source_target_pairs={{0,64},{64,0},{1,65},{65,1},{2,66},{66,2},{3,67},{67,3},{4,68},{68... | collective-permute-start | bytes 4718600 | tf_op jit(solution)/shard_map/ppermute | solution.py:33
  116.3 18.3 %copy-start.10 = (f32[8,256]{1,0:T(8,128)S(1)}, f32[8,256]{1,0:T(8,128)}, u32[]{:S(2)}) copy-start(f32[8,256]{1,0:T(8,128)} %get-tuple-element.25) | copy-start | bytes 24580
  116.3 29.4 %collective-permute-start.11 = (bf16[3072,256]{1,0:T(8,128)(2,1)}, bf16[3072,256]{1,0:T(8,128)(2,1)}, u32[]{:S(2)}, u32[]{:S(2)}) collective-permute-start(bf16[3072,256]{1,0:T(8,128)(2,1)} %get-tuple-element.26.refs_4_.refs_5_), channel_id=1, source_target_pairs={{0,64},{64,0},{1,65},{65,1},{2,66},{66,2},{3,67},{67,3},{4,68},{68... | collective-permute-start | bytes 4718600 | tf_op jit(solution)/shard_map/ppermute | solution.py:33
  127.6 18.2 %copy-start.6 = (bf16[8,400,256]{2,1,0:T(8,128)(2,1)}, bf16[8,400,256]{2,1,0:T(8,128)(2,1)S(1)}, u32[]{:S(2)}) copy-start(bf16[8,400,256]{2,1,0:T(8,128)(2,1)S(1)} %all-to-all-done.3.got_ref) | copy-start | bytes 4915204
  128.6 16.5 %all-to-all-start.4 = ((f32[8,32,256]{2,1,0:T(8,128)}), f32[8,32,256]{2,1,0:T(8,128)S(1)}, u32[]{:S(2)}, u32[]{:S(2)}) async-start(f32[8,32,256]{2,1,0:T(8,128)} %bitcast.12), calls=%async_computation.4 | async-start | bytes 524288 | tf_op jit(solution)/shard_map/all_to_all | solution.py:25
  134.7 5.2 %collective-permute-start.7 = (f32[8,256]{1,0:T(8,128)S(1)}, f32[8,256]{1,0:T(8,128)S(1)}, u32[]{:S(2)}, u32[]{:S(2)}) collective-permute-start(f32[8,256]{1,0:T(8,128)S(1)} %copy-done.10), channel_id=1, source_target_pairs={{0,128},{128,0},{1,129},{129,1},{2,130},{130,2},{3,131},{131,3},{4... | collective-permute-start | bytes 24584 | tf_op jit(solution)/shard_map/ppermute | solution.py:33
  137.5 2.4 %collective-permute-start.6 = (f32[8,256]{1,0:T(8,128)S(1)}, f32[8,256]{1,0:T(8,128)S(1)}, u32[]{:S(2)}, u32[]{:S(2)}) collective-permute-start(f32[8,256]{1,0:T(8,128)S(1)} %copy-done.10), channel_id=1, source_target_pairs={{0,64},{64,0},{1,65},{65,1},{2,66},{66,2},{3,67},{67,3},{4,68},{68... | collective-permute-start | bytes 24584 | tf_op jit(solution)/shard_map/ppermute | solution.py:33
  139.9 1.2 collective-permute-start.8

commit v9 on v8

--- a/solution.py
+++ b/solution.py
@@ -18,6 +18,7 @@
 DEPTH = 3
 PARAMS = pltpu.CompilerParams(vmem_limit_bytes=16 * 1024 * 1024)
 WIDE = pltpu.CompilerParams(vmem_limit_bytes=57 * 1024 * 1024)
+BASE = pltpu.CompilerParams(vmem_limit_bytes=60 * 1024 * 1024)
 FULL = pltpu.CompilerParams(vmem_limit_bytes=62 * 1024 * 1024)
 
 
@@ -234,7 +235,7 @@
 
 def part_kernel(
     where_ref, tgt_ref, own_ref, stats_ref, near_ref, x0, r1, r2, r3, c0, table_ref,
-    out_ref, loss_ref, w_ref, lhs, tab, buf, sems, out_sems,
+    out_ref, loss_ref, w_ref, near, lhs, tab, buf, sems, out_sems,
 ):
     tokens = tgt_ref.shape[1]
     count, width = table_ref.shape
@@ -250,6 +251,8 @@
         at = pl.ds(j * 2, 2)
         return pltpu.make_async_copy(buf.at[at], out_ref.at[at], out_sems.at[j])
 
+    given = pltpu.make_async_copy(near_ref.at[pl.ds(0, count)], near, sems.at[turns])
+    given.start()
     for j in range(DEPTH):
         load(j).start()
 
@@ -263,9 +266,10 @@
     w_ref[...] = jnp.concatenate(
         [w, tgt_ref[...].astype(F32), jnp.zeros((7 - chunks, tokens), F32)], axis=0
     )
+    given.wait()
     for i in range(chunks):
         index = lax.broadcasted_iota(I32, (CHUNK, tokens), 0) + (where_ref[0] + i * CHUNK)
-        e = near_ref[i * CHUNK : (i + 1) * CHUNK, :].astype(F32)
+        e = near[i * CHUNK : (i + 1) * CHUNK, :].astype(F32)
         residual = e * w[i : i + 1, :] - jnp.where(index == tgt_ref[...], 1.0, 0.0)
         lhs[i * CHUNK : (i + 1) * CHUNK, :] = residual.astype(BF16)
 
@@ -316,13 +320,16 @@
     shape = (plane, width // plane + 144, tokens)
     return pl.pallas_call(
         part_kernel,
-        in_specs=[pl.BlockSpec(memory_space=pltpu.SMEM), *[whole] * 9, anywhere],
+        in_specs=[
+            pl.BlockSpec(memory_space=pltpu.SMEM), *[whole] * 3, anywhere, *[whole] * 5, anywhere
+        ],
         out_specs=[pl.BlockSpec(memory_space=pltpu.HBM), whole, whole],
         scratch_shapes=[
             pltpu.VMEM((count, tokens), BF16),
+            pltpu.VMEM((count, tokens), BF16),
             pltpu.VMEM((width // wide, count, wide), BF16),
             pltpu.VMEM(shape, BF16),
-            pltpu.SemaphoreType.DMA((width // wide,)),
+            pltpu.SemaphoreType.DMA((width // wide + 1,)),
             pltpu.SemaphoreType.DMA((plane // 2,)),
         ],
         out_shape=[
@@ -336,7 +343,7 @@
     )(where, targets, own, stats, near, *riders, table)
 
 
-def table_kernel(where_ref, w_ref, got_ref, *refs):
+def table_kernel(where_ref, got_ref, base_ref, *refs):
     out_ref, rows, place = refs[-3:]
     count = out_ref.shape[0]
     first = pl.program_id(0) * count
@@ -369,10 +376,37 @@
         spot = jnp.sum(jnp.where(mine, found, 0.0), axis=0, keepdims=True) - 1.0
         place[...] = jnp.broadcast_to(spot, place.shape).astype(I32)
 
-    near = lax.broadcasted_iota(I32, (count, 256), 0) + (first + where_ref[0])
     spots = lax.broadcasted_iota(I32, (count, place.shape[1]), 0) + first
     match = jnp.where(spots == place[0:1, :], 1.0, 0.0).astype(BF16)
-    total = jnp.dot(match, rows[...], preferred_element_type=F32)
+    total = base_ref[...] + jnp.dot(match, rows[...], preferred_element_type=F32)
+    out_ref[...] = total.astype(BF16)
+
+
+def table_call(where, got, base):
+    count, block = base.shape
+    part = pl.BlockSpec((CHUNK, block), lambda i, s: (i, 0))
+    return pl.pallas_call(
+        table_kernel,
+        grid_spec=pltpu.PrefetchScalarGridSpec(
+            num_scalar_prefetch=1,
+            grid=(count // CHUNK,),
+            in_specs=[pl.BlockSpec(got.shape, lambda i, s: (0, 0, 0)), part],
+            out_specs=part,
+            scratch_shapes=[pltpu.VMEM((512, block), BF16), pltpu.VMEM((8, 512), I32)],
+        ),
+        out_shape=jax.ShapeDtypeStruct((count, block), BF16),
+        compiler_params=FULL,
+        cost_estimate=cost(2 * count * block * 512, 6 * count * block),
+        name="table_grad",
+    )(where, got, base)
+
+
+def base_kernel(where_ref, w_ref, *refs):
+    out_ref = refs[-1]
+    count = out_ref.shape[0]
+    first = where_ref[0] + pl.program_id(0) * count
+    near = lax.broadcasted_iota(I32, (count, 256), 0) + first
+    total = jnp.zeros(out_ref.shape, F32)
     for g in range(4):
         e = refs[2 * g][...].astype(F32)
         w = w_ref[g, pl.ds(pl.program_id(0), 1), :]
@@ -381,10 +415,10 @@
         total += lax.dot_general(
             res, refs[2 * g + 1][...], (((1,), (1,)), ((), ())), preferred_element_type=F32
         )
-    out_ref[...] = total.astype(BF16)
-
-
-def table_call(where, w, got, packs, count):
+    out_ref[...] = total
+
+
+def base_call(where, w, packs, count):
     tokens = packs[0].shape[1]
     block = 512
     specs, operands = [], []
@@ -393,23 +427,18 @@
         specs.append(pl.BlockSpec((block, tokens), lambda i, s: (4 + s[2], 0)))
         operands += [pack, pack]
     return pl.pallas_call(
-        table_kernel,
+        base_kernel,
         grid_spec=pltpu.PrefetchScalarGridSpec(
             num_scalar_prefetch=1,
             grid=(count // CHUNK,),
-            in_specs=[
-                pl.BlockSpec(w.shape, lambda i, s: (0, 0, 0)),
-                pl.BlockSpec(got.shape, lambda i, s: (0, 0, 0)),
-                *specs,
-            ],
+            in_specs=[pl.BlockSpec(w.shape, lambda i, s: (0, 0, 0)), *specs],
             out_specs=pl.BlockSpec((CHUNK, block), lambda i, s: (i, 0)),
-            scratch_shapes=[pltpu.VMEM((512, block), BF16), pltpu.VMEM((8, 512), I32)],
         ),
-        out_shape=jax.ShapeDtypeStruct((count, block), BF16),
-        compiler_params=WIDE,
-        cost_estimate=cost(2 * count * block * 1536, 8 * count * 256 + 2 * count * block),
-        name="table_grad",
-    )(where, w, got, *operands)
+        out_shape=jax.ShapeDtypeStruct((count, block), F32),
+        compiler_params=BASE,
+        cost_estimate=cost(2 * count * block * 1024, 8 * count * 256 + 4 * count * block),
+        name="base",
+    )(where, w, *operands)
 
 
 def inner(hidden, table, targets, input_ids, cotangent):
@@ -461,9 +490,8 @@
 
     w_far = swap(w, "xh")
     w_all = jnp.stack([w, swap(w, "c"), w_far, swap(w_far, "c")])
-    table_grad = table_call(
-        where, w_all, got, (near, near_sib, far, far_sib), vocab_rows
-    )
+    base = base_call(where, w_all, (near, near_sib, far, far_sib), vocab_rows)
+    table_grad = table_call(where, got, base)
     return loss.reshape(tokens), hidden_grad, table_grad
 
 

time: 157 us -> 163 us (1.038)
  Pallas kernels: 33.7 us -> 39.8 us
    pallas_call x0 -> x1, Pallas kernels: none -> 8.13 us  [base_call(): pl.pallas_call(base_kernel, grid_spec=pltpu.PrefetchScalarGridSpec(num_sc...]
    pallas_call x1, Pallas kernels: 9.11 us -> 7.24 us  [table_call(): pl.pallas_call(table_kernel, grid_spec=pltpu.PrefetchScalarGridSpec(num_s...]
  transfers between devices with their start and end apart: 17 -> 17, of which waited for: 9 -> 9; matrix products, arithmetic and copies ran while one was open for 2% -> 2% of each run, Pallas kernels for 16% -> 15%
where the time goes in v9:
time: 163 us; the launch traced here: 161 us
  waiting for transfers between devices  65.7 us (40%)
  starting transfers between devices  48.3 us (30%)
  Pallas kernels  39.8 us (24%)
  local copies, waits for them, and re-layouts  3.36 us (2%)
  other arithmetic  2.91 us (2%)
    all_to_all x5, starting transfers between devices, exchange(): return lax.all_to_all(pieces, axes, 0, 0, tiled=True)  35 us
    ppermute x3, waiting for transfers between devices, partner(): return lax.ppermute(value, 'z', [(i, i ^ bit) for i in range(size)])  25.4 us
    all_to_all x5, waiting for transfers between devices, exchange(): return lax.all_to_all(pieces, axes, 0, 0, tiled=True)  22.5 us
    ppermute x9, waiting for transfers between devices, swap(): return lax.ppermute(value, axis, [(0, 1), (1, 0)])  17.8 us
    pallas_call x2, Pallas kernels, logits_call(): pl.pallas_call(logits_kernel, in_specs=[pl.BlockSpec(memory_space=pltpu.S...  15.6 us
    pallas_call x1, Pallas kernels, base_call(): pl.pallas_call(base_kernel, grid_spec=pltpu.PrefetchScalarGridSpec(num_sc...  8.13 us
    pallas_call x1, Pallas kernels, part_call(): pl.pallas_call(part_kernel, in_specs=[pl.BlockSpec(memory_space=pltpu.SME...  7.66 us
    pallas_call x1, Pallas kernels, table_call(): pl.pallas_call(table_kernel, grid_spec=pltpu.PrefetchScalarGridSpec(num_s...  7.24 us
  transfers between devices with their start and end apart: 17, of which 9 were waited for; matrix products, arithmetic and copies ran while one was open for 2% of the time, Pallas kernels for 15%

profile of v9, /device:TPU:8, one launch (start us, length us, event | category | flops | bytes accessed | tf_op | source)
XLA Modules:
  0.0 161.0 jit_solution(3247996010237082186)
XLA Ops:
  0.6 1.4 broadcast_in_dim.6
  2.0 8.5 %all-to-all-start = ((bf16[8,32,256]{2,1,0:T(8,128)(2,1)}), bf16[8,32,256]{2,1,0:T(8,128)(2,1)S(1)}, u32[]{:S(2)}, u32[]{:S(2)}) async-start(bf16[8,32,256]{2,1,0:T(8,128)(2,1)} %broadcast_in_dim.6), calls=%async_computation | async-start | bytes 262144 | tf_op jit(solution)/shard_map/all_to_all | solution.py:26
  10.5 0.7 convert_bitcast_fusion.3
  11.1 8.4 %all-to-all-done = bf16[8,32,256]{2,1,0:T(8,128)(2,1)S(1)} async-done(((bf16[8,32,256]{2,1,0:T(8,128)(2,1)}), bf16[8,32,256]{2,1,0:T(8,128)(2,1)S(1)}, u32[]{:S(2)}, u32[]{:S(2)}) %all-to-all-start) | async-done | bytes 131104 | tf_op jit(solution)/shard_map/all_to_all | solution.py:26
  19.6 1.0 broadcast_in_dim.7
  20.6 5.8 %all-to-all-start.1 = ((bf16[8,256,256]{2,1,0:T(8,128)(2,1)}), bf16[8,256,256]{2,1,0:T(8,128)(2,1)}, u32[]{:S(2)}, u32[]{:S(2)}) async-start(bf16[8,256,256]{2,1,0:T(8,128)(2,1)} %broadcast_in_dim.7), calls=%async_computation.1 | async-start | bytes 2097152 | tf_op jit(solution)/shard_map/all_to_all | solution.py:26
  26.5 2.8 %collective-permute-start.1 = (bf16[72,1024]{1,0:T(8,128)(2,1)S(1)}, bf16[72,1024]{1,0:T(8,128)(2,1)S(1)}, u32[]{:S(2)}, u32[]{:S(2)}) collective-permute-start(bf16[72,1024]{1,0:T(8,128)(2,1)S(1)} %get-tuple-element.29), channel_id=1, source_target_pairs={{0,128},{128,0},{1,129},{129,1},{2,130},{130,2},{3,131},{131,3},{4... | collective-permute-start | bytes 442376 | tf_op jit(solution)/shard_map/ppermute | solution.py:34
  29.4 13.0 %collective-permute-done.1.refs_2_ = bf16[72,1024]{1,0:T(8,128)(2,1)S(1)} collective-permute-done((bf16[72,1024]{1,0:T(8,128)(2,1)S(1)}, bf16[72,1024]{1,0:T(8,128)(2,1)S(1)}, u32[]{:S(2)}, u32[]{:S(2)}) %collective-permute-start.1) | collective-permute-done | bytes 147488 | tf_op jit(solution)/shard_map/ppermute | solution.py:34
  42.4 1.3 collective-permute-done.2.refs_3_
  43.7 1.1 select.28
  44.9 1.0 collective-permute-start.3
  45.8 14.0 %collective-permute-done.3.refs_1_.refs_3_.refs_5_.r1 = bf16[528,256]{1,0:T(8,128)(2,1)S(1)} collective-permute-done((bf16[528,256]{1,0:T(8,128)(2,1)S(1)}, bf16[528,256]{1,0:T(8,128)(2,1)S(1)}, u32[]{:S(2)}, u32[]{:S(2)}) %collective-permute-start.3) | collective-permute-done | bytes 270368 | tf_op jit(solution)/shard_map/ppermute | solution.py:43
  59.8 3.8 %collective-permute-start.4 = (bf16[544,256]{1,0:T(8,128)(2,1)S(1)}, bf16[544,256]{1,0:T(8,128)(2,1)S(1)}, u32[]{:S(2)}, u32[]{:S(2)}) collective-permute-start(bf16[544,256]{1,0:T(8,128)(2,1)S(1)} %join.2), channel_id=1, source_target_pairs={{0,4},{2,6},{4,0},{6,2},{8,12},{10,14},{12,8},{14,10},{1,5},{3,7},... | collective-permute-start | bytes 835592 | tf_op jit(solution)/shard_map/ppermute | solution.py:43
  63.7 0.8 collective-permute-start.10
  64.5 7.9 %logits.2 = (bf16[3072,256]{1,0:T(8,128)(2,1)}, f32[64,4,256]{2,1,0:T(4,128)}, f32[8,256]{1,0:T(8,128)}) custom-call(s32[5]{0:T(128)} %copy-done.4, s32[1,256]{1,0:T(1,128)} %bitcast.26, bf16[8,256,256]{2,1,0:T(8,128)(2,1)} %all-to-all-done.1.got_ref, bf16[2000,2048]{1,0:T(8,128)(2,1)} %table_ref.5), custom_call_target="tpu_custom_call" | custom-call | flops 2097152000 | bytes 11337728 | tf_op jit(solution)/shard_map/logits/pallas_call | solution.py:211
  72.3 8.6 %all-to-all-start.2 = ((f32[64,4,256]{2,1,0:T(4,128)}), f32[64,4,256]{2,1,0:T(4,128)S(1)}, u32[]{:S(2)}, u32[]{:S(2)}) async-start(f32[64,4,256]{2,1,0:T(4,128)} %get-tuple-element.16), calls=%async_computation.2 | async-start | bytes 524288 | tf_op jit(solution)/shard_map/all_to_all | solution.py:26
  81.1 1.6 collective-permute-start.5
  82.6 11.4 %collective-permute-done.5.r3 = bf16[576,256]{1,0:T(8,128)(2,1)S(1)} collective-permute-done((bf16[576,256]{1,0:T(8,128)(2,1)S(1)}, bf16[576,256]{1,0:T(8,128)(2,1)S(1)}, u32[]{:S(2)}, u32[]{:S(2)}) %collective-permute-start.5) | collective-permute-done | bytes 294944 | tf_op jit(solution)/shard_map/ppermute | solution.py:43
  94.0 0.7 copy-done.8
  94.8 7.7 %part.1 = (bf16[8,400,256]{2,1,0:T(8,128)(2,1)}, f32[1,256]{1,0:T(1,128)}, f32[8,256]{1,0:T(8,128)}) custom-call(s32[5]{0:T(128)} %copy-done.4, s32[1,256]{1,0:T(1,128)} %bitcast.27, f32[8,256]{1,0:T(8,128)} %get-tuple-element.15.own_ref, f32[64,4,256]{2,1,0:T(4,128)} %copy-done.7, bf16[3072,256]{1,0:T(8,128)(2,1)} %get-tuple-element.17.near_ref.refs_0_.refs_1_, ...), custom_call_target="tpu_custom_call" | custom-call | flops 2097152000 | bytes 9240576 | tf_op jit(solution)/shard_map/part/pallas_call | solution.py:321
  102.5 6.0 %all-to-all-start.3 = ((bf16[8,400,256]{2,1,0:T(8,128)(2,1)}), bf16[8,400,256]{2,1,0:T(8,128)(2,1)S(1)}, u32[]{:S(2)}, u32[]{:S(2)}) async-start(bf16[8,400,256]{2,1,0:T(8,128)(2,1)} %get-tuple-element.24), calls=%async_computation.3 | async-start | bytes 3276800 | tf_op jit(solution)/shard_map/all_to_all | solution.py:26
  108.5 7.7 %logits.3 = (bf16[3072,256]{1,0:T(8,128)(2,1)}, f32[1,4,256]{2,1,0:T(4,128)}, f32[8,256]{1,0:T(8,128)}) custom-call(s32[5]{0:T(128)} %copy-done.4, s32[1,256]{1,0:T(1,128)} %bitcast.28, bf16[8,256,256]{2,1,0:T(8,128)(2,1)} %collective-permute-done.10.got_ref, bf16[2000,2048]{1,0:T(8,128)(2,1)} %table_ref.5), custom_call_target="tpu_custom_call" | custom-call | flops 2097152000 | bytes 11337728 | tf_op jit(solution)/shard_map/logits/pallas_call | solution.py:211
  116.8 10.7 %all-to-all-done.3.got_ref = bf16[8,400,256]{2,1,0:T(8,128)(2,1)S(1)} async-done(((bf16[8,400,256]{2,1,0:T(8,128)(2,1)}), bf16[8,400,256]{2,1,0:T(8,128)(2,1)S(1)}, u32[]{:S(2)}, u32[]{:S(2)}) %all-to-all-start.3) | async-done | bytes 1638432 | tf_op jit(solution)/shard_map/all_to_all | solution.py:26
  127.5 1.0 convert_reduce_fusion
  128.4 6.1 %all-to-all-start.4 = ((f32[8,32,256]{2,1,0:T(8,128)}), f32[8,32,256]{2,1,0:T(8,128)S(1)}, u32[]{:S(2)}, u32[]{:S(2)}) async-start(f32[8,32,256]{2,1,0:T(8,128)} %bitcast.12), calls=%async_computation.4 | async-start | bytes 524288 | tf_op jit(solution)/shard_map/all_to_all | solution.py:26
  134.5 2.8 %collective-permute-start.7 = (f32[8,256]{1,0:T(8,128)S(1)}, f32[8,256]{1,0:T(8,128)S(1)}, u32[]{:S(2)}, u32[]{:S(2)}) collective-permute-start(f32[8,256]{1,0:T(8,128)S(1)} %copy-done.10), channel_id=1, source_target_pairs={{0,128},{128,0},{1,129},{129,1},{2,130},{130,2},{3,131},{131,3},{4... | collective-permute-start | bytes 24584 | tf_op jit(solution)/shard_map/ppermute | solution.py:34
  137.3 2.4 %collective-permute-done.7 = f32[8,256]{1,0:T(8,128)S(1)} collective-permute-done((f32[8,256]{1,0:T(8,128)S(1)}, f32[8,256]{1,0:T(8,128)S(1)}, u32[]{:S(2)}, u32[]{:S(2)}) %collective-permute-start.7) | collective-permute-done | bytes 8224 | tf_op jit(solution)/shard_map/ppermute | solution.py:34
  139.7 1.2 collective-permute-done.8
  140.9 0.6 pad_maximum_fusion.1.w_ref
  141.5 3.4 %all-to-all-done.4 = f32[8,32,256]{2,1,0:T(8,128)S(1)} async-done(((f32[8,32,256]{2,1,0:T(8,128)}), f32[8,32,256]{2,1,0:T(8,128)S(1)}, u32[]{:S(2)}, u32[]{:S(2)}) %all-to-all-start.4) | async-done | bytes 262176 | tf_op jit(solution)/shard_map/all_to_all | solution.py:26
  145.6 8.1 %base.1.base_ref = f32[2000,512]{1,0:T(8,128)} custom-call(s32[5]{0:T(128)} %copy-done.4, f32[4,8,256]{2,1,0:T(8,128)} %pad_maximum_fusion.1.w_ref, bf16[3072,256]{1,0:T(8,128)(2,1)} %get-tuple-element.17.near_ref.refs_0_.refs_1_, bf16[3072,256]{1,0:T(8,128)(2,1)} %get-tuple-element.17.near_ref.refs_0_.refs_1_, ...), custom_call_target="tpu_custom_call" | custom-call | flops 2097152000 | bytes 8192000 | tf_op jit(solution)/shard_map/base/pallas_call | solution.py:429
  153.7 7.2 %table_grad.1 = bf16[2000,512]{1,0:T(8,128)(2,1)} custom-call(s32[5]{0:T(128)} %copy-done.4, bf16[8,400,256]{2,1,0:T(8,128)(2,1)} %copy-done.6, f32[2000,512]{1,0:T(8,128)} %base.1.base_ref), custom_call_target="tpu_custom_call" | custom-call | flops 1048576000 | bytes 6144000 | tf_op jit(solution)/shard_map/table_grad/pallas_call | solution.py:388
  (42 shorter events, 1.6 us)
Async XLA Ops:
  2.0 17.6 %all-to-all-start = ((bf16[8,32,256]{2,1,0:T(8,128)(2,1)}), bf16[8,32,256]{2,1,0:T(8,128)(2,1)S(1)}, u32[]{:S(2)}, u32[]{:S(2)}) async-start(bf16[8,32,256]{2,1,0:T(8,128)(2,1)} %broadcast_in_dim.6), calls=%async_computation | async-start | bytes 262144 | tf_op jit(solution)/shard_map/all_to_all | solution.py:26
  19.6 6.9 %copy-start.9 = (bf16[64,2048]{1,0:T(8,128)(2,1)S(1)}, bf16[64,2048]{1,0:T(8,128)(2,1)}, u32[]{:S(2)}) copy-start(bf16[64,2048]{1,0:T(8,128)(2,1)} %param.9) | copy-start | bytes 786436
  20.6 43.1 %all-to-all-start.1 = ((bf16[8,256,256]{2,1,0:T(8,128)(2,1)}), bf16[8,256,256]{2,1,0:T(8,128)(2,1)}, u32[]{:S(2)}, u32[]{:S(2)}) async-start(bf16[8,256,256]{2,1,0:T(8,128)(2,1)} %broadcast_in_dim.7), calls=%async_computation.1 | async-start | bytes 2097152 | tf_op jit(solution)/shard_map/all_to_all | solution.py:26
  26.5 15.8 %collective-permute-start.1 = (bf16[72,1024]{1,0:T(8,128)(2,1)S(1)}, bf16[72,1024]{1,0:T(8,128)(2,1)S(1)}, u32[]{:S(2)}, u32[]{:S(2)}) collective-permute-start(bf16[72,1024]{1,0:T(8,128)(2,1)S(1)} %get-tuple-element.29), channel_id=1, source_target_pairs={{0,128},{128,0},{1,129},{129,1},{2,130},{130,2},{3,131},{131,3},{4... | collective-permute-start | bytes 442376 | tf_op jit(solution)/shard_map/ppermute | solution.py:34
  29.4 13.1 %collective-permute-start = (bf16[72,1024]{1,0:T(8,128)(2,1)S(1)}, bf16[72,1024]{1,0:T(8,128)(2,1)S(1)}, u32[]{:S(2)}, u32[]{:S(2)}) collective-permute-start(bf16[72,1024]{1,0:T(8,128)(2,1)S(1)} %get-tuple-element.30.refs_0_), channel_id=1, source_target_pairs={{0,64},{64,0},{1,65},{65,1},{2,66},{66,2},{3,67},{67,3},{4,68},{68... | collective-permute-start | bytes 442376 | tf_op jit(solution)/shard_map/ppermute | solution.py:34
  42.3 1.4 collective-permute-start.2
  42.4 22.1 %copy-start.4 = (s32[5]{0:T(128)}, s32[5]{0:T(128)S(1)}, u32[]{:S(2)}) copy-start(s32[5]{0:T(128)S(1)} %stack.54.where_ref) | copy-start | bytes 64
  44.9 15.0 %copy-start.3 = (bf16[128,256]{1,0:T(8,128)(2,1)}, bf16[128,256]{1,0:T(8,128)(2,1)S(1)}, u32[]{:S(2)}) copy-start(bf16[128,256]{1,0:T(8,128)(2,1)S(1)} %get-tuple-element.18.x0) | copy-start | bytes 196612
  44.9 36.1 %copy-start.2 = (bf16[16,256]{1,0:T(8,128)(2,1)}, bf16[16,256]{1,0:T(8,128)(2,1)S(1)}, u32[]{:S(2)}) copy-start(bf16[16,256]{1,0:T(8,128)(2,1)S(1)} %get-tuple-element.21.refs_2_.refs_4_.c0) | copy-start | bytes 24580
  44.9 14.9 %collective-permute-start.3 = (bf16[528,256]{1,0:T(8,128)(2,1)S(1)}, bf16[528,256]{1,0:T(8,128)(2,1)S(1)}, u32[]{:S(2)}, u32[]{:S(2)}) collective-permute-start(bf16[528,256]{1,0:T(8,128)(2,1)S(1)} %get-tuple-element.19), channel_id=1, source_target_pairs={{0,8},{2,10},{4,12},{6,14},{8,0},{10,2},{12,4},{14,6},{1,9},{3,11}... | collective-permute-start | bytes 811016 | tf_op jit(solution)/shard_map/ppermute | solution.py:43
  59.8 21.2 %copy-start = (bf16[528,256]{1,0:T(8,128)(2,1)}, bf16[528,256]{1,0:T(8,128)(2,1)S(1)}, u32[]{:S(2)}) copy-start(bf16[528,256]{1,0:T(8,128)(2,1)S(1)} %collective-permute-done.3.refs_1_.refs_3_.refs_5_.r1) | copy-start | bytes 811012
  59.8 21.2 %collective-permute-start.4 = (bf16[544,256]{1,0:T(8,128)(2,1)S(1)}, bf16[544,256]{1,0:T(8,128)(2,1)S(1)}, u32[]{:S(2)}, u32[]{:S(2)}) collective-permute-start(bf16[544,256]{1,0:T(8,128)(2,1)S(1)} %join.2), channel_id=1, source_target_pairs={{0,4},{2,6},{4,0},{6,2},{8,12},{10,14},{12,8},{14,10},{1,5},{3,7},... | collective-permute-start | bytes 835592 | tf_op jit(solution)/shard_map/ppermute | solution.py:43
  63.7 44.8 %collective-permute-start.10 = (bf16[8,256,256]{2,1,0:T(8,128)(2,1)}, bf16[8,256,256]{2,1,0:T(8,128)(2,1)}, u32[]{:S(2)}, u32[]{:S(2)}) collective-permute-start(bf16[8,256,256]{2,1,0:T(8,128)(2,1)} %all-to-all-done.1.got_ref), channel_id=1, source_target_pairs={{0,128},{128,0},{1,129},{129,1},{2,130},{130,2},{3,131},{131,3},{4... | collective-permute-start | bytes 3145736 | tf_op jit(solution)/shard_map/ppermute | solution.py:34
  72.3 21.7 %all-to-all-start.2 = ((f32[64,4,256]{2,1,0:T(4,128)}), f32[64,4,256]{2,1,0:T(4,128)S(1)}, u32[]{:S(2)}, u32[]{:S(2)}) async-start(f32[64,4,256]{2,1,0:T(4,128)} %get-tuple-element.16), calls=%async_computation.2 | async-start | bytes 524288 | tf_op jit(solution)/shard_map/all_to_all | solution.py:26
  81.0 13.0 %copy-start.1 = (bf16[544,256]{1,0:T(8,128)(2,1)}, bf16[544,256]{1,0:T(8,128)(2,1)S(1)}, u32[]{:S(2)}) copy-start(bf16[544,256]{1,0:T(8,128)(2,1)S(1)} %collective-permute-done.4.refs_2_.refs_3_.refs_6_.r2) | copy-start | bytes 835588
  81.1 12.9 %collective-permute-start.5 = (bf16[576,256]{1,0:T(8,128)(2,1)S(1)}, bf16[576,256]{1,0:T(8,128)(2,1)S(1)}, u32[]{:S(2)}, u32[]{:S(2)}) collective-permute-start(bf16[576,256]{1,0:T(8,128)(2,1)S(1)} %join.3), channel_id=1, source_target_pairs={{0,2},{2,0},{4,6},{6,4},{8,10},{10,8},{12,14},{14,12},{1,3},{3,1},... | collective-permute-start | bytes 884744 | tf_op jit(solution)/shard_map/ppermute | solution.py:43
  94.0 0.7 copy-start.8
  94.0 0.8 copy-start.7
  102.5 6.0 %copy-start.5 = (bf16[3072,256]{1,0:T(8,128)(2,1)S(1)}, bf16[3072,256]{1,0:T(8,128)(2,1)}, u32[]{:S(2)}) copy-start(bf16[3072,256]{1,0:T(8,128)(2,1)} %get-tuple-element.17.near_ref.refs_0_.refs_1_) | copy-start | bytes 4718596
  102.5 25.0 %all-to-all-start.3 = ((bf16[8,400,256]{2,1,0:T(8,128)(2,1)}), bf16[8,400,256]{2,1,0:T(8,128)(2,1)S(1)}, u32[]{:S(2)}, u32[]{:S(2)}) async-start(bf16[8,400,256]{2,1,0:T(8,128)(2,1)} %get-tuple-element.24), calls=%async_computation.3 | async-start | bytes 3276800 | tf_op jit(solution)/shard_map/all_to_all | solution.py:26
  108.4 37.1 %collective-permute-start.9 = (bf16[3072,256]{1,0:T(8,128)(2,1)S(1)}, bf16[3072,256]{1,0:T(8,128)(2,1)}, u32[]{:S(2)}, u32[]{:S(2)}) collective-permute-start(bf16[3072,256]{1,0:T(8,128)(2,1)S(1)} %copy-done.5), channel_id=1, source_target_pairs={{0,64},{64,0},{1,65},{65,1},{2,66},{66,2},{3,67},{67,3},{4,68},{68... | collective-permute-start | bytes 4718600 | tf_op jit(solution)/shard_map/ppermute | solution.py:34
  116.2 18.3 %copy-start.10 = (f32[8,256]{1,0:T(8,128)S(1)}, f32[8,256]{1,0:T(8,128)}, u32[]{:S(2)}) copy-start(f32[8,256]{1,0:T(8,128)} %get-tuple-element.25) | copy-start | bytes 24580
  116.2 29.4 %collective-permute-start.11 = (bf16[3072,256]{1,0:T(8,128)(2,1)}, bf16[3072,256]{1,0:T(8,128)(2,1)}, u32[]{:S(2)}, u32[]{:S(2)}) collective-permute-start(bf16[3072,256]{1,0:T(8,128)(2,1)} %get-tuple-element.26.refs_4_.refs_5_), channel_id=1, source_target_pairs={{0,64},{64,0},{1,65},{65,1},{2,66},{66,2},{3,67},{67,3},{4,68},{68... | collective-permute-start | bytes 4718600 | tf_op jit(solution)/shard_map/ppermute | solution.py:34
  127.5 26.3 %copy-start.6 = (bf16[8,400,256]{2,1,0:T(8,128)(2,1)}, bf16[8,400,256]{2,1,0:T(8,128)(2,1)S(1)}, u32[]{:S(2)}) copy-start(bf16[8,400,256]{2,1,0:T(8,128)(2,1)S(1)} %all-to-all-done.3.got_ref) | copy-start | bytes 4915204
  128.4 16.5 %all-to-all-start.4 = ((f32[8,32,256]{2,1,0:T(8,128)}), f32[8,32,256]{2,1,0:T(8,128)S(1)}, u32[]{:S(2)}, u32[]{:S(2)}) async-start(f32[8,32,256]{2,1,0:T(8,128)} %bitcast.12), calls=%async_computation.4 | async-start | bytes 524288 | tf_op jit(solution)/shard_map/all_to_all | solution.py:26
  134.5 5.2 %collective-permute-start.7 = (f32[8,256]{1,0:T(8,128)S(1)}, f32[8,256]{1,0:T(8,128)S(1)}, u32[]{:S(2)}, u32[]{:S(2)}) collective-permute-start(f32[8,256]{1,0:T(8,128)S(1)} %copy-done.10), channel_id=1, source_target_pairs={{0,128},{128,0},{1,129},{129,1},{2,130},{130,2},{3,131},{131,3},{4... | collective-permute-start | bytes 24584 | tf_op jit(solution)/shard_map/ppermute | solution.py:34
  137.3 2.4 %collective-permute-start.6 = (f32[8,256]{1,0:T(8,128)S(1)}, f32[8,256]{1,0:T(8,128)S(1)}, u32[]{:S(2)}, u32[]{:S(2)}) collective-permute-start(f32[8,256]{1,0:T(8,128)S(1)} %copy-done.10), channel_id=1, source_target_pairs={{0,64},{64,0},{1,65},{65,1},{2,66},{66,2},{3,67},{67,3},{4,68},{68... | collective-permute-start | bytes 24584 | tf_op jit(solution)/shard_map/ppermute | solution.py:34
  139.7 1.2 collective-permute-start.8

commit v10 on v8

--- a/solution.py
+++ b/solution.py
@@ -17,7 +17,8 @@
 CHUNK = 400
 DEPTH = 3
 PARAMS = pltpu.CompilerParams(vmem_limit_bytes=16 * 1024 * 1024)
-WIDE = pltpu.CompilerParams(vmem_limit_bytes=57 * 1024 * 1024)
+SIDE = pltpu.CompilerParams(vmem_limit_bytes=57 * 1024 * 1024)
+WIDE = pltpu.CompilerParams(vmem_limit_bytes=63 * 1024 * 1024)
 FULL = pltpu.CompilerParams(vmem_limit_bytes=62 * 1024 * 1024)
 
 
@@ -42,23 +43,23 @@
     return lax.ppermute(value, "z", [(i, i ^ bit) for i in range(size)])
 
 
-def join_kernel(cuts, *refs):
-    out, at = refs[-1], 0
-    for ref, (first, size) in zip(refs, cuts):
-        out[at : at + size, :] = ref[first : first + size, :]
-        at += size
-
-
-def join_call(*parts):
-    cuts = tuple((first, size) for _, first, size in parts)
-    shape = (sum(size for _, size in cuts), parts[0][0].shape[1])
+def join_kernel(one, middle, r1, c0, *outs):
+    for k, out in enumerate(outs):
+        source, at = ((one, 0), (middle, 0), (middle, 128))[k]
+        out[0:128, :] = source[at : at + 128, :]
+        out[128:256, :] = r1[128 * (k + 1) : 128 * (k + 2), :]
+        out[256:272, :] = c0[...]
+        out[272:288, :] = r1[512:528, :]
+
+
+def join_call(one, middle, r1, c0):
     return pl.pallas_call(
-        functools.partial(join_kernel, cuts),
-        out_shape=jax.ShapeDtypeStruct(shape, BF16),
+        join_kernel,
+        out_shape=[jax.ShapeDtypeStruct((288, 256), BF16)] * 3,
         compiler_params=PARAMS,
         cost_estimate=cost(10**6, 2**19),
         name="join",
-    )(*(array for array, _, _ in parts))
+    )(one, middle, r1, c0)
 
 
 def select_kernel(vocab_rows, where_ref, *refs):
@@ -229,11 +230,11 @@
     )(where, targets, got, table)
 
 
-QUOTA = (0, 4, 2, 6, 1, 5, 3, 7)
+QUOTA = (0, 4, 1, 5, 2, 6, 3, 7)
 
 
 def part_kernel(
-    where_ref, tgt_ref, own_ref, stats_ref, near_ref, x0, r1, r2, r3, c0, table_ref,
+    where_ref, tgt_ref, own_ref, stats_ref, near_ref, x0, r1, p1, p2, p3, c0, table_ref,
     out_ref, loss_ref, w_ref, lhs, tab, buf, sems, out_sems,
 ):
     tokens = tgt_ref.shape[1]
@@ -269,13 +270,13 @@
         residual = e * w[i : i + 1, :] - jnp.where(index == tgt_ref[...], 1.0, 0.0)
         lhs[i * CHUNK : (i + 1) * CHUNK, :] = residual.astype(BF16)
 
-    marks = [c0[...], r1[512:528, :], r2[512:528, :], r2[528:544, :]]
-    marks += [r3[k : k + 16, :] for k in range(512, 576, 16)]
+    marks = [c0[...], r1[512:528, :]]
+    marks += [ref[k : k + 16, :] for ref in (p1, p2, p3) for k in (256, 272)]
     group = lax.broadcasted_iota(I32, (16, tokens), 1) >> 4
     mixed = jnp.zeros((16, tokens), F32)
     for q, mark in zip(QUOTA, marks):
         mixed += jnp.where(group == q, mark.astype(F32), 0.0)
-    pieces = ((x0, 0), (r1, 0), (r2, 0), (r2, 256), (r3, 0), (r3, 128), (r3, 256), (r3, 384))
+    pieces = ((x0, 0), (r1, 0), (p1, 0), (p1, 128), (p2, 0), (p2, 128), (p3, 0), (p3, 128))
     for p in range(plane):
         for i, (ref, at) in enumerate(pieces):
             to = depth + 16 * i
@@ -316,7 +317,7 @@
     shape = (plane, width // plane + 144, tokens)
     return pl.pallas_call(
         part_kernel,
-        in_specs=[pl.BlockSpec(memory_space=pltpu.SMEM), *[whole] * 9, anywhere],
+        in_specs=[pl.BlockSpec(memory_space=pltpu.SMEM), *[whole] * 10, anywhere],
         out_specs=[pl.BlockSpec(memory_space=pltpu.HBM), whole, whole],
         scratch_shapes=[
             pltpu.VMEM((count, tokens), BF16),
@@ -349,7 +350,7 @@
         mark = lax.broadcasted_iota(I32, (128, slots), 0)
         lane = lax.broadcasted_iota(I32, (128, slots), 1)
         i = (lane >> 3) & 7
-        quota = ((i & 1) << 2) | (i & 2) | ((i >> 2) & 1)
+        quota = ((i & 1) << 2) | (i >> 1)
         at = quota * 16 + where_ref[4]
         digit = jnp.where(mark == at, 64.0, jnp.where(mark == at + 8, 1.0, 0.0))
         found = jnp.zeros((16, slots), F32)
@@ -406,7 +407,7 @@
             scratch_shapes=[pltpu.VMEM((512, block), BF16), pltpu.VMEM((8, 512), I32)],
         ),
         out_shape=jax.ShapeDtypeStruct((count, block), BF16),
-        compiler_params=WIDE,
+        compiler_params=SIDE,
         cost_estimate=cost(2 * count * block * 1536, 8 * count * 256 + 2 * count * block),
         name="table_grad",
     )(where, w, got, *operands)
@@ -436,11 +437,8 @@
     packs = (near_rows, swap(near_rows, "c"), far_rows, swap(far_rows, "c"))
     away, middle, one, x0, c0 = select_call(where, packs, vocab_rows)
     r1 = partner(away, 4)
-    r2 = partner(join_call((middle, 0, 256), (r1, 256, 256), (c0, 0, 16), (r1, 512, 16)), 2)
-    r3 = join_call(
-        (one, 0, 128), (r1, 128, 128), (r2, 128, 128), (r2, 384, 128), (c0, 0, 16), (r1, 512, 16), (r2, 512, 32)
-    )
-    r3 = partner(r3, 1)
+    sent = join_call(one, middle, r1, c0)
+    got1, got2, got3 = (partner(value, k + 1) for k, value in enumerate(sent))
 
     mine = hidden.T
     stage = exchange(to_each(mine, nz), "z").reshape(-1, tokens)
@@ -452,7 +450,7 @@
     far, _, _ = logits_call(where, goal, far_stage, table, 1)
     near_sib = swap(near, "c")
     far_sib = swap(far, "c")
-    part, loss, w = part_call(where, goal, own, stats, near, (x0, r1, r2, r3, c0), table)
+    part, loss, w = part_call(where, goal, own, stats, near, (x0, r1, got1, got2, got3, c0), table)
 
     got = exchange(part, PLANE)
     part = jnp.sum(got[:, : width // plane].astype(F32), axis=0).reshape(nz, -1, tokens)

time: 157 us -> 158 us (level)
  blocking collectives: 0 us -> 17.4 us
  waiting for transfers between devices: 65.8 us -> 55.2 us
  starting transfers between devices: 48.3 us -> 40.6 us
    all_to_all x0 -> x1, blocking collectives: none -> 17.4 us  [exchange(): return lax.all_to_all(pieces, axes, 0, 0, tiled=True)]
    all_to_all x5 -> x4, starting transfers between devices: 35 us -> 23.6 us  [exchange(): return lax.all_to_all(pieces, axes, 0, 0, tiled=True)]
    all_to_all x5 -> x4, waiting for transfers between devices: 22.6 us -> 13.6 us  [exchange(): return lax.all_to_all(pieces, axes, 0, 0, tiled=True)]
    ppermute x3 -> x4, starting transfers between devices: 6.33 us -> 9.96 us  [partner(): return lax.ppermute(value, 'z', [(i, i ^ bit) for i in range(size)])]
    ppermute x9, waiting for transfers between devices: 17.8 us -> 15.9 us  [swap(): return lax.ppermute(value, axis, [(0, 1), (1, 0)])]
    ppermute x3 -> x4, waiting for transfers between devices: 25.4 us -> 25.7 us  [partner(): return lax.ppermute(value, 'z', [(i, i ^ bit) for i in range(size)])]
  transfers between devices with their start and end apart: 17 -> 17, of which waited for: 9 -> 8; matrix products, arithmetic and copies ran while one was open for 2% -> 3% of each run, Pallas kernels for 16% -> 16%
where the time goes in v10:
time: 158 us; the launch traced here: 155 us
  waiting for transfers between devices  55.2 us (35%)
  starting transfers between devices  40.6 us (26%)
  Pallas kernels  33.6 us (21%)
  blocking collectives  17.4 us (11%)
  local copies, waits for them, and re-layouts  4.4 us (3%)
  other arithmetic  3.36 us (2%)
    ppermute x4, waiting for transfers between devices, partner(): return lax.ppermute(value, 'z', [(i, i ^ bit) for i in range(size)])  25.7 us
    all_to_all x4, starting transfers between devices, exchange(): return lax.all_to_all(pieces, axes, 0, 0, tiled=True)  23.6 us
    all_to_all x1, blocking collectives, exchange(): return lax.all_to_all(pieces, axes, 0, 0, tiled=True)  17.4 us
    ppermute x9, waiting for transfers between devices, swap(): return lax.ppermute(value, axis, [(0, 1), (1, 0)])  15.9 us
    pallas_call x2, Pallas kernels, logits_call(): pl.pallas_call(logits_kernel, in_specs=[pl.BlockSpec(memory_space=pltpu.S...  15.6 us
    all_to_all x4, waiting for transfers between devices, exchange(): return lax.all_to_all(pieces, axes, 0, 0, tiled=True)  13.6 us
    ppermute x4, starting transfers between devices, partner(): return lax.ppermute(value, 'z', [(i, i ^ bit) for i in range(size)])  9.96 us
    pallas_call x1, Pallas kernels, table_call(): pl.pallas_call(table_kernel, grid_spec=pltpu.PrefetchScalarGridSpec(num_s...  9.1 us
  transfers between devices with their start and end apart: 17, of which 8 were waited for; matrix products, arithmetic and copies ran while one was open for 3% of the time, Pallas kernels for 16%

profile of v10, /device:TPU:8, one launch (start us, length us, event | category | flops | bytes accessed | tf_op | source)
XLA Modules:
  0.0 155.3 jit_solution(13892156185938614901)
XLA Ops:
  0.6 0.7 broadcast_in_dim.6
  1.4 17.4 %all_to_all.25 = bf16[8,32,256]{2,1,0:T(8,128)(2,1)S(1)} all-to-all(bf16[8,32,256]{2,1,0:T(8,128)(2,1)S(1)} %broadcast_in_dim.6), channel_id=1, replica_groups=mesh['xh'=2,'c'=2,'y'=4,'z'=8,'xl'=2] {'z'}, dimensions={0} | all-to-all | bytes 262144 | tf_op jit(solution)/shard_map/all_to_all | solution.py:26
  18.7 1.0 broadcast_in_dim.7
  19.8 5.8 %all-to-all-start.1 = ((bf16[8,256,256]{2,1,0:T(8,128)(2,1)}), bf16[8,256,256]{2,1,0:T(8,128)(2,1)}, u32[]{:S(2)}, u32[]{:S(2)}) async-start(bf16[8,256,256]{2,1,0:T(8,128)(2,1)} %broadcast_in_dim.7), calls=%async_computation.1 | async-start | bytes 2097152 | tf_op jit(solution)/shard_map/all_to_all | solution.py:26
  25.7 2.8 %collective-permute-start.1 = (bf16[72,1024]{1,0:T(8,128)(2,1)S(1)}, bf16[72,1024]{1,0:T(8,128)(2,1)S(1)}, u32[]{:S(2)}, u32[]{:S(2)}) collective-permute-start(bf16[72,1024]{1,0:T(8,128)(2,1)S(1)} %get-tuple-element.35), channel_id=1, source_target_pairs={{0,128},{128,0},{1,129},{129,1},{2,130},{130,2},{3,131},{131,3},{4... | collective-permute-start | bytes 442376 | tf_op jit(solution)/shard_map/ppermute | solution.py:34
  28.5 0.7 stack.54.where_ref
  29.2 12.3 %collective-permute-done.1.refs_2_ = bf16[72,1024]{1,0:T(8,128)(2,1)S(1)} collective-permute-done((bf16[72,1024]{1,0:T(8,128)(2,1)S(1)}, bf16[72,1024]{1,0:T(8,128)(2,1)S(1)}, u32[]{:S(2)}, u32[]{:S(2)}) %collective-permute-start.1) | collective-permute-done | bytes 147488 | tf_op jit(solution)/shard_map/ppermute | solution.py:34
  41.5 0.8 collective-permute-start.11
  42.3 7.9 %logits.2 = (bf16[3072,256]{1,0:T(8,128)(2,1)}, f32[64,4,256]{2,1,0:T(4,128)}, f32[8,256]{1,0:T(8,128)}) custom-call(s32[5]{0:T(128)} %stack.54.where_ref, s32[1,256]{1,0:T(1,128)} %bitcast.26, bf16[8,256,256]{2,1,0:T(8,128)(2,1)} %all-to-all-done.1.got_ref, bf16[2000,2048]{1,0:T(8,128)(2,1)} %table_ref.5), custom_call_target="tpu_custom_call" | custom-call | flops 2097152000 | bytes 11337728 | tf_op jit(solution)/shard_map/logits/pallas_call | solution.py:211
  50.2 7.0 %all-to-all-start.2 = ((f32[64,4,256]{2,1,0:T(4,128)}), f32[64,4,256]{2,1,0:T(4,128)S(1)}, u32[]{:S(2)}, u32[]{:S(2)}) async-start(f32[64,4,256]{2,1,0:T(4,128)} %get-tuple-element.19), calls=%async_computation.2 | async-start | bytes 524288 | tf_op jit(solution)/shard_map/all_to_all | solution.py:26
  57.2 1.2 select.28
  58.4 5.5 %collective-permute-start.3 = (bf16[528,256]{1,0:T(8,128)(2,1)S(1)}, bf16[528,256]{1,0:T(8,128)(2,1)S(1)}, u32[]{:S(2)}, u32[]{:S(2)}) collective-permute-start(bf16[528,256]{1,0:T(8,128)(2,1)S(1)} %get-tuple-element.22), channel_id=1, source_target_pairs={{0,8},{2,10},{4,12},{6,14},{8,0},{10,2},{12,4},{14,6},{1,9},{3,11}... | collective-permute-start | bytes 811016 | tf_op jit(solution)/shard_map/ppermute | solution.py:43
  63.9 16.4 %collective-permute-done.3.r1 = bf16[528,256]{1,0:T(8,128)(2,1)S(1)} collective-permute-done((bf16[528,256]{1,0:T(8,128)(2,1)S(1)}, bf16[528,256]{1,0:T(8,128)(2,1)S(1)}, u32[]{:S(2)}, u32[]{:S(2)}) %collective-permute-start.3) | collective-permute-done | bytes 270368 | tf_op jit(solution)/shard_map/ppermute | solution.py:43
  80.9 3.9 %collective-permute-start.6 = (bf16[288,256]{1,0:T(8,128)(2,1)S(1)}, bf16[288,256]{1,0:T(8,128)(2,1)S(1)}, u32[]{:S(2)}, u32[]{:S(2)}) collective-permute-start(bf16[288,256]{1,0:T(8,128)(2,1)S(1)} %get-tuple-element.28), channel_id=1, source_target_pairs={{0,6},{2,4},{4,2},{6,0},{8,14},{10,12},{12,10},{14,8},{1,7},{3,5},... | collective-permute-start | bytes 442376 | tf_op jit(solution)/shard_map/ppermute | solution.py:43
  84.7 2.3 %collective-permute-done.4.p1 = bf16[288,256]{1,0:T(8,128)(2,1)S(1)} collective-permute-done((bf16[288,256]{1,0:T(8,128)(2,1)S(1)}, bf16[288,256]{1,0:T(8,128)(2,1)S(1)}, u32[]{:S(2)}, u32[]{:S(2)}) %collective-permute-start.4) | collective-permute-done | bytes 147488 | tf_op jit(solution)/shard_map/ppermute | solution.py:43
  87.0 7.1 %collective-permute-done.5.p2 = bf16[288,256]{1,0:T(8,128)(2,1)S(1)} collective-permute-done((bf16[288,256]{1,0:T(8,128)(2,1)S(1)}, bf16[288,256]{1,0:T(8,128)(2,1)S(1)}, u32[]{:S(2)}, u32[]{:S(2)}) %collective-permute-start.5) | collective-permute-done | bytes 147488 | tf_op jit(solution)/shard_map/ppermute | solution.py:43
  94.1 0.6 copy-done.8
  94.9 7.8 %part.1 = (bf16[8,400,256]{2,1,0:T(8,128)(2,1)}, f32[1,256]{1,0:T(1,128)}, f32[8,256]{1,0:T(8,128)}) custom-call(s32[5]{0:T(128)} %stack.54.where_ref, s32[1,256]{1,0:T(1,128)} %bitcast.27, f32[8,256]{1,0:T(8,128)} %get-tuple-element.18.own_ref, f32[64,4,256]{2,1,0:T(4,128)} %copy-done.5, bf16[3072,256]{1,0:T(8,128)(2,1)} %get-tuple-element.20.near_ref.refs_0_.refs_1_, ...), custom_call_target="tpu_custom_call" | custom-call | flops 2097152000 | bytes 9240576 | tf_op jit(solution)/shard_map/part/pallas_call | solution.py:318
  102.6 5.8 %all-to-all-start.3 = ((bf16[8,400,256]{2,1,0:T(8,128)(2,1)}), bf16[8,400,256]{2,1,0:T(8,128)(2,1)}, u32[]{:S(2)}, u32[]{:S(2)}) async-start(bf16[8,400,256]{2,1,0:T(8,128)(2,1)} %get-tuple-element.30), calls=%async_computation.3 | async-start | bytes 3276800 | tf_op jit(solution)/shard_map/all_to_all | solution.py:26
  108.4 7.7 %logits.3 = (bf16[3072,256]{1,0:T(8,128)(2,1)}, f32[1,4,256]{2,1,0:T(4,128)}, f32[8,256]{1,0:T(8,128)}) custom-call(s32[5]{0:T(128)} %stack.54.where_ref, s32[1,256]{1,0:T(1,128)} %bitcast.28, bf16[8,256,256]{2,1,0:T(8,128)(2,1)} %collective-permute-done.11.got_ref, bf16[2000,2048]{1,0:T(8,128)(2,1)} %table_ref.5), custom_call_target="tpu_custom_call" | custom-call | flops 2097152000 | bytes 11337728 | tf_op jit(solution)/shard_map/logits/pallas_call | solution.py:211
  116.2 0.6 collective-permute-start.12
  116.8 10.1 %all-to-all-done.3.got_ref = bf16[8,400,256]{2,1,0:T(8,128)(2,1)} async-done(((bf16[8,400,256]{2,1,0:T(8,128)(2,1)}), bf16[8,400,256]{2,1,0:T(8,128)(2,1)}, u32[]{:S(2)}, u32[]{:S(2)}) %all-to-all-start.3) | async-done | bytes 1638432 | tf_op jit(solution)/shard_map/all_to_all | solution.py:26
  126.9 2.1 %convert_reduce_fusion = f32[256,256]{1,0:T(8,128)} fusion(bf16[8,400,256]{2,1,0:T(8,128)(2,1)} %all-to-all-done.3.got_ref), kind=kLoop, calls=%fused_computation | loop fusion | flops 983040 | bytes 1310720 | tf_op jit(solution)/shard_map/reduce_sum | solution.py:456
  129.0 5.0 %all-to-all-start.4 = ((f32[8,32,256]{2,1,0:T(8,128)}), f32[8,32,256]{2,1,0:T(8,128)S(1)}, u32[]{:S(2)}, u32[]{:S(2)}) async-start(f32[8,32,256]{2,1,0:T(8,128)} %bitcast.12), calls=%async_computation.4 | async-start | bytes 524288 | tf_op jit(solution)/shard_map/all_to_all | solution.py:26
  133.9 2.8 %collective-permute-start.8 = (f32[8,256]{1,0:T(8,128)S(1)}, f32[8,256]{1,0:T(8,128)S(1)}, u32[]{:S(2)}, u32[]{:S(2)}) collective-permute-start(f32[8,256]{1,0:T(8,128)S(1)} %copy-done.10), channel_id=1, source_target_pairs={{0,128},{128,0},{1,129},{129,1},{2,130},{130,2},{3,131},{131,3},{4... | collective-permute-start | bytes 24584 | tf_op jit(solution)/shard_map/ppermute | solution.py:34
  136.8 2.4 %collective-permute-done.8 = f32[8,256]{1,0:T(8,128)S(1)} collective-permute-done((f32[8,256]{1,0:T(8,128)S(1)}, f32[8,256]{1,0:T(8,128)S(1)}, u32[]{:S(2)}, u32[]{:S(2)}) %collective-permute-start.8) | collective-permute-done | bytes 8224 | tf_op jit(solution)/shard_map/ppermute | solution.py:34
  139.2 1.2 collective-permute-done.9
  140.4 0.6 pad_maximum_fusion.1.w_ref
  141.0 3.5 %all-to-all-done.4 = f32[8,32,256]{2,1,0:T(8,128)S(1)} async-done(((f32[8,32,256]{2,1,0:T(8,128)}), f32[8,32,256]{2,1,0:T(8,128)S(1)}, u32[]{:S(2)}, u32[]{:S(2)}) %all-to-all-start.4) | async-done | bytes 262176 | tf_op jit(solution)/shard_map/all_to_all | solution.py:26
  144.4 0.6 reduce_sum.19
  145.0 1.2 copy-done.4
  146.2 9.1 %table_grad.1 = bf16[2000,512]{1,0:T(8,128)(2,1)} custom-call(s32[5]{0:T(128)} %stack.54.where_ref, f32[4,8,256]{2,1,0:T(8,128)} %pad_maximum_fusion.1.w_ref, bf16[8,400,256]{2,1,0:T(8,128)(2,1)} %all-to-all-done.3.got_ref, bf16[3072,256]{1,0:T(8,128)(2,1)} %get-tuple-element.20.near_ref.refs_0_.refs_1_, ...), custom_call_target="tpu_custom_call" | custom-call | flops 3145728000 | bytes 6144000 | tf_op jit(solution)/shard_map/table_grad/pallas_call | solution.py:396
  (43 shorter events, 0.9 us)
Async XLA Ops:
  18.7 6.9 %copy-start.11 = (s32[64]{0:T(128)S(1)}, s32[64]{0:T(128)}, u32[]{:S(2)}) copy-start(s32[64]{0:T(128)} %param.8) | copy-start | bytes 772
  18.7 6.9 %copy-start.6 = (bf16[64,2048]{1,0:T(8,128)(2,1)S(1)}, bf16[64,2048]{1,0:T(8,128)(2,1)}, u32[]{:S(2)}) copy-start(bf16[64,2048]{1,0:T(8,128)(2,1)} %param.9) | copy-start | bytes 786436
  19.8 21.7 %all-to-all-start.1 = ((bf16[8,256,256]{2,1,0:T(8,128)(2,1)}), bf16[8,256,256]{2,1,0:T(8,128)(2,1)}, u32[]{:S(2)}, u32[]{:S(2)}) async-start(bf16[8,256,256]{2,1,0:T(8,128)(2,1)} %broadcast_in_dim.7), calls=%async_computation.1 | async-start | bytes 2097152 | tf_op jit(solution)/shard_map/all_to_all | solution.py:26
  25.7 15.8 %collective-permute-start.1 = (bf16[72,1024]{1,0:T(8,128)(2,1)S(1)}, bf16[72,1024]{1,0:T(8,128)(2,1)S(1)}, u32[]{:S(2)}, u32[]{:S(2)}) collective-permute-start(bf16[72,1024]{1,0:T(8,128)(2,1)S(1)} %get-tuple-element.35), channel_id=1, source_target_pairs={{0,128},{128,0},{1,129},{129,1},{2,130},{130,2},{3,131},{131,3},{4... | collective-permute-start | bytes 442376 | tf_op jit(solution)/shard_map/ppermute | solution.py:34
  28.5 28.6 %collective-permute-start = (bf16[72,1024]{1,0:T(8,128)(2,1)S(1)}, bf16[72,1024]{1,0:T(8,128)(2,1)S(1)}, u32[]{:S(2)}, u32[]{:S(2)}) collective-permute-start(bf16[72,1024]{1,0:T(8,128)(2,1)S(1)} %get-tuple-element.36.refs_0_), channel_id=1, source_target_pairs={{0,64},{64,0},{1,65},{65,1},{2,66},{66,2},{3,67},{67,3},{4,68},{68... | collective-permute-start | bytes 442376 | tf_op jit(solution)/shard_map/ppermute | solution.py:34
  41.5 15.7 %collective-permute-start.2 = (bf16[72,1024]{1,0:T(8,128)(2,1)S(1)}, bf16[72,1024]{1,0:T(8,128)(2,1)S(1)}, u32[]{:S(2)}, u32[]{:S(2)}) collective-permute-start(bf16[72,1024]{1,0:T(8,128)(2,1)S(1)} %collective-permute-done.1.refs_2_), channel_id=1, source_target_pairs={{0,64},{64,0},{1,65},{65,1},{2,66},{66,2},{3,67},{67,3},{4,68},{68... | collective-permute-start | bytes 442376 | tf_op jit(solution)/shard_map/ppermute | solution.py:34
  41.5 66.9 %collective-permute-start.11 = (bf16[8,256,256]{2,1,0:T(8,128)(2,1)}, bf16[8,256,256]{2,1,0:T(8,128)(2,1)}, u32[]{:S(2)}, u32[]{:S(2)}) collective-permute-start(bf16[8,256,256]{2,1,0:T(8,128)(2,1)} %all-to-all-done.1.got_ref), channel_id=1, source_target_pairs={{0,128},{128,0},{1,129},{129,1},{2,130},{130,2},{3,131},{131,3},{4... | collective-permute-start | bytes 3145736 | tf_op jit(solution)/shard_map/ppermute | solution.py:34
  42.3 14.9 %copy-start.3 = (s32[5]{0:T(128)S(1)}, s32[5]{0:T(128)}, u32[]{:S(2)}) copy-start(s32[5]{0:T(128)} %stack.54.where_ref) | copy-start | bytes 64
  50.2 43.9 %all-to-all-start.2 = ((f32[64,4,256]{2,1,0:T(4,128)}), f32[64,4,256]{2,1,0:T(4,128)S(1)}, u32[]{:S(2)}, u32[]{:S(2)}) async-start(f32[64,4,256]{2,1,0:T(4,128)} %get-tuple-element.19), calls=%async_computation.2 | async-start | bytes 524288 | tf_op jit(solution)/shard_map/all_to_all | solution.py:26
  58.4 21.9 %copy-start.1 = (bf16[128,256]{1,0:T(8,128)(2,1)}, bf16[128,256]{1,0:T(8,128)(2,1)S(1)}, u32[]{:S(2)}) copy-start(bf16[128,256]{1,0:T(8,128)(2,1)S(1)} %get-tuple-element.21.x0) | copy-start | bytes 196612
  58.4 35.7 %copy-start.2 = (bf16[16,256]{1,0:T(8,128)(2,1)}, bf16[16,256]{1,0:T(8,128)(2,1)S(1)}, u32[]{:S(2)}) copy-start(bf16[16,256]{1,0:T(8,128)(2,1)S(1)} %get-tuple-element.25.c0) | copy-start | bytes 24580
  58.4 21.8 %collective-permute-start.3 = (bf16[528,256]{1,0:T(8,128)(2,1)S(1)}, bf16[528,256]{1,0:T(8,128)(2,1)S(1)}, u32[]{:S(2)}, u32[]{:S(2)}) collective-permute-start(bf16[528,256]{1,0:T(8,128)(2,1)S(1)} %get-tuple-element.22), channel_id=1, source_target_pairs={{0,8},{2,10},{4,12},{6,14},{8,0},{10,2},{12,4},{14,6},{1,9},{3,11}... | collective-permute-start | bytes 811016 | tf_op jit(solution)/shard_map/ppermute | solution.py:43
  80.2 13.9 %copy-start = (bf16[528,256]{1,0:T(8,128)(2,1)}, bf16[528,256]{1,0:T(8,128)(2,1)S(1)}, u32[]{:S(2)}) copy-start(bf16[528,256]{1,0:T(8,128)(2,1)S(1)} %collective-permute-done.3.r1) | copy-start | bytes 811012
  80.3 6.7 %collective-permute-start.4 = (bf16[288,256]{1,0:T(8,128)(2,1)S(1)}, bf16[288,256]{1,0:T(8,128)(2,1)S(1)}, u32[]{:S(2)}, u32[]{:S(2)}) collective-permute-start(bf16[288,256]{1,0:T(8,128)(2,1)S(1)} %get-tuple-element.26), channel_id=1, source_target_pairs={{0,2},{2,0},{4,6},{6,4},{8,10},{10,8},{12,14},{14,12},{1,3},{3,1},... | collective-permute-start | bytes 442376 | tf_op jit(solution)/shard_map/ppermute | solution.py:43
  80.9 13.2 %collective-permute-start.5 = (bf16[288,256]{1,0:T(8,128)(2,1)S(1)}, bf16[288,256]{1,0:T(8,128)(2,1)S(1)}, u32[]{:S(2)}, u32[]{:S(2)}) collective-permute-start(bf16[288,256]{1,0:T(8,128)(2,1)S(1)} %get-tuple-element.27), channel_id=1, source_target_pairs={{0,4},{2,6},{4,0},{6,2},{8,12},{10,14},{12,8},{14,10},{1,5},{3,7},... | collective-permute-start | bytes 442376 | tf_op jit(solution)/shard_map/ppermute | solution.py:43
  80.9 13.2 %collective-permute-start.6 = (bf16[288,256]{1,0:T(8,128)(2,1)S(1)}, bf16[288,256]{1,0:T(8,128)(2,1)S(1)}, u32[]{:S(2)}, u32[]{:S(2)}) collective-permute-start(bf16[288,256]{1,0:T(8,128)(2,1)S(1)} %get-tuple-element.28), channel_id=1, source_target_pairs={{0,6},{2,4},{4,2},{6,0},{8,14},{10,12},{12,10},{14,8},{1,7},{3,5},... | collective-permute-start | bytes 442376 | tf_op jit(solution)/shard_map/ppermute | solution.py:43
  87.0 7.1 %copy-start.7 = (bf16[288,256]{1,0:T(8,128)(2,1)}, bf16[288,256]{1,0:T(8,128)(2,1)S(1)}, u32[]{:S(2)}) copy-start(bf16[288,256]{1,0:T(8,128)(2,1)S(1)} %collective-permute-done.4.p1) | copy-start | bytes 442372
  94.1 0.7 copy-start.8
  94.1 0.7 copy-start.9
  94.1 0.8 copy-start.5
  102.6 24.3 %all-to-all-start.3 = ((bf16[8,400,256]{2,1,0:T(8,128)(2,1)}), bf16[8,400,256]{2,1,0:T(8,128)(2,1)}, u32[]{:S(2)}, u32[]{:S(2)}) async-start(bf16[8,400,256]{2,1,0:T(8,128)(2,1)} %get-tuple-element.30), calls=%async_computation.3 | async-start | bytes 3276800 | tf_op jit(solution)/shard_map/all_to_all | solution.py:26
  108.4 36.6 %collective-permute-start.10 = (bf16[3072,256]{1,0:T(8,128)(2,1)}, bf16[3072,256]{1,0:T(8,128)(2,1)}, u32[]{:S(2)}, u32[]{:S(2)}) collective-permute-start(bf16[3072,256]{1,0:T(8,128)(2,1)} %get-tuple-element.20.near_ref.refs_0_.refs_1_), channel_id=1, source_target_pairs={{0,64},{64,0},{1,65},{65,1},{2,66},{66,2},{3,67},{67,3},{4,68},{68... | collective-permute-start | bytes 4718600 | tf_op jit(solution)/shard_map/ppermute | solution.py:34
  116.2 17.8 %copy-start.10 = (f32[8,256]{1,0:T(8,128)S(1)}, f32[8,256]{1,0:T(8,128)}, u32[]{:S(2)}) copy-start(f32[8,256]{1,0:T(8,128)} %get-tuple-element.31) | copy-start | bytes 24580
  116.2 28.9 %collective-permute-start.12 = (bf16[3072,256]{1,0:T(8,128)(2,1)}, bf16[3072,256]{1,0:T(8,128)(2,1)S(1)}, u32[]{:S(2)}, u32[]{:S(2)}) collective-permute-start(bf16[3072,256]{1,0:T(8,128)(2,1)} %get-tuple-element.32.refs_4_.refs_5_), channel_id=1, source_target_pairs={{0,64},{64,0},{1,65},{65,1},{2,66},{66,2},{3,67},{67,3},{4,68},{68... | collective-permute-start | bytes 4718600 | tf_op jit(solution)/shard_map/ppermute | solution.py:34
  129.0 15.4 %all-to-all-start.4 = ((f32[8,32,256]{2,1,0:T(8,128)}), f32[8,32,256]{2,1,0:T(8,128)S(1)}, u32[]{:S(2)}, u32[]{:S(2)}) async-start(f32[8,32,256]{2,1,0:T(8,128)} %bitcast.12), calls=%async_computation.4 | async-start | bytes 524288 | tf_op jit(solution)/shard_map/all_to_all | solution.py:26
  133.9 5.2 %collective-permute-start.8 = (f32[8,256]{1,0:T(8,128)S(1)}, f32[8,256]{1,0:T(8,128)S(1)}, u32[]{:S(2)}, u32[]{:S(2)}) collective-permute-start(f32[8,256]{1,0:T(8,128)S(1)} %copy-done.10), channel_id=1, source_target_pairs={{0,128},{128,0},{1,129},{129,1},{2,130},{130,2},{3,131},{131,3},{4... | collective-permute-start | bytes 24584 | tf_op jit(solution)/shard_map/ppermute | solution.py:34
  136.7 2.4 %collective-permute-start.7 = (f32[8,256]{1,0:T(8,128)S(1)}, f32[8,256]{1,0:T(8,128)S(1)}, u32[]{:S(2)}, u32[]{:S(2)}) collective-permute-start(f32[8,256]{1,0:T(8,128)S(1)} %copy-done.10), channel_id=1, source_target_pairs={{0,64},{64,0},{1,65},{65,1},{2,66},{66,2},{3,67},{67,3},{4,68},{68... | collective-permute-start | bytes 24584 | tf_op jit(solution)/shard_map/ppermute | solution.py:34
  139.2 1.2 collective-permute-start.9
  145.0 1.2 copy-start.4

commit v11 on v10

--- a/solution.py
+++ b/solution.py
@@ -17,7 +17,7 @@
 CHUNK = 400
 DEPTH = 3
 PARAMS = pltpu.CompilerParams(vmem_limit_bytes=16 * 1024 * 1024)
-SIDE = pltpu.CompilerParams(vmem_limit_bytes=57 * 1024 * 1024)
+SIDE = pltpu.CompilerParams(vmem_limit_bytes=16 * 1024 * 1024)
 WIDE = pltpu.CompilerParams(vmem_limit_bytes=63 * 1024 * 1024)
 FULL = pltpu.CompilerParams(vmem_limit_bytes=62 * 1024 * 1024)
 
@@ -457,8 +457,9 @@
     part = jnp.sum(exchange(part, "z"), axis=0)
     hidden_grad = part.astype(BF16).T
 
-    w_far = swap(w, "xh")
-    w_all = jnp.stack([w, swap(w, "c"), w_far, swap(w_far, "c")])
+    w_near = jnp.stack([w, swap(w, "c")])
+    w_far = swap(w_near, "xh")
+    w_all = jnp.concatenate([w_near, w_far], axis=0)
     table_grad = table_call(
         where, w_all, got, (near, near_sib, far, far_sib), vocab_rows
     )

time: 158 us -> 156 us (0.987)
    ppermute x9 -> x8, waiting for transfers between devices: 15.9 us -> 16 us  [swap(): return lax.ppermute(value, axis, [(0, 1), (1, 0)])]
    ppermute x9 -> x8, starting transfers between devices: 7.03 us -> 7.03 us  [swap(): return lax.ppermute(value, axis, [(0, 1), (1, 0)])]
  transfers between devices with their start and end apart: 17 -> 16, of which waited for: 8 -> 8; matrix products, arithmetic and copies ran while one was open for 3% -> 2% of each run, Pallas kernels for 16% -> 16%
where the time goes in v11:
time: 156 us; the launch traced here: 153 us
  waiting for transfers between devices  55.8 us (36%)
  starting transfers between devices  40.6 us (26%)
  Pallas kernels  32.8 us (21%)
  blocking collectives  17.4 us (11%)
  local copies, waits for them, and re-layouts  3.2 us (2%)
  other arithmetic  2.76 us (2%)
    ppermute x4, waiting for transfers between devices, partner(): return lax.ppermute(value, 'z', [(i, i ^ bit) for i in range(size)])  25.7 us
    all_to_all x4, starting transfers between devices, exchange(): return lax.all_to_all(pieces, axes, 0, 0, tiled=True)  23.6 us
    all_to_all x1, blocking collectives, exchange(): return lax.all_to_all(pieces, axes, 0, 0, tiled=True)  17.4 us
    ppermute x8, waiting for transfers between devices, swap(): return lax.ppermute(value, axis, [(0, 1), (1, 0)])  16 us
    pallas_call x2, Pallas kernels, logits_call(): pl.pallas_call(logits_kernel, in_specs=[pl.BlockSpec(memory_space=pltpu.S...  15.6 us
    all_to_all x4, waiting for transfers between devices, exchange(): return lax.all_to_all(pieces, axes, 0, 0, tiled=True)  14.1 us
    ppermute x4, starting transfers between devices, partner(): return lax.ppermute(value, 'z', [(i, i ^ bit) for i in range(size)])  9.96 us
    pallas_call x1, Pallas kernels, table_call(): pl.pallas_call(table_kernel, grid_spec=pltpu.PrefetchScalarGridSpec(num_s...  8.32 us
  transfers between devices with their start and end apart: 16, of which 8 were waited for; matrix products, arithmetic and copies ran while one was open for 2% of the time, Pallas kernels for 16%

profile of v11, /device:TPU:8, one launch (start us, length us, event | category | flops | bytes accessed | tf_op | source)
XLA Modules:
  0.0 153.4 jit_solution(15937397924378116698)
XLA Ops:
  0.6 0.7 broadcast_in_dim.6
  1.4 17.4 %all_to_all.25 = bf16[8,32,256]{2,1,0:T(8,128)(2,1)S(1)} all-to-all(bf16[8,32,256]{2,1,0:T(8,128)(2,1)S(1)} %broadcast_in_dim.6), channel_id=1, replica_groups=mesh['xh'=2,'c'=2,'y'=4,'z'=8,'xl'=2] {'z'}, dimensions={0} | all-to-all | bytes 262144 | tf_op jit(solution)/shard_map/all_to_all | solution.py:26
  18.7 1.0 broadcast_in_dim.7
  19.8 5.8 %all-to-all-start.1 = ((bf16[8,256,256]{2,1,0:T(8,128)(2,1)}), bf16[8,256,256]{2,1,0:T(8,128)(2,1)}, u32[]{:S(2)}, u32[]{:S(2)}) async-start(bf16[8,256,256]{2,1,0:T(8,128)(2,1)} %broadcast_in_dim.7), calls=%async_computation.1 | async-start | bytes 2097152 | tf_op jit(solution)/shard_map/all_to_all | solution.py:26
  25.7 2.8 %collective-permute-start.1 = (bf16[72,1024]{1,0:T(8,128)(2,1)S(1)}, bf16[72,1024]{1,0:T(8,128)(2,1)S(1)}, u32[]{:S(2)}, u32[]{:S(2)}) collective-permute-start(bf16[72,1024]{1,0:T(8,128)(2,1)S(1)} %get-tuple-element.35), channel_id=1, source_target_pairs={{0,128},{128,0},{1,129},{129,1},{2,130},{130,2},{3,131},{131,3},{4... | collective-permute-start | bytes 442376 | tf_op jit(solution)/shard_map/ppermute | solution.py:34
  28.5 0.6 stack.48.where_ref
  29.2 12.3 %collective-permute-done.1.refs_2_ = bf16[72,1024]{1,0:T(8,128)(2,1)S(1)} collective-permute-done((bf16[72,1024]{1,0:T(8,128)(2,1)S(1)}, bf16[72,1024]{1,0:T(8,128)(2,1)S(1)}, u32[]{:S(2)}, u32[]{:S(2)}) %collective-permute-start.1) | collective-permute-done | bytes 147488 | tf_op jit(solution)/shard_map/ppermute | solution.py:34
  41.5 0.8 collective-permute-start.10
  42.3 7.9 %logits.2 = (bf16[3072,256]{1,0:T(8,128)(2,1)}, f32[64,4,256]{2,1,0:T(4,128)}, f32[8,256]{1,0:T(8,128)}) custom-call(s32[5]{0:T(128)} %stack.48.where_ref, s32[1,256]{1,0:T(1,128)} %bitcast.28, bf16[8,256,256]{2,1,0:T(8,128)(2,1)} %all-to-all-done.1.got_ref, bf16[2000,2048]{1,0:T(8,128)(2,1)} %table_ref.5), custom_call_target="tpu_custom_call" | custom-call | flops 2097152000 | bytes 11337728 | tf_op jit(solution)/shard_map/logits/pallas_call | solution.py:211
  50.2 7.0 %all-to-all-start.2 = ((f32[64,4,256]{2,1,0:T(4,128)}), f32[64,4,256]{2,1,0:T(4,128)S(1)}, u32[]{:S(2)}, u32[]{:S(2)}) async-start(f32[64,4,256]{2,1,0:T(4,128)} %get-tuple-element.19), calls=%async_computation.2 | async-start | bytes 524288 | tf_op jit(solution)/shard_map/all_to_all | solution.py:26
  57.2 1.2 select.28
  58.4 5.5 %collective-permute-start.3 = (bf16[528,256]{1,0:T(8,128)(2,1)S(1)}, bf16[528,256]{1,0:T(8,128)(2,1)S(1)}, u32[]{:S(2)}, u32[]{:S(2)}) collective-permute-start(bf16[528,256]{1,0:T(8,128)(2,1)S(1)} %get-tuple-element.22), channel_id=1, source_target_pairs={{0,8},{2,10},{4,12},{6,14},{8,0},{10,2},{12,4},{14,6},{1,9},{3,11}... | collective-permute-start | bytes 811016 | tf_op jit(solution)/shard_map/ppermute | solution.py:43
  63.9 16.4 %collective-permute-done.3.r1 = bf16[528,256]{1,0:T(8,128)(2,1)S(1)} collective-permute-done((bf16[528,256]{1,0:T(8,128)(2,1)S(1)}, bf16[528,256]{1,0:T(8,128)(2,1)S(1)}, u32[]{:S(2)}, u32[]{:S(2)}) %collective-permute-start.3) | collective-permute-done | bytes 270368 | tf_op jit(solution)/shard_map/ppermute | solution.py:43
  80.3 0.6 collective-permute-start.4
  80.9 3.9 %collective-permute-start.6 = (bf16[288,256]{1,0:T(8,128)(2,1)S(1)}, bf16[288,256]{1,0:T(8,128)(2,1)S(1)}, u32[]{:S(2)}, u32[]{:S(2)}) collective-permute-start(bf16[288,256]{1,0:T(8,128)(2,1)S(1)} %get-tuple-element.28), channel_id=1, source_target_pairs={{0,6},{2,4},{4,2},{6,0},{8,14},{10,12},{12,10},{14,8},{1,7},{3,5},... | collective-permute-start | bytes 442376 | tf_op jit(solution)/shard_map/ppermute | solution.py:43
  84.7 2.3 %collective-permute-done.4.p1 = bf16[288,256]{1,0:T(8,128)(2,1)S(1)} collective-permute-done((bf16[288,256]{1,0:T(8,128)(2,1)S(1)}, bf16[288,256]{1,0:T(8,128)(2,1)S(1)}, u32[]{:S(2)}, u32[]{:S(2)}) %collective-permute-start.4) | collective-permute-done | bytes 147488 | tf_op jit(solution)/shard_map/ppermute | solution.py:43
  87.0 7.1 %collective-permute-done.5.p2 = bf16[288,256]{1,0:T(8,128)(2,1)S(1)} collective-permute-done((bf16[288,256]{1,0:T(8,128)(2,1)S(1)}, bf16[288,256]{1,0:T(8,128)(2,1)S(1)}, u32[]{:S(2)}, u32[]{:S(2)}) %collective-permute-start.5) | collective-permute-done | bytes 147488 | tf_op jit(solution)/shard_map/ppermute | solution.py:43
  94.1 0.6 copy-done.9
  94.9 7.8 %part.1 = (bf16[8,400,256]{2,1,0:T(8,128)(2,1)}, f32[1,256]{1,0:T(1,128)}, f32[8,256]{1,0:T(8,128)}) custom-call(s32[5]{0:T(128)} %stack.48.where_ref, s32[1,256]{1,0:T(1,128)} %bitcast.29, f32[8,256]{1,0:T(8,128)} %get-tuple-element.18.own_ref, f32[64,4,256]{2,1,0:T(4,128)} %copy-done.6, bf16[3072,256]{1,0:T(8,128)(2,1)} %get-tuple-element.20.near_ref.refs_0_.refs_1_, ...), custom_call_target="tpu_custom_call" | custom-call | flops 2097152000 | bytes 9240576 | tf_op jit(solution)/shard_map/part/pallas_call | solution.py:318
  102.6 5.8 %all-to-all-start.3 = ((bf16[8,400,256]{2,1,0:T(8,128)(2,1)}), bf16[8,400,256]{2,1,0:T(8,128)(2,1)}, u32[]{:S(2)}, u32[]{:S(2)}) async-start(bf16[8,400,256]{2,1,0:T(8,128)(2,1)} %get-tuple-element.30), calls=%async_computation.3 | async-start | bytes 3276800 | tf_op jit(solution)/shard_map/all_to_all | solution.py:26
  108.4 7.7 %logits.3 = (bf16[3072,256]{1,0:T(8,128)(2,1)}, f32[1,4,256]{2,1,0:T(4,128)}, f32[8,256]{1,0:T(8,128)}) custom-call(s32[5]{0:T(128)} %stack.48.where_ref, s32[1,256]{1,0:T(1,128)} %bitcast.30, bf16[8,256,256]{2,1,0:T(8,128)(2,1)} %collective-permute-done.10.got_ref, bf16[2000,2048]{1,0:T(8,128)(2,1)} %table_ref.5), custom_call_target="tpu_custom_call" | custom-call | flops 2097152000 | bytes 11337728 | tf_op jit(solution)/shard_map/logits/pallas_call | solution.py:211
  116.2 0.6 collective-permute-start.11
  116.8 10.1 %all-to-all-done.3.got_ref = bf16[8,400,256]{2,1,0:T(8,128)(2,1)} async-done(((bf16[8,400,256]{2,1,0:T(8,128)(2,1)}), bf16[8,400,256]{2,1,0:T(8,128)(2,1)}, u32[]{:S(2)}, u32[]{:S(2)}) %all-to-all-start.3) | async-done | bytes 1638432 | tf_op jit(solution)/shard_map/all_to_all | solution.py:26
  126.9 2.1 %convert_reduce_fusion = f32[256,256]{1,0:T(8,128)} fusion(bf16[8,400,256]{2,1,0:T(8,128)(2,1)} %all-to-all-done.3.got_ref), kind=kLoop, calls=%fused_computation | loop fusion | flops 983040 | bytes 1310720 | tf_op jit(solution)/shard_map/reduce_sum | solution.py:456
  129.0 5.0 %all-to-all-start.4 = ((f32[8,32,256]{2,1,0:T(8,128)}), f32[8,32,256]{2,1,0:T(8,128)S(1)}, u32[]{:S(2)}, u32[]{:S(2)}) async-start(f32[8,32,256]{2,1,0:T(8,128)} %bitcast.12), calls=%async_computation.4 | async-start | bytes 524288 | tf_op jit(solution)/shard_map/all_to_all | solution.py:26
  133.9 0.1 collective-permute-start.7
  134.0 1.2 collective-permute-done.7
  135.2 2.7 %collective-permute-start.8 = (f32[2,8,256]{2,1,0:T(8,128)S(1)}, f32[2,8,256]{2,1,0:T(8,128)S(1)}, u32[]{:S(2)}, u32[]{:S(2)}) collective-permute-start(f32[2,8,256]{2,1,0:T(8,128)S(1)} %pad_maximum_fusion.2), channel_id=1, source_target_pairs={{0,128},{128,0},{1,129},{129,1},{2,130},{130,2},{3,131},{131,3},{4... | collective-permute-start | bytes 49160 | tf_op jit(solution)/shard_map/ppermute | solution.py:34
  137.9 2.5 %collective-permute-done.8 = f32[2,8,256]{2,1,0:T(8,128)S(1)} collective-permute-done((f32[2,8,256]{2,1,0:T(8,128)S(1)}, f32[2,8,256]{2,1,0:T(8,128)S(1)}, u32[]{:S(2)}, u32[]{:S(2)}) %collective-permute-start.8) | collective-permute-done | bytes 16416 | tf_op jit(solution)/shard_map/ppermute | solution.py:34
  140.4 4.0 %all-to-all-done.4 = f32[8,32,256]{2,1,0:T(8,128)S(1)} async-done(((f32[8,32,256]{2,1,0:T(8,128)}), f32[8,32,256]{2,1,0:T(8,128)S(1)}, u32[]{:S(2)}, u32[]{:S(2)}) %all-to-all-start.4) | async-done | bytes 262176 | tf_op jit(solution)/shard_map/all_to_all | solution.py:26
  144.4 0.6 reduce_sum.19
  145.1 8.3 %table_grad.1 = bf16[2000,512]{1,0:T(8,128)(2,1)} custom-call(s32[5]{0:T(128)S(1)} %copy-done.5, f32[4,8,256]{2,1,0:T(8,128)S(1)} %pad_maximum_fusion.1.w_ref, bf16[8,400,256]{2,1,0:T(8,128)(2,1)} %all-to-all-done.3.got_ref, bf16[3072,256]{1,0:T(8,128)(2,1)} %get-tuple-element.20.near_ref.refs_0_.refs_1_, ...), custom_call_target="tpu_custom_call" | custom-call | flops 3145728000 | bytes 6144000 | tf_op jit(solution)/shard_map/table_grad/pallas_call | solution.py:396
  (44 shorter events, 0.3 us)
Async XLA Ops:
  18.7 6.9 %copy-start.12 = (s32[64]{0:T(128)S(1)}, s32[64]{0:T(128)}, u32[]{:S(2)}) copy-start(s32[64]{0:T(128)} %param.8) | copy-start | bytes 772
  18.7 6.9 %copy-start.7 = (bf16[64,2048]{1,0:T(8,128)(2,1)S(1)}, bf16[64,2048]{1,0:T(8,128)(2,1)}, u32[]{:S(2)}) copy-start(bf16[64,2048]{1,0:T(8,128)(2,1)} %param.9) | copy-start | bytes 786436
  19.8 21.7 %all-to-all-start.1 = ((bf16[8,256,256]{2,1,0:T(8,128)(2,1)}), bf16[8,256,256]{2,1,0:T(8,128)(2,1)}, u32[]{:S(2)}, u32[]{:S(2)}) async-start(bf16[8,256,256]{2,1,0:T(8,128)(2,1)} %broadcast_in_dim.7), calls=%async_computation.1 | async-start | bytes 2097152 | tf_op jit(solution)/shard_map/all_to_all | solution.py:26
  25.7 15.8 %collective-permute-start.1 = (bf16[72,1024]{1,0:T(8,128)(2,1)S(1)}, bf16[72,1024]{1,0:T(8,128)(2,1)S(1)}, u32[]{:S(2)}, u32[]{:S(2)}) collective-permute-start(bf16[72,1024]{1,0:T(8,128)(2,1)S(1)} %get-tuple-element.35), channel_id=1, source_target_pairs={{0,128},{128,0},{1,129},{129,1},{2,130},{130,2},{3,131},{131,3},{4... | collective-permute-start | bytes 442376 | tf_op jit(solution)/shard_map/ppermute | solution.py:34
  28.5 28.6 %collective-permute-start = (bf16[72,1024]{1,0:T(8,128)(2,1)S(1)}, bf16[72,1024]{1,0:T(8,128)(2,1)S(1)}, u32[]{:S(2)}, u32[]{:S(2)}) collective-permute-start(bf16[72,1024]{1,0:T(8,128)(2,1)S(1)} %get-tuple-element.36.refs_0_), channel_id=1, source_target_pairs={{0,64},{64,0},{1,65},{65,1},{2,66},{66,2},{3,67},{67,3},{4,68},{68... | collective-permute-start | bytes 442376 | tf_op jit(solution)/shard_map/ppermute | solution.py:34
  41.5 15.7 %collective-permute-start.2 = (bf16[72,1024]{1,0:T(8,128)(2,1)S(1)}, bf16[72,1024]{1,0:T(8,128)(2,1)S(1)}, u32[]{:S(2)}, u32[]{:S(2)}) collective-permute-start(bf16[72,1024]{1,0:T(8,128)(2,1)S(1)} %collective-permute-done.1.refs_2_), channel_id=1, source_target_pairs={{0,64},{64,0},{1,65},{65,1},{2,66},{66,2},{3,67},{67,3},{4,68},{68... | collective-permute-start | bytes 442376 | tf_op jit(solution)/shard_map/ppermute | solution.py:34
  41.5 66.9 %collective-permute-start.10 = (bf16[8,256,256]{2,1,0:T(8,128)(2,1)}, bf16[8,256,256]{2,1,0:T(8,128)(2,1)}, u32[]{:S(2)}, u32[]{:S(2)}) collective-permute-start(bf16[8,256,256]{2,1,0:T(8,128)(2,1)} %all-to-all-done.1.got_ref), channel_id=1, source_target_pairs={{0,128},{128,0},{1,129},{129,1},{2,130},{130,2},{3,131},{131,3},{4... | collective-permute-start | bytes 3145736 | tf_op jit(solution)/shard_map/ppermute | solution.py:34
  42.3 14.9 %copy-start.4 = (s32[5]{0:T(128)S(1)}, s32[5]{0:T(128)}, u32[]{:S(2)}) copy-start(s32[5]{0:T(128)} %stack.48.where_ref) | copy-start | bytes 64
  50.2 43.9 %all-to-all-start.2 = ((f32[64,4,256]{2,1,0:T(4,128)}), f32[64,4,256]{2,1,0:T(4,128)S(1)}, u32[]{:S(2)}, u32[]{:S(2)}) async-start(f32[64,4,256]{2,1,0:T(4,128)} %get-tuple-element.19), calls=%async_computation.2 | async-start | bytes 524288 | tf_op jit(solution)/shard_map/all_to_all | solution.py:26
  58.4 21.9 %copy-start.2 = (bf16[128,256]{1,0:T(8,128)(2,1)}, bf16[128,256]{1,0:T(8,128)(2,1)S(1)}, u32[]{:S(2)}) copy-start(bf16[128,256]{1,0:T(8,128)(2,1)S(1)} %get-tuple-element.21.x0) | copy-start | bytes 196612
  58.4 35.7 %copy-start.3 = (bf16[16,256]{1,0:T(8,128)(2,1)}, bf16[16,256]{1,0:T(8,128)(2,1)S(1)}, u32[]{:S(2)}) copy-start(bf16[16,256]{1,0:T(8,128)(2,1)S(1)} %get-tuple-element.25.c0) | copy-start | bytes 24580
  58.4 21.8 %collective-permute-start.3 = (bf16[528,256]{1,0:T(8,128)(2,1)S(1)}, bf16[528,256]{1,0:T(8,128)(2,1)S(1)}, u32[]{:S(2)}, u32[]{:S(2)}) collective-permute-start(bf16[528,256]{1,0:T(8,128)(2,1)S(1)} %get-tuple-element.22), channel_id=1, source_target_pairs={{0,8},{2,10},{4,12},{6,14},{8,0},{10,2},{12,4},{14,6},{1,9},{3,11}... | collective-permute-start | bytes 811016 | tf_op jit(solution)/shard_map/ppermute | solution.py:43
  80.2 13.9 %copy-start.1 = (bf16[528,256]{1,0:T(8,128)(2,1)}, bf16[528,256]{1,0:T(8,128)(2,1)S(1)}, u32[]{:S(2)}) copy-start(bf16[528,256]{1,0:T(8,128)(2,1)S(1)} %collective-permute-done.3.r1) | copy-start | bytes 811012
  80.3 6.7 %collective-permute-start.4 = (bf16[288,256]{1,0:T(8,128)(2,1)S(1)}, bf16[288,256]{1,0:T(8,128)(2,1)S(1)}, u32[]{:S(2)}, u32[]{:S(2)}) collective-permute-start(bf16[288,256]{1,0:T(8,128)(2,1)S(1)} %get-tuple-element.26), channel_id=1, source_target_pairs={{0,2},{2,0},{4,6},{6,4},{8,10},{10,8},{12,14},{14,12},{1,3},{3,1},... | collective-permute-start | bytes 442376 | tf_op jit(solution)/shard_map/ppermute | solution.py:43
  80.9 13.2 %collective-permute-start.5 = (bf16[288,256]{1,0:T(8,128)(2,1)S(1)}, bf16[288,256]{1,0:T(8,128)(2,1)S(1)}, u32[]{:S(2)}, u32[]{:S(2)}) collective-permute-start(bf16[288,256]{1,0:T(8,128)(2,1)S(1)} %get-tuple-element.27), channel_id=1, source_target_pairs={{0,4},{2,6},{4,0},{6,2},{8,12},{10,14},{12,8},{14,10},{1,5},{3,7},... | collective-permute-start | bytes 442376 | tf_op jit(solution)/shard_map/ppermute | solution.py:43
  80.9 13.2 %collective-permute-start.6 = (bf16[288,256]{1,0:T(8,128)(2,1)S(1)}, bf16[288,256]{1,0:T(8,128)(2,1)S(1)}, u32[]{:S(2)}, u32[]{:S(2)}) collective-permute-start(bf16[288,256]{1,0:T(8,128)(2,1)S(1)} %get-tuple-element.28), channel_id=1, source_target_pairs={{0,6},{2,4},{4,2},{6,0},{8,14},{10,12},{12,10},{14,8},{1,7},{3,5},... | collective-permute-start | bytes 442376 | tf_op jit(solution)/shard_map/ppermute | solution.py:43
  87.0 7.1 %copy-start.8 = (bf16[288,256]{1,0:T(8,128)(2,1)}, bf16[288,256]{1,0:T(8,128)(2,1)S(1)}, u32[]{:S(2)}) copy-start(bf16[288,256]{1,0:T(8,128)(2,1)S(1)} %collective-permute-done.4.p1) | copy-start | bytes 442372
  94.1 0.7 copy-start.9
  94.1 0.7 copy-start.10
  94.1 0.8 copy-start.6
  102.6 24.3 %all-to-all-start.3 = ((bf16[8,400,256]{2,1,0:T(8,128)(2,1)}), bf16[8,400,256]{2,1,0:T(8,128)(2,1)}, u32[]{:S(2)}, u32[]{:S(2)}) async-start(bf16[8,400,256]{2,1,0:T(8,128)(2,1)} %get-tuple-element.30), calls=%async_computation.3 | async-start | bytes 3276800 | tf_op jit(solution)/shard_map/all_to_all | solution.py:26
  108.4 36.6 %collective-permute-start.9 = (bf16[3072,256]{1,0:T(8,128)(2,1)}, bf16[3072,256]{1,0:T(8,128)(2,1)}, u32[]{:S(2)}, u32[]{:S(2)}) collective-permute-start(bf16[3072,256]{1,0:T(8,128)(2,1)} %get-tuple-element.20.near_ref.refs_0_.refs_1_), channel_id=1, source_target_pairs={{0,64},{64,0},{1,65},{65,1},{2,66},{66,2},{3,67},{67,3},{4,68},{68... | collective-permute-start | bytes 4718600 | tf_op jit(solution)/shard_map/ppermute | solution.py:34
  116.2 17.8 %copy-start.11 = (f32[8,256]{1,0:T(8,128)S(1)}, f32[8,256]{1,0:T(8,128)}, u32[]{:S(2)}) copy-start(f32[8,256]{1,0:T(8,128)} %get-tuple-element.31) | copy-start | bytes 24580
  116.2 28.9 %copy-start = (bf16[3072,256]{1,0:T(8,128)(2,1)S(1)}, bf16[3072,256]{1,0:T(8,128)(2,1)}, u32[]{:S(2)}) copy-start(bf16[3072,256]{1,0:T(8,128)(2,1)} %get-tuple-element.32.refs_4_.refs_5_) | copy-start | bytes 4718596
  116.2 28.9 %copy-start.5 = (s32[5]{0:T(128)S(1)}, s32[5]{0:T(128)}, u32[]{:S(2)}) copy-start(s32[5]{0:T(128)} %stack.48.where_ref) | copy-start | bytes 64
  116.2 28.9 %collective-permute-start.11 = (bf16[3072,256]{1,0:T(8,128)(2,1)}, bf16[3072,256]{1,0:T(8,128)(2,1)S(1)}, u32[]{:S(2)}, u32[]{:S(2)}) collective-permute-start(bf16[3072,256]{1,0:T(8,128)(2,1)} %get-tuple-element.32.refs_4_.refs_5_), channel_id=1, source_target_pairs={{0,64},{64,0},{1,65},{65,1},{2,66},{66,2},{3,67},{67,3},{4,68},{68... | collective-permute-start | bytes 4718600 | tf_op jit(solution)/shard_map/ppermute | solution.py:34
  129.0 15.4 %all-to-all-start.4 = ((f32[8,32,256]{2,1,0:T(8,128)}), f32[8,32,256]{2,1,0:T(8,128)S(1)}, u32[]{:S(2)}, u32[]{:S(2)}) async-start(f32[8,32,256]{2,1,0:T(8,128)} %bitcast.12), calls=%async_computation.4 | async-start | bytes 524288 | tf_op jit(solution)/shard_map/all_to_all | solution.py:26
  133.9 1.3 collective-permute-start.7
  135.2 5.2 %collective-permute-start.8 = (f32[2,8,256]{2,1,0:T(8,128)S(1)}, f32[2,8,256]{2,1,0:T(8,128)S(1)}, u32[]{:S(2)}, u32[]{:S(2)}) collective-permute-start(f32[2,8,256]{2,1,0:T(8,128)S(1)} %pad_maximum_fusion.2), channel_id=1, source_target_pairs={{0,128},{128,0},{1,129},{129,1},{2,130},{130,2},{3,131},{131,3},{4... | collective-permute-start | bytes 49160 | tf_op jit(solution)/shard_map/ppermute | solution.py:34
